TPU v7x, 32 devices: a whole 2x2x4 slice. The times are simulated.
32 devices in a mesh: dp: 4 (over x, core), seq: 2 (over y), tensor: 4 (over z).
Axes of the slice: x: 2, y: 2, z: 4, core: 2. Of those that a mesh axis runs over, the one named last changes fastest.
Arguments:
- tokens: bfloat16 [2048, 4096], P(('dp', 'seq')), may hold values from -6 to 6
- seg_ids: int32 [2048], P('dp'), may hold values from 0 to 15, as said below
- gain_attn: bfloat16 [4096], P(('dp', 'seq')), may hold values from 0.5 to 1.5
- w_query: bfloat16 [4096, 4096], P(('dp', 'seq'), 'tensor'), may hold values from -1.5 to 1.5
- kv_weight: bfloat16 [4096, 512], P(('dp', 'seq')), may hold values from -1.5 to 1.5
- w_out: bfloat16 [4096, 4096], P('tensor', ('dp', 'seq')), may hold values from -0.375 to 0.375
- gain_ffn: bfloat16 [4096], P(('dp', 'seq')), may hold values from 0.5 to 1.5
- w_gate: bfloat16 [4096, 12288], P(('dp', 'seq'), 'tensor'), may hold values from -0.09375 to 0.09375
- w_up: bfloat16 [4096, 12288], P(('dp', 'seq'), 'tensor'), may hold values from -0.09375 to 0.09375
- w_down: bfloat16 [12288, 4096], P('tensor', ('dp', 'seq')), may hold values from -0.0546875 to 0.0546875
- d_out: bfloat16 [2048, 4096], P(('dp', 'seq')), may hold values from -6 to 6
Outputs:
- out: bfloat16 [2048, 4096], P(('dp', 'seq'))
- d_tokens: float32 [2048, 4096], P(('dp', 'seq'))
- d_gain_attn: float32 [4096], P(('dp', 'seq'))
- d_w_query: float32 [4096, 4096], P(('dp', 'seq'), 'tensor')
- d_kv_weight: float32 [4096, 512], P(('dp', 'seq'))
- d_w_out: float32 [4096, 4096], P('tensor', ('dp', 'seq'))
- d_gain_ffn: float32 [4096], P(('dp', 'seq'))
- d_w_gate: float32 [4096, 12288], P(('dp', 'seq'), 'tensor')
- d_w_up: float32 [4096, 12288], P(('dp', 'seq'), 'tensor')
- d_w_down: float32 [12288, 4096], P('tensor', ('dp', 'seq'))
Inputs may be any that keep to these rules, and one draw needn't show every extreme that they name: `seg_ids`: within each group of 512 tokens g (from 0) the ids never fall, take values from 4 g to 4 g + 3 and start at 4 g; some group other than the last holds one sequence.
All inputs are finite; a program needn't handle non-finite values.
Results may differ from a plain program's by a relative error of at most 0.02.
Values may be sent and summed in bfloat16 or wider, within the bound.
A program may use at most 384 MiB of HBM per device.

v0:
```python
import math

import jax
import jax.numpy as jnp
from jax import lax
from jax.sharding import PartitionSpec as P

HD = 256


EPS = 1e-06
NEG = -1e30


def place_tables(segs):
    length = segs.shape[0]
    index = jnp.arange(length, dtype=jnp.int32)
    flags = jnp.concatenate([jnp.ones((1,), dtype=bool), segs[1:] != segs[:-1]])
    starts = lax.cummax(jnp.where(flags, index, jnp.zeros_like(index)), axis=0)
    places = index - starts
    half_size = HD // 2
    freqs = jnp.exp(jnp.arange(half_size, dtype=jnp.float32) * (-math.log(10000.0) / half_size))
    angles = places.astype(jnp.float32)[:, None] * freqs[None, :]
    return (places, jnp.cos(angles), jnp.sin(angles))


def rotate(vector, cos_table, sin_table):
    half_size = vector.shape[-1] // 2
    leading = vector[..., :half_size]
    trailing = vector[..., half_size:]
    return jnp.concatenate(
        [leading * cos_table - trailing * sin_table, trailing * cos_table + leading * sin_table],
        axis=-1,
    )


def rotate_back(vector, cos_table, sin_table):
    half_size = vector.shape[-1] // 2
    leading = vector[..., :half_size]
    trailing = vector[..., half_size:]
    return jnp.concatenate(
        [leading * cos_table + trailing * sin_table, trailing * cos_table - leading * sin_table],
        axis=-1,
    )


def matmul(left, right):
    return jnp.dot(left, right, preferred_element_type=jnp.float32)


def matmul_nt(left, right):
    return lax.dot_general(
        left, right, (((1,), (1,)), ((), ())), preferred_element_type=jnp.float32
    )


def matmul_tn(left, right):
    return lax.dot_general(
        left, right, (((0,), (0,)), ((), ())), preferred_element_type=jnp.float32
    )


def gelu_tanh(values):
    return jax.nn.gelu(values, approximate=True)


def norm_back(d_act, normed, rms_val, gain_val):
    scaled = d_act * gain_val
    return rms_val * (scaled - normed * jnp.mean(scaled * normed, axis=-1, keepdims=True))


def shards(
    tokens, seg_ids, gain_attn, w_query, kv_weight, w_out, gain_ffn, w_gate, w_up, w_down, d_out
):
    rows = tokens.shape[0]
    scale_factor = 1.0 / math.sqrt(HD)
    offset = lax.axis_index("seq") * rows
    places, cos_table, sin_table = place_tables(seg_ids)
    own_places = lax.dynamic_slice_in_dim(places, offset, rows, 0)
    own_segs = lax.dynamic_slice_in_dim(seg_ids, offset, rows, 0)
    own_cos = lax.dynamic_slice_in_dim(cos_table, offset, rows, 0)
    own_sin = lax.dynamic_slice_in_dim(sin_table, offset, rows, 0)
    allowed = (own_segs[:, None] == seg_ids[None, :]) & (own_places[:, None] >= places[None, :])
    full_query, full_out, full_kv, full_gain_one = (
        lax.all_gather(w_query, ("dp", "seq"), axis=0, tiled=True),
        lax.all_gather(w_out, ("dp", "seq"), axis=1, tiled=True),
        lax.all_gather(kv_weight, ("dp", "seq"), axis=0, tiled=True),
        lax.all_gather(gain_attn, ("dp", "seq"), axis=0, tiled=True),
    )
    gain_one = full_gain_one.astype(jnp.float32)
    inputs = tokens.astype(jnp.float32)
    rms_one = lax.rsqrt(jnp.mean(inputs * inputs, axis=-1, keepdims=True) + EPS)
    norm_one = inputs * rms_one
    act_one = (norm_one * gain_one).astype(jnp.bfloat16)
    query_pre = matmul(act_one, full_query)
    heads = query_pre.shape[1] // HD
    kv_pre = matmul(act_one, full_kv)
    queries = (
        rotate(query_pre.reshape(rows, heads, HD), own_cos[:, None, :], own_sin[:, None, :])
        * scale_factor
    ).astype(jnp.bfloat16)
    own_kv = jnp.concatenate(
        [rotate(kv_pre[:, :HD], own_cos, own_sin), kv_pre[:, HD:]], axis=1
    ).astype(jnp.bfloat16)
    all_kv = lax.all_gather(own_kv, "seq", axis=0, tiled=True)
    keys = all_kv[:, :HD]
    values_all = all_kv[:, HD:]
    scores = jnp.einsum("rhd,kd->hrk", queries, keys, preferred_element_type=jnp.float32)
    scores = jnp.where(allowed[None], scores, NEG)
    top_score = jnp.max(scores, axis=-1, keepdims=True)
    expd = jnp.exp(scores - top_score)
    total = jnp.sum(expd, axis=-1, keepdims=True)
    log_total = top_score + jnp.log(total)
    probs_low = (expd / total).astype(jnp.bfloat16)
    mixed = (
        jnp.einsum("hrk,kd->rhd", probs_low, values_all, preferred_element_type=jnp.float32)
        .reshape(rows, heads * HD)
        .astype(jnp.bfloat16)
    )
    attn = lax.psum(matmul(mixed, full_out), "tensor")
    resid = inputs + attn
    full_gate, full_up, full_down, full_gain_two = (
        lax.all_gather(w_gate, ("dp", "seq"), axis=0, tiled=True),
        lax.all_gather(w_up, ("dp", "seq"), axis=0, tiled=True),
        lax.all_gather(w_down, ("dp", "seq"), axis=1, tiled=True),
        lax.all_gather(gain_ffn, ("dp", "seq"), axis=0, tiled=True),
    )
    gain_two = full_gain_two.astype(jnp.float32)
    rms_two = lax.rsqrt(jnp.mean(resid * resid, axis=-1, keepdims=True) + EPS)
    norm_two = resid * rms_two
    act_two = (norm_two * gain_two).astype(jnp.bfloat16)
    gate = matmul(act_two, full_gate)
    up_val = matmul(act_two, full_up)
    gelu_val, gelu_pull = jax.vjp(gelu_tanh, gate)
    hidden = (gelu_val * up_val).astype(jnp.bfloat16)
    ffn = lax.psum(matmul(hidden, full_down).astype(jnp.bfloat16), "tensor").astype(jnp.float32)
    out = (resid + ffn).astype(jnp.bfloat16)
    back_gate, back_up, back_down = (
        lax.all_gather(w_gate, ("dp", "seq"), axis=0, tiled=True),
        lax.all_gather(w_up, ("dp", "seq"), axis=0, tiled=True),
        lax.all_gather(w_down, ("dp", "seq"), axis=1, tiled=True),
    )
    d_hidden = matmul_nt(d_out, back_down)
    grad_down = matmul_tn(hidden, d_out)
    d_gate = gelu_pull(d_hidden * up_val)[0].astype(jnp.bfloat16)
    d_up = (d_hidden * gelu_val).astype(jnp.bfloat16)
    grad_gate = matmul_tn(act_two, d_gate)
    grad_up = matmul_tn(act_two, d_up)
    d_act_two = lax.psum(matmul_nt(d_gate, back_gate) + matmul_nt(d_up, back_up), "tensor")
    grad_gain_two = jnp.sum(d_act_two * norm_two, axis=0)
    d_resid = d_out.astype(jnp.float32) + norm_back(d_act_two, norm_two, rms_two, gain_two)
    ffn_grads = (
        lax.psum_scatter(
            grad_gate.astype(jnp.bfloat16), ("dp", "seq"), scatter_dimension=0, tiled=True
        ).astype(jnp.float32),
        lax.psum_scatter(
            grad_up.astype(jnp.bfloat16), ("dp", "seq"), scatter_dimension=0, tiled=True
        ).astype(jnp.float32),
        lax.psum_scatter(
            grad_down.astype(jnp.bfloat16), ("dp", "seq"), scatter_dimension=1, tiled=True
        ).astype(jnp.float32),
        lax.psum_scatter(
            grad_gain_two.astype(jnp.bfloat16), ("dp", "seq"), scatter_dimension=0, tiled=True
        ).astype(jnp.float32),
    )
    back_query, back_out, back_kv = (
        lax.all_gather(w_query, ("dp", "seq"), axis=0, tiled=True),
        lax.all_gather(w_out, ("dp", "seq"), axis=1, tiled=True),
        lax.all_gather(kv_weight, ("dp", "seq"), axis=0, tiled=True),
    )
    d_attn = d_resid.astype(jnp.bfloat16)
    grad_out = matmul_tn(mixed, d_attn)
    d_mixed = matmul_nt(d_attn, back_out).astype(jnp.bfloat16).reshape(rows, heads, HD)
    scores_again = jnp.einsum("rhd,kd->hrk", queries, keys, preferred_element_type=jnp.float32)
    probs = jnp.where(allowed[None], jnp.exp(scores_again - log_total), 0.0)
    d_probs = jnp.einsum("rhd,kd->hrk", d_mixed, values_all, preferred_element_type=jnp.float32)
    delta = jnp.sum(probs * d_probs, axis=-1, keepdims=True)
    d_scores = (probs * (d_probs - delta)).astype(jnp.bfloat16)
    d_queries = (
        jnp.einsum("hrk,kd->rhd", d_scores, keys, preferred_element_type=jnp.float32) * scale_factor
    )
    d_query_pre = (
        rotate_back(d_queries, own_cos[:, None, :], own_sin[:, None, :])
        .reshape(rows, heads * HD)
        .astype(jnp.bfloat16)
    )
    d_keys_part = jnp.einsum("hrk,rhd->kd", d_scores, queries, preferred_element_type=jnp.float32)
    d_values_part = jnp.einsum(
        "hrk,rhd->kd", probs.astype(jnp.bfloat16), d_mixed, preferred_element_type=jnp.float32
    )
    own_kv_grad = lax.psum_scatter(
        jnp.concatenate([d_keys_part, d_values_part], axis=1).astype(jnp.bfloat16),
        "seq",
        scatter_dimension=0,
        tiled=True,
    )
    d_act_query = matmul_nt(d_query_pre, back_query)
    d_act_sum, kv_grad = (
        lax.psum(d_act_query.astype(jnp.bfloat16), "tensor").astype(jnp.float32),
        lax.psum(own_kv_grad, "tensor").astype(jnp.float32),
    )
    d_kv_pre = jnp.concatenate(
        [rotate_back(kv_grad[:, :HD], own_cos, own_sin), kv_grad[:, HD:]], axis=1
    ).astype(jnp.bfloat16)
    d_act_one = d_act_sum + matmul_nt(d_kv_pre, back_kv)
    grad_query = matmul_tn(act_one, d_query_pre)
    grad_kv = matmul_tn(act_one, d_kv_pre)
    grad_gain_one = jnp.sum(d_act_one * norm_one, axis=0)
    d_tokens = d_resid + norm_back(d_act_one, norm_one, rms_one, gain_one)
    attn_grads = (
        lax.psum_scatter(
            grad_query.astype(jnp.bfloat16), ("dp", "seq"), scatter_dimension=0, tiled=True
        ).astype(jnp.float32),
        lax.psum_scatter(
            grad_out.astype(jnp.bfloat16), ("dp", "seq"), scatter_dimension=1, tiled=True
        ).astype(jnp.float32),
        lax.psum_scatter(
            grad_kv.astype(jnp.bfloat16), ("dp", "seq"), scatter_dimension=0, tiled=True
        ).astype(jnp.float32),
        lax.psum_scatter(
            grad_gain_one.astype(jnp.bfloat16), ("dp", "seq"), scatter_dimension=0, tiled=True
        ).astype(jnp.float32),
    )
    return (
        out,
        d_tokens,
        attn_grads[3],
        attn_grads[0],
        attn_grads[2],
        attn_grads[1],
        ffn_grads[3],
        ffn_grads[0],
        ffn_grads[1],
        ffn_grads[2],
    )


def solution(mesh):
    in_specs = (
        P(("dp", "seq"), None),
        P("dp"),
        P(("dp", "seq")),
        P(("dp", "seq"), "tensor"),
        P(("dp", "seq"), None),
        P("tensor", ("dp", "seq")),
        P(("dp", "seq")),
        P(("dp", "seq"), "tensor"),
        P(("dp", "seq"), "tensor"),
        P("tensor", ("dp", "seq")),
        P(("dp", "seq"), None),
    )
    out_specs = (
        P(("dp", "seq"), None),
        P(("dp", "seq"), None),
        P(("dp", "seq")),
        P(("dp", "seq"), "tensor"),
        P(("dp", "seq"), None),
        P("tensor", ("dp", "seq")),
        P(("dp", "seq")),
        P(("dp", "seq"), "tensor"),
        P(("dp", "seq"), "tensor"),
        P("tensor", ("dp", "seq")),
    )
    return jax.shard_map(shards, mesh=mesh, in_specs=in_specs, out_specs=out_specs, check_vma=False)
```

profile of v0, /device:TPU:0, one launch (start us, length us, event | category | flops | bytes accessed | tf_op | source)
XLA Modules:
  0.0 1815.9 jit_solution(10553113912535316646)
XLA Ops:
  10.2 0.8 slice_compare_fusion
  12.5 18.0 all-gather
  31.5 17.9 all-gather.9.cloned.1.call-done
  49.4 3.5 fusion.48
  53.7 10.2 all_gather.35
  63.8 42.2 %all-gather.11.cloned.1.call-done = bf16[4096,1024]{1,0:T(8,128)(2,1)} async-done(((bf16[512,1024]{1,0:T(8,128)(2,1)}), bf16[4096,1024]{1,0:T(8,128)(2,1)}) %all-gather.11.cloned.1.call-update) | async-done | bytes 8388624 | tf_op jit(solution)/shard_map/all_gather | solution.py:85
  106.1 6.8 fusion.46
  113.0 1.0 pad_maximum_fusion
  114.1 1.7 copy.57
  115.8 1.5 fusion.23
  117.7 0.9 copy-done.4
  119.2 1.5 convolution_convert_fusion.9
  120.8 43.1 %all-gather.13.cloned.1.call-done = bf16[1024,4096]{1,0:T(8,128)(2,1)} async-done(((bf16[1024,512]{1,0:T(8,128)(2,1)}), bf16[1024,4096]{1,0:T(8,128)(2,1)}) %all-gather.13.cloned.1.call-update) | async-done | bytes 8388624 | tf_op jit(solution)/shard_map/all_gather | solution.py:86
  163.8 8.0 fusion.51
  173.8 16.6 all-gather.1
  190.5 136.5 %all-reduce.8.cloned.1.call-done = f32[256,4096]{1,0:T(8,128)} async-done(((f32[256,4096]{1,0:T(8,128)}), f32[256,4096]{1,0:T(8,128)}) %all-reduce.8.cloned.1.call-update) | async-done | bytes 4194320 | tf_op jit(solution)/shard_map/psum | solution.py:120
  327.0 2.8 multiply_reduce_fusion.2
  329.8 2.0 copy-done
  331.8 1.9 multiply_convert_fusion
  333.7 119.2 %all-gather.17.cloned.1.call-done = bf16[4096,3072]{1,0:T(8,128)(2,1)} async-done(((bf16[512,3072]{1,0:T(8,128)(2,1)}), bf16[4096,3072]{1,0:T(8,128)(2,1)}) %all-gather.17.cloned.1.call-update) | async-done | bytes 25165840 | tf_op jit(solution)/shard_map/all_gather | solution.py:124
  452.9 13.7 fusion.53
  466.6 113.3 %all-gather.15.cloned.1.call-done = bf16[4096,3072]{1,0:T(8,128)(2,1)} async-done(((bf16[512,3072]{1,0:T(8,128)(2,1)}), bf16[4096,3072]{1,0:T(8,128)(2,1)}) %all-gather.15.cloned.1.call-update) | async-done | bytes 25165840 | tf_op jit(solution)/shard_map/all_gather | solution.py:123
  579.8 13.6 fusion.52
  593.4 118.5 %all-gather.19.cloned.1.call-done = bf16[3072,4096]{1,0:T(8,128)(2,1)} async-done(((bf16[3072,512]{1,0:T(8,128)(2,1)}), bf16[3072,4096]{1,0:T(8,128)(2,1)}) %all-gather.19.cloned.1.call-update) | async-done | bytes 25165840 | tf_op jit(solution)/shard_map/all_gather | solution.py:125
  711.9 17.4 multiply_convert_fusion.1
  729.3 13.4 fusion.54
  742.7 14.7 convolution_add_fusion.1
  757.5 1.3 log_add_fusion
  758.8 13.8 convolution_convert_fusion.7
  772.6 140.0 %all-reduce.10.cloned.1.call-done = f32[256,4096]{1,0:T(8,128)} async-done(((f32[256,4096]{1,0:T(8,128)}), f32[256,4096]{1,0:T(8,128)}) %all-reduce.10.cloned.1.call-update) | async-done | bytes 4194320 | tf_op jit(solution)/shard_map/psum | solution.py:149
  912.6 5.4 multiply_reduce_fusion
  918.5 3.1 multiply_add_fusion
  921.6 2.0 copy-done.3
  923.7 6.5 convolution_convert_fusion.8
  930.2 2.0 copy.83
  932.2 2.3 fusion.28
  937.0 0.8 pad_maximum_fusion.2
  938.1 1.0 add_convert_fusion.1
  939.2 7.1 convolution_convert_fusion.6
  946.3 5.3 reduce-scatter.8.cloned.1.call-done
  951.7 166.4 %all-reduce.12.cloned.1.call-done = (bf16[256,4096]{1,0:T(8,128)(2,1)}, bf16[256,4096]{1,0:T(8,128)(2,1)}, bf16[256,512]{1,0:T(8,128)(2,1)}) async-done(((bf16[256,4096]{1,0:T(8,128)(2,1)}, bf16[256,4096]{1,0:T(8,128)(2,1)}, bf16[256,512]{1,0:T(8,128)(2,1)}), (bf16[256,4096]{1,0:T(8,128)(2,1)}, bf16[256,4096]{1,0:T(8,128)(2,1)}, bf16[256,512]{1,0:T(8,128)(2,1)})) %all-reduce.12.cloned.1.call-update) | async-done | bytes 4456464 | tf_op jit(solution)/shard_map/psum | solution.py:136
  1118.1 0.9 slice.84
  1119.0 1.0 convert_element_type.159
  1120.8 3.5 convolution_convert_fusion.5
  1124.3 1.0 copy-done.9
  1125.3 8.3 convolution_convert_fusion.3
  1133.7 5.8 convolution_convert_fusion.4
  1140.0 13.7 convolution_convert_fusion
  1153.7 13.9 convolution_convert_fusion.1
  1167.7 13.5 convolution_convert_fusion.2
  1183.1 7.2 fusion.9
  1190.3 25.7 %all-reduce.2 = (bf16[4096]{0:T(1024)(128)(2,1)S(1)}, bf16[4096]{0:T(1024)(128)(2,1)S(1)}) all-reduce(bf16[4096]{0:T(1024)(128)(2,1)S(1)} %get-tuple-element.12, bf16[4096]{0:T(1024)(128)(2,1)S(1)} %copy-done.22), channel_id=3, replica_groups=mesh['dp'=4,'seq'=2,'tensor'=4] {'dp','seq'}, use_global_device_ids=true, to_apply=%region_16.17.clone | all-reduce | flops 8192 | bytes 32768
  1216.6 10.6 fusion.8
  1227.2 2.1 convert_element_type.165
  1229.4 20.3 %reduce-scatter.14.cloned.1.call-done = bf16[1024,512]{1,0:T(8,128)(2,1)} async-done(((bf16[1024,4096]{1,0:T(8,128)(2,1)}), bf16[1024,512]{1,0:T(8,128)(2,1)}) %reduce-scatter.14.cloned.1.call-update) | async-done | bytes 1048592 | tf_op jit(solution)/shard_map/reduce_scatter | solution.py:214
  1249.7 2.8 convert_element_type.167
  1252.5 72.2 %reduce-scatter.10.cloned.1.call-done = bf16[512,1024]{1,0:T(8,128)(2,1)} async-done(((bf16[4096,1024]{1,0:T(8,128)(2,1)}), bf16[512,1024]{1,0:T(8,128)(2,1)}) %reduce-scatter.10.cloned.1.call-update) | async-done | bytes 1048592 | tf_op jit(solution)/shard_map/reduce_scatter | solution.py:211
  1324.7 2.8 convert_element_type.163
  1327.4 156.7 %reduce-scatter.20.cloned.1.call-done = bf16[3072,512]{1,0:T(8,128)(2,1)} async-done(((bf16[3072,4096]{1,0:T(8,128)(2,1)}), bf16[3072,512]{1,0:T(8,128)(2,1)}) %reduce-scatter.20.cloned.1.call-update) | async-done | bytes 3145744 | tf_op jit(solution)/shard_map/reduce_scatter | solution.py:159
  1484.2 5.5 convert_element_type.175
  1489.7 154.3 %reduce-scatter.18.cloned.1.call-done = bf16[512,3072]{1,0:T(8,128)(2,1)} async-done(((bf16[4096,3072]{1,0:T(8,128)(2,1)}), bf16[512,3072]{1,0:T(8,128)(2,1)}) %reduce-scatter.18.cloned.1.call-update) | async-done | bytes 3145744 | tf_op jit(solution)/shard_map/reduce_scatter | solution.py:156
  1644.0 5.4 convert_element_type.173
  1649.4 154.4 %reduce-scatter.16.cloned.1.call-done = bf16[512,3072]{1,0:T(8,128)(2,1)} async-done(((bf16[4096,3072]{1,0:T(8,128)(2,1)}), bf16[512,3072]{1,0:T(8,128)(2,1)}) %reduce-scatter.16.cloned.1.call-update) | async-done | bytes 3145744 | tf_op jit(solution)/shard_map/reduce_scatter | solution.py:153
  1803.8 5.4 convert_element_type.171
  (127 shorter events, 15.8 us)
Async XLA Ops:
  7.2 23.9 %copy-start.23 = (s32[512]{0:T(512)S(1)}, s32[512]{0:T(512)}, u32[]{:S(2)}) copy-start(s32[512]{0:T(512)} %param.12) | copy-start | bytes 6148
  7.2 23.4 %copy-start.2 = (bf16[256,4096]{1,0:T(8,128)(2,1)S(1)}, bf16[256,4096]{1,0:T(8,128)(2,1)}, u32[]{:S(2)}) copy-start(bf16[256,4096]{1,0:T(8,128)(2,1)} %param.11) | copy-start | bytes 6291460
  7.2 42.2 %all-gather.9.cloned.1.call-start = ((), (), s32[]{:S(2)}) async-start(), calls=%async_computation.7 | async-start | bytes 4718592 | tf_op jit(solution)/shard_map/all_gather | solution.py:87
  7.9 98.1 %all-gather.11.cloned.1.call-start = ((), (), s32[]{:S(2)}) async-start(), calls=%async_computation.8 | async-start | bytes 9437184 | tf_op jit(solution)/shard_map/all_gather | solution.py:85
  8.7 155.2 %all-gather.13.cloned.1.call-start = ((), (), s32[]{:S(2)}) async-start(), calls=%async_computation.9 | async-start | bytes 9437184 | tf_op jit(solution)/shard_map/all_gather | solution.py:86
  9.4 317.5 %all-reduce.8.cloned.1.call-start = ((), (), s32[]{:S(2)}) async-start(), calls=%async_computation.10 | async-start | bytes 8388608 | tf_op jit(solution)/shard_map/psum | solution.py:120
  30.5 75.5 %copy-start.14 = (f32[8,1,512]{2,1,0:T(1,128)}, f32[8,1,512]{2,1,0:T(1,128)S(1)}, u32[]{:S(2)}) copy-start(f32[8,1,512]{2,1,0:T(1,128)S(1)} %convert_element_type.176) | copy-start | bytes 49156
  31.1 21.7 %copy-start.27 = (f32[256]{0:T(256)}, f32[256]{0:T(256)S(1)}, u32[]{:S(2)}) copy-start(f32[256]{0:T(256)S(1)} %add_rsqrt_fusion.1) | copy-start | bytes 3076
  53.5 59.4 %copy-start.11 = (f32[256,128]{0,1:T(8,128)}, f32[256,128]{0,1:T(8,128)S(1)}, u32[]{:S(2)}) copy-start(f32[256,128]{0,1:T(8,128)S(1)} %copy.54) | copy-start | bytes 393220
  53.6 59.3 %copy-start.13 = (f32[256,128]{0,1:T(8,128)}, f32[256,128]{0,1:T(8,128)S(1)}, u32[]{:S(2)}) copy-start(f32[256,128]{0,1:T(8,128)S(1)} %copy.56) | copy-start | bytes 393220
  115.8 3.5 copy-start.7
  117.3 1.3 copy-start.4
  117.3 1.3 copy-start.20
  118.6 0.6 copy-start.24
  171.8 281.1 %all-gather.17.cloned.1.call-start = ((), (), s32[]{:S(2)}) async-start(), calls=%async_computation.12 | async-start | bytes 28311552 | tf_op jit(solution)/shard_map/all_gather | solution.py:124
  172.4 1.4 copy-start.29
  172.4 407.4 %all-gather.15.cloned.1.call-start = ((), (), s32[]{:S(2)}) async-start(), calls=%async_computation.11 | async-start | bytes 28311552 | tf_op jit(solution)/shard_map/all_gather | solution.py:123
  173.0 538.9 %all-gather.19.cloned.1.call-start = ((), (), s32[]{:S(2)}) async-start(), calls=%async_computation.13 | async-start | bytes 28311552 | tf_op jit(solution)/shard_map/all_gather | solution.py:125
  173.8 738.8 %all-reduce.10.cloned.1.call-start = ((), (), s32[]{:S(2)}) async-start(), calls=%async_computation.14 | async-start | bytes 8388608 | tf_op jit(solution)/shard_map/psum | solution.py:149
  329.8 2.0 copy-start
  329.8 2.0 copy-start.25
  757.4 194.2 %reduce-scatter.8.cloned.1.call-start = ((), (), s32[]{:S(2)}) async-start(), calls=%async_computation.15 | async-start | bytes 786432 | tf_op jit(solution)/shard_map/reduce_scatter | solution.py:191
  912.6 5.4 copy-start.1
  912.6 5.9 copy-start.6
  912.6 5.9 copy-start.26
  921.6 2.0 copy-start.3
  923.6 8.6 copy-start.21
  932.2 2.4 copy-start.5
  932.2 2.5 copy-start.8
  932.2 2.6 copy-start.10
  936.0 2.1 copy-start.12
  937.8 180.3 %all-reduce.12.cloned.1.call-start = ((), (), s32[]{:S(2)}) async-start(), calls=%async_computation.22 | async-start | bytes 8912896 | tf_op jit(solution)/shard_map/psum | solution.py:136
  946.3 174.5 %copy-start.15 = (f32[8,1,512]{2,1,0:T(1,128)S(1)}, f32[8,1,512]{2,1,0:T(1,128)}, u32[]{:S(2)}) copy-start(f32[8,1,512]{2,1,0:T(1,128)} %copy-done.14) | copy-start | bytes 49156
  946.3 174.5 %copy-start.28 = (f32[256]{0:T(256)S(1)}, f32[256]{0:T(256)}, u32[]{:S(2)}) copy-start(f32[256]{0:T(256)} %copy-done.27) | copy-start | bytes 3076
  951.6 275.6 %reduce-scatter.12.cloned.1.call-start = ((), (), s32[]{:S(2)}) async-start(), calls=%async_computation.17 | async-start | bytes 4718592 | tf_op jit(solution)/shard_map/reduce_scatter | solution.py:217
  1119.0 1.1 copy-start.16
  1120.1 0.6 copy-start.18
  1124.2 1.0 copy-start.9
  1124.3 125.4 %reduce-scatter.14.cloned.1.call-start = ((), (), s32[]{:S(2)}) async-start(), calls=%async_computation.18 | async-start | bytes 9437184 | tf_op jit(solution)/shard_map/reduce_scatter | solution.py:214
  1133.6 191.0 %reduce-scatter.10.cloned.1.call-start = ((), (), s32[]{:S(2)}) async-start(), calls=%async_computation.16 | async-start | bytes 9437184 | tf_op jit(solution)/shard_map/reduce_scatter | solution.py:211
  1139.5 344.7 %reduce-scatter.20.cloned.1.call-start = ((), (), s32[]{:S(2)}) async-start(), calls=%async_computation.21 | async-start | bytes 28311552 | tf_op jit(solution)/shard_map/reduce_scatter | solution.py:159
  1153.7 490.3 %reduce-scatter.18.cloned.1.call-start = ((), (), s32[]{:S(2)}) async-start(), calls=%async_computation.20 | async-start | bytes 28311552 | tf_op jit(solution)/shard_map/reduce_scatter | solution.py:156
  1167.6 636.2 %reduce-scatter.16.cloned.1.call-start = ((), (), s32[]{:S(2)}) async-start(), calls=%async_computation.19 | async-start | bytes 28311552 | tf_op jit(solution)/shard_map/reduce_scatter | solution.py:153
  1181.1 0.7 copy-start.30
  1181.1 1.9 copy-start.17
  1181.1 1.9 copy-start.19
  1183.0 7.2 copy-start.22
Sparse Core Ops, SparseCore 0:
  9.9 39.4 all-gather.8
  51.2 54.7 all-gather.10
  107.9 55.8 all-gather.12
  171.9 154.9 all-reduce.7
  328.7 124.1 all-gather.16
  454.6 125.1 all-gather.14
  581.7 130.1 all-gather.18
  757.6 154.9 all-reduce.9
  938.0 13.5 reduce-scatter.7
  954.6 163.4 all-reduce.11
  1124.4 50.1 reduce-scatter.11
  1177.9 71.7 reduce-scatter.13
  1253.1 71.4 reduce-scatter.9
  1328.1 156.0 reduce-scatter.19
  1487.6 156.2 reduce-scatter.17
  1647.4 156.2 reduce-scatter.15
where the time goes:
time: 1820 us
  waiting for transfers between devices  1460 us (80%)
  matrix products  191 us (10%)
  blocking collectives  70.5 us (4%)
  other arithmetic  57.7 us (3%)
    psum x1, waiting for transfers between devices, shards(): lax.psum(matmul(hidden, full_down).astype(jnp.bfloat16), 'tensor')  166 us
    reduce_scatter x1, waiting for transfers between devices, shards(): lax.psum_scatter(grad_down.astype(jnp.bfloat16), ('dp', 'seq'), scatter_d...  157 us
    reduce_scatter x1, waiting for transfers between devices, shards(): lax.psum_scatter(grad_gate.astype(jnp.bfloat16), ('dp', 'seq'), scatter_d...  154 us
    reduce_scatter x1, waiting for transfers between devices, shards(): lax.psum_scatter(grad_up.astype(jnp.bfloat16), ('dp', 'seq'), scatter_dim...  154 us
    psum x1, waiting for transfers between devices, shards(): lax.psum(matmul_nt(d_gate, back_gate) + matmul_nt(d_up, back_up), 'tensor')  140 us
    psum x1, waiting for transfers between devices, shards(): attn = lax.psum(matmul(mixed, full_out), 'tensor')  136 us
    all_gather x1, waiting for transfers between devices, shards(): lax.all_gather(w_up, ('dp', 'seq'), axis=0, tiled=True)  119 us
    all_gather x1, waiting for transfers between devices, shards(): lax.all_gather(w_down, ('dp', 'seq'), axis=1, tiled=True)  118 us
  transfers between devices with their start and end apart: 16, of which 15 were waited for; matrix products, arithmetic and copies ran while one was open for 9% of the time, Pallas kernels for 0%

commit v1 on v0

--- a/solution.py
+++ b/solution.py
@@ -69,7 +69,7 @@
     return rms_val * (scaled - normed * jnp.mean(scaled * normed, axis=-1, keepdims=True))
 
 
-def shards(
+def weights_move(
     tokens, seg_ids, gain_attn, w_query, kv_weight, w_out, gain_ffn, w_gate, w_up, w_down, d_out
 ):
     rows = tokens.shape[0]
@@ -235,6 +235,212 @@
     )
 
 
+AXES = ("dp", "seq")
+LANES = 128
+
+
+def gather_rows(block):
+    return lax.all_gather(block, AXES, axis=0, tiled=True)
+
+
+def scatter_rows(block):
+    return lax.psum_scatter(block, AXES, scatter_dimension=0, tiled=True)
+
+
+def to_columns(block):
+    return lax.all_to_all(block, AXES, split_axis=1, concat_axis=0, tiled=True)
+
+
+def lane_sums(values):
+    return jnp.sum(values.reshape(values.shape[0], -1, LANES), axis=1)
+
+
+def to_tokens(partial, rest, parts, rows):
+    depth = lax.axis_size("tensor")
+    width = partial.shape[1]
+    share = rows // depth
+    summed = lax.psum_scatter(
+        partial.astype(jnp.bfloat16).reshape(parts, depth, share, width),
+        "tensor",
+        scatter_dimension=1,
+        tiled=False,
+    )
+    own_rest = lax.dynamic_index_in_dim(
+        rest.reshape(parts, depth, share, width), lax.axis_index("tensor"), 1, keepdims=False
+    )
+    whole = (summed.astype(jnp.float32) + own_rest).astype(jnp.bfloat16)
+    moved = lax.all_to_all(whole, AXES, split_axis=0, concat_axis=0, tiled=True)
+    by_row = jnp.transpose(moved, (1, 0, 2)).reshape(share, parts * width)
+    return lax.all_gather(by_row, "tensor", axis=0, tiled=True)
+
+
+def acts_move(
+    tokens, seg_ids, gain_attn, w_query, kv_weight, w_out, gain_ffn, w_gate, w_up, w_down, d_out
+):
+    low = jnp.bfloat16
+    rows, width = tokens.shape
+    seqs = lax.axis_size("seq")
+    parts = lax.axis_size("dp") * seqs
+    scale_factor = 1.0 / math.sqrt(HD)
+    offset = lax.axis_index("seq") * rows
+    places, cos_table, sin_table = place_tables(seg_ids)
+    own_places = lax.dynamic_slice_in_dim(places, offset, rows, 0)
+    own_segs = lax.dynamic_slice_in_dim(seg_ids, offset, rows, 0)
+    own_cos = lax.dynamic_slice_in_dim(cos_table, offset, rows, 0)
+    own_sin = lax.dynamic_slice_in_dim(sin_table, offset, rows, 0)
+    allowed = (own_segs[:, None] == seg_ids[None, :]) & (own_places[:, None] >= places[None, :])
+    gain_one = gain_attn.astype(jnp.float32)
+    gain_two = gain_ffn.astype(jnp.float32)
+    qw = w_query.shape[1]
+    heads = qw // HD
+    ff = w_gate.shape[1]
+
+    x_low = to_columns(tokens)
+    g_low = to_columns(d_out)
+    x_col = x_low.astype(jnp.float32)
+    own_x = tokens.astype(jnp.float32)
+    rms_one = lax.rsqrt(jnp.mean(own_x * own_x, axis=-1, keepdims=True) + EPS)
+    act_one = (x_col * gain_one).astype(low)
+    qkv = scatter_rows(
+        jnp.concatenate([matmul(act_one, w_query), matmul(act_one, kv_weight)], axis=1).astype(low)
+    )
+    qkv = qkv.astype(jnp.float32) * rms_one
+    queries = (
+        rotate(qkv[:, :qw].reshape(rows, heads, HD), own_cos[:, None, :], own_sin[:, None, :])
+        * scale_factor
+    ).astype(low)
+    rms_high = rms_one.astype(low)
+    rms_rest = (rms_one - rms_high.astype(jnp.float32)).astype(low)
+    half = (rows, LANES // 2)
+    own_kv = jnp.concatenate(
+        [
+            rotate(qkv[:, qw : qw + HD], own_cos, own_sin).astype(low),
+            qkv[:, qw + HD :].astype(low),
+            jnp.broadcast_to(rms_high, half),
+            jnp.broadcast_to(rms_rest, half),
+        ],
+        axis=1,
+    )
+    all_kv = lax.all_gather(own_kv, "seq", axis=0, tiled=True)
+    keys = all_kv[:, :HD]
+    values_all = all_kv[:, HD : 2 * HD]
+    rms_group = all_kv[:, 2 * HD : 2 * HD + 1].astype(jnp.float32) + all_kv[
+        :, 2 * HD + LANES // 2 : 2 * HD + LANES // 2 + 1
+    ].astype(jnp.float32)
+    scores = jnp.einsum("rhd,kd->hrk", queries, keys, preferred_element_type=jnp.float32)
+    scores = jnp.where(allowed[None], scores, NEG)
+    top_score = jnp.max(scores, axis=-1, keepdims=True)
+    expd = jnp.exp(scores - top_score)
+    total = jnp.sum(expd, axis=-1, keepdims=True)
+    probs = expd / total
+    probs_low = probs.astype(low)
+    mixed = (
+        jnp.einsum("hrk,kd->rhd", probs_low, values_all, preferred_element_type=jnp.float32)
+        .reshape(rows, heads * HD)
+        .astype(low)
+    )
+    mixed_all = gather_rows(mixed)
+    attn = lax.psum(matmul(mixed_all, w_out).astype(low), "tensor")
+    d_hidden = scatter_rows(matmul_nt(g_low, w_down).astype(low)).astype(jnp.float32)
+    resid = x_col + attn.astype(jnp.float32)
+    act_two = (resid * gain_two).astype(low)
+    both = scatter_rows(
+        jnp.concatenate(
+            [matmul(act_two, w_gate), matmul(act_two, w_up), lane_sums(resid * resid)], axis=1
+        ).astype(low)
+    ).astype(jnp.float32)
+    mean_two = jnp.sum(both[:, 2 * ff :], axis=-1, keepdims=True) / width
+    rms_two = lax.rsqrt(mean_two + EPS)
+    gate = both[:, :ff] * rms_two
+    up_val = both[:, ff : 2 * ff] * rms_two
+    gelu_val, gelu_pull = jax.vjp(gelu_tanh, gate)
+    hidden = (gelu_val * up_val).astype(low)
+    d_gate = gelu_pull(d_hidden * up_val)[0]
+    d_up = d_hidden * gelu_val
+    dots_two = lane_sums(d_gate * gate + d_up * up_val) * (rms_two * rms_two / width)
+    back = gather_rows(
+        jnp.concatenate(
+            [(d_gate * rms_two).astype(low), (d_up * rms_two).astype(low), dots_two.astype(low)],
+            axis=1,
+        )
+    )
+    hidden_all = gather_rows(hidden)
+    d_gate_all = back[:, :ff]
+    d_up_all = back[:, ff : 2 * ff]
+    dot_two = jnp.sum(back[:, 2 * ff :].astype(jnp.float32), axis=-1, keepdims=True)
+    d_act_two = matmul_nt(d_gate_all, w_gate) + matmul_nt(d_up_all, w_up)
+    grad_gain_two = jnp.sum(d_act_two * resid, axis=0)
+    d_norm = lax.psum((d_act_two * gain_two - resid * dot_two).astype(low), "tensor")
+    d_resid = g_low.astype(jnp.float32) + d_norm.astype(jnp.float32)
+    d_attn = d_resid.astype(low)
+    d_mixed = scatter_rows(matmul_nt(d_attn, w_out).astype(low)).reshape(rows, heads, HD)
+    grad_gate = matmul_tn(act_two, d_gate_all)
+    grad_up = matmul_tn(act_two, d_up_all)
+    grad_down = matmul_tn(hidden_all, g_low)
+    out = to_tokens(matmul(hidden_all, w_down), resid, parts, rows)
+    grad_out = matmul_tn(mixed_all, d_attn)
+
+    d_probs = jnp.einsum("rhd,kd->hrk", d_mixed, values_all, preferred_element_type=jnp.float32)
+    delta = jnp.sum(probs * d_probs, axis=-1, keepdims=True)
+    d_scores = (probs * (d_probs - delta)).astype(low)
+    d_queries = (
+        jnp.einsum("hrk,kd->rhd", d_scores, keys, preferred_element_type=jnp.float32) * scale_factor
+    )
+    d_query_pre = (
+        rotate_back(d_queries, own_cos[:, None, :], own_sin[:, None, :]).reshape(rows, heads * HD)
+        * rms_one
+    ).astype(low)
+    query_dots = lane_sums(
+        (d_queries * queries.astype(jnp.float32)).reshape(rows, heads * HD)
+    ) * (rms_one * rms_one / (width * scale_factor))
+    d_keys = jnp.einsum("hrk,rhd->kd", d_scores, queries, preferred_element_type=jnp.float32)
+    d_values = jnp.einsum("hrk,rhd->kd", probs_low, d_mixed, preferred_element_type=jnp.float32)
+    kv_dots = lane_sums(
+        jnp.concatenate(
+            [d_keys * keys.astype(jnp.float32), d_values * values_all.astype(jnp.float32)], axis=1
+        )
+    ) * (rms_group * rms_group / width)
+    d_kv = jnp.concatenate(
+        [
+            rotate_back(d_keys, cos_table, sin_table) * rms_group,
+            d_values * rms_group,
+            kv_dots,
+        ],
+        axis=1,
+    ).astype(low)
+    kvw = d_kv.shape[1]
+    pieces = [d_kv[at * rows : (at + 1) * rows] for at in range(seqs)]
+    home = gather_rows(
+        jnp.concatenate([d_query_pre, query_dots.astype(low)] + pieces, axis=1)
+    )
+    d_query_all = home[:, :qw]
+    kv_parts = home[:, qw + LANES :].reshape(parts // seqs, seqs, rows, seqs, kvw)
+    kv_sum = jnp.sum(kv_parts.astype(jnp.float32), axis=1)
+    kv_sum = jnp.transpose(kv_sum, (0, 2, 1, 3)).reshape(parts * rows, kvw)
+    d_kv_all = kv_sum[:, : 2 * HD].astype(low)
+    dot_one = jnp.sum(
+        home[:, qw : qw + LANES].astype(jnp.float32) + kv_sum[:, 2 * HD :], axis=-1, keepdims=True
+    )
+    d_act_one = matmul_nt(d_query_all, w_query) + matmul_nt(d_kv_all, kv_weight)
+    grad_gain_one = jnp.sum(d_act_one * x_col, axis=0)
+    d_tokens = to_tokens(d_act_one * gain_one - x_col * dot_one, d_resid, parts, rows)
+    grad_query = matmul_tn(act_one, d_query_all)
+    grad_kv = lax.psum(matmul_tn(act_one, d_kv_all).astype(low), "tensor").astype(jnp.float32)
+    gains = lax.psum(jnp.stack([grad_gain_one, grad_gain_two]), "tensor")
+    return (
+        out,
+        d_tokens.astype(jnp.float32),
+        gains[0],
+        grad_query,
+        grad_kv,
+        grad_out,
+        gains[1],
+        grad_gate,
+        grad_up,
+        grad_down,
+    )
+
+
 def solution(mesh):
     in_specs = (
         P(("dp", "seq"), None),
@@ -261,4 +467,11 @@
         P(("dp", "seq"), "tensor"),
         P("tensor", ("dp", "seq")),
     )
+
+    def shards(*arrays):
+        tokens = arrays[0]
+        count = tokens.shape[0] * mesh.shape["dp"] * mesh.shape["seq"]
+        plan = acts_move if count <= tokens.shape[1] else weights_move
+        return plan(*arrays)
+
     return jax.shard_map(shards, mesh=mesh, in_specs=in_specs, out_specs=out_specs, check_vma=False)

time: 1820 us -> 1410 us (0.77)
  waiting for transfers between devices: 1460 us -> 979 us
  other arithmetic: 57.7 us -> 113 us
  local copies, waits for them, and re-layouts: 15.7 us -> 65.4 us
  matrix products: 191 us -> 158 us
    psum x3 -> x2, waiting for transfers between devices: 443 us -> 172 us  [the longest x1 86.2 us: acts_move(): lax.psum((d_act_two * gain_two - resid * dot_two).astype(low), 'tensor')]
    reduce_scatter x7 -> x4, waiting for transfers between devices: 563 us -> 308 us  [scatter_rows(): return lax.psum_scatter(block, AXES, scatter_dimension=0, tiled=True)]
    unnamed x16 -> x14, waiting for transfers between devices: 3.97 us -> 172 us
    all_gather x6, waiting for transfers between devices: 454 us -> 301 us  [the longest x4 275 us: gather_rows(): return lax.all_gather(block, AXES, axis=0, tiled=True)]
    all_to_all x0 -> x2, blocking collectives: none -> 41.8 us  [the longest x1 29.6 us: to_columns(): return lax.all_to_all(block, AXES, split_axis=1, concat_axis=0, tiled=True)]
    all_gather x3 -> x1, blocking collectives: 44.8 us -> 11.7 us  [acts_move(): all_kv = lax.all_gather(own_kv, 'seq', axis=0, tiled=True)]
    all_to_all x0 -> x2, waiting for transfers between devices: none -> 25.8 us  [the longest x1 25.8 us: to_columns(): return lax.all_to_all(block, AXES, split_axis=1, concat_axis=0, tiled=True)]
    unnamed x1 -> x0, blocking collectives: 25.7 us -> none
  transfers between devices with their start and end apart: 16 -> 15, of which waited for: 15 -> 13; matrix products, arithmetic and copies ran while one was open for 9% -> 7% of each run, Pallas kernels for 0% -> 0%
where the time goes in v1:
time: 1410 us; the launch traced here: 1400 us
  waiting for transfers between devices  979 us (69%)
  matrix products  158 us (11%)
  other arithmetic  113 us (8%)
  local copies, waits for them, and re-layouts  65.4 us (5%)
  blocking collectives  63.3 us (4%)
  between operations  15.1 us (1%)
    reduce_scatter x4, waiting for transfers between devices, scatter_rows(): return lax.psum_scatter(block, AXES, scatter_dimension=0, tiled=True)  308 us
    all_gather x4, waiting for transfers between devices, gather_rows(): return lax.all_gather(block, AXES, axis=0, tiled=True)  275 us
    unnamed x14, waiting for transfers between devices  172 us
    psum x1, waiting for transfers between devices, acts_move(): lax.psum((d_act_two * gain_two - resid * dot_two).astype(low), 'tensor')  86.2 us
    psum x1, waiting for transfers between devices, acts_move(): attn = lax.psum(matmul(mixed_all, w_out).astype(low), 'tensor')  86.1 us
    dot_general x6, matrix products, matmul_nt(): lax.dot_general(left, right, (((1,), (1,)), ((), ())), preferred_element_...  51 us
    dot_general x6, matrix products, matmul_tn(): lax.dot_general(left, right, (((0,), (0,)), ((), ())), preferred_element_...  50.4 us
    dot_general x6, matrix products, matmul(): return jnp.dot(left, right, preferred_element_type=jnp.float32)  43.2 us
  transfers between devices with their start and end apart: 15, of which 13 were waited for; matrix products, arithmetic and copies ran while one was open for 7% of the time, Pallas kernels for 0%

profile of v1, /device:TPU:0, one launch (start us, length us, event | category | flops | bytes accessed | tf_op | source)
XLA Modules:
  0.0 1404.2 jit_solution(3917099636171890622)
XLA Ops:
  7.2 3.3 copy.126
  10.5 5.3 all-to-all-start
  15.9 25.8 %all-to-all-done = bf16[256,8,512]{2,0,1:T(8,128)(2,1)} async-done(((bf16[256,8,512]{2,0,1:T(8,128)(2,1)}), bf16[256,8,512]{2,0,1:T(8,128)(2,1)}, u32[]{:S(2)}, u32[]{:S(2)}) %all-to-all-start) | async-done | bytes 2097184 | tf_op jit(solution)/shard_map/all_to_all | solution.py:251
  41.7 2.1 fusion.9
  45.7 2.4 convolution_convert_fusion.4
  48.2 3.5 pad_maximum_fusion.1
  53.3 2.1 multiply_reduce_fusion.1
  58.6 55.6 %reduce-scatter.11.cloned.1.call-done = bf16[256,1536]{0,1:T(8,128)(2,1)} async-done(((bf16[2048,1536]{0,1:T(8,128)(2,1)}), bf16[256,1536]{0,1:T(8,128)(2,1)}) %reduce-scatter.11.cloned.1.call-update) | async-done | bytes 786448 | tf_op jit(solution)/shard_map/reduce_scatter | solution.py:247
  123.0 11.7 all_gather.21
  134.7 2.2 fusion.76
  136.9 2.1 copy.115
  139.0 2.0 copy.114
  144.2 3.3 fusion.79
  147.5 3.2 convolution_convert_fusion.9
  150.7 37.4 %all-gather.7.cloned.1.call-done = bf16[2048,1024]{0,1:T(8,128)(2,1)} async-done(((bf16[256,1024]{0,1:T(8,128)(2,1)}), bf16[2048,1024]{0,1:T(8,128)(2,1)}) %all-gather.7.cloned.1.call-update) | async-done | bytes 4194320 | tf_op jit(solution)/shard_map/all_gather | solution.py:243
  188.2 6.2 convolution_convert_fusion.5
  194.6 86.1 %all-reduce.7.cloned.1.call-done = bf16[2048,512]{1,0:T(8,128)(2,1)} async-done(((bf16[2048,512]{1,0:T(8,128)(2,1)}), bf16[2048,512]{1,0:T(8,128)(2,1)}) %all-reduce.7.cloned.1.call-update) | async-done | bytes 2097168 | tf_op jit(solution)/shard_map/psum | solution.py:343
  280.7 5.8 multiply_convert_fusion
  286.5 5.2 reshape.230
  291.7 12.1 convolution_convert_fusion.1
  303.8 9.7 convolution_convert_fusion.2
  313.5 10.0 reduce_sum.119
  323.5 18.0 %pad_maximum_fusion = bf16[2048,6272]{1,0:T(8,128)(2,1)} fusion(bf16[2048,128]{1,0:T(8,128)(2,1)} %reduce_sum.119, bf16[2048,3072]{1,0:T(8,128)(2,1)} %convolution_convert_fusion.1, bf16[2048,3072]{1,0:T(8,128)(2,1)} %convolution_convert_fusion.2), kind=kLoop, calls=%fused_computation.1 | loop fusion | flops 77070336 | bytes 51380224 | tf_op jit(solution)/shard_map/concatenate | solution.py:348
  343.4 29.6 %all_to_all.42 = bf16[256,8,512]{2,0,1:T(8,128)(2,1)S(1)} all-to-all(bf16[256,8,512]{2,0,1:T(8,128)(2,1)S(1)} %bitcast.200), channel_id=1, replica_groups=mesh['dp'=4,'seq'=2,'tensor'=4] {'dp','seq'}, dimensions={1} | all-to-all | bytes 4194304 | tf_op jit(solution)/shard_map/all_to_all | solution.py:251
  374.3 10.2 convolution_convert_fusion
  384.6 114.8 %reduce-scatter.13.cloned.1.call-done = bf16[256,6272]{1,0:T(8,128)(2,1)} async-done(((bf16[2048,6272]{1,0:T(8,128)(2,1)}), bf16[256,6272]{1,0:T(8,128)(2,1)}) %reduce-scatter.13.cloned.1.call-update) | async-done | bytes 3211280 | tf_op jit(solution)/shard_map/reduce_scatter | solution.py:247
  499.4 2.3 convert_element_type.215
  501.7 2.7 copy-done.2
  505.1 89.9 %reduce-scatter.15.cloned.1.call-done = bf16[256,3072]{1,0:T(8,128)(2,1)} async-done(((bf16[2048,3072]{1,0:T(8,128)(2,1)}), bf16[256,3072]{1,0:T(8,128)(2,1)}) %reduce-scatter.15.cloned.1.call-update) | async-done | bytes 1572880 | tf_op jit(solution)/shard_map/reduce_scatter | solution.py:247
  595.1 5.0 multiply_convert_fusion.2
  600.6 3.0 multiply_convert_fusion.1
  607.2 127.3 %all-gather.13.cloned.1.call-done = bf16[2048,6272]{1,0:T(8,128)(2,1)} async-done(((bf16[256,6272]{1,0:T(8,128)(2,1)}), bf16[2048,6272]{1,0:T(8,128)(2,1)}) %all-gather.13.cloned.1.call-update) | async-done | bytes 25690128 | tf_op jit(solution)/shard_map/all_gather | solution.py:243
  735.8 10.8 fusion.3
  746.5 12.1 subtract_convert_fusion
  758.7 86.2 %all-reduce.9.cloned.1.call-done = bf16[2048,512]{1,0:T(8,128)(2,1)} async-done(((bf16[2048,512]{1,0:T(8,128)(2,1)}), bf16[2048,512]{1,0:T(8,128)(2,1)}) %all-reduce.9.cloned.1.call-update) | async-done | bytes 2097168 | tf_op jit(solution)/shard_map/psum | solution.py:373
  845.0 2.2 convert_add_fusion
  847.2 2.0 copy-done.11
  849.2 4.4 convolution_convert_fusion.3
  856.2 47.8 %reduce-scatter.17.cloned.1.call-done = bf16[256,1024]{1,0:T(8,128)(2,1)} async-done(((bf16[2048,1024]{1,0:T(8,128)(2,1)}), bf16[256,1024]{1,0:T(8,128)(2,1)}) %reduce-scatter.17.cloned.1.call-update) | async-done | bytes 524304 | tf_op jit(solution)/shard_map/reduce_scatter | solution.py:247
  909.7 3.4 convert_multiply_fusion.5
  921.4 57.1 %all-gather.9.cloned.1.call-done = bf16[2048,3072]{1,0:T(8,128)(2,1)} async-done(((bf16[256,3072]{1,0:T(8,128)(2,1)}), bf16[2048,3072]{1,0:T(8,128)(2,1)}) %all-gather.9.cloned.1.call-update) | async-done | bytes 12582928 | tf_op jit(solution)/shard_map/all_gather | solution.py:243
  978.5 11.5 convolution_convert_fusion.7
  990.0 53.7 %all-gather.15.cloned.1.call-done = bf16[2048,2432]{0,1:T(8,128)(2,1)} async-done(((bf16[256,2432]{0,1:T(8,128)(2,1)}), bf16[2048,2432]{0,1:T(8,128)(2,1)}) %all-gather.15.cloned.1.call-update) | async-done | bytes 9961488 | tf_op jit(solution)/shard_map/all_gather | solution.py:243
  1043.7 7.8 slice_convert_fusion
  1051.5 14.3 %reshape.243 = f32[4,2,256,2,640]{2,1,0,4,3:T(2,128)} reshape(f32[2048,1280]{0,1:T(8,128)} %slice_convert_fusion) | data formatting | bytes 20971520 | tf_op jit(solution)/shard_map/convert_element_type | solution.py:418
  1065.8 17.4 %reduce_sum.126 = f32[4,256,2,640]{1,0,3,2:T(4,128)} reduce(f32[4,2,256,2,640]{2,1,0,4,3:T(2,128)} %reshape.243, f32[]{:T(128)} %constant.24.clone.1), dimensions={1}, to_apply=%region_19.20 | reduce | flops 1310720 | bytes 15728644 | tf_op jit(solution)/shard_map/reduce_sum | solution.py:418
  1083.2 7.4 copy.98
  1090.6 2.4 slice.164
  1093.0 4.3 convolution_convert_fusion.8
  1098.9 5.1 fusion.15
  1105.2 8.4 fusion.12
  1114.9 170.9 %all-reduce.11.cloned.1.call-done = (bf16[8,4,64,512]{3,2,1,0:T(8,128)(2,1)}, bf16[8,4,64,512]{3,2,1,0:T(8,128)(2,1)}, bf16[512,512]{1,0:T(8,128)(2,1)}) async-done(((bf16[8,4,64,512]{3,2,1,0:T(8,128)(2,1)}, bf16[8,4,64,512]{3,2,1,0:T(8,128)(2,1)}, bf16[512,512]{1,0:T(8,128)(2,1)}), (bf16[8,4,64,512]{3,2,1,0:T(8,128)(2,1)}, bf16[8,4,64,512]{3,2,1,0:T(8,128)(2,1)}, ...) | async-done | bytes 4718608
  1285.8 2.2 fusion.37
  1288.0 12.3 all_to_all.43
  1301.1 12.0 fusion.84
  1313.1 3.0 fusion.38
  1316.1 3.5 all-to-all-start.3
  1319.6 12.3 fusion.5
  1332.9 12.2 fusion.1
  1345.1 3.6 fusion.32
  1348.7 9.8 psum.30
  1359.1 6.0 fusion.13
  1366.2 25.5 %all-gather.17.cloned.1.call-done = bf16[256,4096]{1,0:T(8,128)(2,1)} async-done(((bf16[64,4096]{1,0:T(8,128)(2,1)}), bf16[256,4096]{1,0:T(8,128)(2,1)}) %all-gather.17.cloned.1.call-update) | async-done | bytes 2097168 | tf_op jit(solution)/shard_map/all_gather | solution.py:274
  1391.6 4.2 convert_element_type.247
  (194 shorter events, 53.4 us)
Async XLA Ops:
  7.2 296.6 %copy-start = (bf16[512,3072]{1,0:T(8,128)(2,1)S(1)}, bf16[512,3072]{1,0:T(8,128)(2,1)}, u32[]{:S(2)}) copy-start(bf16[512,3072]{1,0:T(8,128)(2,1)} %param.18) | copy-start | bytes 9437188
  10.5 5.4 copy-start.44
  10.5 31.2 %all-to-all-start = ((bf16[256,8,512]{2,0,1:T(8,128)(2,1)}), bf16[256,8,512]{2,0,1:T(8,128)(2,1)}, u32[]{:S(2)}, u32[]{:S(2)}) async-start(bf16[256,8,512]{2,0,1:T(8,128)(2,1)} %bitcast.199), calls=%async_computation | async-start | bytes 4194304 | tf_op jit(solution)/shard_map/all_to_all | solution.py:251
  15.8 98.5 %reduce-scatter.11.cloned.1.call-start = ((), (), s32[]{:S(2)}) async-start(), calls=%async_computation.8 | async-start | bytes 7077888 | tf_op jit(solution)/shard_map/reduce_scatter | solution.py:247
  15.9 29.2 %copy-start.35 = (f32[512]{0:T(512)}, f32[512]{0:T(512)S(1)}, u32[]{:S(2)}) copy-start(f32[512]{0:T(512)S(1)} %convert_element_type.198) | copy-start | bytes 6148
  41.7 2.1 copy-start.28
  43.7 1.4 copy-start.4
  43.7 2.0 copy-start.49
  51.7 0.7 copy-start.34
  51.7 136.5 %all-gather.7.cloned.1.call-start = ((), (), s32[]{:S(2)}) async-start(), calls=%async_computation.9 | async-start | bytes 4718592 | tf_op jit(solution)/shard_map/all_gather | solution.py:243
  53.3 63.4 %copy-start.41 = (f32[128]{0:T(128)}, f32[128]{0:T(128)S(1)}, u32[]{:S(2)}) copy-start(f32[128]{0:T(128)S(1)} %multiply_exponential_fusion) | copy-start | bytes 1540
  56.0 61.7 %copy-start.37 = (f32[256]{0:T(256)}, f32[256]{0:T(256)S(1)}, u32[]{:S(2)}) copy-start(f32[256]{0:T(256)S(1)} %get-tuple-element.52) | copy-start | bytes 3076
  114.3 2.8 copy-start.26
  114.3 2.8 copy-start.27
  115.6 1.5 copy-start.10
  136.9 7.2 copy-start.33
  142.4 0.8 copy-start.14
  142.4 1.0 copy-start.16
  150.7 43.9 %copy-start.45 = (bf16[512]{0:T(512)(128)(2,1)S(1)}, bf16[512]{0:T(512)(128)(2,1)}, u32[]{:S(2)}) copy-start(bf16[512]{0:T(512)(128)(2,1)} %param.17) | copy-start | bytes 3076
  150.7 130.0 %all-reduce.7.cloned.1.call-start = ((), (), s32[]{:S(2)}) async-start(), calls=%async_computation.10 | async-start | bytes 4194304 | tf_op jit(solution)/shard_map/psum | solution.py:343
  194.4 305.0 %reduce-scatter.13.cloned.1.call-start = ((), (), s32[]{:S(2)}) async-start(), calls=%async_computation.11 | async-start | bytes 28901376 | tf_op jit(solution)/shard_map/reduce_scatter | solution.py:247
  291.7 12.1 copy-start.23
  341.5 253.6 %reduce-scatter.15.cloned.1.call-start = ((), (), s32[]{:S(2)}) async-start(), calls=%async_computation.14 | async-start | bytes 14155776 | tf_op jit(solution)/shard_map/reduce_scatter | solution.py:247
  343.3 30.9 %copy-start.47 = (bf16[3072,512]{1,0:T(8,128)(2,1)S(1)}, bf16[3072,512]{1,0:T(8,128)(2,1)}, u32[]{:S(2)}) copy-start(bf16[3072,512]{1,0:T(8,128)(2,1)} %param.20) | copy-start | bytes 9437188
  372.9 1.3 copy-start.8
  384.5 350.0 %all-gather.13.cloned.1.call-start = ((), (), s32[]{:S(2)}) async-start(), calls=%async_computation.15 | async-start | bytes 28901376 | tf_op jit(solution)/shard_map/all_gather | solution.py:243
  501.7 2.7 copy-start.2
  595.1 5.1 copy-start.3
  595.1 5.6 copy-start.13
  604.2 0.7 copy-start.39
  606.9 238.0 %all-reduce.9.cloned.1.call-start = ((), (), s32[]{:S(2)}) async-start(), calls=%async_computation.16 | async-start | bytes 4194304 | tf_op jit(solution)/shard_map/psum | solution.py:373
  735.8 10.8 copy-start.6
  758.6 86.3 %copy-start.9 = (bf16[256,8,512]{2,0,1:T(8,128)(2,1)S(1)}, bf16[256,8,512]{2,0,1:T(8,128)(2,1)}, u32[]{:S(2)}) copy-start(bf16[256,8,512]{2,0,1:T(8,128)(2,1)} %copy-done.8) | copy-start | bytes 6291460
  758.7 90.5 %copy-start.48 = (bf16[1024,512]{1,0:T(8,128)(2,1)S(1)}, bf16[1024,512]{1,0:T(8,128)(2,1)}, u32[]{:S(2)}) copy-start(bf16[1024,512]{1,0:T(8,128)(2,1)} %param.16) | copy-start | bytes 3145732
  758.7 145.3 %reduce-scatter.17.cloned.1.call-start = ((), (), s32[]{:S(2)}) async-start(), calls=%async_computation.17 | async-start | bytes 4718592 | tf_op jit(solution)/shard_map/reduce_scatter | solution.py:247
  847.2 2.0 copy-start.11
  853.6 51.6 %copy-start.19 = (f32[4,256,512]{1,2,0:T(8,128)S(1)}, f32[4,256,512]{1,2,0:T(8,128)}, u32[]{:S(2)}) copy-start(f32[4,256,512]{1,2,0:T(8,128)} %get-tuple-element.56) | copy-start | bytes 6291460
  853.7 124.9 %all-gather.9.cloned.1.call-start = ((), (), s32[]{:S(2)}) async-start(), calls=%async_computation.12 | async-start | bytes 14155776 | tf_op jit(solution)/shard_map/all_gather | solution.py:243
  854.4 189.3 %all-gather.15.cloned.1.call-start = ((), (), s32[]{:S(2)}) async-start(), calls=%async_computation.18 | async-start | bytes 11206656 | tf_op jit(solution)/shard_map/all_gather | solution.py:243
  905.3 1.6 copy-start.31
  906.9 1.0 copy-start.21
  906.9 1.5 copy-start.42
  908.0 1.7 copy-start.22
  908.0 1.7 copy-start.32
  908.0 1.7 copy-start.43
  914.5 2.6 copy-start.15
  914.6 2.6 copy-start.17
  917.8 1.0 copy-start.25
  917.8 2.0 copy-start.40
  917.9 2.0 copy-start.38
  921.2 364.6 %all-reduce.11.cloned.1.call-start = ((), (), s32[]{:S(2)}) async-start(), calls=%async_computation.20 | async-start | bytes 9437184
  1090.6 2.4 copy-start.5
  1098.9 6.3 copy-start.7
  1098.9 6.3 copy-start.18
  1098.9 6.3 copy-start.29
  1098.9 6.3 copy-start.36
  1113.7 252.5 %all-gather.11.cloned.1.call-start = ((), (), s32[]{:S(2)}) async-start(), calls=%async_computation.13 | async-start | bytes 2621440 | tf_op jit(solution)/shard_map/all_gather | solution.py:274
  1316.1 15.9 %all-to-all-start.3 = ((bf16[8,64,512]{2,1,0:T(8,128)(2,1)}), bf16[8,64,512]{2,1,0:T(8,128)(2,1)S(1)}, u32[]{:S(2)}, u32[]{:S(2)}) async-start(bf16[8,64,512]{2,1,0:T(8,128)(2,1)} %fusion.38), calls=%async_computation.7 | async-start | bytes 1048576 | tf_op jit(solution)/shard_map/all_to_all | solution.py:272
  1319.6 72.0 %all-gather.17.cloned.1.call-start = ((), (), s32[]{:S(2)}) async-start(), calls=%async_computation.19 | async-start | bytes 2621440 | tf_op jit(solution)/shard_map/all_gather | solution.py:274
  1332.8 12.2 copy-start.12
  1332.9 12.2 copy-start.46
  1359.1 6.0 copy-start.30
  1391.6 4.3 copy-start.20
  1391.6 5.6 copy-start.1
  (2 other events, 1.3 us)
Sparse Core Ops, SparseCore 0:
  51.8 62.3 reduce-scatter.10
  150.8 37.2 all-gather.6
  194.5 86.1 all-reduce.6
  341.6 157.7 reduce-scatter.12
  502.7 92.2 reduce-scatter.14
  607.1 127.3 all-gather.12
  758.8 86.1 all-reduce.8
  853.8 50.1 reduce-scatter.16
  906.5 71.9 all-gather.8
  980.8 62.8 all-gather.14
  1113.8 171.9 all-reduce.10
  1301.2 43.7 all-gather.10
  1347.1 44.4 all-gather.16

commit v2 on v1

--- a/solution.py
+++ b/solution.py
@@ -1,8 +1,11 @@
+import functools
 import math
 
 import jax
 import jax.numpy as jnp
 from jax import lax
+from jax.experimental import pallas as pl
+from jax.experimental.pallas import tpu as pltpu
 from jax.sharding import PartitionSpec as P
 
 HD = 256
@@ -235,6 +238,462 @@
     )
 
 
+MESH = pl.DeviceIdType.MESH
+VMEM_LIMIT = 66000 * 1024
+
+
+class Place:
+    def __init__(self):
+        self.dp = lax.axis_index("dp")
+        self.seq = lax.axis_index("seq")
+        self.z = lax.axis_index("tensor")
+        self.core = lax.rem(self.dp, 2)
+        self.chip = lax.div(self.dp, 2)
+
+    def device(self, across, other):
+        chip = (self.chip + across) % 2
+        seq = (self.seq + across // 2) % 2
+        core = (self.core + other) % 2
+        return chip * 2 + core, seq, self.z
+
+    def shard(self, across, other):
+        dp, seq, _ = self.device(across, other)
+        return dp * 2 + seq
+
+
+def greet(peers):
+    barrier = pltpu.get_barrier_semaphore()
+    for peer in peers:
+        pl.semaphore_signal(barrier, inc=1, device_id=peer, device_id_type=MESH)
+    pl.semaphore_wait(barrier, len(peers))
+
+
+def remote(src, dst, send, recv, peer):
+    return pltpu.make_async_remote_copy(
+        src_ref=src, dst_ref=dst, send_sem=send, recv_sem=recv, device_id=peer, device_id_type=MESH
+    )
+
+
+def scatter_kernel(rows, width, counts, nt, shared, act, *refs):
+    w0 = refs[0]
+    w1 = w0 if shared else refs[1]
+    tiny, out, tiny_all, held, sib_out, sib_in, from_x, from_y, sib_send, sib_recv = refs[1 if shared else 2 :][:10]
+    x_send, x_recv, y_send, y_recv, tiny_send, tiny_recv = refs[-6:]
+    here = Place()
+    sib, xdev, ydev = here.device(0, 1), here.device(1, 0), here.device(2, 0)
+    peers = [here.device(a, o) for a in range(4) for o in range(2) if a + o > 0]
+    greet(peers)
+    weights = (w0, w1)
+
+    def tiny_copy(at):
+        across, other = (at + 1) // 2, (at + 1) % 2
+        return remote(tiny.at[here.shard(across, other)], tiny_all.at[here.shard(0, 0)],
+                      tiny_send.at[at], tiny_recv.at[at], peers[at])
+
+    for at in range(7):
+        tiny_copy(at).start()
+    tiny_all[here.shard(0, 0)] = tiny[here.shard(0, 0)]
+    half_cols = counts * width
+    stages = (((3, 0), (3, 1)), ((1, 0), (2, 1)), ((0, 0), (0, 1)), ((1, 1), (2, 0)))
+
+    def product(across, other, half, at):
+        row = pl.multiple_of(here.shard(across, other) * rows, rows)
+        first = half * half_cols if shared else 0
+        cols = pl.ds(pl.multiple_of(first + at * width, width), width)
+        block = act[pl.ds(row, rows), :]
+        if nt:
+            return lax.dot_general(block, weights[half][cols, :], (((1,), (1,)), ((), ())),
+                                   preferred_element_type=jnp.float32)
+        return jnp.dot(block, weights[half][:, cols], preferred_element_type=jnp.float32)
+
+    def to_sib(stage, stream, at):
+        return remote(sib_out.at[stage, stream, at], sib_in.at[stage, stream, at],
+                      sib_send.at[stage, stream, at], sib_recv.at[stage, stream, at], sib)
+
+    def to_x(step, at, stage):
+        return remote(held.at[stage, 0, at], from_x.at[step, at], x_send.at[step, at],
+                      x_recv.at[step, at], xdev)
+
+    def to_y(step, at, stage):
+        return remote(held.at[stage, 1, at], from_y.at[step, at], y_send.at[step, at],
+                      y_recv.at[step, at], ydev)
+
+    step_of = {0: 0, 1: 1, 3: 2}
+
+    for stage, streams in enumerate(stages):
+        def compute(at, stage=stage, streams=streams):
+            for stream, (across, half) in enumerate(streams):
+                sib_out[stage, stream, at] = product(across, 1, half, at).astype(jnp.bfloat16)
+                held[stage, stream, at] = product(across, 0, half, at).astype(jnp.bfloat16)
+
+        def finish(at, stage=stage):
+            for stream in range(2):
+                to_sib(stage, stream, at).wait_recv()
+                total = held[stage, stream, at].astype(jnp.float32) + sib_in[
+                    stage, stream, at].astype(jnp.float32)
+                if stage == 3:
+                    if stream == 0:
+                        to_y(0, at, 0).wait_recv()
+                        total += from_y[0, at].astype(jnp.float32)
+                    else:
+                        to_x(0, at, 0).wait_recv()
+                        total += from_x[0, at].astype(jnp.float32)
+                if stage == 2:
+                    cols = pl.ds(pl.multiple_of(stream * half_cols + at * width, width), width)
+                    out[:, cols] = total
+                else:
+                    held[stage, stream, at] = total.astype(jnp.bfloat16)
+            if stage != 2:
+                to_x(step_of[stage], at, stage).start()
+                to_y(step_of[stage], at, stage).start()
+
+        def body(at, _, compute=compute, finish=finish, stage=stage):
+            compute(at)
+            for stream in range(2):
+                to_sib(stage, stream, at).start()
+
+            @pl.when(at > 0)
+            def _():
+                finish(at - 1)
+            return 0
+
+        lax.fori_loop(0, counts, body, 0)
+        finish(counts - 1)
+
+    def last(at, _):
+        for half in range(2):
+            cols = pl.ds(pl.multiple_of(half * half_cols + at * width, width), width)
+            xs, ys = (1, 2) if half == 0 else (2, 1)
+            to_x(xs, at, 0).wait_recv()
+            to_y(ys, at, 0).wait_recv()
+            out[:, cols] += from_x[xs, at].astype(jnp.float32) + from_y[ys, at].astype(jnp.float32)
+        for stage in range(4):
+            for stream in range(2):
+                to_sib(stage, stream, at).wait_send()
+        for step in range(3):
+            to_x(step, at, 0).wait_send()
+            to_y(step, at, 0).wait_send()
+        return 0
+
+    lax.fori_loop(0, counts, last, 0)
+    for at in range(7):
+        tiny_copy(at).wait()
+
+
+def scatter_product(act, weights, tiny, width, nt, cid):
+    total, depth = act.shape
+    rows = total // 8
+    shared = len(weights) == 1
+    half = weights[0].shape[0 if nt else 1] // (2 if shared else 1)
+    counts = half // width
+    low = jnp.bfloat16
+    dma = pltpu.SemaphoreType.DMA
+    vm = pl.BlockSpec(memory_space=pltpu.VMEM)
+    return pl.pallas_call(
+        functools.partial(scatter_kernel, rows, width, counts, nt, shared),
+        out_shape=(
+            jax.ShapeDtypeStruct((rows, 2 * half), jnp.float32),
+            jax.ShapeDtypeStruct(tiny.shape, jnp.float32),
+        ),
+        in_specs=[vm] * (2 + len(weights)),
+        out_specs=(vm, vm),
+        scratch_shapes=[
+            pltpu.VMEM((4, 2, counts, rows, width), low),
+            pltpu.VMEM((4, 2, counts, rows, width), low),
+            pltpu.VMEM((4, 2, counts, rows, width), low),
+            pltpu.VMEM((3, counts, rows, width), low),
+            pltpu.VMEM((3, counts, rows, width), low),
+            dma((4, 2, counts)), dma((4, 2, counts)),
+            dma((3, counts)), dma((3, counts)), dma((3, counts)), dma((3, counts)),
+            dma((7,)), dma((7,)),
+        ],
+        compiler_params=pltpu.CompilerParams(collective_id=cid, has_side_effects=True,
+                                             vmem_limit_bytes=VMEM_LIMIT),
+        name=f"scatter_product_{cid}",
+    )(act, *weights, tiny)
+
+
+def line_kernel(chunk, counts, own, out, from_end, mine, from_mid, end_send, end_recv, mid_send, mid_recv,
+                back_send, back_recv):
+    here = Place()
+    z = here.z
+    outer = jnp.logical_or(z == 0, z == 3)
+    mate = z + 1 - 2 * (z % 2)
+    other = 3 - z
+    mate_dev = (here.dp, here.seq, mate)
+    other_dev = (here.dp, here.seq, other)
+
+    def rows(at):
+        return pl.ds(pl.multiple_of(at * chunk, chunk), chunk)
+
+    def up(at):
+        return remote(own.at[rows(at), :], from_end.at[at], end_send.at[at], end_recv.at[at], mate_dev)
+
+    def over(at):
+        return remote(mine.at[at], from_mid.at[at], mid_send.at[at], mid_recv.at[at], other_dev)
+
+    def down(at):
+        return remote(out.at[rows(at), :], out.at[rows(at), :], back_send.at[at], back_recv.at[at], mate_dev)
+
+    barrier = pltpu.get_barrier_semaphore()
+    pl.semaphore_signal(barrier, inc=1, device_id=mate_dev, device_id_type=MESH)
+
+    @pl.when(outer)
+    def _():
+        pl.semaphore_wait(barrier, 1)
+
+        def send(at, _):
+            up(at).start()
+            return 0
+
+        def take(at, _):
+            up(at).wait_send()
+            down(at).wait_recv()
+            return 0
+
+        lax.fori_loop(0, counts, send, 0)
+        lax.fori_loop(0, counts, take, 0)
+
+    @pl.when(jnp.logical_not(outer))
+    def _():
+        pl.semaphore_signal(barrier, inc=1, device_id=other_dev, device_id_type=MESH)
+        pl.semaphore_wait(barrier, 2)
+
+        def second(at):
+            over(at).wait_recv()
+            out[rows(at), :] = (mine[at].astype(jnp.float32) + from_mid[at].astype(jnp.float32)).astype(out.dtype)
+            down(at).start()
+
+        def first(at, _):
+            up(at).wait_recv()
+            mine[at] = (own[rows(at), :].astype(jnp.float32) + from_end[at].astype(jnp.float32)).astype(mine.dtype)
+            over(at).start()
+
+            @pl.when(at > 1)
+            def _():
+                second(at - 2)
+            return 0
+
+        lax.fori_loop(0, counts, first, 0)
+        second(counts - 2)
+        second(counts - 1)
+
+        def drain(at, _):
+            over(at).wait_send()
+            down(at).wait_send()
+            return 0
+
+        lax.fori_loop(0, counts, drain, 0)
+
+
+def line_sum(own, cid, counts=16):
+    total, width = own.shape
+    chunk = total // counts
+    low = own.dtype
+    dma = pltpu.SemaphoreType.DMA
+    vm = pl.BlockSpec(memory_space=pltpu.VMEM)
+    buf = pltpu.VMEM((counts, chunk, width), low)
+    return pl.pallas_call(
+        functools.partial(line_kernel, chunk, counts),
+        out_shape=jax.ShapeDtypeStruct((total, width), low),
+        in_specs=[vm],
+        out_specs=vm,
+        scratch_shapes=[buf, buf, buf] + [dma((counts,))] * 6,
+        compiler_params=pltpu.CompilerParams(collective_id=cid, has_side_effects=True,
+                                             vmem_limit_bytes=VMEM_LIMIT),
+        name=f"line_sum_{cid}",
+    )(own)
+
+
+def gather_kernel(rows, width, counts, act_t, w0, w1, g0, g1, tiny, d_act, gw0, gw1, tiny_all, got,
+                  x_send, x_recv, y_send, y_recv, sib_send, sib_recv, tiny_send, tiny_recv):
+    here = Place()
+    sib, xdev, ydev = here.device(0, 1), here.device(1, 0), here.device(2, 0)
+    peers = [here.device(a, o) for a in range(4) for o in range(2) if a + o > 0]
+    greet(peers)
+    core = here.core
+    own, weights, grads = (g0, g1), (w0, w1), (gw0, gw1)
+    stages = (((1, 0), (2, 1)), ((1, 1), (2, 0)), ((3, 1), (3, 0)))
+
+    def part(half, at):
+        return own[half].at[:, pl.ds(pl.multiple_of(at * width, width), width)]
+
+    def x_copy(step, at):
+        src = part(step, at) if step < 2 else got.at[2, core, 1, at]
+        dst = got.at[1, core, step, at] if step < 2 else got.at[3, core, 1, at]
+        return remote(src, dst, x_send.at[step, at], x_recv.at[step, at], xdev)
+
+    def y_copy(step, at):
+        src = part(1 - step, at) if step < 2 else got.at[1, core, 0, at]
+        dst = got.at[2, core, 1 - step, at] if step < 2 else got.at[3, core, 0, at]
+        return remote(src, dst, y_send.at[step, at], y_recv.at[step, at], ydev)
+
+    def sib_copy(stage, stream, at):
+        if stage == 3:
+            src, (across, half) = part(stream, at), (0, stream)
+        else:
+            across, half = stages[stage][stream]
+            src = got.at[across, core, half, at]
+        return remote(src, got.at[across, core, half, at], sib_send.at[stage, stream, at],
+                      sib_recv.at[stage, stream, at], sib)
+
+    def tiny_copy(at, peer):
+        return remote(tiny, tiny_all.at[here.shard(0, 0)], tiny_send.at[at], tiny_recv.at[at], peer)
+
+    def begin(at, _):
+        x_copy(0, at).start()
+        y_copy(0, at).start()
+        return 0
+
+    def begin_sib(at, _):
+        sib_copy(3, 0, at).start()
+        sib_copy(3, 1, at).start()
+        return 0
+
+    for at, peer in enumerate(peers):
+        tiny_copy(at, peer).start()
+    lax.fori_loop(0, counts, begin, 0)
+    lax.fori_loop(0, counts, begin_sib, 0)
+    tiny_all[here.shard(0, 0)] = tiny[...]
+    d_act[...] = jnp.zeros_like(d_act)
+
+    def blocks(across, half, at, mine):
+        cols = pl.ds(pl.multiple_of(at * width, width), width)
+        gained = None
+        for other in range(2):
+            row = pl.ds(pl.multiple_of(here.shard(across, other) * rows, rows), rows)
+            if mine and other == 0:
+                block = own[half][:, cols]
+            else:
+                block = got[across, (core + other) % 2, half, at]
+            d_act[row, :] += lax.dot_general(block, weights[half][:, cols], (((1,), (1,)), ((), ())),
+                                             preferred_element_type=jnp.float32)
+            more = jnp.dot(act_t[:, row], block, preferred_element_type=jnp.float32)
+            gained = more if gained is None else gained + more
+        if mine:
+            grads[half][:, cols] = gained
+        else:
+            grads[half][:, cols] += gained
+
+    def own_step(at, _):
+        for half in range(2):
+            sib_copy(3, half, at).wait_recv()
+            blocks(0, half, at, True)
+        return 0
+
+    lax.fori_loop(0, counts, own_step, 0)
+
+    def work(stage, at):
+        for stream, (across, half) in enumerate(stages[stage]):
+            sib_copy(stage, stream, at).wait_recv()
+            blocks(across, half, at, False)
+
+    for stage in range(3):
+        def body(at, _, stage=stage):
+            x_copy(stage, at).wait_recv()
+            sib_copy(stage, 0, at).start()
+            y_copy(stage, at).wait_recv()
+            sib_copy(stage, 1, at).start()
+            if stage < 2:
+                x_copy(stage + 1, at).start()
+                y_copy(stage + 1, at).start()
+
+            @pl.when(at > 0)
+            def _():
+                work(stage, at - 1)
+            return 0
+
+        lax.fori_loop(0, counts, body, 0)
+        work(stage, counts - 1)
+
+    def drain(at, _):
+        for step in range(3):
+            x_copy(step, at).wait_send()
+            y_copy(step, at).wait_send()
+        for stage in range(4):
+            sib_copy(stage, 0, at).wait_send()
+            sib_copy(stage, 1, at).wait_send()
+        return 0
+
+    lax.fori_loop(0, counts, drain, 0)
+    for at, peer in enumerate(peers):
+        tiny_copy(at, peer).wait()
+
+
+def gather_product(act_t, w0, w1, g0, g1, tiny, width, cid):
+    depth, total = act_t.shape
+    rows, half = g0.shape
+    counts = half // width
+    low = jnp.bfloat16
+    dma = pltpu.SemaphoreType.DMA
+    vm = pl.BlockSpec(memory_space=pltpu.VMEM)
+    f32 = jnp.float32
+    return pl.pallas_call(
+        functools.partial(gather_kernel, rows, width, counts),
+        out_shape=(
+            jax.ShapeDtypeStruct((total, depth), f32),
+            jax.ShapeDtypeStruct((depth, half), f32),
+            jax.ShapeDtypeStruct((depth, half), f32),
+            jax.ShapeDtypeStruct((8,) + tiny.shape, f32),
+        ),
+        in_specs=[vm] * 6,
+        out_specs=(vm,) * 4,
+        scratch_shapes=[
+            pltpu.VMEM((4, 2, 2, counts, rows, width), low),
+            dma((3, counts)), dma((3, counts)), dma((3, counts)), dma((3, counts)),
+            dma((4, 2, counts)), dma((4, 2, counts)), dma((7,)), dma((7,)),
+        ],
+        compiler_params=pltpu.CompilerParams(collective_id=cid, has_side_effects=True,
+                                             vmem_limit_bytes=VMEM_LIMIT),
+        name=f"gather_product_{cid}",
+    )(act_t, w0, w1, g0, g1, tiny)
+
+
+def turn_kernel(rows, cols, back, src, out, own_sem, send, recv):
+    here = Place()
+    peers = [(a, o) for a in (3, 1, 2, 0) for o in range(2) if a + o > 0]
+    greet([here.device(a, o) for a, o in peers])
+
+    def by_row(ref, shard):
+        return ref.at[pl.ds(pl.multiple_of(shard * rows, rows), rows), :]
+
+    def by_col(ref, shard):
+        return ref.at[:, pl.ds(pl.multiple_of(shard * cols, cols), cols)]
+
+    take, put = (by_row, by_col) if back else (by_col, by_row)
+    me = here.shard(0, 0)
+
+    def copy(at):
+        across, other = peers[at]
+        return remote(take(src, here.shard(across, other)), put(out, me), send.at[at], recv.at[at],
+                      here.device(across, other))
+
+    for at in range(7):
+        copy(at).start()
+    own = pltpu.make_async_copy(take(src, me), put(out, me), own_sem)
+    own.start()
+    own.wait()
+    for at in range(7):
+        copy(at).wait()
+
+
+def turn(src, back, cid):
+    rows, cols = (src.shape[0] // 8, src.shape[1]) if back else (src.shape[0], src.shape[1] // 8)
+    shape = (rows, 8 * cols) if back else (8 * rows, cols)
+    dma = pltpu.SemaphoreType.DMA
+    vm = pl.BlockSpec(memory_space=pltpu.VMEM)
+    return pl.pallas_call(
+        functools.partial(turn_kernel, rows, cols, back),
+        out_shape=jax.ShapeDtypeStruct(shape, src.dtype),
+        in_specs=[vm],
+        out_specs=vm,
+        scratch_shapes=[dma(()), dma((7,)), dma((7,))],
+        compiler_params=pltpu.CompilerParams(collective_id=cid, has_side_effects=True,
+                                             vmem_limit_bytes=VMEM_LIMIT),
+        name=f"turn_{cid}",
+    )(src)
+
+
 AXES = ("dp", "seq")
 LANES = 128
 
@@ -243,35 +702,13 @@
     return lax.all_gather(block, AXES, axis=0, tiled=True)
 
 
-def scatter_rows(block):
-    return lax.psum_scatter(block, AXES, scatter_dimension=0, tiled=True)
-
-
-def to_columns(block):
-    return lax.all_to_all(block, AXES, split_axis=1, concat_axis=0, tiled=True)
-
-
 def lane_sums(values):
     return jnp.sum(values.reshape(values.shape[0], -1, LANES), axis=1)
 
 
-def to_tokens(partial, rest, parts, rows):
-    depth = lax.axis_size("tensor")
-    width = partial.shape[1]
-    share = rows // depth
-    summed = lax.psum_scatter(
-        partial.astype(jnp.bfloat16).reshape(parts, depth, share, width),
-        "tensor",
-        scatter_dimension=1,
-        tiled=False,
-    )
-    own_rest = lax.dynamic_index_in_dim(
-        rest.reshape(parts, depth, share, width), lax.axis_index("tensor"), 1, keepdims=False
-    )
-    whole = (summed.astype(jnp.float32) + own_rest).astype(jnp.bfloat16)
-    moved = lax.all_to_all(whole, AXES, split_axis=0, concat_axis=0, tiled=True)
-    by_row = jnp.transpose(moved, (1, 0, 2)).reshape(share, parts * width)
-    return lax.all_gather(by_row, "tensor", axis=0, tiled=True)
+def pack_rows(values):
+    parts = values.reshape(8, -1, LANES)
+    return jnp.pad(parts, ((0, 0), (0, 8 - parts.shape[1]), (0, 0)))
 
 
 def acts_move(
@@ -295,16 +732,15 @@
     heads = qw // HD
     ff = w_gate.shape[1]
 
-    x_low = to_columns(tokens)
-    g_low = to_columns(d_out)
+    none = jnp.zeros((8, 8, LANES), jnp.float32)
+    x_low = turn(tokens, False, 1)
+    g_low = turn(d_out, False, 2)
     x_col = x_low.astype(jnp.float32)
     own_x = tokens.astype(jnp.float32)
     rms_one = lax.rsqrt(jnp.mean(own_x * own_x, axis=-1, keepdims=True) + EPS)
     act_one = (x_col * gain_one).astype(low)
-    qkv = scatter_rows(
-        jnp.concatenate([matmul(act_one, w_query), matmul(act_one, kv_weight)], axis=1).astype(low)
-    )
-    qkv = qkv.astype(jnp.float32) * rms_one
+    w_qkv = jnp.concatenate([w_query, kv_weight], axis=1)
+    qkv = scatter_product(act_one, (w_qkv,), none, 256, False, 3)[0] * rms_one
     queries = (
         rotate(qkv[:, :qw].reshape(rows, heads, HD), own_cos[:, None, :], own_sin[:, None, :])
         * scale_factor
@@ -340,16 +776,13 @@
         .astype(low)
     )
     mixed_all = gather_rows(mixed)
-    attn = lax.psum(matmul(mixed_all, w_out).astype(low), "tensor")
-    d_hidden = scatter_rows(matmul_nt(g_low, w_down).astype(low)).astype(jnp.float32)
+    attn = line_sum(matmul(mixed_all, w_out).astype(low), 4)
+    d_hidden = scatter_product(g_low, (w_down,), none, 512, True, 5)[0]
     resid = x_col + attn.astype(jnp.float32)
     act_two = (resid * gain_two).astype(low)
-    both = scatter_rows(
-        jnp.concatenate(
-            [matmul(act_two, w_gate), matmul(act_two, w_up), lane_sums(resid * resid)], axis=1
-        ).astype(low)
-    ).astype(jnp.float32)
-    mean_two = jnp.sum(both[:, 2 * ff :], axis=-1, keepdims=True) / width
+    squares = pack_rows(jnp.sum(resid * resid, axis=-1))
+    both, squares_all = scatter_product(act_two, (w_gate, w_up), squares, 512, False, 6)
+    mean_two = jnp.sum(squares_all[:, : rows // LANES], axis=0).reshape(rows, 1) / width
     rms_two = lax.rsqrt(mean_two + EPS)
     gate = both[:, :ff] * rms_two
     up_val = both[:, ff : 2 * ff] * rms_two
@@ -357,27 +790,31 @@
     hidden = (gelu_val * up_val).astype(low)
     d_gate = gelu_pull(d_hidden * up_val)[0]
     d_up = d_hidden * gelu_val
-    dots_two = lane_sums(d_gate * gate + d_up * up_val) * (rms_two * rms_two / width)
-    back = gather_rows(
-        jnp.concatenate(
-            [(d_gate * rms_two).astype(low), (d_up * rms_two).astype(low), dots_two.astype(low)],
-            axis=1,
-        )
+    dots_two = jnp.sum(d_gate * gate + d_up * up_val, axis=-1, keepdims=True) * (
+        rms_two * rms_two / width
+    )
+    dots_own = jnp.pad(dots_two.reshape(-1, LANES), ((0, 8 - rows // LANES), (0, 0)))
+    d_act_two, grad_gate, grad_up, dots_all = gather_product(
+        act_two.T,
+        w_gate,
+        w_up,
+        (d_gate * rms_two).astype(low),
+        (d_up * rms_two).astype(low),
+        dots_own,
+        512,
+        7,
     )
     hidden_all = gather_rows(hidden)
-    d_gate_all = back[:, :ff]
-    d_up_all = back[:, ff : 2 * ff]
-    dot_two = jnp.sum(back[:, 2 * ff :].astype(jnp.float32), axis=-1, keepdims=True)
-    d_act_two = matmul_nt(d_gate_all, w_gate) + matmul_nt(d_up_all, w_up)
+    dot_two = dots_all[:, : rows // LANES].reshape(parts * rows, 1)
     grad_gain_two = jnp.sum(d_act_two * resid, axis=0)
-    d_norm = lax.psum((d_act_two * gain_two - resid * dot_two).astype(low), "tensor")
+    d_norm = line_sum((d_act_two * gain_two - resid * dot_two).astype(low), 8)
     d_resid = g_low.astype(jnp.float32) + d_norm.astype(jnp.float32)
     d_attn = d_resid.astype(low)
-    d_mixed = scatter_rows(matmul_nt(d_attn, w_out).astype(low)).reshape(rows, heads, HD)
-    grad_gate = matmul_tn(act_two, d_gate_all)
-    grad_up = matmul_tn(act_two, d_up_all)
+    d_mixed = scatter_product(d_attn, (w_out,), none, 256, True, 9)[0]
+    d_mixed = d_mixed.astype(low).reshape(rows, heads, HD)
     grad_down = matmul_tn(hidden_all, g_low)
-    out = to_tokens(matmul(hidden_all, w_down), resid, parts, rows)
+    ffn = lax.psum(matmul(hidden_all, w_down).astype(low), "tensor")
+    out = turn((resid + ffn.astype(jnp.float32)).astype(low), True, 10)
     grad_out = matmul_tn(mixed_all, d_attn)
 
     d_probs = jnp.einsum("rhd,kd->hrk", d_mixed, values_all, preferred_element_type=jnp.float32)
@@ -423,7 +860,8 @@
     )
     d_act_one = matmul_nt(d_query_all, w_query) + matmul_nt(d_kv_all, kv_weight)
     grad_gain_one = jnp.sum(d_act_one * x_col, axis=0)
-    d_tokens = to_tokens(d_act_one * gain_one - x_col * dot_one, d_resid, parts, rows)
+    d_norm_one = line_sum((d_act_one * gain_one - x_col * dot_one).astype(low), 11)
+    d_tokens = turn((d_resid + d_norm_one.astype(jnp.float32)).astype(low), True, 12)
     grad_query = matmul_tn(act_one, d_query_all)
     grad_kv = lax.psum(matmul_tn(act_one, d_kv_all).astype(low), "tensor").astype(jnp.float32)
     gains = lax.psum(jnp.stack([grad_gain_one, grad_gain_two]), "tensor")
@@ -470,8 +908,9 @@
 
     def shards(*arrays):
         tokens = arrays[0]
-        count = tokens.shape[0] * mesh.shape["dp"] * mesh.shape["seq"]
-        plan = acts_move if count <= tokens.shape[1] else weights_move
+        sizes = tuple(mesh.shape[name] for name in ("dp", "seq", "tensor"))
+        count = tokens.shape[0] * sizes[0] * sizes[1]
+        plan = acts_move if sizes == (4, 2, 4) and count <= tokens.shape[1] else weights_move
         return plan(*arrays)
 
     return jax.shard_map(shards, mesh=mesh, in_specs=in_specs, out_specs=out_specs, check_vma=False)

time: 1410 us -> 1070 us (0.76)
  waiting for transfers between devices: 979 us -> 154 us
  Pallas kernels: 0 us -> 669 us
  matrix products: 158 us -> 73.3 us
  blocking collectives: 63.3 us -> 19.6 us
  other arithmetic: 113 us -> 80.8 us
    pallas_call x0 -> x12, Pallas kernels: none -> 669 us  [the longest x4 245 us: scatter_product(): pl.pallas_call(functools.partial(scatter_kernel, rows, width, counts, nt,...]
    reduce_scatter x4 -> x0, waiting for transfers between devices: 308 us -> none  [scatter_rows(): return lax.psum_scatter(block, AXES, scatter_dimension=0, tiled=True)]
    all_gather x4 -> x3, waiting for transfers between devices: 275 us -> 78 us  [gather_rows(): return lax.all_gather(block, AXES, axis=0, tiled=True)]
    unnamed x14 -> x4, waiting for transfers between devices: 172 us -> 0.73 us
    psum x2 -> x1, waiting for transfers between devices: 172 us -> 75 us  [acts_move(): ffn = lax.psum(matmul(hidden_all, w_down).astype(low), 'tensor')]
    all_to_all x2 -> x0, blocking collectives: 41.8 us -> none  [the longest x1 29.6 us: to_columns(): return lax.all_to_all(block, AXES, split_axis=1, concat_axis=0, tiled=True)]
    dot_general x6 -> x2, matrix products: 51 us -> 15.1 us  [matmul_nt(): lax.dot_general(left, right, (((1,), (1,)), ((), ())), preferred_element_...]
    all_to_all x2 -> x0, waiting for transfers between devices: 25.8 us -> none  [the longest x1 25.8 us: to_columns(): return lax.all_to_all(block, AXES, split_axis=1, concat_axis=0, tiled=True)]
  transfers between devices with their start and end apart: 15 -> 4, of which waited for: 13 -> 3; matrix products, arithmetic and copies ran while one was open for 7% -> 8% of each run, Pallas kernels for 0% -> 9%
where the time goes in v2:
time: 1070 us
  Pallas kernels  669 us (63%)
  waiting for transfers between devices  154 us (14%)
  other arithmetic  80.8 us (8%)
  matrix products  73.3 us (7%)
  local copies, waits for them, and re-layouts  53.6 us (5%)
  blocking collectives  19.6 us (2%)
  between operations  15 us (1%)
    pallas_call x4, Pallas kernels, scatter_product(): pl.pallas_call(functools.partial(scatter_kernel, rows, width, counts, nt,...  245 us
    pallas_call x3, Pallas kernels, line_sum(): pl.pallas_call(functools.partial(line_kernel, chunk, counts), out_shape=j...  182 us
    pallas_call x4, Pallas kernels, turn(): pl.pallas_call(functools.partial(turn_kernel, rows, cols, back), out_shap...  123 us
    pallas_call x1, Pallas kernels, gather_product(): pl.pallas_call(functools.partial(gather_kernel, rows, width, counts), out...  119 us
    all_gather x3, waiting for transfers between devices, gather_rows(): return lax.all_gather(block, AXES, axis=0, tiled=True)  78 us
    psum x1, waiting for transfers between devices, acts_move(): ffn = lax.psum(matmul(hidden_all, w_down).astype(low), 'tensor')  75 us
    dot_general x4, matrix products, matmul_tn(): lax.dot_general(left, right, (((0,), (0,)), ((), ())), preferred_element_...  27.9 us
  transfers between devices with their start and end apart: 4, of which 3 were waited for; matrix products, arithmetic and copies ran while one was open for 8% of the time, Pallas kernels for 9%

profile of v2, /device:TPU:0, one launch (start us, length us, event | category | flops | bytes accessed | tf_op | source)
XLA Modules:
  0.0 1065.9 jit_solution(98720722884033159)
XLA Ops:
  7.2 30.9 %turn_1.1 = bf16[2048,512]{1,0:T(8,128)(2,1)} custom-call(bf16[256,4096]{1,0:T(8,128)(2,1)} %src.2), custom_call_target="tpu_custom_call" | custom-call | tf_op jit(solution)/shard_map/turn_1/pallas_call | solution.py:685
  38.2 2.2 multiply_reduce_fusion.2
  42.2 1.8 fusion.1.act
  44.0 1.2 pad_maximum_fusion.refs_0_
  45.9 35.3 %scatter_product_3.1 = (f32[256,1536]{1,0:T(8,128)}, f32[8,8,128]{2,1,0:T(8,128)}) custom-call(bf16[2048,512]{1,0:T(8,128)(2,1)} %fusion.1.act, bf16[512,1536]{1,0:T(8,128)(2,1)} %pad_maximum_fusion.refs_0_, f32[8,8,128]{2,1,0:T(8,128)} %broadcast_in_dim.16.refs_1_), custom_call_target="tpu_custom_call" | custom-call | tf_op jit(solution)/shard_map/scatter_product_3/pallas_call | solution.py:392
  81.2 1.6 broadcast_multiply_fusion
  83.7 1.4 reshape.205
  85.2 1.3 fusion.57
  86.5 1.0 multiply_sine_fusion
  88.0 10.1 all_gather.12
  98.3 0.8 copy-done.6
  99.5 2.1 fusion.60
  101.6 1.9 convolution_convert_fusion.3
  104.4 33.7 %turn_2.1.act = bf16[2048,512]{1,0:T(8,128)(2,1)} custom-call(bf16[256,4096]{1,0:T(8,128)(2,1)} %src.3), custom_call_target="tpu_custom_call" | custom-call | tf_op jit(solution)/shard_map/turn_2/pallas_call | solution.py:685
  138.1 67.1 %scatter_product_5.1 = (f32[256,3072]{1,0:T(8,128)}, f32[8,8,128]{2,1,0:T(8,128)}) custom-call(bf16[2048,512]{1,0:T(8,128)(2,1)} %turn_2.1.act, bf16[3072,512]{1,0:T(8,128)(2,1)} %refs_0_.4, f32[8,8,128]{2,1,0:T(8,128)} %broadcast_in_dim.16.refs_1_), custom_call_target="tpu_custom_call" | custom-call | tf_op jit(solution)/shard_map/scatter_product_5/pallas_call | solution.py:392
  205.3 1.9 fusion.33
  207.1 6.2 convolution_convert_fusion.own
  213.3 62.4 %line_sum_4.1 = bf16[2048,512]{1,0:T(8,128)(2,1)} custom-call(bf16[2048,512]{1,0:T(8,128)(2,1)} %convolution_convert_fusion.own), custom_call_target="tpu_custom_call" | custom-call | tf_op jit(solution)/shard_map/line_sum_4/pallas_call | solution.py:496
  275.7 4.4 multiply_reduce_fusion.1
  280.8 115.8 %scatter_product_6.1 = (f32[256,6144]{1,0:T(8,128)}, f32[8,8,128]{2,1,0:T(8,128)}) custom-call(bf16[2048,512]{1,0:T(8,128)(2,1)} %get-tuple-element.46.act, bf16[512,3072]{1,0:T(8,128)(2,1)} %w0.1, bf16[512,3072]{1,0:T(8,128)(2,1)} %w1.1, f32[8,8,128]{2,1,0:T(8,128)} %pad.8.refs_2_), custom_call_target="tpu_custom_call" | custom-call | tf_op jit(solution)/shard_map/scatter_product_6/pallas_call | solution.py:392
  397.4 7.4 add_reduce_fusion
  405.4 1.5 multiply_convert_fusion.2.g0
  406.9 2.4 copy.87.act_t
  409.2 119.4 %gather_product_7.1 = (f32[2048,512]{1,0:T(8,128)}, f32[512,3072]{1,0:T(8,128)}, f32[512,3072]{1,0:T(8,128)}, f32[8,8,128]{2,1,0:T(8,128)}) custom-call(bf16[512,2048]{1,0:T(8,128)(2,1)} %copy.87.act_t, bf16[512,3072]{1,0:T(8,128)(2,1)} %w0.1, bf16[512,3072]{1,0:T(8,128)(2,1)} %w1.1, bf16[256,3072]{1,0:T(8,128)(2,1)} %multiply_convert_fusion.2.g0, ...), custom_call_target="tpu_custom_call" | custom-call | tf_op jit(solution)/shard_map/gather_product_7/pallas_call | solution.py:631
  529.4 5.7 subtract_convert_fusion.own
  535.1 61.0 %line_sum_8.1 = bf16[2048,512]{1,0:T(8,128)(2,1)} custom-call(bf16[2048,512]{1,0:T(8,128)(2,1)} %subtract_convert_fusion.own), custom_call_target="tpu_custom_call" | custom-call | tf_op jit(solution)/shard_map/line_sum_8/pallas_call | solution.py:496
  596.1 4.1 fusion.5.act
  600.2 26.5 %scatter_product_9.1 = (f32[256,1024]{1,0:T(8,128)}, f32[8,8,128]{2,1,0:T(8,128)}) custom-call(bf16[2048,512]{1,0:T(8,128)(2,1)} %fusion.5.act, bf16[1024,512]{1,0:T(8,128)(2,1)} %refs_0_.5, f32[8,8,128]{2,1,0:T(8,128)} %broadcast_in_dim.16.refs_1_), custom_call_target="tpu_custom_call" | custom-call | tf_op jit(solution)/shard_map/scatter_product_9/pallas_call | solution.py:392
  626.7 1.3 convert_element_type.192
  628.3 2.3 fusion.16
  631.1 1.5 convolution_multiply_fusion
  632.6 1.2 convolution_bitcast_fusion.1
  635.5 0.9 fusion.21
  637.4 1.1 multiply_add_fusion.2
  638.6 3.3 convert_multiply_fusion.5
  644.3 1.3 copy.104
  645.7 1.1 pad_maximum_fusion.1
  647.6 5.8 fusion.65
  653.4 55.4 %all-gather.8.cloned.1.call-done = bf16[2048,2432]{0,1:T(8,128)(2,1)} async-done(((bf16[256,2432]{0,1:T(8,128)(2,1)}), bf16[2048,2432]{0,1:T(8,128)(2,1)}) %all-gather.8.cloned.1.call-update) | async-done | bytes 9961488 | tf_op jit(solution)/shard_map/all_gather | solution.py:702
  708.8 7.9 slice_convert_fusion
  716.7 14.8 %reshape.211 = f32[4,2,256,2,640]{2,1,0,4,3:T(2,128)} reshape(f32[2048,1280]{0,1:T(8,128)} %slice_convert_fusion) | data formatting | bytes 20971520 | tf_op jit(solution)/shard_map/convert_element_type | solution.py:855
  731.5 17.4 %reduce_sum.119 = f32[4,256,2,640]{1,0,3,2:T(4,128)} reduce(f32[4,2,256,2,640]{2,1,0,4,3:T(2,128)} %reshape.211, f32[]{:T(128)} %constant.22.clone.1), dimensions={1}, to_apply=%region_12.13 | reduce | flops 1310720 | bytes 15728644 | tf_op jit(solution)/shard_map/reduce_sum | solution.py:855
  748.9 7.3 copy.105
  756.2 4.5 convolution_convert_fusion.2
  760.7 22.6 %all-gather.6.cloned.1.call-done = bf16[2048,3072]{1,0:T(8,128)(2,1)} async-done(((bf16[256,3072]{1,0:T(8,128)(2,1)}), bf16[2048,3072]{1,0:T(8,128)(2,1)}) %all-gather.6.cloned.1.call-update) | async-done | bytes 12582928 | tf_op jit(solution)/shard_map/all_gather | solution.py:702
  783.3 11.7 %convolution_convert_fusion.1 = bf16[2048,512]{1,0:T(8,128)(2,1)} fusion(bf16[2048,3072]{1,0:T(8,128)(2,1)} %all-gather.6.cloned.1.call-done, bf16[3072,512]{1,0:T(8,128)(2,1)} %refs_0_.4), kind=kOutput, calls=%fused_computation.40 | convolution fusion | flops 6443499520 | bytes 17825792 | tf_op jit(solution)/shard_map/dot_general | solution.py:51
  795.1 6.6 fusion.8
  801.7 2.3 slice.150
  804.0 1.6 copy.125
  805.5 1.2 add_reduce_fusion.1
  806.7 6.0 fusion.6
  812.8 11.6 %fusion.66 = f32[3072,512]{1,0:T(8,128)} fusion(bf16[2048,3072]{1,0:T(8,128)(2,1)} %all-gather.6.cloned.1.call-done, bf16[2048,512]{1,0:T(8,128)(2,1)S(1)} %copy-done.2), kind=kOutput, calls=%fused_computation.128 | convolution fusion | flops 6442450944 | bytes 20971520 | tf_op jit(solution)/shard_map/dot_general | solution.py:61
  824.3 75.0 %all-reduce.5.cloned.1.call-done = (bf16[2048,512]{1,0:T(8,128)(2,1)}, bf16[512,512]{1,0:T(8,128)(2,1)}) async-done(((bf16[2048,512]{1,0:T(8,128)(2,1)}, bf16[512,512]{1,0:T(8,128)(2,1)}), (bf16[2048,512]{1,0:T(8,128)(2,1)}, bf16[512,512]{1,0:T(8,128)(2,1)})) %all-reduce.5.cloned.1.call-update) | async-done | bytes 2621456 | tf_op jit(solution)/shard_map/psum | solution.py:816
  899.3 8.5 fusion.4
  907.9 9.5 psum.22
  918.0 59.0 %line_sum_11.1 = bf16[2048,512]{1,0:T(8,128)(2,1)} custom-call(bf16[2048,512]{1,0:T(8,128)(2,1)} %get-tuple-element.43.own), custom_call_target="tpu_custom_call" | custom-call | tf_op jit(solution)/shard_map/line_sum_11/pallas_call | solution.py:496
  976.9 5.0 add_convert_fusion.src
  982.0 29.4 %turn_12.1 = bf16[256,4096]{1,0:T(8,128)(2,1)} custom-call(bf16[2048,512]{1,0:T(8,128)(2,1)} %add_convert_fusion.src), custom_call_target="tpu_custom_call" | custom-call | tf_op jit(solution)/shard_map/turn_12/pallas_call | solution.py:685
  1011.4 4.1 convert_element_type.207
  1015.5 28.9 %turn_10.1 = bf16[256,4096]{1,0:T(8,128)(2,1)} custom-call(bf16[2048,512]{1,0:T(8,128)(2,1)} %get-tuple-element.44.src), custom_call_target="tpu_custom_call" | custom-call | tf_op jit(solution)/shard_map/turn_10/pallas_call | solution.py:685
  1044.4 2.1 convert_element_type.209
  1046.5 3.3 copy.136
  1049.8 6.4 copy.137
  1056.2 2.7 copy.138
  (152 shorter events, 15.2 us)
Async XLA Ops:
  7.2 200.0 %all-gather.4.cloned.1.call-start = ((), (), s32[]{:S(2)}) async-start(), calls=%async_computation | async-start | bytes 4718592 | tf_op jit(solution)/shard_map/all_gather | solution.py:702
  38.1 4.1 copy-start
  38.1 5.9 copy-start.12
  38.1 5.9 copy-start.23
  41.6 3.6 copy-start.30
  81.2 1.8 copy-start.29
  82.8 3.7 copy-start.40
  82.9 4.7 copy-start.43
  82.9 4.8 copy-start.42
  83.7 3.8 copy-start.32
  87.6 11.6 %copy-start.18 = (f32[256,128]{1,0:T(8,128)}, f32[256,128]{1,0:T(8,128)S(1)}, u32[]{:S(2)}) copy-start(f32[256,128]{1,0:T(8,128)S(1)} %get-tuple-element.37) | copy-start | bytes 393220
  87.6 11.6 %copy-start.20 = (f32[256,128]{1,0:T(8,128)}, f32[256,128]{1,0:T(8,128)S(1)}, u32[]{:S(2)}) copy-start(f32[256,128]{1,0:T(8,128)S(1)} %get-tuple-element.38) | copy-start | bytes 393220
  98.1 3.5 copy-start.10
  98.3 0.8 copy-start.6
  98.3 1.0 copy-start.8
  99.3 4.3 copy-start.14
  99.5 4.1 copy-start.28
  101.6 2.0 copy-start.36
  101.6 2.2 copy-start.44
  103.6 605.2 %all-gather.8.cloned.1.call-start = ((), (), s32[]{:S(2)}) async-start(), calls=%async_computation.2 | async-start | bytes 11206656 | tf_op jit(solution)/shard_map/all_gather | solution.py:702
  404.8 2.1 copy-start.4
  628.2 2.3 copy-start.25
  628.2 2.5 copy-start.11
  628.2 2.5 copy-start.37
  630.7 1.9 copy-start.15
  631.1 3.1 copy-start.7
  631.1 3.1 copy-start.9
  633.9 0.9 copy-start.19
  633.9 1.0 copy-start.21
  634.8 0.7 copy-start.34
  635.0 1.8 copy-start.33
  635.0 1.8 copy-start.41
  635.5 3.1 copy-start.39
  636.4 1.0 copy-start.22
  636.4 2.2 copy-start.16
  641.9 1.2 copy-start.35
  642.1 1.2 copy-start.26
  642.1 1.2 copy-start.27
  642.5 3.2 copy-start.38
  642.5 3.2 copy-start.17
  644.3 3.3 copy-start.5
  646.8 136.5 %all-gather.6.cloned.1.call-start = ((), (), s32[]{:S(2)}) async-start(), calls=%async_computation.1 | async-start | bytes 14155776 | tf_op jit(solution)/shard_map/all_gather | solution.py:702
  647.5 251.8 %all-reduce.5.cloned.1.call-start = ((), (), s32[]{:S(2)}) async-start(), calls=%async_computation.3 | async-start | bytes 5242880 | tf_op jit(solution)/shard_map/psum | solution.py:816
  748.9 7.3 copy-start.3
  760.7 34.4 %copy-start.24 = (bf16[512,1024]{1,0:T(8,128)(2,1)S(1)}, bf16[512,1024]{1,0:T(8,128)(2,1)}, u32[]{:S(2)}) copy-start(bf16[512,1024]{1,0:T(8,128)(2,1)} %param.14) | copy-start | bytes 3145732
  806.7 6.1 copy-start.2
  812.7 86.6 %copy-start.1 = (bf16[2048,512]{1,0:T(8,128)(2,1)S(1)}, bf16[2048,512]{1,0:T(8,128)(2,1)}, u32[]{:S(2)}) copy-start(bf16[2048,512]{1,0:T(8,128)(2,1)} %turn_1.1) | copy-start | bytes 6291460
  812.7 86.6 %copy-start.13 = (bf16[512,512]{1,0:T(8,128)(2,1)S(1)}, bf16[512,512]{1,0:T(8,128)(2,1)}, u32[]{:S(2)}) copy-start(bf16[512,512]{1,0:T(8,128)(2,1)} %param.15) | copy-start | bytes 1572868
  812.8 86.6 %copy-start.31 = (f32[512]{0:T(512)S(1)}, f32[512]{0:T(512)}, u32[]{:S(2)}) copy-start(f32[512]{0:T(512)} %copy-done.30) | copy-start | bytes 6148
  1046.5 9.7 slice-start
  1049.8 6.4 slice-start.1
Sparse Core Ops, SparseCore 0:
  103.7 55.0 all-gather.3
  646.9 61.8 all-gather.7
  711.3 71.9 all-gather.5
  795.2 104.0 all-reduce.4

commit v3 on v2

--- a/solution.py
+++ b/solution.py
@@ -261,11 +261,20 @@
         return dp * 2 + seq
 
 
-def greet(peers):
+def greet(peers, line=None):
     barrier = pltpu.get_barrier_semaphore()
     for peer in peers:
         pl.semaphore_signal(barrier, inc=1, device_id=peer, device_id_type=MESH)
-    pl.semaphore_wait(barrier, len(peers))
+    if line is None:
+        pl.semaphore_wait(barrier, len(peers))
+        return
+    pl.semaphore_signal(barrier, inc=1, device_id=line.mate, device_id_type=MESH)
+
+    @pl.when(line.inner == 1)
+    def _():
+        pl.semaphore_signal(barrier, inc=1, device_id=line.other, device_id_type=MESH)
+
+    pl.semaphore_wait(barrier, len(peers) + 1 + line.inner)
 
 
 def remote(src, dst, send, recv, peer):
@@ -274,15 +283,116 @@
     )
 
 
-def scatter_kernel(rows, width, counts, nt, shared, act, *refs):
-    w0 = refs[0]
-    w1 = w0 if shared else refs[1]
-    tiny, out, tiny_all, held, sib_out, sib_in, from_x, from_y, sib_send, sib_recv = refs[1 if shared else 2 :][:10]
-    x_send, x_recv, y_send, y_recv, tiny_send, tiny_recv = refs[-6:]
+class Line:
+    def __init__(self, here, counts, refs, place=None):
+        self.own, self.out, self.from_end, self.mine, self.from_mid = refs[:5]
+        self.sems = refs[5:11]
+        self.counts = counts
+        self.chunk = self.own.shape[0] // counts
+        self.place = place
+        z = here.z
+        self.inner = ((z + 1) // 2) % 2
+        self.mate = (here.dp, here.seq, z + 1 - 2 * (z % 2))
+        self.other = (here.dp, here.seq, 3 - z)
+
+    def rows(self, at):
+        at = at if self.place is None else self.place(at)
+        return pl.ds(pl.multiple_of(at * self.chunk, self.chunk), self.chunk)
+
+    def up(self, at):
+        return remote(self.own.at[self.rows(at), :], self.from_end.at[at], self.sems[0].at[at],
+                      self.sems[1].at[at], self.mate)
+
+    def over(self, at):
+        return remote(self.mine.at[at], self.from_mid.at[at], self.sems[2].at[at], self.sems[3].at[at],
+                      self.other)
+
+    def down(self, at):
+        rows = self.rows(at)
+        return remote(self.out.at[rows, :], self.out.at[rows, :], self.sems[4].at[at],
+                      self.sems[5].at[at], self.mate)
+
+    def begin(self):
+        @pl.when(self.inner == 0)
+        def _():
+            def send(at, _):
+                self.up(at).start()
+                return 0
+
+            lax.fori_loop(0, self.counts, send, 0)
+
+    def first(self, at):
+        rows = self.rows(at)
+        self.up(at).wait_recv()
+        total = self.own[rows, :].astype(jnp.float32) + self.from_end[at].astype(jnp.float32)
+        self.mine[at] = total.astype(self.mine.dtype)
+        self.over(at).start()
+
+    def second(self, at):
+        rows = self.rows(at)
+        self.over(at).wait_recv()
+        total = self.mine[at].astype(jnp.float32) + self.from_mid[at].astype(jnp.float32)
+        self.out[rows, :] = total.astype(self.out.dtype)
+        self.down(at).start()
+
+    def step(self, at):
+        @pl.when(jnp.logical_and(self.inner == 1, at < self.counts))
+        def _():
+            self.first(at)
+
+        @pl.when(jnp.logical_and(self.inner == 1, jnp.logical_and(at > 1, at < self.counts + 2)))
+        def _():
+            self.second(at - 2)
+
+    def end(self, done=0):
+        def rest(at, _):
+            self.step(at)
+            return 0
+
+        lax.fori_loop(min(done, self.counts + 2), self.counts + 2, rest, 0)
+
+        @pl.when(self.inner == 0)
+        def _():
+            def take(at, _):
+                self.up(at).wait_send()
+                self.down(at).wait_recv()
+                return 0
+
+            lax.fori_loop(0, self.counts, take, 0)
+
+        @pl.when(self.inner == 1)
+        def _():
+            def drain(at, _):
+                self.over(at).wait_send()
+                self.down(at).wait_send()
+                return 0
+
+            lax.fori_loop(0, self.counts, drain, 0)
+
+
+def line_scratch(counts, shape, low):
+    buf = pltpu.VMEM((counts, shape[0] // counts, shape[1]), low)
+    return [buf, buf, buf] + [pltpu.SemaphoreType.DMA((counts,))] * 6
+
+
+def scatter_kernel(rows, width, counts, nt, shared, line_counts, act, *refs):
+    refs = list(refs)
     here = Place()
+    w0 = refs.pop(0)
+    w1 = w0 if shared else refs.pop(0)
+    tiny = refs.pop(0)
+    line_own = refs.pop(0) if line_counts else None
+    out, tiny_all = refs.pop(0), refs.pop(0)
+    line = None
+    if line_counts:
+        line = Line(here, line_counts, [line_own, refs.pop(0)] + refs[13:])
+    held, sib_out, sib_in, from_x, from_y, sib_send, sib_recv = refs[:7]
+    x_send, x_recv, y_send, y_recv, tiny_send, tiny_recv = refs[7:13]
     sib, xdev, ydev = here.device(0, 1), here.device(1, 0), here.device(2, 0)
     peers = [here.device(a, o) for a in range(4) for o in range(2) if a + o > 0]
-    greet(peers)
+    greet(peers, line)
+    if line:
+        line.begin()
     weights = (w0, w1)
 
     def tiny_copy(at):
@@ -320,7 +430,7 @@
 
     step_of = {0: 0, 1: 1, 3: 2}
 
-    for stage, streams in enumerate(stages):
+    for order, (stage, streams) in enumerate(enumerate(stages)):
         def compute(at, stage=stage, streams=streams):
             for stream, (across, half) in enumerate(streams):
                 sib_out[stage, stream, at] = product(across, 1, half, at).astype(jnp.bfloat16)
@@ -347,7 +457,7 @@
                 to_x(step_of[stage], at, stage).start()
                 to_y(step_of[stage], at, stage).start()
 
-        def body(at, _, compute=compute, finish=finish, stage=stage):
+        def body(at, _, compute=compute, finish=finish, stage=stage, order=0):
             compute(at)
             for stream in range(2):
                 to_sib(stage, stream, at).start()
@@ -355,10 +465,15 @@
             @pl.when(at > 0)
             def _():
                 finish(at - 1)
+
+            if line:
+                line.step(order * counts + at)
             return 0
 
-        lax.fori_loop(0, counts, body, 0)
+        lax.fori_loop(0, counts, functools.partial(body, order=order), 0)
         finish(counts - 1)
+    if line:
+        line.end(4 * counts)
 
     def last(at, _):
         for half in range(2):
@@ -380,7 +495,7 @@
         tiny_copy(at).wait()
 
 
-def scatter_product(act, weights, tiny, width, nt, cid):
+def scatter_product(act, weights, tiny, width, nt, cid, line=None, line_counts=16):
     total, depth = act.shape
     rows = total // 8
     shared = len(weights) == 1
@@ -389,196 +504,149 @@
     low = jnp.bfloat16
     dma = pltpu.SemaphoreType.DMA
     vm = pl.BlockSpec(memory_space=pltpu.VMEM)
+    out_shape = [
+        jax.ShapeDtypeStruct((rows, 2 * half), jnp.float32),
+        jax.ShapeDtypeStruct(tiny.shape, jnp.float32),
+    ]
+    scratch = [
+        pltpu.VMEM((4, 2, counts, rows, width), low),
+        pltpu.VMEM((4, 2, counts, rows, width), low),
+        pltpu.VMEM((4, 2, counts, rows, width), low),
+        pltpu.VMEM((3, counts, rows, width), low),
+        pltpu.VMEM((3, counts, rows, width), low),
+        dma((4, 2, counts)), dma((4, 2, counts)),
+        dma((3, counts)), dma((3, counts)), dma((3, counts)), dma((3, counts)),
+        dma((7,)), dma((7,)),
+    ]
+    operands = [act, *weights, tiny]
+    if line is not None:
+        operands.append(line)
+        out_shape.append(jax.ShapeDtypeStruct(line.shape, line.dtype))
+        scratch += line_scratch(line_counts, line.shape, line.dtype)
     return pl.pallas_call(
-        functools.partial(scatter_kernel, rows, width, counts, nt, shared),
-        out_shape=(
-            jax.ShapeDtypeStruct((rows, 2 * half), jnp.float32),
-            jax.ShapeDtypeStruct(tiny.shape, jnp.float32),
-        ),
-        in_specs=[vm] * (2 + len(weights)),
-        out_specs=(vm, vm),
-        scratch_shapes=[
-            pltpu.VMEM((4, 2, counts, rows, width), low),
-            pltpu.VMEM((4, 2, counts, rows, width), low),
-            pltpu.VMEM((4, 2, counts, rows, width), low),
-            pltpu.VMEM((3, counts, rows, width), low),
-            pltpu.VMEM((3, counts, rows, width), low),
-            dma((4, 2, counts)), dma((4, 2, counts)),
-            dma((3, counts)), dma((3, counts)), dma((3, counts)), dma((3, counts)),
-            dma((7,)), dma((7,)),
-        ],
+        functools.partial(scatter_kernel, rows, width, counts, nt, shared,
+                          0 if line is None else line_counts),
+        out_shape=out_shape,
+        in_specs=[vm] * len(operands),
+        out_specs=[vm] * len(out_shape),
+        scratch_shapes=scratch,
         compiler_params=pltpu.CompilerParams(collective_id=cid, has_side_effects=True,
                                              vmem_limit_bytes=VMEM_LIMIT),
         name=f"scatter_product_{cid}",
-    )(act, *weights, tiny)
-
-
-def line_kernel(chunk, counts, own, out, from_end, mine, from_mid, end_send, end_recv, mid_send, mid_recv,
-                back_send, back_recv):
+    )(*operands)
+
+
+def gather_kernel(rows, width, counts, down, give_cols, n_own, n_out, line_counts, act, *refs):
+    refs = list(refs)
     here = Place()
-    z = here.z
-    outer = jnp.logical_or(z == 0, z == 3)
-    mate = z + 1 - 2 * (z % 2)
-    other = 3 - z
-    mate_dev = (here.dp, here.seq, mate)
-    other_dev = (here.dp, here.seq, other)
-
-    def rows(at):
-        return pl.ds(pl.multiple_of(at * chunk, chunk), chunk)
-
-    def up(at):
-        return remote(own.at[rows(at), :], from_end.at[at], end_send.at[at], end_recv.at[at], mate_dev)
-
-    def over(at):
-        return remote(mine.at[at], from_mid.at[at], mid_send.at[at], mid_recv.at[at], other_dev)
-
-    def down(at):
-        return remote(out.at[rows(at), :], out.at[rows(at), :], back_send.at[at], back_recv.at[at], mate_dev)
-
-    barrier = pltpu.get_barrier_semaphore()
-    pl.semaphore_signal(barrier, inc=1, device_id=mate_dev, device_id_type=MESH)
-
-    @pl.when(outer)
-    def _():
-        pl.semaphore_wait(barrier, 1)
-
-        def send(at, _):
-            up(at).start()
-            return 0
-
-        def take(at, _):
-            up(at).wait_send()
-            down(at).wait_recv()
-            return 0
-
-        lax.fori_loop(0, counts, send, 0)
-        lax.fori_loop(0, counts, take, 0)
-
-    @pl.when(jnp.logical_not(outer))
-    def _():
-        pl.semaphore_signal(barrier, inc=1, device_id=other_dev, device_id_type=MESH)
-        pl.semaphore_wait(barrier, 2)
-
-        def second(at):
-            over(at).wait_recv()
-            out[rows(at), :] = (mine[at].astype(jnp.float32) + from_mid[at].astype(jnp.float32)).astype(out.dtype)
-            down(at).start()
-
-        def first(at, _):
-            up(at).wait_recv()
-            mine[at] = (own[rows(at), :].astype(jnp.float32) + from_end[at].astype(jnp.float32)).astype(mine.dtype)
-            over(at).start()
-
-            @pl.when(at > 1)
-            def _():
-                second(at - 2)
-            return 0
-
-        lax.fori_loop(0, counts, first, 0)
-        second(counts - 2)
-        second(counts - 1)
-
-        def drain(at, _):
-            over(at).wait_send()
-            down(at).wait_send()
-            return 0
-
-        lax.fori_loop(0, counts, drain, 0)
-
-
-def line_sum(own, cid, counts=16):
-    total, width = own.shape
-    chunk = total // counts
-    low = own.dtype
-    dma = pltpu.SemaphoreType.DMA
-    vm = pl.BlockSpec(memory_space=pltpu.VMEM)
-    buf = pltpu.VMEM((counts, chunk, width), low)
-    return pl.pallas_call(
-        functools.partial(line_kernel, chunk, counts),
-        out_shape=jax.ShapeDtypeStruct((total, width), low),
-        in_specs=[vm],
-        out_specs=vm,
-        scratch_shapes=[buf, buf, buf] + [dma((counts,))] * 6,
-        compiler_params=pltpu.CompilerParams(collective_id=cid, has_side_effects=True,
-                                             vmem_limit_bytes=VMEM_LIMIT),
-        name=f"line_sum_{cid}",
-    )(own)
-
-
-def gather_kernel(rows, width, counts, act_t, w0, w1, g0, g1, tiny, d_act, gw0, gw1, tiny_all, got,
-                  x_send, x_recv, y_send, y_recv, sib_send, sib_recv, tiny_send, tiny_recv):
-    here = Place()
+    weights = [refs.pop(0) for _ in range(n_own)]
+    payload = [refs.pop(0) for _ in range(n_own)]
+    give = refs.pop(0) if give_cols else None
+    tiny = refs.pop(0)
+    line_own = refs.pop(0) if line_counts else None
+    sums = refs.pop(0)
+    grads = [refs.pop(0) for _ in range(n_out)]
+    tiny_all = refs.pop(0)
+    line_out = refs.pop(0) if line_counts else None
+    got, x_send, x_recv, y_send, y_recv, sib_send, sib_recv, tiny_send, tiny_recv, own_sem = refs[:10]
+    refs = refs[10:]
+    if give_cols:
+        taken, give_sems = refs[:2]
+        refs = refs[2:]
+    line = Line(here, line_counts, [line_own, line_out] + refs) if line_counts else None
     sib, xdev, ydev = here.device(0, 1), here.device(1, 0), here.device(2, 0)
     peers = [here.device(a, o) for a in range(4) for o in range(2) if a + o > 0]
-    greet(peers)
     core = here.core
-    own, weights, grads = (g0, g1), (w0, w1), (gw0, gw1)
+    half_cols = counts * width
+
+    def part(half, at):
+        first = half * half_cols if n_own == 1 else 0
+        return pl.ds(pl.multiple_of(first + at * width, width), width)
+
+    def weight(half):
+        return weights[half if n_own > 1 else 0]
+
+    def own_copy(half, at):
+        src = payload[half if n_own > 1 else 0].at[:, part(half, at)]
+        return pltpu.make_async_copy(src, got.at[0, core, half, at], own_sem.at[half, at])
+
+    for half in range(2):
+        for at in range(counts):
+            own_copy(half, at).start()
+    greet(peers, line)
     stages = (((1, 0), (2, 1)), ((1, 1), (2, 0)), ((3, 1), (3, 0)))
 
-    def part(half, at):
-        return own[half].at[:, pl.ds(pl.multiple_of(at * width, width), width)]
-
     def x_copy(step, at):
-        src = part(step, at) if step < 2 else got.at[2, core, 1, at]
+        src = got.at[0, core, step, at] if step < 2 else got.at[2, core, 1, at]
         dst = got.at[1, core, step, at] if step < 2 else got.at[3, core, 1, at]
         return remote(src, dst, x_send.at[step, at], x_recv.at[step, at], xdev)
 
     def y_copy(step, at):
-        src = part(1 - step, at) if step < 2 else got.at[1, core, 0, at]
+        src = got.at[0, core, 1 - step, at] if step < 2 else got.at[1, core, 0, at]
         dst = got.at[2, core, 1 - step, at] if step < 2 else got.at[3, core, 0, at]
         return remote(src, dst, y_send.at[step, at], y_recv.at[step, at], ydev)
 
     def sib_copy(stage, stream, at):
-        if stage == 3:
-            src, (across, half) = part(stream, at), (0, stream)
-        else:
-            across, half = stages[stage][stream]
-            src = got.at[across, core, half, at]
-        return remote(src, got.at[across, core, half, at], sib_send.at[stage, stream, at],
-                      sib_recv.at[stage, stream, at], sib)
-
-    def tiny_copy(at, peer):
-        return remote(tiny, tiny_all.at[here.shard(0, 0)], tiny_send.at[at], tiny_recv.at[at], peer)
-
-    def begin(at, _):
+        across, half = (0, stream) if stage == 3 else stages[stage][stream]
+        slot = got.at[across, core, half, at]
+        return remote(slot, slot, sib_send.at[stage, stream, at], sib_recv.at[stage, stream, at], sib)
+
+    def tiny_copy(at):
+        return remote(tiny, tiny_all.at[here.shard(0, 0)], tiny_send.at[at], tiny_recv.at[at], peers[at])
+
+    if give_cols:
+        given = remote(give, taken, give_sems.at[0], give_sems.at[1], ydev)
+        given.start()
+    if line:
+        line.begin()
+    for at in range(counts):
+        for half in range(2):
+            own_copy(half, at).wait()
+    if give_cols:
+        given.wait()
+        for at in range(give_cols // width):
+            slot = counts - give_cols // width + at
+            more = taken[:, at * width : (at + 1) * width].astype(jnp.float32)
+            got[0, core, 1, slot] = (got[0, core, 1, slot].astype(jnp.float32) + more).astype(got.dtype)
+    sums[...] = jnp.zeros_like(sums)
+    for at in range(counts):
         x_copy(0, at).start()
         y_copy(0, at).start()
-        return 0
-
-    def begin_sib(at, _):
+    for at in range(counts):
         sib_copy(3, 0, at).start()
         sib_copy(3, 1, at).start()
-        return 0
-
-    for at, peer in enumerate(peers):
-        tiny_copy(at, peer).start()
-    lax.fori_loop(0, counts, begin, 0)
-    lax.fori_loop(0, counts, begin_sib, 0)
+    for at in range(7):
+        tiny_copy(at).start()
     tiny_all[here.shard(0, 0)] = tiny[...]
-    d_act[...] = jnp.zeros_like(d_act)
-
-    def blocks(across, half, at, mine):
-        cols = pl.ds(pl.multiple_of(at * width, width), width)
+
+    def blocks(across, half, at, fresh):
         gained = None
+        cols = part(half, at)
         for other in range(2):
             row = pl.ds(pl.multiple_of(here.shard(across, other) * rows, rows), rows)
-            if mine and other == 0:
-                block = own[half][:, cols]
+            block = got[across, (core + other) % 2, half, at]
+            if down:
+                sums[row, :] += jnp.dot(block, weight(half)[cols, :], preferred_element_type=jnp.float32)
+                more = lax.dot_general(block, act[row, :], (((0,), (0,)), ((), ())),
+                                       preferred_element_type=jnp.float32)
             else:
-                block = got[across, (core + other) % 2, half, at]
-            d_act[row, :] += lax.dot_general(block, weights[half][:, cols], (((1,), (1,)), ((), ())),
-                                             preferred_element_type=jnp.float32)
-            more = jnp.dot(act_t[:, row], block, preferred_element_type=jnp.float32)
+                sums[row, :] += lax.dot_general(block, weight(half)[:, cols], (((1,), (1,)), ((), ())),
+                                                preferred_element_type=jnp.float32)
+                more = jnp.dot(act[:, row], block, preferred_element_type=jnp.float32)
             gained = more if gained is None else gained + more
-        if mine:
-            grads[half][:, cols] = gained
+        grad = grads[half if n_out > 1 else 0]
+        where = (cols, slice(None)) if down else (slice(None), cols)
+        if fresh:
+            grad[where] = gained
         else:
-            grads[half][:, cols] += gained
+            grad[where] += gained
 
     def own_step(at, _):
         for half in range(2):
             sib_copy(3, half, at).wait_recv()
             blocks(0, half, at, True)
+        if line:
+            line.step(at)
         return 0
 
     lax.fori_loop(0, counts, own_step, 0)
@@ -601,10 +669,15 @@
             @pl.when(at > 0)
             def _():
                 work(stage, at - 1)
+
+            if line:
+                line.step((stage + 1) * counts + at)
             return 0
 
         lax.fori_loop(0, counts, body, 0)
         work(stage, counts - 1)
+    if line:
+        line.end(4 * counts)
 
     def drain(at, _):
         for step in range(3):
@@ -616,37 +689,53 @@
         return 0
 
     lax.fori_loop(0, counts, drain, 0)
-    for at, peer in enumerate(peers):
-        tiny_copy(at, peer).wait()
-
-
-def gather_product(act_t, w0, w1, g0, g1, tiny, width, cid):
-    depth, total = act_t.shape
-    rows, half = g0.shape
+    for at in range(7):
+        tiny_copy(at).wait()
+
+
+def gather_product(act, weights, payload, tiny, width, down, cid, give=None, line=None, line_counts=16):
+    total, depth = act.shape if down else act.shape[::-1]
+    rows = payload[0].shape[0]
+    half = payload[0].shape[1] // (2 if len(payload) == 1 else 1)
     counts = half // width
     low = jnp.bfloat16
+    f32 = jnp.float32
     dma = pltpu.SemaphoreType.DMA
     vm = pl.BlockSpec(memory_space=pltpu.VMEM)
-    f32 = jnp.float32
+    hbm = pl.BlockSpec(memory_space=pl.ANY)
+    out_shape = [jax.ShapeDtypeStruct((total, depth), f32)]
+    out_shape += [jax.ShapeDtypeStruct(w.shape, f32) for w in weights]
+    out_shape.append(jax.ShapeDtypeStruct((8,) + tiny.shape, f32))
+    scratch = [
+        pltpu.VMEM((4, 2, 2, counts, rows, width), low),
+        dma((3, counts)), dma((3, counts)), dma((3, counts)), dma((3, counts)),
+        dma((4, 2, counts)), dma((4, 2, counts)), dma((7,)), dma((7,)), dma((2, counts)),
+    ]
+    operands = [act, *weights, *payload]
+    specs = [vm] * (1 + len(weights)) + [hbm] * len(payload)
+    if give is not None:
+        operands.append(give)
+        specs.append(vm)
+        scratch += [pltpu.VMEM(give.shape, low), dma((2,))]
+    operands.append(tiny)
+    specs.append(vm)
+    if line is not None:
+        operands.append(line)
+        specs.append(vm)
+        out_shape.append(jax.ShapeDtypeStruct(line.shape, line.dtype))
+        scratch += line_scratch(line_counts, line.shape, line.dtype)
     return pl.pallas_call(
-        functools.partial(gather_kernel, rows, width, counts),
-        out_shape=(
-            jax.ShapeDtypeStruct((total, depth), f32),
-            jax.ShapeDtypeStruct((depth, half), f32),
-            jax.ShapeDtypeStruct((depth, half), f32),
-            jax.ShapeDtypeStruct((8,) + tiny.shape, f32),
-        ),
-        in_specs=[vm] * 6,
-        out_specs=(vm,) * 4,
-        scratch_shapes=[
-            pltpu.VMEM((4, 2, 2, counts, rows, width), low),
-            dma((3, counts)), dma((3, counts)), dma((3, counts)), dma((3, counts)),
-            dma((4, 2, counts)), dma((4, 2, counts)), dma((7,)), dma((7,)),
-        ],
+        functools.partial(gather_kernel, rows, width, counts, down,
+                          0 if give is None else give.shape[1], len(weights), len(weights),
+                          0 if line is None else line_counts),
+        out_shape=out_shape,
+        in_specs=specs,
+        out_specs=[vm] * len(out_shape),
+        scratch_shapes=scratch,
         compiler_params=pltpu.CompilerParams(collective_id=cid, has_side_effects=True,
                                              vmem_limit_bytes=VMEM_LIMIT),
         name=f"gather_product_{cid}",
-    )(act_t, w0, w1, g0, g1, tiny)
+    )(*operands)
 
 
 def turn_kernel(rows, cols, back, src, out, own_sem, send, recv):
@@ -694,16 +783,126 @@
     )(src)
 
 
+def close_kernel(rows, cols, per, own, rest, other_own, out, other_out, summed, ready, local_sem, other_send,
+                 other_recv, put_send, put_recv, *line_refs):
+    here = Place()
+    me = here.shard(0, 0)
+    counts = 8 * per
+
+    def target(at):
+        turn_at = at // per
+        return 3 - turn_at // 2, 1 - turn_at % 2
+
+    def place(at):
+        across, other = target(at)
+        return here.shard(across, other) * per + at % per
+
+    line = Line(here, counts, [own, summed] + list(line_refs), place)
+    peers = [(a, o) for a in (3, 2, 1, 0) for o in (1, 0) if a + o > 0]
+    greet([here.device(a, o) for a, o in peers], line)
+    line.begin()
+    columns = pl.ds(pl.multiple_of(me * cols, cols), cols)
+
+    def turn_copy(at):
+        across, other = peers[at]
+        src = other_own.at[pl.ds(pl.multiple_of(here.shard(across, other) * rows, rows), rows), :]
+        return remote(src, other_out.at[:, columns], other_send.at[at], other_recv.at[at],
+                      here.device(across, other))
+
+    for at in range(7):
+        turn_copy(at).start()
+    mine = pltpu.make_async_copy(other_own.at[pl.ds(pl.multiple_of(me * rows, rows), rows), :],
+                                 other_out.at[:, columns], local_sem)
+    mine.start()
+    chunk = line.chunk
+
+    def put(at):
+        across, other = target(at)
+        dst = out.at[pl.ds(pl.multiple_of(at % per * chunk, chunk), chunk), columns]
+        return remote(ready.at[at], dst, put_send.at[at], put_recv.at[at], here.device(across, other))
+
+    def emit(at):
+        total = rest[line.rows(at), :] + summed[line.rows(at), :].astype(jnp.float32)
+
+        @pl.when(at < 7 * per)
+        def _():
+            ready[at] = total.astype(ready.dtype)
+            put(at).start()
+
+        @pl.when(at >= 7 * per)
+        def _():
+            out[pl.ds(pl.multiple_of(at % per * chunk, chunk), chunk), columns] = total.astype(out.dtype)
+
+    @pl.when(line.inner == 1)
+    def _():
+        def both(at, _):
+            line.step(at)
+
+            @pl.when(at > 1)
+            def _():
+                emit(at - 2)
+            return 0
+
+        lax.fori_loop(0, counts + 2, both, 0)
+
+        def drain(at, _):
+            line.over(at).wait_send()
+            line.down(at).wait_send()
+            return 0
+
+        lax.fori_loop(0, counts, drain, 0)
+
+    @pl.when(line.inner == 0)
+    def _():
+        def take(at, _):
+            line.up(at).wait_send()
+            line.down(at).wait_recv()
+            emit(at)
+            return 0
+
+        lax.fori_loop(0, counts, take, 0)
+
+    mine.wait()
+    for at in range(7):
+        turn_copy(at).wait()
+
+    def finish(at, _):
+        put(at).wait()
+        return 0
+
+    lax.fori_loop(0, 7 * per, finish, 0)
+
+
+def close(own, rest, other_own, cid, per=2):
+    total, cols = own.shape
+    rows = total // 8
+    low = own.dtype
+    dma = pltpu.SemaphoreType.DMA
+    vm = pl.BlockSpec(memory_space=pltpu.VMEM)
+    whole = jax.ShapeDtypeStruct((rows, 8 * cols), low)
+    counts = 8 * per
+    return pl.pallas_call(
+        functools.partial(close_kernel, rows, cols, per),
+        out_shape=[whole, whole],
+        in_specs=[vm] * 3,
+        out_specs=[vm] * 2,
+        scratch_shapes=[
+            pltpu.VMEM((total, cols), low),
+            pltpu.VMEM((7 * per, rows // per, cols), low),
+            dma(()), dma((7,)), dma((7,)), dma((7 * per,)), dma((7 * per,)),
+        ] + line_scratch(counts, own.shape, low),
+        compiler_params=pltpu.CompilerParams(collective_id=cid, has_side_effects=True,
+                                             vmem_limit_bytes=VMEM_LIMIT),
+        name=f"close_{cid}",
+    )(own, rest, other_own)
+
+
 AXES = ("dp", "seq")
 LANES = 128
 
 
 def gather_rows(block):
     return lax.all_gather(block, AXES, axis=0, tiled=True)
-
-
-def lane_sums(values):
-    return jnp.sum(values.reshape(values.shape[0], -1, LANES), axis=1)
 
 
 def pack_rows(values):
@@ -776,8 +975,9 @@
         .astype(low)
     )
     mixed_all = gather_rows(mixed)
-    attn = line_sum(matmul(mixed_all, w_out).astype(low), 4)
-    d_hidden = scatter_product(g_low, (w_down,), none, 512, True, 5)[0]
+    d_hidden, _, attn = scatter_product(
+        g_low, (w_down,), none, 512, True, 4, line=matmul(mixed_all, w_out).astype(low)
+    )
     resid = x_col + attn.astype(jnp.float32)
     act_two = (resid * gain_two).astype(low)
     squares = pack_rows(jnp.sum(resid * resid, axis=-1))
@@ -796,25 +996,29 @@
     dots_own = jnp.pad(dots_two.reshape(-1, LANES), ((0, 8 - rows // LANES), (0, 0)))
     d_act_two, grad_gate, grad_up, dots_all = gather_product(
         act_two.T,
-        w_gate,
-        w_up,
-        (d_gate * rms_two).astype(low),
-        (d_up * rms_two).astype(low),
+        (w_gate, w_up),
+        ((d_gate * rms_two).astype(low), (d_up * rms_two).astype(low)),
         dots_own,
         512,
+        False,
         7,
     )
-    hidden_all = gather_rows(hidden)
     dot_two = dots_all[:, : rows // LANES].reshape(parts * rows, 1)
     grad_gain_two = jnp.sum(d_act_two * resid, axis=0)
-    d_norm = line_sum((d_act_two * gain_two - resid * dot_two).astype(low), 8)
+    ffn, grad_down, _, d_norm = gather_product(
+        g_low,
+        (w_down,),
+        (hidden,),
+        none[0],
+        256,
+        True,
+        8,
+        line=(d_act_two * gain_two - resid * dot_two).astype(low),
+    )
     d_resid = g_low.astype(jnp.float32) + d_norm.astype(jnp.float32)
     d_attn = d_resid.astype(low)
     d_mixed = scatter_product(d_attn, (w_out,), none, 256, True, 9)[0]
     d_mixed = d_mixed.astype(low).reshape(rows, heads, HD)
-    grad_down = matmul_tn(hidden_all, g_low)
-    ffn = lax.psum(matmul(hidden_all, w_down).astype(low), "tensor")
-    out = turn((resid + ffn.astype(jnp.float32)).astype(low), True, 10)
     grad_out = matmul_tn(mixed_all, d_attn)
 
     d_probs = jnp.einsum("rhd,kd->hrk", d_mixed, values_all, preferred_element_type=jnp.float32)
@@ -827,44 +1031,55 @@
         rotate_back(d_queries, own_cos[:, None, :], own_sin[:, None, :]).reshape(rows, heads * HD)
         * rms_one
     ).astype(low)
-    query_dots = lane_sums(
-        (d_queries * queries.astype(jnp.float32)).reshape(rows, heads * HD)
+    query_dots = jnp.sum(
+        (d_queries * queries.astype(jnp.float32)).reshape(rows, heads * HD), axis=1, keepdims=True
     ) * (rms_one * rms_one / (width * scale_factor))
     d_keys = jnp.einsum("hrk,rhd->kd", d_scores, queries, preferred_element_type=jnp.float32)
     d_values = jnp.einsum("hrk,rhd->kd", probs_low, d_mixed, preferred_element_type=jnp.float32)
-    kv_dots = lane_sums(
-        jnp.concatenate(
-            [d_keys * keys.astype(jnp.float32), d_values * values_all.astype(jnp.float32)], axis=1
-        )
+    kv_dots = jnp.sum(
+        d_keys * keys.astype(jnp.float32) + d_values * values_all.astype(jnp.float32),
+        axis=1,
+        keepdims=True,
     ) * (rms_group * rms_group / width)
     d_kv = jnp.concatenate(
+        [rotate_back(d_keys, cos_table, sin_table) * rms_group, d_values * rms_group], axis=1
+    ).astype(low)
+    away = rows - offset
+    own_dots = query_dots + lax.dynamic_slice_in_dim(kv_dots, offset, rows, 0)
+    dots_one = jnp.concatenate(
         [
-            rotate_back(d_keys, cos_table, sin_table) * rms_group,
-            d_values * rms_group,
-            kv_dots,
-        ],
-        axis=1,
-    ).astype(low)
-    kvw = d_kv.shape[1]
-    pieces = [d_kv[at * rows : (at + 1) * rows] for at in range(seqs)]
-    home = gather_rows(
-        jnp.concatenate([d_query_pre, query_dots.astype(low)] + pieces, axis=1)
-    )
-    d_query_all = home[:, :qw]
-    kv_parts = home[:, qw + LANES :].reshape(parts // seqs, seqs, rows, seqs, kvw)
-    kv_sum = jnp.sum(kv_parts.astype(jnp.float32), axis=1)
-    kv_sum = jnp.transpose(kv_sum, (0, 2, 1, 3)).reshape(parts * rows, kvw)
-    d_kv_all = kv_sum[:, : 2 * HD].astype(low)
-    dot_one = jnp.sum(
-        home[:, qw : qw + LANES].astype(jnp.float32) + kv_sum[:, 2 * HD :], axis=-1, keepdims=True
-    )
-    d_act_one = matmul_nt(d_query_all, w_query) + matmul_nt(d_kv_all, kv_weight)
+            own_dots.reshape(-1, LANES),
+            lax.dynamic_slice_in_dim(kv_dots, away, rows, 0).reshape(-1, LANES),
+        ]
+    )
+    tiles = rows // LANES
+    d_act_one, grad_qkv, dots_all, ffn_sum = gather_product(
+        act_one.T,
+        (w_qkv,),
+        (jnp.concatenate([d_query_pre, lax.dynamic_slice_in_dim(d_kv, offset, rows, 0)], axis=1),),
+        jnp.pad(dots_one, ((0, 8 - 2 * tiles), (0, 0))),
+        256,
+        False,
+        11,
+        give=lax.dynamic_slice_in_dim(d_kv, away, rows, 0),
+        line=ffn.astype(low),
+    )
+    pairs = dots_all.reshape(parts // 2, 2, 8, LANES)
+    dot_one = (pairs[:, :, :tiles] + pairs[:, ::-1, tiles : 2 * tiles]).reshape(parts * rows, 1)
     grad_gain_one = jnp.sum(d_act_one * x_col, axis=0)
-    d_norm_one = line_sum((d_act_one * gain_one - x_col * dot_one).astype(low), 11)
-    d_tokens = turn((d_resid + d_norm_one.astype(jnp.float32)).astype(low), True, 12)
-    grad_query = matmul_tn(act_one, d_query_all)
-    grad_kv = lax.psum(matmul_tn(act_one, d_kv_all).astype(low), "tensor").astype(jnp.float32)
-    gains = lax.psum(jnp.stack([grad_gain_one, grad_gain_two]), "tensor")
+    d_tokens, out = close(
+        (d_act_one * gain_one - x_col * dot_one).astype(low),
+        d_resid,
+        (resid + ffn_sum.astype(jnp.float32)).astype(low),
+        12,
+    )
+    grad_query = grad_qkv[:, :qw]
+    sums = jnp.concatenate(
+        [grad_qkv[:, qw:], jnp.stack([grad_gain_one, grad_gain_two]), jnp.zeros((14, width // parts))]
+    )
+    sums = lax.psum(sums.astype(low), "tensor").astype(jnp.float32)
+    grad_kv = sums[: width // parts]
+    gains = sums[width // parts :]
     return (
         out,
         d_tokens.astype(jnp.float32),

time: 1070 us -> 838 us (0.78)
  waiting for transfers between devices: 154 us -> 41.5 us
  matrix products: 73.3 us -> 19.6 us
  Pallas kernels: 669 us -> 637 us
  other arithmetic: 80.8 us -> 62.3 us
    all_gather x3 -> x1, waiting for transfers between devices: 78 us -> 10.9 us  [gather_rows(): return lax.all_gather(block, AXES, axis=0, tiled=True)]
    pallas_call x4 -> x2, Pallas kernels: 123 us -> 64.5 us  [turn(): pl.pallas_call(functools.partial(turn_kernel, rows, cols, back), out_shap...]
    psum x1, waiting for transfers between devices: 75 us -> 30.5 us  [acts_move(): sums = lax.psum(sums.astype(low), 'tensor').astype(jnp.float32)]
    pallas_call x4, Pallas kernels: 302 us -> 328 us  [the longest x3 263 us: gather_product(): pl.pallas_call(functools.partial(gather_kernel, rows, width, counts, down...]
    dot_general x4 -> x1, matrix products: 27.9 us -> 3.65 us  [matmul_tn(): lax.dot_general(left, right, (((0,), (0,)), ((), ())), preferred_element_...]
    dot_general x2 -> x0, matrix products: 15.1 us -> none  [matmul_nt(): lax.dot_general(left, right, (((1,), (1,)), ((), ())), preferred_element_...]
    convert_element_type x1 -> x0, local copies, waits for them, and re-layouts: 14.8 us -> none  [acts_move(): kv_sum = jnp.sum(kv_parts.astype(jnp.float32), axis=1)]
    convert_element_type x6 -> x3, other arithmetic: 24.8 us -> 10.7 us  [the longest x1 5.68 us: acts_move(): (d_act_two * gain_two - resid * dot_two).astype(low)]
  transfers between devices with their start and end apart: 4 -> 2, of which waited for: 3 -> 2; matrix products, arithmetic and copies ran while one was open for 8% -> 2% of each run, Pallas kernels for 9% -> 4%
where the time goes in v3:
time: 838 us; the launch traced here: 831 us
  Pallas kernels  637 us (76%)
  other arithmetic  62.3 us (7%)
  local copies, waits for them, and re-layouts  45.3 us (5%)
  waiting for transfers between devices  41.5 us (5%)
  matrix products  19.6 us (2%)
  between operations  15.2 us (2%)
  blocking collectives  10.1 us (1%)
    pallas_call x3, Pallas kernels, gather_product(): pl.pallas_call(functools.partial(gather_kernel, rows, width, counts, down...  263 us
    pallas_call x4, Pallas kernels, scatter_product(): pl.pallas_call(functools.partial(scatter_kernel, rows, width, counts, nt,...  244 us
    pallas_call x1, Pallas kernels, close(): pl.pallas_call(functools.partial(close_kernel, rows, cols, per), out_shap...  65.6 us
    pallas_call x2, Pallas kernels, turn(): pl.pallas_call(functools.partial(turn_kernel, rows, cols, back), out_shap...  64.5 us
    psum x1, waiting for transfers between devices, acts_move(): sums = lax.psum(sums.astype(low), 'tensor').astype(jnp.float32)  30.5 us
    unnamed x93, local copies, waits for them, and re-layouts  20 us
  transfers between devices with their start and end apart: 2, of which 2 were waited for; matrix products, arithmetic and copies ran while one was open for 2% of the time, Pallas kernels for 4%

profile of v3, /device:TPU:0, one launch (start us, length us, event | category | flops | bytes accessed | tf_op | source)
XLA Modules:
  0.0 830.9 jit_solution(13862692926626032448)
XLA Ops:
  7.8 2.7 multiply_reduce_fusion.2
  10.4 30.9 %turn_1.1 = bf16[2048,512]{1,0:T(8,128)(2,1)} custom-call(bf16[256,4096]{1,0:T(8,128)(2,1)} %src.2), custom_call_target="tpu_custom_call" | custom-call | tf_op jit(solution)/shard_map/turn_1/pallas_call | solution.py:774
  41.3 0.8 convert_element_type.147
  42.1 1.3 subtract_convert_fusion.2
  43.4 2.3 constant_dynamic-update-slice_fusion.1
  45.7 1.9 constant_dynamic-update-slice_fusion.refs_0_
  47.5 1.8 fusion.1.act
  49.9 35.3 %scatter_product_3.1 = (f32[256,1536]{1,0:T(8,128)}, f32[8,8,128]{2,1,0:T(8,128)}) custom-call(bf16[2048,512]{1,0:T(8,128)(2,1)} %fusion.1.act, bf16[512,1536]{1,0:T(8,128)(2,1)} %constant_dynamic-update-slice_fusion.refs_0_, f32[8,8,128]{2,1,0:T(8,128)} %broadcast_in_dim.20.refs_1_), custom_call_target="tpu_custom_call" | custom-call | tf_op jit(solution)/shard_map/scatter_product_3/pallas_call | solution.py:526
  85.2 1.6 broadcast_multiply_fusion
  87.9 1.4 reshape.233
  89.3 1.3 fusion.54
  90.6 1.0 multiply_sine_fusion
  92.1 10.1 %all_gather.6 = bf16[512,640]{1,0:T(8,128)(2,1)S(1)} all-gather(bf16[256,640]{1,0:T(8,128)(2,1)S(1)} %concatenate.40), channel_id=1, replica_groups=mesh['dp'=4,'seq'=2,'tensor'=4] {'seq'}, dimensions={0}, use_global_device_ids=true | all-gather | bytes 983040 | tf_op jit(solution)/shard_map/all_gather | solution.py:959
  102.6 0.8 copy-done.5
  103.6 2.1 fusion.56
  105.7 1.9 convolution_convert_fusion.1
  108.5 33.6 %turn_2.1.act = bf16[2048,512]{1,0:T(8,128)(2,1)} custom-call(bf16[256,4096]{1,0:T(8,128)(2,1)} %src.3), custom_call_target="tpu_custom_call" | custom-call | tf_op jit(solution)/shard_map/turn_2/pallas_call | solution.py:774
  142.2 2.1 fusion.74
  144.3 2.4 copy.84.act
  146.7 0.7 pad.18.clone
  147.3 10.9 %all-gather.2.cloned.1.call-done = bf16[2048,1024]{0,1:T(8,128)(2,1)} async-done(((bf16[256,1024]{0,1:T(8,128)(2,1)}), bf16[2048,1024]{0,1:T(8,128)(2,1)}) %all-gather.2.cloned.1.call-update) | async-done | bytes 4194320 | tf_op jit(solution)/shard_map/all_gather | solution.py:905
  158.2 5.9 convolution_convert_fusion.refs_2_
  164.1 67.0 %scatter_product_4.1 = (f32[256,3072]{1,0:T(8,128)}, f32[8,8,128]{2,1,0:T(8,128)}, bf16[2048,512]{1,0:T(8,128)(2,1)}) custom-call(bf16[2048,512]{1,0:T(8,128)(2,1)} %turn_2.1.act, bf16[3072,512]{1,0:T(8,128)(2,1)} %refs_0_.8, f32[8,8,128]{2,1,0:T(8,128)} %broadcast_in_dim.20.refs_1_, bf16[2048,512]{1,0:T(8,128)(2,1)} %convolution_convert_fusion.refs_2_), custom_call_target="tpu_custom_call" | custom-call | tf_op jit(solution)/shard_map/scatter_product_4/pallas_call | solution.py:526
  231.1 3.2 multiply_reduce_fusion.1
  234.3 0.7 pad.12.refs_2_
  234.9 0.7 copy-done.3
  235.6 2.4 copy.67.act
  237.9 115.5 %scatter_product_6.1 = (f32[256,6144]{1,0:T(8,128)}, f32[8,8,128]{2,1,0:T(8,128)}) custom-call(bf16[2048,512]{1,0:T(8,128)(2,1)} %copy-done.3, bf16[512,3072]{1,0:T(8,128)(2,1)} %refs_0_.7, bf16[512,3072]{1,0:T(8,128)(2,1)} %refs_1_.3, f32[8,8,128]{2,1,0:T(8,128)} %pad.12.refs_2_), custom_call_target="tpu_custom_call" | custom-call | tf_op jit(solution)/shard_map/scatter_product_6/pallas_call | solution.py:526
  353.4 0.8 slice_reduce_fusion
  354.2 7.4 add_reduce_fusion
  362.2 1.5 multiply_convert_fusion.2.refs_2_
  363.7 119.2 %gather_product_7.1 = (f32[2048,512]{1,0:T(8,128)}, f32[512,3072]{1,0:T(8,128)}, f32[512,3072]{1,0:T(8,128)}, f32[8,8,128]{2,1,0:T(8,128)}) custom-call(bf16[512,2048]{1,0:T(8,128)(2,1)} %copy.67.act, bf16[512,3072]{1,0:T(8,128)(2,1)} %refs_0_.7, bf16[512,3072]{1,0:T(8,128)(2,1)} %refs_1_.3, bf16[256,3072]{1,0:T(8,128)(2,1)} %multiply_convert_fusion.2.refs_2_, ...), custom_call_target="tpu_custom_call" | custom-call | tf_op jit(solution)/shard_map/gather_product_7/pallas_call | solution.py:727
  483.0 0.8 slice.111
  483.8 5.7 subtract_convert_fusion.refs_3_
  490.0 69.4 %gather_product_8.1 = (f32[2048,512]{1,0:T(8,128)}, f32[3072,512]{1,0:T(8,128)}, f32[8,8,128]{2,1,0:T(8,128)}, bf16[2048,512]{1,0:T(8,128)(2,1)}) custom-call(bf16[2048,512]{1,0:T(8,128)(2,1)} %turn_2.1.act, bf16[3072,512]{1,0:T(8,128)(2,1)} %refs_0_.8, bf16[256,3072]{1,0:T(8,128)(2,1)} %get-tuple-element.60.refs_1_, f32[8,128]{1,0:T(8,128)} %squeeze.9.refs_2_, ...), custom_call_target="tpu_custom_call" | custom-call | tf_op jit(solution)/shard_map/gather_product_8/pallas_call | solution.py:727
  559.4 5.7 convert_add_fusion.1
  565.2 26.3 %scatter_product_9.1 = (f32[256,1024]{1,0:T(8,128)}, f32[8,8,128]{2,1,0:T(8,128)}) custom-call(bf16[2048,512]{1,0:T(8,128)(2,1)} %get-tuple-element.64.act, bf16[1024,512]{1,0:T(8,128)(2,1)} %refs_0_.9, f32[8,8,128]{2,1,0:T(8,128)} %broadcast_in_dim.20.refs_1_), custom_call_target="tpu_custom_call" | custom-call | tf_op jit(solution)/shard_map/scatter_product_9/pallas_call | solution.py:526
  591.6 1.4 convert_element_type.170
  593.2 2.2 fusion.11
  595.7 0.7 copy-done.14
  596.9 2.9 add_reduce_fusion.1
  599.8 1.9 multiply_add_fusion.2
  602.1 3.8 convert_element_type.178.refs_4_
  606.2 0.7 copy-done.6
  608.5 1.2 multiply_multiply_fusion.3
  610.1 0.8 fusion.21
  611.4 0.9 pad_maximum_fusion.refs_1_
  612.4 73.9 %gather_product_11.1 = (f32[2048,512]{1,0:T(8,128)}, f32[512,1536]{1,0:T(8,128)}, f32[8,8,128]{2,1,0:T(8,128)}, bf16[2048,512]{1,0:T(8,128)(2,1)}) custom-call(bf16[512,2048]{1,0:T(8,128)(2,1)} %copy.84.act, bf16[512,1536]{1,0:T(8,128)(2,1)} %constant_dynamic-update-slice_fusion.refs_0_, bf16[256,1536]{1,0:T(8,128)(2,1)} %pad_maximum_fusion.refs_1_, ...), custom_call_target="tpu_custom_call" | custom-call | tf_op jit(solution)/shard_map/gather_product_11/pallas_call | solution.py:727
  686.3 2.1 slice.226
  688.4 3.3 slice.122
  691.8 6.8 fusion.4
  698.6 65.6 %close_12.1 = (bf16[256,4096]{1,0:T(8,128)(2,1)}, bf16[256,4096]{1,0:T(8,128)(2,1)}) custom-call(bf16[2048,512]{1,0:T(8,128)(2,1)} %get-tuple-element.61.own, f32[2048,512]{1,0:T(8,128)} %get-tuple-element.63.rest, bf16[2048,512]{1,0:T(8,128)(2,1)} %get-tuple-element.62.other_own), custom_call_target="tpu_custom_call" | custom-call | tf_op jit(solution)/shard_map/close_12/pallas_call | solution.py:884
  764.1 0.7 stack.8
  764.8 0.7 stack.9
  765.5 2.0 maximum_maximum_fusion
  767.5 4.2 convert_element_type.182
  771.8 3.6 fusion.61
  775.5 30.5 %all-reduce.5.cloned.1.call-done = bf16[528,512]{1,0:T(8,128)(2,1)} async-done(((bf16[528,512]{1,0:T(8,128)(2,1)}), bf16[528,512]{1,0:T(8,128)(2,1)}) %all-reduce.5.cloned.1.call-update) | async-done | bytes 540688 | tf_op jit(solution)/shard_map/psum | solution.py:1080
  806.0 1.4 fusion.55
  807.4 2.1 slice.143
  809.5 1.3 copy.115
  810.8 6.9 copy.116
  817.8 2.8 copy.117
  820.9 2.7 copy.118
  (135 shorter events, 9.8 us)
Async XLA Ops:
  7.2 151.0 %all-gather.2.cloned.1.call-start = ((), (), s32[]{:S(2)}) async-start(), calls=%async_computation | async-start | bytes 4718592 | tf_op jit(solution)/shard_map/all_gather | solution.py:905
  41.3 6.2 copy-start
  42.1 7.2 copy-start.24
  85.2 1.7 copy-start.26
  87.8 2.8 copy-start.27
  87.9 2.8 copy-start.34
  89.3 2.4 copy-start.37
  89.3 2.5 copy-start.36
  91.7 10.9 %copy-start.15 = (f32[256,128]{1,0:T(8,128)}, f32[256,128]{1,0:T(8,128)S(1)}, u32[]{:S(2)}) copy-start(f32[256,128]{1,0:T(8,128)S(1)} %get-tuple-element.55) | copy-start | bytes 393220
  91.7 10.9 %copy-start.17 = (f32[256,128]{1,0:T(8,128)}, f32[256,128]{1,0:T(8,128)S(1)}, u32[]{:S(2)}) copy-start(f32[256,128]{1,0:T(8,128)S(1)} %get-tuple-element.56) | copy-start | bytes 393220
  102.2 3.5 copy-start.9
  102.4 3.3 copy-start.23
  102.5 0.8 copy-start.5
  102.6 1.0 copy-start.7
  103.6 2.1 copy-start.13
  105.7 2.0 copy-start.32
  105.7 2.2 copy-start.38
  107.7 698.3 %all-reduce.5.cloned.1.call-start = ((), (), s32[]{:S(2)}) async-start(), calls=%async_computation.1 | async-start | bytes 1081344 | tf_op jit(solution)/shard_map/psum | solution.py:1080
  144.3 13.9 %copy-start.19 = (bf16[1024,512]{1,0:T(8,128)(2,1)S(1)}, bf16[1024,512]{1,0:T(8,128)(2,1)}, u32[]{:S(2)}) copy-start(bf16[1024,512]{1,0:T(8,128)(2,1)} %refs_0_.9) | copy-start | bytes 3145732
  234.3 1.3 copy-start.3
  591.5 1.6 copy-start.10
  591.6 1.6 copy-start.33
  593.2 2.2 copy-start.11
  595.4 1.0 copy-start.14
  596.9 2.9 copy-start.28
  596.9 2.9 copy-start.35
  605.9 1.0 copy-start.6
  605.9 1.2 copy-start.8
  605.9 1.4 copy-start.29
  605.9 1.4 copy-start.16
  605.9 1.4 copy-start.18
  607.4 0.7 copy-start.30
  607.7 2.2 copy-start.20
  607.7 2.2 copy-start.21
  607.7 2.2 copy-start.22
  686.3 5.4 copy-start.31
  688.4 3.3 copy-start.1
  688.4 3.4 copy-start.2
  688.4 3.4 copy-start.25
  767.5 4.3 copy-start.4
  767.5 4.3 copy-start.39
  775.5 34.1 %copy-start.12 = (bf16[256,4096]{1,0:T(8,128)(2,1)S(1)}, bf16[256,4096]{1,0:T(8,128)(2,1)}, u32[]{:S(2)}) copy-start(bf16[256,4096]{1,0:T(8,128)(2,1)} %get-tuple-element.104) | copy-start | bytes 6291460
  809.5 8.3 slice-start
  810.8 6.9 slice-start.1
  810.8 9.8 %slice-start.2 = ((s8[6291456]{0:T(1024)(128)(4,1)}), s8[4194304]{0:T(1024)(128)(4,1)S(1)}, s32[]{:S(2)}) async-start(s8[6291456]{0:T(1024)(128)(4,1)} %bitcast.116), calls=%async_computation.4 | async-start | bytes 8388608
  817.8 3.1 slice-start.3
Sparse Core Ops, SparseCore 0:
  107.8 50.3 all-gather.1
  767.6 38.3 all-reduce.4

commit v4 on v0

--- a/solution.py
+++ b/solution.py
@@ -1,8 +1,11 @@
+import functools
 import math
 
 import jax
 import jax.numpy as jnp
 from jax import lax
+from jax.experimental import pallas as pl
+from jax.experimental.pallas import tpu as pltpu
 from jax.sharding import PartitionSpec as P
 
 HD = 256
@@ -69,7 +72,7 @@
     return rms_val * (scaled - normed * jnp.mean(scaled * normed, axis=-1, keepdims=True))
 
 
-def shards(
+def weights_move(
     tokens, seg_ids, gain_attn, w_query, kv_weight, w_out, gain_ffn, w_gate, w_up, w_down, d_out
 ):
     rows = tokens.shape[0]
@@ -235,6 +238,1085 @@
     )
 
 
+MESH = pl.DeviceIdType.MESH
+VMEM_LIMIT = 66000 * 1024
+
+
+class Place:
+    def __init__(self):
+        self.dp = lax.axis_index("dp")
+        self.seq = lax.axis_index("seq")
+        self.z = lax.axis_index("tensor")
+        self.core = lax.rem(self.dp, 2)
+        self.chip = lax.div(self.dp, 2)
+
+    def device(self, across, other):
+        chip = (self.chip + across) % 2
+        seq = (self.seq + across // 2) % 2
+        core = (self.core + other) % 2
+        return chip * 2 + core, seq, self.z
+
+    def shard(self, across, other):
+        dp, seq, _ = self.device(across, other)
+        return dp * 2 + seq
+
+
+def greet(here, peers, line=False):
+    barrier = pltpu.get_barrier_semaphore()
+    peers = list(peers)
+    if line:
+        peers += [(here.dp, here.seq, (here.z + step) % 4) for step in range(1, 4)]
+    for peer in peers:
+        pl.semaphore_signal(barrier, inc=1, device_id=peer, device_id_type=MESH)
+    pl.semaphore_wait(barrier, len(peers))
+
+
+def remote(src, dst, send, recv, peer):
+    return pltpu.make_async_remote_copy(
+        src_ref=src, dst_ref=dst, send_sem=send, recv_sem=recv, device_id=peer, device_id_type=MESH
+    )
+
+
+class Line:
+    def __init__(self, here, counts, refs, place=None):
+        self.own, self.out, self.from_end, self.mine, self.from_mid = refs[:5]
+        self.sems = refs[5:11]
+        self.counts = counts
+        self.chunk = self.own.shape[0] // counts
+        self.place = place
+        z = here.z
+        self.inner = ((z + 1) // 2) % 2
+        self.mate = (here.dp, here.seq, z + 1 - 2 * (z % 2))
+        self.other = (here.dp, here.seq, 3 - z)
+
+    def rows(self, at):
+        at = at if self.place is None else self.place(at)
+        return pl.ds(pl.multiple_of(at * self.chunk, self.chunk), self.chunk)
+
+    def up(self, at):
+        return remote(self.own.at[self.rows(at), :], self.from_end.at[at], self.sems[0].at[at],
+                      self.sems[1].at[at], self.mate)
+
+    def over(self, at):
+        return remote(self.mine.at[at], self.from_mid.at[at], self.sems[2].at[at], self.sems[3].at[at],
+                      self.other)
+
+    def down(self, at):
+        rows = self.rows(at)
+        return remote(self.out.at[rows, :], self.out.at[rows, :], self.sems[4].at[at],
+                      self.sems[5].at[at], self.mate)
+
+    def begin(self):
+        @pl.when(self.inner == 0)
+        def _():
+            def send(at, _):
+                self.up(at).start()
+                return 0
+
+            lax.fori_loop(0, self.counts, send, 0)
+
+    def first(self, at):
+        rows = self.rows(at)
+        self.up(at).wait_recv()
+        total = self.own[rows, :].astype(jnp.float32) + self.from_end[at].astype(jnp.float32)
+        self.mine[at] = total.astype(self.mine.dtype)
+        self.over(at).start()
+
+    def second(self, at):
+        rows = self.rows(at)
+        self.over(at).wait_recv()
+        total = self.mine[at].astype(jnp.float32) + self.from_mid[at].astype(jnp.float32)
+        self.out[rows, :] = total.astype(self.out.dtype)
+        self.down(at).start()
+
+    def step(self, at):
+        @pl.when(jnp.logical_and(self.inner == 1, at < self.counts))
+        def _():
+            self.first(at)
+
+        @pl.when(jnp.logical_and(self.inner == 1, jnp.logical_and(at > 1, at < self.counts + 2)))
+        def _():
+            self.second(at - 2)
+
+    def end(self, done=0):
+        def rest(at, _):
+            self.step(at)
+            return 0
+
+        lax.fori_loop(min(done, self.counts + 2), self.counts + 2, rest, 0)
+
+        @pl.when(self.inner == 0)
+        def _():
+            def take(at, _):
+                self.up(at).wait_send()
+                self.down(at).wait_recv()
+                return 0
+
+            lax.fori_loop(0, self.counts, take, 0)
+
+        @pl.when(self.inner == 1)
+        def _():
+            def drain(at, _):
+                self.over(at).wait_send()
+                self.down(at).wait_send()
+                return 0
+
+            lax.fori_loop(0, self.counts, drain, 0)
+
+
+def line_scratch(counts, shape, low):
+    buf = pltpu.VMEM((counts, shape[0] // counts, shape[1]), low)
+    return [buf, buf, buf] + [pltpu.SemaphoreType.DMA((counts,))] * 6
+
+
+def turned(at):
+    return 3 - at // 2, 1 - at % 2
+
+
+def slice_peers(here):
+    return [here.device(*turned(at)) for at in range(7)]
+
+
+def kernel_call(kernel, out_shape, operands, specs, scratch, cid, name):
+    vm = pl.BlockSpec(memory_space=pltpu.VMEM)
+    return pl.pallas_call(
+        kernel,
+        out_shape=out_shape,
+        in_specs=specs,
+        out_specs=[vm] * len(out_shape),
+        scratch_shapes=scratch,
+        compiler_params=pltpu.CompilerParams(
+            collective_id=cid, has_side_effects=True, vmem_limit_bytes=VMEM_LIMIT
+        ),
+        name=f"{name}_{cid}",
+    )(*operands)
+
+
+class Tiny:
+    def __init__(self, here, src, dst, sems, spread):
+        self.here, self.src, self.dst, self.sems, self.spread = here, src, dst, sems, spread
+        self.peers = slice_peers(here)
+        self.me = here.shard(0, 0)
+
+    def tile(self, shard):
+        return self.src.at[shard] if self.spread else self.src
+
+    def copy(self, at):
+        return remote(self.tile(self.here.shard(*turned(at))), self.dst.at[self.me], self.sems[0].at[at],
+                      self.sems[1].at[at], self.peers[at])
+
+    def begin(self):
+        for at in range(7):
+            self.copy(at).start()
+        self.dst[self.me] = self.tile(self.me)[...]
+
+    def end(self):
+        for at in range(7):
+            self.copy(at).wait()
+
+
+class Reduce:
+    def __init__(self, here, counts, width, product, out, refs):
+        self.counts, self.width, self.product, self.out = counts, width, product, out
+        self.held, self.sib_out, self.sib_in, self.from_x, self.from_y = refs[:5]
+        self.sib_sems, self.x_sems, self.y_sems = refs[5:7], refs[7:9], refs[9:11]
+        self.sib, self.xdev, self.ydev = here.device(0, 1), here.device(1, 0), here.device(2, 0)
+        self.stages = (((3, 0), (3, 1)), ((1, 0), (2, 1)), ((0, 0), (0, 1)), ((1, 1), (2, 0)))
+
+    def to_sib(self, stage, stream, at):
+        spot = (stage, stream, at)
+        return remote(self.sib_out.at[spot], self.sib_in.at[spot], self.sib_sems[0].at[spot],
+                      self.sib_sems[1].at[spot], self.sib)
+
+    def to_x(self, step, at, stage=0):
+        return remote(self.held.at[stage, 0, at], self.from_x.at[step, at], self.x_sems[0].at[step, at],
+                      self.x_sems[1].at[step, at], self.xdev)
+
+    def to_y(self, step, at, stage=0):
+        return remote(self.held.at[stage, 1, at], self.from_y.at[step, at], self.y_sems[0].at[step, at],
+                      self.y_sems[1].at[step, at], self.ydev)
+
+    def cols(self, half, at):
+        return pl.ds(pl.multiple_of((half * self.counts + at) * self.width, self.width), self.width)
+
+    def compute(self, stage, at):
+        for stream, (across, half) in enumerate(self.stages[stage]):
+            self.sib_out[stage, stream, at] = self.product(across, 1, half, at).astype(jnp.bfloat16)
+            self.held[stage, stream, at] = self.product(across, 0, half, at).astype(jnp.bfloat16)
+        for stream in range(2):
+            self.to_sib(stage, stream, at).start()
+
+    def finish(self, stage, at):
+        for stream in range(2):
+            self.to_sib(stage, stream, at).wait_recv()
+            total = self.held[stage, stream, at].astype(jnp.float32)
+            total += self.sib_in[stage, stream, at].astype(jnp.float32)
+            if stage == 3 and stream == 0:
+                self.to_y(0, at).wait_recv()
+                total += self.from_y[0, at].astype(jnp.float32)
+            if stage == 3 and stream == 1:
+                self.to_x(0, at).wait_recv()
+                total += self.from_x[0, at].astype(jnp.float32)
+            if stage == 2:
+                self.out[:, self.cols(stream, at)] = total
+            else:
+                self.held[stage, stream, at] = total.astype(jnp.bfloat16)
+        if stage != 2:
+            step = (0, 1, None, 2)[stage]
+            self.to_x(step, at, stage).start()
+            self.to_y(step, at, stage).start()
+
+    def run(self, line=None):
+        for stage in range(4):
+            def body(at, _, stage=stage):
+                self.compute(stage, at)
+
+                @pl.when(at > 0)
+                def _():
+                    self.finish(stage, at - 1)
+
+                if line:
+                    line.step(stage * self.counts + at)
+                return 0
+
+            lax.fori_loop(0, self.counts, body, 0)
+            self.finish(stage, self.counts - 1)
+
+    def end(self):
+        def last(at, _):
+            for half in range(2):
+                xs, ys = (1, 2) if half == 0 else (2, 1)
+                self.to_x(xs, at).wait_recv()
+                self.to_y(ys, at).wait_recv()
+                self.out[:, self.cols(half, at)] += self.from_x[xs, at].astype(
+                    jnp.float32) + self.from_y[ys, at].astype(jnp.float32)
+            for stage in range(4):
+                for stream in range(2):
+                    self.to_sib(stage, stream, at).wait_send()
+            for step in range(3):
+                self.to_x(step, at).wait_send()
+                self.to_y(step, at).wait_send()
+            return 0
+
+        lax.fori_loop(0, self.counts, last, 0)
+
+
+def reduce_scratch(counts, rows, width):
+    low, dma = jnp.bfloat16, pltpu.SemaphoreType.DMA
+    block = pltpu.VMEM((4, 2, counts, rows, width), low)
+    landed = pltpu.VMEM((3, counts, rows, width), low)
+    return [block] * 3 + [landed] * 2 + [dma((4, 2, counts))] * 2 + [dma((3, counts))] * 4
+
+
+class Spread:
+    def __init__(self, here, counts, refs):
+        self.counts = counts
+        self.got = refs[0]
+        self.x_sems, self.y_sems, self.sib_sems = refs[1:3], refs[3:5], refs[5:7]
+        self.core = here.core
+        self.sib, self.xdev, self.ydev = here.device(0, 1), here.device(1, 0), here.device(2, 0)
+        self.stages = (((1, 0), (2, 1)), ((1, 1), (2, 0)), ((3, 1), (3, 0)))
+
+    def slot(self, across, half, at):
+        return self.got.at[across, self.core, half, at]
+
+    def x_copy(self, step, at):
+        src = self.slot(0, step, at) if step < 2 else self.slot(2, 1, at)
+        dst = self.slot(1, step, at) if step < 2 else self.slot(3, 1, at)
+        return remote(src, dst, self.x_sems[0].at[step, at], self.x_sems[1].at[step, at], self.xdev)
+
+    def y_copy(self, step, at):
+        src = self.slot(0, 1 - step, at) if step < 2 else self.slot(1, 0, at)
+        dst = self.slot(2, 1 - step, at) if step < 2 else self.slot(3, 0, at)
+        return remote(src, dst, self.y_sems[0].at[step, at], self.y_sems[1].at[step, at], self.ydev)
+
+    def sib_copy(self, stage, stream, at):
+        across, half = (0, stream) if stage == 3 else self.stages[stage][stream]
+        slot = self.slot(across, half, at)
+        spot = (stage, stream, at)
+        return remote(slot, slot, self.sib_sems[0].at[spot], self.sib_sems[1].at[spot], self.sib)
+
+    def begin(self):
+        for at in range(self.counts):
+            self.x_copy(0, at).start()
+            self.y_copy(0, at).start()
+        for at in range(self.counts):
+            self.sib_copy(3, 0, at).start()
+            self.sib_copy(3, 1, at).start()
+
+    def run(self, blocks, line=None, done=0):
+        def own(at, _):
+            for half in range(2):
+                self.sib_copy(3, half, at).wait_recv()
+                blocks(0, half, at, True)
+            if line:
+                line.step(done + at)
+            return 0
+
+        lax.fori_loop(0, self.counts, own, 0)
+
+        def work(stage, at):
+            for stream, (across, half) in enumerate(self.stages[stage]):
+                self.sib_copy(stage, stream, at).wait_recv()
+                blocks(across, half, at, False)
+
+        for stage in range(3):
+            def body(at, _, stage=stage):
+                self.x_copy(stage, at).wait_recv()
+                self.sib_copy(stage, 0, at).start()
+                self.y_copy(stage, at).wait_recv()
+                self.sib_copy(stage, 1, at).start()
+                if stage < 2:
+                    self.x_copy(stage + 1, at).start()
+                    self.y_copy(stage + 1, at).start()
+
+                @pl.when(at > 0)
+                def _():
+                    work(stage, at - 1)
+
+                if line:
+                    line.step(done + (stage + 1) * self.counts + at)
+                return 0
+
+            lax.fori_loop(0, self.counts, body, 0)
+            work(stage, self.counts - 1)
+
+    def end(self):
+        def drain(at, _):
+            for step in range(3):
+                self.x_copy(step, at).wait_send()
+                self.y_copy(step, at).wait_send()
+            for stage in range(4):
+                self.sib_copy(stage, 0, at).wait_send()
+                self.sib_copy(stage, 1, at).wait_send()
+            return 0
+
+        lax.fori_loop(0, self.counts, drain, 0)
+
+
+def spread_scratch(counts, rows, width):
+    dma = pltpu.SemaphoreType.DMA
+    return [pltpu.VMEM((4, 2, 2, counts, rows, width), jnp.bfloat16)] + [dma((3, counts))] * 4 + [
+        dma((4, 2, counts))] * 2
+
+
+def row_span(here, across, other, rows):
+    return pl.ds(pl.multiple_of(here.shard(across, other) * rows, rows), rows)
+
+
+def dot_nt(left, right):
+    return lax.dot_general(left, right, (((1,), (1,)), ((), ())), preferred_element_type=jnp.float32)
+
+
+def dot_tn(left, right):
+    return lax.dot_general(left, right, (((0,), (0,)), ((), ())), preferred_element_type=jnp.float32)
+
+
+def dot_nn(left, right):
+    return jnp.dot(left, right, preferred_element_type=jnp.float32)
+
+
+def products(here, act, weight_of, nt, rows, width, half_cols, shared):
+    def product(across, other, half, at):
+        first = half * half_cols if shared else 0
+        cols = pl.ds(pl.multiple_of(first + at * width, width), width)
+        block = act[row_span(here, across, other, rows), :]
+        weight = weight_of(half)
+        return dot_nt(block, weight[cols, :]) if nt else dot_nn(block, weight[:, cols])
+
+    return product
+
+
+def scatter_kernel(rows, width, counts, nt, shared, line_counts, act, *refs):
+    refs = list(refs)
+    here = Place()
+    w0 = refs.pop(0)
+    w1 = w0 if shared else refs.pop(0)
+    tiny_own = refs.pop(0)
+    line_own = refs.pop(0) if line_counts else None
+    out, tiny_all = refs.pop(0), refs.pop(0)
+    line = None
+    if line_counts:
+        line = Line(here, line_counts, [line_own, refs.pop(0)] + refs[13:])
+    weights = (w0, w1)
+    product = products(here, act, lambda half: weights[half], nt, rows, width, counts * width, shared)
+    total = Reduce(here, counts, width, product, out, refs[:11])
+    tiny = Tiny(here, tiny_own, tiny_all, refs[11:13], True)
+    greet(here, tiny.peers, line is not None)
+    if line:
+        line.begin()
+    tiny.begin()
+    total.run(line)
+    if line:
+        line.end(4 * counts)
+    total.end()
+    tiny.end()
+
+
+def scatter_product(act, weights, tiny, width, nt, cid, line=None, line_counts=16):
+    total, depth = act.shape
+    rows = total // 8
+    shared = len(weights) == 1
+    half = weights[0].shape[0 if nt else 1] // (2 if shared else 1)
+    counts = half // width
+    dma = pltpu.SemaphoreType.DMA
+    vm = pl.BlockSpec(memory_space=pltpu.VMEM)
+    out_shape = [
+        jax.ShapeDtypeStruct((rows, 2 * half), jnp.float32),
+        jax.ShapeDtypeStruct(tiny.shape, jnp.float32),
+    ]
+    scratch = reduce_scratch(counts, rows, width) + [dma((7,))] * 2
+    operands = [act, *weights, tiny]
+    if line is not None:
+        operands.append(line)
+        out_shape.append(jax.ShapeDtypeStruct(line.shape, line.dtype))
+        scratch += line_scratch(line_counts, line.shape, line.dtype)
+    kernel = functools.partial(scatter_kernel, rows, width, counts, nt, shared,
+                               0 if line is None else line_counts)
+    return kernel_call(kernel, out_shape, operands, [vm] * len(operands), scratch, cid, "scatter_product")
+
+
+def gather_kernel(rows, width, counts, down, n_own, line_counts, act, *refs):
+    refs = list(refs)
+    here = Place()
+    weights = [refs.pop(0) for _ in range(n_own)]
+    payload = [refs.pop(0) for _ in range(n_own)]
+    tiny_own = refs.pop(0)
+    line_own = refs.pop(0) if line_counts else None
+    sums = refs.pop(0)
+    grads = [refs.pop(0) for _ in range(n_own)]
+    tiny_all = refs.pop(0)
+    line_out = refs.pop(0) if line_counts else None
+    spread = Spread(here, counts, refs[:7])
+    tiny = Tiny(here, tiny_own, tiny_all, refs[7:9], False)
+    own_sem = refs[9]
+    line = Line(here, line_counts, [line_own, line_out] + refs[10:]) if line_counts else None
+    got, core = spread.got, here.core
+
+    def part(half, at):
+        first = half * counts * width if n_own == 1 else 0
+        return pl.ds(pl.multiple_of(first + at * width, width), width)
+
+    def own_copy(half, at):
+        src = payload[half if n_own > 1 else 0].at[:, part(half, at)]
+        return pltpu.make_async_copy(src, got.at[0, core, half, at], own_sem.at[half, at])
+
+    for half in range(2):
+        for at in range(counts):
+            own_copy(half, at).start()
+    greet(here, tiny.peers, line is not None)
+    if line:
+        line.begin()
+    for at in range(counts):
+        for half in range(2):
+            own_copy(half, at).wait()
+    spread.begin()
+    tiny.begin()
+    sums[...] = jnp.zeros_like(sums)
+
+    def blocks(across, half, at, fresh):
+        gained = None
+        cols = part(half, at)
+        weight = weights[half if n_own > 1 else 0]
+        for other in range(2):
+            row = row_span(here, across, other, rows)
+            block = got[across, (core + other) % 2, half, at]
+            if down:
+                sums[row, :] += dot_nn(block, weight[cols, :])
+                more = dot_tn(block, act[row, :])
+            else:
+                sums[row, :] += dot_nt(block, weight[:, cols])
+                more = dot_nn(act[:, row], block)
+            gained = more if gained is None else gained + more
+        grad = grads[half if n_own > 1 else 0]
+        where = (cols, slice(None)) if down else (slice(None), cols)
+        if fresh:
+            grad[where] = gained
+        else:
+            grad[where] += gained
+
+    spread.run(blocks, line)
+    if line:
+        line.end(4 * counts)
+    spread.end()
+    tiny.end()
+
+
+def gather_product(act, weights, payload, tiny, width, down, cid, line=None, line_counts=16):
+    total, depth = act.shape if down else act.shape[::-1]
+    rows = payload[0].shape[0]
+    half = payload[0].shape[1] // (2 if len(payload) == 1 else 1)
+    counts = half // width
+    f32 = jnp.float32
+    dma = pltpu.SemaphoreType.DMA
+    vm = pl.BlockSpec(memory_space=pltpu.VMEM)
+    hbm = pl.BlockSpec(memory_space=pl.ANY)
+    out_shape = [jax.ShapeDtypeStruct((total, depth), f32)]
+    out_shape += [jax.ShapeDtypeStruct(w.shape, f32) for w in weights]
+    out_shape.append(jax.ShapeDtypeStruct((8,) + tiny.shape, f32))
+    scratch = spread_scratch(counts, rows, width) + [dma((7,))] * 2 + [dma((2, counts))]
+    operands = [act, *weights, *payload, tiny]
+    specs = [vm] * (1 + len(weights)) + [hbm] * len(payload) + [vm]
+    if line is not None:
+        operands.append(line)
+        specs.append(vm)
+        out_shape.append(jax.ShapeDtypeStruct(line.shape, line.dtype))
+        scratch += line_scratch(line_counts, line.shape, line.dtype)
+    kernel = functools.partial(gather_kernel, rows, width, counts, down, len(weights),
+                               0 if line is None else line_counts)
+    return kernel_call(kernel, out_shape, operands, specs, scratch, cid, "gather_product")
+
+
+def attend_kernel(rows, heads, cols, qkv, rms, cos, sin, mask, w_out, cot, tiny_own, part, mixed_all, g_col, kv,
+                  probs, queries, tiny_pair, *refs):
+    here = Place()
+    spread = Spread(here, heads // 2, refs[:7])
+    sums, pair_sems, turn_send, turn_recv, local_sem = refs[7:12]
+    got, core = spread.got, here.core
+    greet(here, slice_peers(here))
+    me = here.shard(0, 0)
+
+    def turn_copy(at):
+        across, other = turned(at)
+        first = pl.multiple_of(here.shard(across, other) * cols, cols)
+        return remote(cot.at[:, pl.ds(first, cols)], g_col.at[pl.ds(pl.multiple_of(me * rows, rows), rows), :],
+                      turn_send.at[at], turn_recv.at[at], here.device(across, other))
+
+    own_turn = pltpu.make_async_copy(cot.at[:, pl.ds(pl.multiple_of(me * cols, cols), cols)],
+                                     g_col.at[pl.ds(pl.multiple_of(me * rows, rows), rows), :], local_sem)
+    own_turn.start()
+    half = HD // 2
+    scale = 1.0 / math.sqrt(HD)
+    wide = heads * HD
+
+    def rotated(first):
+        lead = qkv[:, first : first + half] * rms[...]
+        trail = qkv[:, first + half : first + HD] * rms[...]
+        return lead * cos[...] - trail * sin[...], trail * cos[...] + lead * sin[...]
+
+    low_k, high_k = rotated(wide)
+    kv[0, :, :half] = low_k.astype(kv.dtype)
+    kv[0, :, half:HD] = high_k.astype(kv.dtype)
+    for at in range(2):
+        first = HD + at * half
+        kv[0, :, first : first + half] = (qkv[:, wide + first : wide + first + half] * rms[...]).astype(kv.dtype)
+    tiny_pair[0] = tiny_own[...]
+    pair = remote(kv.at[0], kv.at[1], pair_sems.at[0], pair_sems.at[1], spread.ydev)
+    tiny = remote(tiny_own, tiny_pair.at[1], pair_sems.at[2], pair_sems.at[3], spread.ydev)
+    for head in range(heads):
+        if head == 1:
+            pair.start()
+            tiny.start()
+            turn_copy(2 * (3 - 1)).start()
+            turn_copy(2 * (3 - 1) + 1).start()
+        lead, trail = rotated(head * HD)
+        queries[:, head * HD : head * HD + half] = (lead * scale).astype(queries.dtype)
+        queries[:, head * HD + half : (head + 1) * HD] = (trail * scale).astype(queries.dtype)
+    pair.wait()
+    for at in range(7):
+        if at // 2 != 2:
+            turn_copy(at).start()
+
+    def one_head(head, _):
+        query = queries[:, pl.ds(pl.multiple_of(head * HD, HD), HD)]
+        scores = jnp.concatenate([dot_nt(query, kv[0, :, :HD]), dot_nt(query, kv[1, :, :HD])], axis=1)
+        scores = jnp.where(mask[...] > 0, scores, NEG)
+        expd = jnp.exp(scores - jnp.max(scores, axis=-1, keepdims=True))
+        prob = expd / jnp.sum(expd, axis=-1, keepdims=True)
+        probs[head] = prob
+        prob_low = prob.astype(jnp.bfloat16)
+        mixed = dot_nn(prob_low[:, :rows], kv[0, :, HD:]) + dot_nn(prob_low[:, rows:], kv[1, :, HD:])
+        got[0, core, head // (heads // 2), head % (heads // 2)] = mixed.astype(got.dtype)
+        return 0
+
+    lax.fori_loop(0, heads, one_head, 0)
+    sums[...] = jnp.zeros_like(sums)
+    spread.begin()
+
+    def blocks(across, half_at, at, fresh):
+        span = pl.ds(pl.multiple_of((half_at * (heads // 2) + at) * HD, HD), HD)
+        for other in range(2):
+            row = row_span(here, across, other, rows)
+            block = got[across, (core + other) % 2, half_at, at]
+            mixed_all[row, span] = block
+            sums[row, :] += dot_nn(block, w_out[span, :])
+
+    spread.run(blocks)
+    part[...] = sums[...].astype(part.dtype)
+    spread.end()
+    tiny.wait()
+    own_turn.wait()
+    for at in range(7):
+        turn_copy(at).wait()
+
+
+def attend(qkv, rms, cos, sin, mask, w_out, cot, tiny, cid):
+    rows = qkv.shape[0]
+    wide, cols = w_out.shape
+    heads = wide // HD
+    low, f32 = jnp.bfloat16, jnp.float32
+    dma = pltpu.SemaphoreType.DMA
+    vm = pl.BlockSpec(memory_space=pltpu.VMEM)
+    out_shape = [
+        jax.ShapeDtypeStruct((8 * rows, cols), low),
+        jax.ShapeDtypeStruct((8 * rows, wide), low),
+        jax.ShapeDtypeStruct((8 * rows, cols), low),
+        jax.ShapeDtypeStruct((2, rows, 2 * HD), low),
+        jax.ShapeDtypeStruct((heads, rows, 2 * rows), f32),
+        jax.ShapeDtypeStruct((rows, wide), low),
+        jax.ShapeDtypeStruct((2,) + tiny.shape, f32),
+    ]
+    scratch = spread_scratch(heads // 2, rows, HD) + [
+        pltpu.VMEM((8 * rows, cols), f32), dma((4,)), dma((7,)), dma((7,)), dma(())]
+    kernel = functools.partial(attend_kernel, rows, heads, cols)
+    return kernel_call(kernel, out_shape, [qkv, rms, cos, sin, mask, w_out, cot, tiny], [vm] * 8, scratch, cid,
+                       "attend")
+
+
+def home_kernel(rows, heads, line_counts, d_attn, w_out, queries, kv, probs, rms, cos, sin, act_t, w_qkv, line_own,
+                sums, grad, tiny_all, line_out, *refs):
+    here = Place()
+    width = HD
+    counts, out_counts = heads // 2, (heads + 2) // 2
+    refs = list(refs)
+    total_refs, refs = refs[:11], refs[11:]
+    spread = Spread(here, out_counts, refs[:7])
+    d_mixed, tiny_own, d_kv, give, taken, give_sems, tiny_send, tiny_recv = refs[7:15]
+    line = Line(here, line_counts, [line_own, line_out] + refs[15:])
+    tiny = Tiny(here, tiny_own, tiny_all, (tiny_send, tiny_recv), False)
+    got, core = spread.got, here.core
+    product = products(here, d_attn, lambda half: w_out, True, rows, width, counts * width, True)
+    total = Reduce(here, counts, width, product, d_mixed, total_refs)
+    greet(here, tiny.peers, True)
+    line.begin()
+    total.run(line)
+    done = 4 * counts
+    total.end()
+    half = HD // 2
+    scale = 1.0 / math.sqrt(HD)
+    depth = w_qkv.shape[0] * 8
+    d_kv[...] = jnp.zeros_like(d_kv)
+
+    def one_head(head, dots):
+        span = pl.ds(pl.multiple_of(head * HD, HD), HD)
+        query = queries[:, span]
+        cot = d_mixed[:, span].astype(jnp.bfloat16)
+        prob = probs[head]
+        d_prob = jnp.concatenate([dot_nt(cot, kv[0, :, HD:]), dot_nt(cot, kv[1, :, HD:])], axis=1)
+        delta = jnp.sum(prob * d_prob, axis=-1, keepdims=True)
+        d_score = (prob * (d_prob - delta)).astype(jnp.bfloat16)
+        prob_low = prob.astype(jnp.bfloat16)
+        d_query = (dot_nn(d_score[:, :rows], kv[0, :, :HD]) + dot_nn(d_score[:, rows:], kv[1, :, :HD])) * scale
+        for side in range(2):
+            keys = slice(side * rows, (side + 1) * rows)
+            d_kv[side, :, :HD] += dot_tn(d_score[:, keys], query)
+            d_kv[side, :, HD:] += dot_tn(prob_low[:, keys], cot)
+        dots = dots + jnp.sum(d_query * query.astype(jnp.float32), axis=-1, keepdims=True)
+        lead, trail = d_query[:, :half], d_query[:, half:]
+        slot = got.at[0, core, head // out_counts, head % out_counts]
+        slot[:, :half] = ((lead * cos[0] + trail * sin[0]) * rms[0]).astype(got.dtype)
+        slot[:, half:] = ((trail * cos[0] - lead * sin[0]) * rms[0]).astype(got.dtype)
+
+        @pl.when(done + head < line_counts + 2)
+        def _():
+            line.step(done + head)
+        return dots
+
+    dots = lax.fori_loop(0, heads, one_head, jnp.zeros((rows, 1), jnp.float32))
+    done += heads
+    eye = (lax.broadcasted_iota(jnp.int32, (LANES, LANES), 0) ==
+           lax.broadcasted_iota(jnp.int32, (LANES, LANES), 1)).astype(jnp.float32)
+    tiny_own[...] = jnp.zeros_like(tiny_own)
+    for side in (1, 0):
+        d_key, d_value = d_kv[side, :, :HD], d_kv[side, :, HD:]
+        own = jnp.sum(d_key * kv[side, :, :HD].astype(jnp.float32) +
+                      d_value * kv[side, :, HD:].astype(jnp.float32), axis=-1, keepdims=True)
+        if side == 0:
+            own = own + dots * (1.0 / scale)
+        own = own * (rms[side] * rms[side] * (1.0 / depth))
+        for at in range(rows // LANES):
+            tile = own[at * LANES : (at + 1) * LANES, :] * eye
+            spot = side * (rows // LANES) + at
+            tiny_own[spot : spot + 1, :] = jnp.sum(tile, axis=0, keepdims=True)
+        lead, trail = d_key[:, :half], d_key[:, half:]
+        parts = [(lead * cos[side] + trail * sin[side]) * rms[side],
+                 (trail * cos[side] - lead * sin[side]) * rms[side],
+                 d_value[:, :half] * rms[side], d_value[:, half:] * rms[side]]
+        for at, value in enumerate(parts):
+            if side == 1:
+                give[:, at * half : (at + 1) * half] = value.astype(give.dtype)
+            else:
+                d_kv[0, :, at * half : (at + 1) * half] = value
+    given = remote(give, taken, give_sems.at[0], give_sems.at[1], spread.ydev)
+    given.start()
+    sums[...] = jnp.zeros_like(sums)
+    given.wait()
+    for at in range(2):
+        span = slice(at * HD, (at + 1) * HD)
+        value = d_kv[0, :, span] + taken[:, span].astype(jnp.float32)
+        got[0, core, 1, out_counts - 2 + at] = value.astype(got.dtype)
+    tiny.begin()
+    spread.begin()
+
+    def blocks(across, half_at, at, fresh):
+        span = pl.ds(pl.multiple_of((half_at * out_counts + at) * width, width), width)
+        gained = None
+        for other in range(2):
+            row = row_span(here, across, other, rows)
+            block = got[across, (core + other) % 2, half_at, at]
+            sums[row, :] += dot_nt(block, w_qkv[:, span])
+            more = dot_nn(act_t[:, row], block)
+            gained = more if gained is None else gained + more
+        if fresh:
+            grad[:, span] = gained
+        else:
+            grad[:, span] += gained
+
+    spread.run(blocks, line, done)
+    line.end(done + 4 * out_counts)
+    spread.end()
+    tiny.end()
+
+
+def home(d_attn, w_out, queries, kv, probs, rms, cos, sin, act_t, w_qkv, line, cid, line_counts=16):
+    total, cols = d_attn.shape
+    rows = total // 8
+    wide = w_out.shape[0]
+    heads = wide // HD
+    low, f32 = jnp.bfloat16, jnp.float32
+    dma = pltpu.SemaphoreType.DMA
+    vm = pl.BlockSpec(memory_space=pltpu.VMEM)
+    out_shape = [
+        jax.ShapeDtypeStruct((total, cols), f32),
+        jax.ShapeDtypeStruct(w_qkv.shape, f32),
+        jax.ShapeDtypeStruct((8, 8, LANES), f32),
+        jax.ShapeDtypeStruct(line.shape, line.dtype),
+    ]
+    scratch = reduce_scratch(heads // 2, rows, HD) + spread_scratch((heads + 2) // 2, rows, HD)
+    scratch += [
+        pltpu.VMEM((rows, wide), f32),
+        pltpu.VMEM((8, LANES), f32),
+        pltpu.VMEM((2, rows, 2 * HD), f32),
+        pltpu.VMEM((rows, 2 * HD), low),
+        pltpu.VMEM((rows, 2 * HD), low),
+        dma((2,)), dma((7,)), dma((7,)),
+    ] + line_scratch(line_counts, line.shape, low)
+    operands = [d_attn, w_out, queries, kv, probs, rms, cos, sin, act_t, w_qkv, line]
+    kernel = functools.partial(home_kernel, rows, heads, line_counts)
+    return kernel_call(kernel, out_shape, operands, [vm] * len(operands), scratch, cid, "home")
+
+
+def turn_kernel(rows, cols, back, src, out, own_sem, send, recv):
+    here = Place()
+    peers = [(a, o) for a in (3, 1, 2, 0) for o in range(2) if a + o > 0]
+    greet(here, [here.device(a, o) for a, o in peers])
+
+    def by_row(ref, shard):
+        return ref.at[pl.ds(pl.multiple_of(shard * rows, rows), rows), :]
+
+    def by_col(ref, shard):
+        return ref.at[:, pl.ds(pl.multiple_of(shard * cols, cols), cols)]
+
+    take, put = (by_row, by_col) if back else (by_col, by_row)
+    me = here.shard(0, 0)
+
+    def copy(at):
+        across, other = peers[at]
+        return remote(take(src, here.shard(across, other)), put(out, me), send.at[at], recv.at[at],
+                      here.device(across, other))
+
+    for at in range(7):
+        copy(at).start()
+    own = pltpu.make_async_copy(take(src, me), put(out, me), own_sem)
+    own.start()
+    own.wait()
+    for at in range(7):
+        copy(at).wait()
+
+
+def turn(src, back, cid):
+    rows, cols = (src.shape[0] // 8, src.shape[1]) if back else (src.shape[0], src.shape[1] // 8)
+    shape = (rows, 8 * cols) if back else (8 * rows, cols)
+    dma = pltpu.SemaphoreType.DMA
+    vm = pl.BlockSpec(memory_space=pltpu.VMEM)
+    return pl.pallas_call(
+        functools.partial(turn_kernel, rows, cols, back),
+        out_shape=jax.ShapeDtypeStruct(shape, src.dtype),
+        in_specs=[vm],
+        out_specs=vm,
+        scratch_shapes=[dma(()), dma((7,)), dma((7,))],
+        compiler_params=pltpu.CompilerParams(collective_id=cid, has_side_effects=True,
+                                             vmem_limit_bytes=VMEM_LIMIT),
+        name=f"turn_{cid}",
+    )(src)
+
+def close_kernel(rows, cols, per, extra, own, rest, other_own, tile, out, other_out, summed, tiles, ready, local_sem,
+                 other_send, other_recv, put_send, put_recv, tile_send, tile_recv, *line_refs):
+    here = Place()
+    me = here.shard(0, 0)
+    counts = 8 * per
+
+    def target(at):
+        turn_at = at // per
+        return 3 - turn_at // 2, 1 - turn_at % 2
+
+    def place(at):
+        across, other = target(jnp.minimum(at, counts - 1))
+        return jnp.where(at < counts, here.shard(across, other) * per + at % per, at)
+
+    line = Line(here, counts + extra, [own, summed] + list(line_refs), place)
+    peers = [turned(at) for at in range(7)]
+    greet(here, slice_peers(here), True)
+    line.begin()
+
+    def tile_copy(step):
+        return remote(tile, tiles.at[here.z], tile_send.at[step], tile_recv.at[step],
+                      (here.dp, here.seq, (here.z + step + 1) % 4))
+
+    for step in range(3):
+        tile_copy(step).start()
+    tiles[here.z] = tile[...]
+    columns = pl.ds(pl.multiple_of(me * cols, cols), cols)
+
+    def turn_copy(at):
+        across, other = peers[at]
+        src = other_own.at[pl.ds(pl.multiple_of(here.shard(across, other) * rows, rows), rows), :]
+        return remote(src, other_out.at[:, columns], other_send.at[at], other_recv.at[at],
+                      here.device(across, other))
+
+    for at in range(7):
+        turn_copy(at).start()
+    mine = pltpu.make_async_copy(other_own.at[pl.ds(pl.multiple_of(me * rows, rows), rows), :],
+                                 other_out.at[:, columns], local_sem)
+    mine.start()
+    chunk = line.chunk
+
+    def put(at):
+        across, other = target(at)
+        dst = out.at[pl.ds(pl.multiple_of(at % per * chunk, chunk), chunk), columns]
+        return remote(ready.at[at], dst, put_send.at[at], put_recv.at[at], here.device(across, other))
+
+    def emit(at):
+        total = rest[line.rows(at), :] + summed[line.rows(at), :].astype(jnp.float32)
+
+        @pl.when(at < 7 * per)
+        def _():
+            ready[at] = total.astype(ready.dtype)
+            put(at).start()
+
+        @pl.when(at >= 7 * per)
+        def _():
+            out[pl.ds(pl.multiple_of(at % per * chunk, chunk), chunk), columns] = total.astype(out.dtype)
+
+    @pl.when(line.inner == 1)
+    def _():
+        def both(at, _):
+            line.step(at)
+
+            @pl.when(jnp.logical_and(at > 1, at < counts + 2))
+            def _():
+                emit(at - 2)
+            return 0
+
+        lax.fori_loop(0, counts + extra + 2, both, 0)
+
+        def drain(at, _):
+            line.over(at).wait_send()
+            line.down(at).wait_send()
+            return 0
+
+        lax.fori_loop(0, counts + extra, drain, 0)
+
+    @pl.when(line.inner == 0)
+    def _():
+        def take(at, _):
+            line.up(at).wait_send()
+            line.down(at).wait_recv()
+
+            @pl.when(at < counts)
+            def _():
+                emit(at)
+            return 0
+
+        lax.fori_loop(0, counts + extra, take, 0)
+
+    mine.wait()
+    for at in range(7):
+        turn_copy(at).wait()
+
+    def finish(at, _):
+        put(at).wait()
+        return 0
+
+    lax.fori_loop(0, 7 * per, finish, 0)
+    for step in range(3):
+        tile_copy(step).wait()
+
+
+def close(own, rest, other_own, tile, cid, per=2):
+    total, cols = rest.shape
+    rows = total // 8
+    low = own.dtype
+    dma = pltpu.SemaphoreType.DMA
+    vm = pl.BlockSpec(memory_space=pltpu.VMEM)
+    whole = jax.ShapeDtypeStruct((rows, 8 * cols), low)
+    chunk = rows // per
+    extra = (own.shape[0] - total) // chunk
+    counts = 8 * per
+    out_shape = [whole, whole, jax.ShapeDtypeStruct(own.shape, low), jax.ShapeDtypeStruct((4,) + tile.shape, tile.dtype)]
+    scratch = [
+        pltpu.VMEM((7 * per, chunk, cols), low),
+        dma(()), dma((7,)), dma((7,)), dma((7 * per,)), dma((7 * per,)), dma((3,)), dma((3,)),
+    ] + line_scratch(counts + extra, own.shape, low)
+    kernel = functools.partial(close_kernel, rows, cols, per, extra)
+    return kernel_call(kernel, out_shape, [own, rest, other_own, tile], [vm] * 4, scratch, cid, "close")
+
+
+LANES = 128
+
+
+def pack_rows(values):
+    parts = values.reshape(8, -1, LANES)
+    return jnp.pad(parts, ((0, 0), (0, 8 - parts.shape[1]), (0, 0)))
+
+
+def acts_move(
+    tokens, seg_ids, gain_attn, w_query, kv_weight, w_out, gain_ffn, w_gate, w_up, w_down, d_out
+):
+    low = jnp.bfloat16
+    rows, width = tokens.shape
+    seqs = lax.axis_size("seq")
+    parts = lax.axis_size("dp") * seqs
+    offset = lax.axis_index("seq") * rows
+    places, cos_table, sin_table = place_tables(seg_ids)
+    away = rows - offset
+
+    def own_first(table):
+        return jnp.stack(
+            [
+                lax.dynamic_slice_in_dim(table, offset, rows, 0),
+                lax.dynamic_slice_in_dim(table, away, rows, 0),
+            ]
+        )
+
+    pair_places = own_first(places)
+    pair_segs = own_first(seg_ids)
+    pair_cos = own_first(cos_table)
+    pair_sin = own_first(sin_table)
+    allowed = (pair_segs[0][:, None] == pair_segs.reshape(1, -1)) & (
+        pair_places[0][:, None] >= pair_places.reshape(1, -1)
+    )
+    gain_one = gain_attn.astype(jnp.float32)
+    gain_two = gain_ffn.astype(jnp.float32)
+    qw = w_query.shape[1]
+    ff = w_gate.shape[1]
+
+    none = jnp.zeros((8, 8, LANES), jnp.float32)
+    x_low = turn(tokens, False, 1)
+    x_col = x_low.astype(jnp.float32)
+    own_x = tokens.astype(jnp.float32)
+    rms_one = lax.rsqrt(jnp.mean(own_x * own_x, axis=-1, keepdims=True) + EPS)
+    act_one = (x_col * gain_one).astype(low)
+    w_qkv = jnp.concatenate([w_query, kv_weight], axis=1)
+    qkv = scatter_product(act_one, (w_qkv,), none, 256, False, 2)[0]
+    tiles = rows // LANES
+    attn_part, mixed_all, g_low, kv, probs, queries, rms_tiles = attend(
+        qkv,
+        jnp.broadcast_to(rms_one, (rows, LANES)),
+        pair_cos[0],
+        pair_sin[0],
+        allowed.astype(jnp.float32),
+        w_out,
+        d_out,
+        jnp.pad(rms_one.reshape(tiles, LANES), ((0, 8 - tiles), (0, 0))),
+        3,
+    )
+    pair_rms = jnp.broadcast_to(rms_tiles[:, :tiles].reshape(2, rows, 1), (2, rows, LANES))
+    d_hidden, _, attn = scatter_product(g_low, (w_down,), none, 512, True, 4, line=attn_part)
+    resid = x_col + attn.astype(jnp.float32)
+    act_two = (resid * gain_two).astype(low)
+    squares = pack_rows(jnp.sum(resid * resid, axis=-1))
+    both, squares_all = scatter_product(act_two, (w_gate, w_up), squares, 512, False, 6)
+    mean_two = jnp.sum(squares_all[:, : rows // LANES], axis=0).reshape(rows, 1) / width
+    rms_two = lax.rsqrt(mean_two + EPS)
+    gate = both[:, :ff] * rms_two
+    up_val = both[:, ff : 2 * ff] * rms_two
+    gelu_val, gelu_pull = jax.vjp(gelu_tanh, gate)
+    hidden = (gelu_val * up_val).astype(low)
+    d_gate = gelu_pull(d_hidden * up_val)[0]
+    d_up = d_hidden * gelu_val
+    dots_two = jnp.sum(d_gate * gate + d_up * up_val, axis=-1, keepdims=True) * (
+        rms_two * rms_two / width
+    )
+    dots_own = jnp.pad(dots_two.reshape(-1, LANES), ((0, 8 - rows // LANES), (0, 0)))
+    d_act_two, grad_gate, grad_up, dots_all = gather_product(
+        act_two.T,
+        (w_gate, w_up),
+        ((d_gate * rms_two).astype(low), (d_up * rms_two).astype(low)),
+        dots_own,
+        512,
+        False,
+        7,
+    )
+    dot_two = dots_all[:, : rows // LANES].reshape(parts * rows, 1)
+    grad_gain_two = jnp.sum(d_act_two * resid, axis=0)
+    ffn, grad_down, _, d_norm = gather_product(
+        g_low,
+        (w_down,),
+        (hidden,),
+        none[0],
+        256,
+        True,
+        8,
+        line=(d_act_two * gain_two - resid * dot_two).astype(low),
+    )
+    d_resid = g_low.astype(jnp.float32) + d_norm.astype(jnp.float32)
+    d_attn = d_resid.astype(low)
+    grad_out = matmul_tn(mixed_all, d_attn)
+
+    d_act_one, grad_qkv, dots_all, ffn_sum = home(
+        d_attn,
+        w_out,
+        queries,
+        kv,
+        probs,
+        pair_rms,
+        pair_cos,
+        pair_sin,
+        act_one.T,
+        w_qkv,
+        ffn.astype(low),
+        9,
+    )
+    pairs = dots_all.reshape(parts // 2, 2, 8, LANES)
+    dot_one = (pairs[:, :, :tiles] + pairs[:, ::-1, tiles : 2 * tiles]).reshape(parts * rows, 1)
+    grad_gain_one = jnp.sum(d_act_one * x_col, axis=0)
+    d_tokens, out, summed, gain_tiles = close(
+        jnp.concatenate(
+            [(d_act_one * gain_one - x_col * dot_one).astype(low), grad_qkv[:, qw:].astype(low)]
+        ),
+        d_resid,
+        (resid + ffn_sum.astype(jnp.float32)).astype(low),
+        jnp.stack([grad_gain_one, grad_gain_two]).reshape(8, LANES),
+        10,
+    )
+    grad_query = grad_qkv[:, :qw]
+    grad_kv = summed[parts * rows :].astype(jnp.float32)
+    gains = jnp.sum(gain_tiles, axis=0).reshape(2, -1)
+    return (
+        out,
+        d_tokens.astype(jnp.float32),
+        gains[0],
+        grad_query,
+        grad_kv,
+        grad_out,
+        gains[1],
+        grad_gate,
+        grad_up,
+        grad_down,
+    )
+
+
 def solution(mesh):
     in_specs = (
         P(("dp", "seq"), None),
@@ -261,4 +1343,12 @@
         P(("dp", "seq"), "tensor"),
         P("tensor", ("dp", "seq")),
     )
+
+    def shards(*arrays):
+        tokens = arrays[0]
+        sizes = tuple(mesh.shape[name] for name in ("dp", "seq", "tensor"))
+        count = tokens.shape[0] * sizes[0] * sizes[1]
+        plan = acts_move if sizes == (4, 2, 4) and count <= tokens.shape[1] else weights_move
+        return plan(*arrays)
+
     return jax.shard_map(shards, mesh=mesh, in_specs=in_specs, out_specs=out_specs, check_vma=False)

time: 1820 us -> 778 us (0.43)
  waiting for transfers between devices: 1460 us -> 0 us
  Pallas kernels: 0 us -> 674 us
  matrix products: 191 us -> 3.68 us
  blocking collectives: 70.5 us -> 0 us
  local copies, waits for them, and re-layouts: 15.7 us -> 37.9 us
    pallas_call x0 -> x9, Pallas kernels: none -> 674 us  [the longest x8 643 us: kernel_call(): pl.pallas_call(kernel, out_shape=out_shape, in_specs=specs, out_specs=[vm...]
    reduce_scatter x7 -> x0, waiting for transfers between devices: 563 us -> none  [the longest x1 157 us: shards(): lax.psum_scatter(grad_down.astype(jnp.bfloat16), ('dp', 'seq'), scatter_d...]
    all_gather x6 -> x0, waiting for transfers between devices: 454 us -> none  [the longest x1 119 us: shards(): lax.all_gather(w_up, ('dp', 'seq'), axis=0, tiled=True)]
    psum x3 -> x0, waiting for transfers between devices: 443 us -> none  [the longest x1 166 us: shards(): lax.psum(matmul(hidden, full_down).astype(jnp.bfloat16), 'tensor')]
    dot_general x17 -> x0, matrix products: 126 us -> none  [the longest x6 66.3 us: matmul_nt(): lax.dot_general(left, right, (((1,), (1,)), ((), ())), preferred_element_...]
    dot_general x6 -> x1, matrix products: 58.6 us -> 3.68 us  [matmul_tn(): lax.dot_general(left, right, (((0,), (0,)), ((), ())), preferred_element_...]
    all_gather x3 -> x0, blocking collectives: 44.8 us -> none  [the longest x1 18 us: shards(): lax.all_gather(gain_attn, ('dp', 'seq'), axis=0, tiled=True)]
    unnamed x1 -> x0, blocking collectives: 25.7 us -> none
  transfers between devices with their start and end apart: 16 -> 0, of which waited for: 15 -> 0; matrix products, arithmetic and copies ran while one was open for 9% -> 0% of each run, Pallas kernels for 0% -> 0%
where the time goes in v4:
time: 778 us; the launch traced here: 773 us
  Pallas kernels  674 us (87%)
  other arithmetic  56.8 us (7%)
  local copies, waits for them, and re-layouts  37.9 us (5%)
    pallas_call x8, Pallas kernels, kernel_call(): pl.pallas_call(kernel, out_shape=out_shape, in_specs=specs, out_specs=[vm...  643 us
    pallas_call x1, Pallas kernels, turn(): pl.pallas_call(functools.partial(turn_kernel, rows, cols, back), out_shap...  30.9 us
    unnamed x45, local copies, waits for them, and re-layouts  17.7 us

profile of v4, /device:TPU:0, one launch (start us, length us, event | category | flops | bytes accessed | tf_op | source)
XLA Modules:
  0.0 773.3 jit_solution(18418463584570926491)
XLA Ops:
  0.7 0.9 slice_compare_fusion
  1.5 2.1 multiply_reduce_fusion.2
  3.6 0.1 add_select_fusion
  3.7 0.3 reduce-window.9
  4.0 1.3 convert_element_type.77
  5.3 1.3 convert_element_type.84
  6.6 0.1 slice_reduce_fusion.1
  6.8 0.6 pad.11.tiny_own
  7.4 0.8 fusion.15
  8.3 0.8 broadcast_in_dim.11.rms
  9.1 0.9 and_convert_fusion.mask
  10.0 1.0 multiply_sine_fusion
  11.1 0.6 copy-done.7
  11.7 0.7 pad_maximum_fusion.2.sin
  12.4 0.7 pad_maximum_fusion.1.cos
  13.2 1.0 constant_dynamic-update-slice_fusion.1
  14.2 0.8 constant_dynamic-update-slice_fusion.refs_0_.w_qkv
  15.0 30.9 %turn_1.1 = bf16[2048,512]{1,0:T(8,128)(2,1)} custom-call(bf16[256,4096]{1,0:T(8,128)(2,1)} %src.1), custom_call_target="tpu_custom_call" | custom-call | tf_op jit(solution)/shard_map/turn_1/pallas_call | solution.py:1042
  45.9 3.3 fusion.20
  49.2 4.1 copy.24.act_t
  53.3 1.8 fusion.act
  55.0 0.6 broadcast_in_dim.10.refs_1_
  55.7 35.3 %scatter_product_2.1 = (f32[256,1536]{1,0:T(8,128)}, f32[8,8,128]{2,1,0:T(8,128)}) custom-call(bf16[2048,512]{1,0:T(8,128)(2,1)} %fusion.act, bf16[512,1536]{1,0:T(8,128)(2,1)} %constant_dynamic-update-slice_fusion.refs_0_.w_qkv, f32[8,8,128]{2,1,0:T(8,128)} %broadcast_in_dim.10.refs_1_), custom_call_target="tpu_custom_call" | custom-call | tf_op jit(solution)/shard_map/scatter_product_2/pallas_call | solution.py:382
  91.0 59.1 %attend_3.1 = (bf16[2048,512]{1,0:T(8,128)(2,1)}, bf16[2048,1024]{1,0:T(8,128)(2,1)}, bf16[2048,512]{1,0:T(8,128)(2,1)}, bf16[2,256,512]{2,1,0:T(8,128)(2,1)}, f...) custom-call(f32[256,1536]{1,0:T(8,128)} %get-tuple-element.37.qkv, ...), custom_call_target="tpu_custom_call" | custom-call | tf_op jit(solution)/shard_map/attend_3/pallas_call | solution.py:382
  150.1 0.7 slice_bitcast_fusion.2
  150.8 0.8 broadcast_in_dim.14.rms
  151.7 76.7 %scatter_product_4.1 = (f32[256,3072]{1,0:T(8,128)}, f32[8,8,128]{2,1,0:T(8,128)}, bf16[2048,512]{1,0:T(8,128)(2,1)}) custom-call(bf16[2048,512]{1,0:T(8,128)(2,1)} %get-tuple-element.38.act, bf16[3072,512]{1,0:T(8,128)(2,1)} %refs_0_.7, f32[8,8,128]{2,1,0:T(8,128)} %broadcast_in_dim.10.refs_1_, bf16[2048,512]{1,0:T(8,128)(2,1)} %get-tuple-element.39.refs_2_), custom_call_target="tpu_custom_call" | custom-call | tf_op jit(solution)/shard_map/scatter_product_4/pallas_call | solution.py:382
  228.3 3.2 multiply_reduce_fusion.1
  231.5 0.7 pad.12.refs_2_
  232.2 0.7 copy-done.3
  232.9 2.4 copy.23.act
  235.2 115.5 %scatter_product_6.1 = (f32[256,6144]{1,0:T(8,128)}, f32[8,8,128]{2,1,0:T(8,128)}) custom-call(bf16[2048,512]{1,0:T(8,128)(2,1)} %copy-done.3, bf16[512,3072]{1,0:T(8,128)(2,1)} %refs_0_.6, bf16[512,3072]{1,0:T(8,128)(2,1)} %refs_1_.3, f32[8,8,128]{2,1,0:T(8,128)} %pad.12.refs_2_), custom_call_target="tpu_custom_call" | custom-call | tf_op jit(solution)/shard_map/scatter_product_6/pallas_call | solution.py:382
  350.7 0.8 slice_reduce_fusion
  351.5 7.4 add_reduce_fusion
  358.9 0.6 pad.13.refs_4_
  359.5 1.5 multiply_convert_fusion.2.refs_2_
  361.0 118.9 %gather_product_7.1 = (f32[2048,512]{1,0:T(8,128)}, f32[512,3072]{1,0:T(8,128)}, f32[512,3072]{1,0:T(8,128)}, f32[8,8,128]{2,1,0:T(8,128)}) custom-call(bf16[512,2048]{1,0:T(8,128)(2,1)} %copy.23.act, bf16[512,3072]{1,0:T(8,128)(2,1)} %refs_0_.6, bf16[512,3072]{1,0:T(8,128)(2,1)} %refs_1_.3, bf16[256,3072]{1,0:T(8,128)(2,1)} %multiply_convert_fusion.2.refs_2_, ...), custom_call_target="tpu_custom_call" | custom-call | tf_op jit(solution)/shard_map/gather_product_7/pallas_call | solution.py:382
  480.0 0.8 slice.59
  480.7 5.7 subtract_convert_fusion.refs_3_
  486.4 0.6 squeeze.9.refs_2_
  487.0 69.5 %gather_product_8.1 = (f32[2048,512]{1,0:T(8,128)}, f32[3072,512]{1,0:T(8,128)}, f32[8,8,128]{2,1,0:T(8,128)}, bf16[2048,512]{1,0:T(8,128)(2,1)}) custom-call(bf16[2048,512]{1,0:T(8,128)(2,1)} %get-tuple-element.38.act, bf16[3072,512]{1,0:T(8,128)(2,1)} %refs_0_.7, bf16[256,3072]{1,0:T(8,128)(2,1)} %get-tuple-element.71.refs_1_, f32[8,128]{1,0:T(8,128)} %squeeze.9.refs_2_, ...), custom_call_target="tpu_custom_call" | custom-call | tf_op jit(solution)/shard_map/gather_product_8/pallas_call | solution.py:382
  556.5 3.9 convert_element_type.92.line_own
  560.5 2.9 convert_add_fusion.1
  563.4 1.3 copy-done.2
  564.7 3.7 fusion.17
  568.4 80.2 %home_9.1 = (f32[2048,512]{1,0:T(8,128)}, f32[512,1536]{1,0:T(8,128)}, f32[8,8,128]{2,1,0:T(8,128)}, bf16[2048,512]{1,0:T(8,128)(2,1)}) custom-call(bf16[2048,512]{1,0:T(8,128)(2,1)} %copy-done.2, bf16[1024,512]{1,0:T(8,128)(2,1)} %w_out.3, bf16[256,1024]{1,0:T(8,128)(2,1)} %get-tuple-element.47.queries, bf16[2,256,512]{2,1,0:T(8,128)(2,1)} %get-tuple-element.48.kv, ...), custom_call_target="tpu_custom_call" | custom-call | tf_op jit(solution)/shard_map/home_9/pallas_call | solution.py:382
  648.6 0.8 slice.69
  649.4 0.8 slice_add_fusion
  650.2 7.2 fusion.3
  657.4 0.6 reshape.124.tile
  658.0 1.3 slice.107
  659.3 3.2 slice.65
  662.5 1.7 pad_maximum_fusion.own
  664.1 87.7 %close_10.1 = (bf16[256,4096]{1,0:T(8,128)(2,1)}, bf16[256,4096]{1,0:T(8,128)(2,1)}, bf16[2560,512]{1,0:T(8,128)(2,1)}, f32[4,8,128]{2,1,0:T(8,128)}) custom-call(bf16[2560,512]{1,0:T(8,128)(2,1)} %pad_maximum_fusion.own, f32[2048,512]{1,0:T(8,128)} %get-tuple-element.74.rest, bf16[2048,512]{1,0:T(8,128)(2,1)} %get-tuple-element.73.other_own, ...), custom_call_target="tpu_custom_call" | custom-call | tf_op jit(solution)/shard_map/close_10/pallas_call | solution.py:382
  751.9 0.7 reduce_sum.72
  752.6 0.6 slice_bitcast_fusion
  753.2 2.3 slice_convert_fusion.1
  755.5 4.2 convert_element_type.96
  759.7 1.3 copy.35
  761.1 3.2 copy.36
  764.3 1.5 slice-done.1
  765.8 3.2 copy.37
  769.0 1.4 slice-done.5
  770.4 2.7 copy.38
  (48 shorter events, 0.4 us)
Async XLA Ops:
  0.6 12.5 %copy-start.9 = (bf16[512,1024]{1,0:T(8,128)(2,1)S(1)}, bf16[512,1024]{1,0:T(8,128)(2,1)}, u32[]{:S(2)}) copy-start(bf16[512,1024]{1,0:T(8,128)(2,1)} %param.14) | copy-start | bytes 3145732
  3.6 10.6 %copy-start.10 = (bf16[512,512]{1,0:T(8,128)(2,1)S(1)}, bf16[512,512]{1,0:T(8,128)(2,1)}, u32[]{:S(2)}) copy-start(bf16[512,512]{1,0:T(8,128)(2,1)} %param.15) | copy-start | bytes 1572868
  11.0 0.7 copy-start.7
  11.1 1.4 copy-start.8
  49.2 4.1 copy-start
  49.2 4.1 copy-start.11
  231.5 1.3 copy-start.3
  556.5 4.0 copy-start.1
  556.5 4.0 copy-start.5
  560.5 4.2 copy-start.4
  563.4 1.3 copy-start.2
  753.2 6.6 copy-start.6
  753.2 7.9 %slice-start.2 = ((s8[6291456]{0:T(1024)(128)(4,1)}), s8[4194304]{0:T(1024)(128)(4,1)S(1)}, s32[]{:S(2)}) async-start(s8[6291456]{0:T(1024)(128)(4,1)} %bitcast.52), calls=%async_computation.2 | async-start | bytes 8388608
  755.5 5.6 slice-start.3
  759.7 4.6 slice-start
  761.1 4.7 slice-start.1
  761.1 7.9 %slice-start.4 = ((s8[6291456]{0:T(1024)(128)(4,1)}), s8[2097152]{0:T(1024)(128)(4,1)S(1)}, s32[]{:S(2)}) async-start(s8[6291456]{0:T(1024)(128)(4,1)} %bitcast.54), calls=%async_computation.4 | async-start | bytes 4194304
  765.8 4.6 slice-start.5

commit v5 on v4

--- a/solution.py
+++ b/solution.py
@@ -279,8 +279,8 @@
 
 class Line:
     def __init__(self, here, counts, refs, place=None):
-        self.own, self.out, self.from_end, self.mine, self.from_mid = refs[:5]
-        self.sems = refs[5:11]
+        self.own, self.out, self.from_end, self.from_mid = refs[:4]
+        self.sems = refs[4:10]
         self.counts = counts
         self.chunk = self.own.shape[0] // counts
         self.place = place
@@ -298,53 +298,59 @@
                       self.sems[1].at[at], self.mate)
 
     def over(self, at):
-        return remote(self.mine.at[at], self.from_mid.at[at], self.sems[2].at[at], self.sems[3].at[at],
-                      self.other)
+        return remote(self.out.at[self.rows(at), :], self.from_mid.at[at], self.sems[2].at[at],
+                      self.sems[3].at[at], self.other)
 
     def down(self, at):
         rows = self.rows(at)
         return remote(self.out.at[rows, :], self.out.at[rows, :], self.sems[4].at[at],
                       self.sems[5].at[at], self.mate)
 
-    def begin(self):
+    def launch(self, first, count):
         @pl.when(self.inner == 0)
         def _():
             def send(at, _):
-                self.up(at).start()
+                self.up(first + at).start()
                 return 0
 
-            lax.fori_loop(0, self.counts, send, 0)
+            lax.fori_loop(0, count, send, 0)
+
+    def begin(self):
+        self.launch(0, self.counts)
 
     def first(self, at):
         rows = self.rows(at)
         self.up(at).wait_recv()
         total = self.own[rows, :].astype(jnp.float32) + self.from_end[at].astype(jnp.float32)
-        self.mine[at] = total.astype(self.mine.dtype)
+        self.out[rows, :] = total.astype(self.out.dtype)
         self.over(at).start()
 
     def second(self, at):
         rows = self.rows(at)
-        self.over(at).wait_recv()
-        total = self.mine[at].astype(jnp.float32) + self.from_mid[at].astype(jnp.float32)
+        self.over(at).wait()
+        total = self.out[rows, :].astype(jnp.float32) + self.from_mid[at].astype(jnp.float32)
         self.out[rows, :] = total.astype(self.out.dtype)
         self.down(at).start()
 
-    def step(self, at):
-        @pl.when(jnp.logical_and(self.inner == 1, at < self.counts))
+    def step(self, at, start=0, count=None):
+        count = self.counts if count is None else count
+
+        @pl.when(jnp.logical_and(self.inner == 1, at < count))
         def _():
-            self.first(at)
-
-        @pl.when(jnp.logical_and(self.inner == 1, jnp.logical_and(at > 1, at < self.counts + 2)))
+            self.first(start + at)
+
+        @pl.when(jnp.logical_and(self.inner == 1, jnp.logical_and(at > 1, at < count + 2)))
         def _():
-            self.second(at - 2)
-
-    def end(self, done=0):
+            self.second(start + at - 2)
+
+    def steps(self, first, last, start=0, count=None):
         def rest(at, _):
-            self.step(at)
+            self.step(at, start, count)
             return 0
 
-        lax.fori_loop(min(done, self.counts + 2), self.counts + 2, rest, 0)
-
+        lax.fori_loop(first, last, rest, 0)
+
+    def settle(self):
         @pl.when(self.inner == 0)
         def _():
             def take(at, _):
@@ -357,16 +363,19 @@
         @pl.when(self.inner == 1)
         def _():
             def drain(at, _):
-                self.over(at).wait_send()
                 self.down(at).wait_send()
                 return 0
 
             lax.fori_loop(0, self.counts, drain, 0)
 
+    def end(self, done=0):
+        self.steps(min(done, self.counts + 2), self.counts + 2)
+        self.settle()
+
 
 def line_scratch(counts, shape, low):
     buf = pltpu.VMEM((counts, shape[0] // counts, shape[1]), low)
-    return [buf, buf, buf] + [pltpu.SemaphoreType.DMA((counts,))] * 6
+    return [buf, buf] + [pltpu.SemaphoreType.DMA((counts,))] * 6
 
 
 def turned(at):
@@ -544,16 +553,22 @@
             self.sib_copy(3, 0, at).start()
             self.sib_copy(3, 1, at).start()
 
-    def run(self, blocks, line=None, done=0):
+    def run(self, blocks, line=None, hook=None, between=None):
+        if hook is None:
+            def hook(stage, at):
+                if line:
+                    line.step((stage + 1) * self.counts + at)
+
         def own(at, _):
             for half in range(2):
                 self.sib_copy(3, half, at).wait_recv()
                 blocks(0, half, at, True)
-            if line:
-                line.step(done + at)
+            hook(-1, at)
             return 0
 
         lax.fori_loop(0, self.counts, own, 0)
+        if between:
+            between(-1)
 
         def work(stage, at):
             for stream, (across, half) in enumerate(self.stages[stage]):
@@ -574,12 +589,13 @@
                 def _():
                     work(stage, at - 1)
 
-                if line:
-                    line.step(done + (stage + 1) * self.counts + at)
+                hook(stage, at)
                 return 0
 
             lax.fori_loop(0, self.counts, body, 0)
             work(stage, self.counts - 1)
+            if between:
+                between(stage)
 
     def end(self):
         def drain(at, _):
@@ -873,16 +889,42 @@
                        "attend")
 
 
-def home_kernel(rows, heads, line_counts, d_attn, w_out, queries, kv, probs, rms, cos, sin, act_t, w_qkv, line_own,
-                sums, grad, tiny_all, line_out, *refs):
+def tail_kernel(rows, heads, per, d_attn, w_out, queries, kv, probs, rms, cos, sin, act_t, w_qkv, ffn, x_low,
+                resid, gain, gain_grad, d_tok, out, grad, kv_sum, gain_tiles, *refs):
     here = Place()
     width = HD
     counts, out_counts = heads // 2, (heads + 2) // 2
     refs = list(refs)
-    total_refs, refs = refs[:11], refs[11:]
-    spread = Spread(here, out_counts, refs[:7])
-    d_mixed, tiny_own, d_kv, give, taken, give_sems, tiny_send, tiny_recv = refs[7:15]
-    line = Line(here, line_counts, [line_own, line_out] + refs[15:])
+    line_counts = 8 * per
+    cols = d_attn.shape[1]
+    extra = cols // (rows // per)
+
+    def take(count):
+        taken_refs = refs[:count]
+        del refs[:count]
+        return taken_refs
+
+    total_refs = take(11)
+    spread = Spread(here, out_counts, take(7))
+    d_mixed, tiny_own, tiny_all, d_kv, give, taken, give_sems, tiny_send, tiny_recv = take(9)
+    sums, gain_sum, tile, tile_send, tile_recv, put_sems, local_sems = take(7)
+
+    def far(at):
+        return turned(at // per)
+
+    def near(at):
+        return at // (2 * per), at // per % 2
+
+    def place_ffn(at):
+        return here.shard(*far(at)) * per + at % per
+
+    def place_tok(at):
+        return jnp.where(at < line_counts, here.shard(*near(jnp.minimum(at, line_counts - 1))) * per + at % per, at)
+
+    ffn_sum = take(1)[0]
+    line = Line(here, line_counts, [ffn, ffn_sum] + take(8), place_ffn)
+    contrib, summed = take(2)
+    line_tok = Line(here, line_counts + extra, [contrib, summed] + take(8), place_tok)
     tiny = Tiny(here, tiny_own, tiny_all, (tiny_send, tiny_recv), False)
     got, core = spread.got, here.core
     product = products(here, d_attn, lambda half: w_out, True, rows, width, counts * width, True)
@@ -917,9 +959,7 @@
         slot[:, :half] = ((lead * cos[0] + trail * sin[0]) * rms[0]).astype(got.dtype)
         slot[:, half:] = ((trail * cos[0] - lead * sin[0]) * rms[0]).astype(got.dtype)
 
-        @pl.when(done + head < line_counts + 2)
-        def _():
-            line.step(done + head)
+        line.step(done + head)
         return dots
 
     dots = lax.fori_loop(0, heads, one_head, jnp.zeros((rows, 1), jnp.float32))
@@ -935,9 +975,9 @@
             own = own + dots * (1.0 / scale)
         own = own * (rms[side] * rms[side] * (1.0 / depth))
         for at in range(rows // LANES):
-            tile = own[at * LANES : (at + 1) * LANES, :] * eye
+            spot_values = own[at * LANES : (at + 1) * LANES, :] * eye
             spot = side * (rows // LANES) + at
-            tiny_own[spot : spot + 1, :] = jnp.sum(tile, axis=0, keepdims=True)
+            tiny_own[spot : spot + 1, :] = jnp.sum(spot_values, axis=0, keepdims=True)
         lead, trail = d_key[:, :half], d_key[:, half:]
         parts = [(lead * cos[side] + trail * sin[side]) * rms[side],
                  (trail * cos[side] - lead * sin[side]) * rms[side],
@@ -957,6 +997,7 @@
         got[0, core, 1, out_counts - 2 + at] = value.astype(got.dtype)
     tiny.begin()
     spread.begin()
+    gain_sum[...] = jnp.zeros_like(gain_sum)
 
     def blocks(across, half_at, at, fresh):
         span = pl.ds(pl.multiple_of((half_at * out_counts + at) * width, width), width)
@@ -972,13 +1013,182 @@
         else:
             grad[:, span] += gained
 
-    spread.run(blocks, line, done)
-    line.end(done + 4 * out_counts)
+    def column(values):
+        return jnp.sum(eye * values, axis=1, keepdims=True)
+
+    def contribute(chip):
+        def shard_rows(other, _):
+            shard, partner = here.shard(chip, other), here.shard((chip + 2) % 4, other)
+            for at in range(rows // LANES):
+                row = pl.ds(pl.multiple_of(shard * rows + at * LANES, LANES), LANES)
+                kept = rows // LANES + at
+                dot = column(tiny_all[shard, at : at + 1, :] + tiny_all[partner, kept : kept + 1, :])
+                value, x_rows = sums[row, :], x_low[row, :].astype(jnp.float32)
+                contrib[row, :] = (value * gain[...] - x_rows * dot).astype(contrib.dtype)
+                gain_sum[...] += jnp.sum(value * x_rows, axis=0, keepdims=True)
+            return 0
+
+        lax.fori_loop(0, 2, shard_rows, 0)
+        line_tok.launch(2 * per * chip, 2 * per)
+
+    first_part = 2 * per
+
+    def hook(stage, at):
+        if stage < 0:
+            line.step(done + at)
+        elif stage < 2:
+            line_tok.step(stage * out_counts + at, 0, first_part)
+        else:
+            line_tok.step(at, first_part, line_counts + extra - first_part)
+
+    def between(stage):
+        if stage < 0:
+            tiny.end()
+            contribute(0)
+            line.steps(min(done + out_counts, line_counts + 2), line_counts + 2)
+        elif stage == 1:
+            line_tok.steps(2 * out_counts, first_part + 2, 0, first_part)
+            contribute(1)
+            contribute(2)
+        elif stage == 2:
+            contribute(3)
+
+    spread.run(blocks, hook=hook, between=between)
+    for half_at in range(cols // (rows // per)):
+        span = pl.ds(line_counts * (rows // per) + half_at * (rows // per), rows // per)
+        source = slice(half_at * (rows // per), (half_at + 1) * (rows // per))
+        contrib[span, :] = grad[source, heads * HD :].astype(contrib.dtype)
+    line_tok.launch(line_counts, extra)
+    for at in range(cols // LANES):
+        tile[at : at + 1, :] = gain_sum[:, at * LANES : (at + 1) * LANES]
+        spot = cols // LANES + at
+        tile[spot : spot + 1, :] = gain_grad[:, at * LANES : (at + 1) * LANES]
+
+    def tile_copy(step):
+        return remote(tile, gain_tiles.at[here.z], tile_send.at[step], tile_recv.at[step],
+                      (here.dp, here.seq, (here.z + step + 1) % 4))
+
+    line.settle()
+    me = here.shard(0, 0)
+    columns = pl.ds(pl.multiple_of(me * cols, cols), cols)
+    chunk = line.chunk
+
+    def put(which, at):
+        kind = (line, line_tok)[which]
+        goal = here.device(*(far, near)[which](at))
+        dst = (out, d_tok)[which].at[pl.ds(pl.multiple_of(at % per * chunk, chunk), chunk), columns]
+        return remote(kind.from_end.at[at], dst, put_sems.at[which, 0, at], put_sems.at[which, 1, at], goal)
+
+    def emit(which, at):
+        kind = (line, line_tok)[which]
+        row = kind.rows(at)
+        base = (resid, d_attn)[which][row, :].astype(jnp.float32)
+        kind.from_end[at] = (base + kind.out[row, :].astype(jnp.float32)).astype(out.dtype)
+
+    def is_own(which, at):
+        return at >= 7 * per if which == 0 else at < per
+
+    def send(which, at):
+        own = is_own(which, at)
+
+        @pl.when(own)
+        def _():
+            dst = (out, d_tok)[which].at[pl.ds(pl.multiple_of(at % per * chunk, chunk), chunk), columns]
+            pltpu.make_async_copy((line, line_tok)[which].from_end.at[at], dst, local_sems.at[which, at % per]).start()
+
+        @pl.when(jnp.logical_not(own))
+        def _():
+            put(which, at).start()
+
+    for step in range(3):
+        tile_copy(step).start()
+    gain_tiles[here.z] = tile[...]
+    left = line_counts + extra - first_part
+
+    @pl.when(line.inner == 1)
+    def _():
+        def early(at, _):
+            emit(1, at)
+            return 0
+
+        lax.fori_loop(0, first_part, early, 0)
+
+        def both(at, _):
+            line_tok.step(at, first_part, left)
+            spot = at - out_counts
+            ready = first_part + at - out_counts
+
+            @pl.when(jnp.logical_and(spot > 0, spot <= line_counts))
+            def _():
+                send(0, spot - 1)
+
+            @pl.when(jnp.logical_and(spot > 0, spot <= first_part))
+            def _():
+                send(1, spot - 1)
+
+            @pl.when(jnp.logical_and(ready > first_part, ready <= line_counts))
+            def _():
+                send(1, ready - 1)
+
+            @pl.when(spot < line_counts)
+            def _():
+                emit(0, spot)
+
+            @pl.when(ready < line_counts)
+            def _():
+                emit(1, ready)
+            return 0
+
+        lax.fori_loop(out_counts, out_counts + line_counts + 1, both, 0)
+        line_tok.steps(out_counts + line_counts + 1, left + 2, first_part, left)
+
+        def drain(at, _):
+            line_tok.down(at).wait_send()
+            return 0
+
+        lax.fori_loop(0, line_counts + extra, drain, 0)
+
+    @pl.when(line.inner == 0)
+    def _():
+        def arrive(at, _):
+            line_tok.up(at).wait_send()
+            line_tok.down(at).wait_recv()
+
+            @pl.when(jnp.logical_and(at > 0, at <= line_counts))
+            def _():
+                send(0, at - 1)
+                send(1, at - 1)
+
+            @pl.when(at < line_counts)
+            def _():
+                emit(0, at)
+                emit(1, at)
+            return 0
+
+        lax.fori_loop(0, line_counts + extra, arrive, 0)
+
+    for half_at in range(extra):
+        span = pl.ds((line_counts + half_at) * chunk, chunk)
+        kv_sum[half_at * chunk : (half_at + 1) * chunk, :] = summed[span, :].astype(jnp.float32)
     spread.end()
-    tiny.end()
-
-
-def home(d_attn, w_out, queries, kv, probs, rms, cos, sin, act_t, w_qkv, line, cid, line_counts=16):
+    for which in range(2):
+        def finish(at, _, which=which):
+            @pl.when(jnp.logical_not(is_own(which, at)))
+            def _():
+                put(which, at).wait()
+            return 0
+
+        lax.fori_loop(0, line_counts, finish, 0)
+        for at in range(per):
+            dst = (out, d_tok)[which].at[at * chunk : (at + 1) * chunk, columns]
+            spot = (7 * per if which == 0 else 0) + at
+            pltpu.make_async_copy((line, line_tok)[which].from_end.at[spot], dst, local_sems.at[which, at]).wait()
+    for step in range(3):
+        tile_copy(step).wait()
+
+
+def tail(d_attn, w_out, queries, kv, probs, rms, cos, sin, act_t, w_qkv, ffn, x_low, resid, gain, gain_grad, cid,
+         per=2):
     total, cols = d_attn.shape
     rows = total // 8
     wide = w_out.shape[0]
@@ -986,24 +1196,36 @@
     low, f32 = jnp.bfloat16, jnp.float32
     dma = pltpu.SemaphoreType.DMA
     vm = pl.BlockSpec(memory_space=pltpu.VMEM)
+    counts = 8 * per
+    chunk = rows // per
+    extra = cols // chunk
+    long = (total + cols, cols)
     out_shape = [
-        jax.ShapeDtypeStruct((total, cols), f32),
+        jax.ShapeDtypeStruct((rows, 8 * cols), low),
+        jax.ShapeDtypeStruct((rows, 8 * cols), low),
         jax.ShapeDtypeStruct(w_qkv.shape, f32),
-        jax.ShapeDtypeStruct((8, 8, LANES), f32),
-        jax.ShapeDtypeStruct(line.shape, line.dtype),
+        jax.ShapeDtypeStruct((cols, 2 * HD), f32),
+        jax.ShapeDtypeStruct((4, 8, LANES), f32),
     ]
     scratch = reduce_scratch(heads // 2, rows, HD) + spread_scratch((heads + 2) // 2, rows, HD)
     scratch += [
         pltpu.VMEM((rows, wide), f32),
         pltpu.VMEM((8, LANES), f32),
+        pltpu.VMEM((8, 8, LANES), f32),
         pltpu.VMEM((2, rows, 2 * HD), f32),
         pltpu.VMEM((rows, 2 * HD), low),
         pltpu.VMEM((rows, 2 * HD), low),
         dma((2,)), dma((7,)), dma((7,)),
-    ] + line_scratch(line_counts, line.shape, low)
-    operands = [d_attn, w_out, queries, kv, probs, rms, cos, sin, act_t, w_qkv, line]
-    kernel = functools.partial(home_kernel, rows, heads, line_counts)
-    return kernel_call(kernel, out_shape, operands, [vm] * len(operands), scratch, cid, "home")
+        pltpu.VMEM((total, cols), f32),
+        pltpu.VMEM((1, cols), f32),
+        pltpu.VMEM((8, LANES), f32),
+        dma((3,)), dma((3,)), dma((2, 2, counts)), dma((2, per)),
+        pltpu.VMEM((total, cols), low),
+    ] + line_scratch(counts, (total, cols), low)
+    scratch += [pltpu.VMEM(long, low), pltpu.VMEM(long, low)] + line_scratch(counts + extra, long, low)
+    operands = [d_attn, w_out, queries, kv, probs, rms, cos, sin, act_t, w_qkv, ffn, x_low, resid, gain, gain_grad]
+    kernel = functools.partial(tail_kernel, rows, heads, per)
+    return kernel_call(kernel, out_shape, operands, [vm] * len(operands), scratch, cid, "tail")
 
 
 def turn_kernel(rows, cols, back, src, out, own_sem, send, recv):
@@ -1049,127 +1271,6 @@
                                              vmem_limit_bytes=VMEM_LIMIT),
         name=f"turn_{cid}",
     )(src)
-
-def close_kernel(rows, cols, per, extra, own, rest, other_own, tile, out, other_out, summed, tiles, ready, local_sem,
-                 other_send, other_recv, put_send, put_recv, tile_send, tile_recv, *line_refs):
-    here = Place()
-    me = here.shard(0, 0)
-    counts = 8 * per
-
-    def target(at):
-        turn_at = at // per
-        return 3 - turn_at // 2, 1 - turn_at % 2
-
-    def place(at):
-        across, other = target(jnp.minimum(at, counts - 1))
-        return jnp.where(at < counts, here.shard(across, other) * per + at % per, at)
-
-    line = Line(here, counts + extra, [own, summed] + list(line_refs), place)
-    peers = [turned(at) for at in range(7)]
-    greet(here, slice_peers(here), True)
-    line.begin()
-
-    def tile_copy(step):
-        return remote(tile, tiles.at[here.z], tile_send.at[step], tile_recv.at[step],
-                      (here.dp, here.seq, (here.z + step + 1) % 4))
-
-    for step in range(3):
-        tile_copy(step).start()
-    tiles[here.z] = tile[...]
-    columns = pl.ds(pl.multiple_of(me * cols, cols), cols)
-
-    def turn_copy(at):
-        across, other = peers[at]
-        src = other_own.at[pl.ds(pl.multiple_of(here.shard(across, other) * rows, rows), rows), :]
-        return remote(src, other_out.at[:, columns], other_send.at[at], other_recv.at[at],
-                      here.device(across, other))
-
-    for at in range(7):
-        turn_copy(at).start()
-    mine = pltpu.make_async_copy(other_own.at[pl.ds(pl.multiple_of(me * rows, rows), rows), :],
-                                 other_out.at[:, columns], local_sem)
-    mine.start()
-    chunk = line.chunk
-
-    def put(at):
-        across, other = target(at)
-        dst = out.at[pl.ds(pl.multiple_of(at % per * chunk, chunk), chunk), columns]
-        return remote(ready.at[at], dst, put_send.at[at], put_recv.at[at], here.device(across, other))
-
-    def emit(at):
-        total = rest[line.rows(at), :] + summed[line.rows(at), :].astype(jnp.float32)
-
-        @pl.when(at < 7 * per)
-        def _():
-            ready[at] = total.astype(ready.dtype)
-            put(at).start()
-
-        @pl.when(at >= 7 * per)
-        def _():
-            out[pl.ds(pl.multiple_of(at % per * chunk, chunk), chunk), columns] = total.astype(out.dtype)
-
-    @pl.when(line.inner == 1)
-    def _():
-        def both(at, _):
-            line.step(at)
-
-            @pl.when(jnp.logical_and(at > 1, at < counts + 2))
-            def _():
-                emit(at - 2)
-            return 0
-
-        lax.fori_loop(0, counts + extra + 2, both, 0)
-
-        def drain(at, _):
-            line.over(at).wait_send()
-            line.down(at).wait_send()
-            return 0
-
-        lax.fori_loop(0, counts + extra, drain, 0)
-
-    @pl.when(line.inner == 0)
-    def _():
-        def take(at, _):
-            line.up(at).wait_send()
-            line.down(at).wait_recv()
-
-            @pl.when(at < counts)
-            def _():
-                emit(at)
-            return 0
-
-        lax.fori_loop(0, counts + extra, take, 0)
-
-    mine.wait()
-    for at in range(7):
-        turn_copy(at).wait()
-
-    def finish(at, _):
-        put(at).wait()
-        return 0
-
-    lax.fori_loop(0, 7 * per, finish, 0)
-    for step in range(3):
-        tile_copy(step).wait()
-
-
-def close(own, rest, other_own, tile, cid, per=2):
-    total, cols = rest.shape
-    rows = total // 8
-    low = own.dtype
-    dma = pltpu.SemaphoreType.DMA
-    vm = pl.BlockSpec(memory_space=pltpu.VMEM)
-    whole = jax.ShapeDtypeStruct((rows, 8 * cols), low)
-    chunk = rows // per
-    extra = (own.shape[0] - total) // chunk
-    counts = 8 * per
-    out_shape = [whole, whole, jax.ShapeDtypeStruct(own.shape, low), jax.ShapeDtypeStruct((4,) + tile.shape, tile.dtype)]
-    scratch = [
-        pltpu.VMEM((7 * per, chunk, cols), low),
-        dma(()), dma((7,)), dma((7,)), dma((7 * per,)), dma((7 * per,)), dma((3,)), dma((3,)),
-    ] + line_scratch(counts + extra, own.shape, low)
-    kernel = functools.partial(close_kernel, rows, cols, per, extra)
-    return kernel_call(kernel, out_shape, [own, rest, other_own, tile], [vm] * 4, scratch, cid, "close")
 
 
 LANES = 128
@@ -1274,7 +1375,7 @@
     d_attn = d_resid.astype(low)
     grad_out = matmul_tn(mixed_all, d_attn)
 
-    d_act_one, grad_qkv, dots_all, ffn_sum = home(
+    d_tokens, out, grad_qkv, grad_kv, gain_tiles = tail(
         d_attn,
         w_out,
         queries,
@@ -1286,22 +1387,13 @@
         act_one.T,
         w_qkv,
         ffn.astype(low),
+        x_low,
+        resid.astype(low),
+        gain_one[None, :],
+        grad_gain_two[None, :],
         9,
     )
-    pairs = dots_all.reshape(parts // 2, 2, 8, LANES)
-    dot_one = (pairs[:, :, :tiles] + pairs[:, ::-1, tiles : 2 * tiles]).reshape(parts * rows, 1)
-    grad_gain_one = jnp.sum(d_act_one * x_col, axis=0)
-    d_tokens, out, summed, gain_tiles = close(
-        jnp.concatenate(
-            [(d_act_one * gain_one - x_col * dot_one).astype(low), grad_qkv[:, qw:].astype(low)]
-        ),
-        d_resid,
-        (resid + ffn_sum.astype(jnp.float32)).astype(low),
-        jnp.stack([grad_gain_one, grad_gain_two]).reshape(8, LANES),
-        10,
-    )
     grad_query = grad_qkv[:, :qw]
-    grad_kv = summed[parts * rows :].astype(jnp.float32)
     gains = jnp.sum(gain_tiles, axis=0).reshape(2, -1)
     return (
         out,

time: 778 us -> 741 us (0.952)
  Pallas kernels: 674 us -> 652 us
  other arithmetic: 56.8 us -> 40.9 us
    pallas_call x8 -> x7, Pallas kernels: 643 us -> 621 us  [kernel_call(): pl.pallas_call(kernel, out_shape=out_shape, in_specs=specs, out_specs=[vm...]
    unnamed x45 -> x54, local copies, waits for them, and re-layouts: 17.7 us -> 17.6 us
where the time goes in v5:
time: 741 us; the launch traced here: 730 us
  Pallas kernels  652 us (88%)
  other arithmetic  40.9 us (6%)
  local copies, waits for them, and re-layouts  32.4 us (4%)
    pallas_call x7, Pallas kernels, kernel_call(): pl.pallas_call(kernel, out_shape=out_shape, in_specs=specs, out_specs=[vm...  621 us
    pallas_call x1, Pallas kernels, turn(): pl.pallas_call(functools.partial(turn_kernel, rows, cols, back), out_shap...  30.9 us
    unnamed x54, local copies, waits for them, and re-layouts  17.6 us

profile of v5, /device:TPU:0, one launch (start us, length us, event | category | flops | bytes accessed | tf_op | source)
XLA Modules:
  0.0 729.7 jit_solution(11569821491526950012)
XLA Ops:
  0.6 0.8 slice_compare_fusion
  1.5 0.1 add_select_fusion
  1.6 0.3 reduce-window.9
  1.9 0.1 slice.41
  2.0 0.1 slice_reduce_fusion.1
  2.1 0.1 fusion.11
  2.2 0.8 fusion.12
  3.1 0.9 and_convert_fusion.mask
  4.0 1.0 multiply_sine_fusion
  5.0 0.8 dynamic-slice_bitcast_fusion
  5.8 30.9 %turn_1.1.x_low = bf16[2048,512]{1,0:T(8,128)(2,1)} custom-call(bf16[256,4096]{1,0:T(8,128)(2,1)} %src.1), custom_call_target="tpu_custom_call" | custom-call | tf_op jit(solution)/shard_map/turn_1/pallas_call | solution.py:1264
  36.7 0.0 copy-start.9
  36.7 0.8 convert_element_type.67
  37.5 3.4 fusion.act
  40.8 1.0 constant_dynamic-update-slice_fusion.1
  41.9 0.0 copy-done.11
  41.9 0.8 constant_dynamic-update-slice_fusion.refs_0_.w_qkv
  42.7 0.6 broadcast_in_dim.14.refs_1_
  43.3 35.4 %scatter_product_2.1 = (f32[256,1536]{1,0:T(8,128)}, f32[8,8,128]{2,1,0:T(8,128)}) custom-call(bf16[2048,512]{1,0:T(8,128)(2,1)} %fusion.act, bf16[512,1536]{1,0:T(8,128)(2,1)} %constant_dynamic-update-slice_fusion.refs_0_.w_qkv, f32[8,8,128]{2,1,0:T(8,128)} %broadcast_in_dim.14.refs_1_), custom_call_target="tpu_custom_call" | custom-call | tf_op jit(solution)/shard_map/scatter_product_2/pallas_call | solution.py:391
  78.7 2.1 multiply_reduce_fusion.2
  80.8 0.8 broadcast_in_dim.15.rms
  81.6 0.6 pad.11.tiny_own
  82.2 59.1 %attend_3.1 = (bf16[2048,512]{1,0:T(8,128)(2,1)}, bf16[2048,1024]{1,0:T(8,128)(2,1)}, bf16[2048,512]{1,0:T(8,128)(2,1)}, bf16[2,256,512]{2,1,0:T(8,128)(2,1)}, f...) custom-call(f32[256,1536]{1,0:T(8,128)} %get-tuple-element.34.qkv, ...), custom_call_target="tpu_custom_call" | custom-call | tf_op jit(solution)/shard_map/attend_3/pallas_call | solution.py:391
  141.3 76.5 %scatter_product_4.1 = (f32[256,3072]{1,0:T(8,128)}, f32[8,8,128]{2,1,0:T(8,128)}, bf16[2048,512]{1,0:T(8,128)(2,1)}) custom-call(bf16[2048,512]{1,0:T(8,128)(2,1)} %get-tuple-element.35.act, bf16[3072,512]{1,0:T(8,128)(2,1)} %refs_0_.7, f32[8,8,128]{2,1,0:T(8,128)} %broadcast_in_dim.14.refs_1_, bf16[2048,512]{1,0:T(8,128)(2,1)} %get-tuple-element.36.refs_2_), custom_call_target="tpu_custom_call" | custom-call | tf_op jit(solution)/shard_map/scatter_product_4/pallas_call | solution.py:391
  217.8 0.7 convert_element_type.74
  218.5 4.4 multiply_reduce_fusion.1
  222.9 0.6 pad.12.refs_2_
  223.5 115.5 %scatter_product_6.1 = (f32[256,6144]{1,0:T(8,128)}, f32[8,8,128]{2,1,0:T(8,128)}) custom-call(bf16[2048,512]{1,0:T(8,128)(2,1)} %get-tuple-element.68.act, bf16[512,3072]{1,0:T(8,128)(2,1)} %refs_0_.6, bf16[512,3072]{1,0:T(8,128)(2,1)} %refs_1_.3, f32[8,8,128]{2,1,0:T(8,128)} %pad.12.refs_2_), custom_call_target="tpu_custom_call" | custom-call | tf_op jit(solution)/shard_map/scatter_product_6/pallas_call | solution.py:391
  339.0 0.8 slice_reduce_fusion
  339.8 7.4 %add_reduce_fusion = (f32[256]{0:T(256)S(1)}, f32[256,3072]{1,0:T(8,128)S(1)}, bf16[256,3072]{1,0:T(8,128)(2,1)}, bf16[256,3072]{1,0:T(8,128)(2,1)}) fusion(f32[256,6144]{1,0:T(8,128)} %get-tuple-element.38, f32[256]{0:T(256)S(1)} %fusion.8, f32[256,3072]{1,0:T(8,128)} %get-tuple-element.40), kind=kLoop, calls=%fused_computation.18 | loop fusion | flops 25165568 | bytes 15730688 | tf_op jit(solution)/shard_map/reduce_sum | solution.py:1349
  347.2 0.6 pad.13.refs_4_
  347.8 1.5 multiply_convert_fusion.2.refs_2_
  349.3 2.4 copy.23.act
  351.7 118.9 %gather_product_7.1 = (f32[2048,512]{1,0:T(8,128)}, f32[512,3072]{1,0:T(8,128)}, f32[512,3072]{1,0:T(8,128)}, f32[8,8,128]{2,1,0:T(8,128)}) custom-call(bf16[512,2048]{1,0:T(8,128)(2,1)} %copy.23.act, bf16[512,3072]{1,0:T(8,128)(2,1)} %refs_0_.6, bf16[512,3072]{1,0:T(8,128)(2,1)} %refs_1_.3, bf16[256,3072]{1,0:T(8,128)(2,1)} %multiply_convert_fusion.2.refs_2_, ...), custom_call_target="tpu_custom_call" | custom-call | tf_op jit(solution)/shard_map/gather_product_7/pallas_call | solution.py:391
  470.5 0.8 slice.46
  471.3 5.9 multiply_reduce_fusion
  477.2 0.6 squeeze.9.refs_2_
  477.8 69.4 %gather_product_8.1 = (f32[2048,512]{1,0:T(8,128)}, f32[3072,512]{1,0:T(8,128)}, f32[8,8,128]{2,1,0:T(8,128)}, bf16[2048,512]{1,0:T(8,128)(2,1)}) custom-call(bf16[2048,512]{1,0:T(8,128)(2,1)} %get-tuple-element.35.act, bf16[3072,512]{1,0:T(8,128)(2,1)} %refs_0_.7, bf16[256,3072]{1,0:T(8,128)(2,1)} %get-tuple-element.65.refs_1_, f32[8,128]{1,0:T(8,128)} %squeeze.9.refs_2_, ...), custom_call_target="tpu_custom_call" | custom-call | tf_op jit(solution)/shard_map/gather_product_8/pallas_call | solution.py:391
  547.2 3.0 add_convert_fusion.d_attn
  550.2 0.0 copy-start.1
  550.2 0.4 copy-done.4
  550.7 3.7 fusion.14
  554.4 0.0 copy-done.3
  554.4 0.0 copy-start.7
  554.4 0.0 copy-start.12
  554.4 0.0 copy-start
  554.4 1.6 convert_element_type.82.ffn
  556.0 0.7 slice_bitcast_fusion.2
  556.7 0.8 broadcast_in_dim.35.rms
  557.6 0.7 pad_maximum_fusion.cos
  558.3 0.7 pad_maximum_fusion.1.sin
  559.0 0.4 fusion.17
  559.5 2.4 copy.24.act_t
  561.8 146.1 %tail_9.1 = (bf16[256,4096]{1,0:T(8,128)(2,1)}, bf16[256,4096]{1,0:T(8,128)(2,1)}, f32[512,1536]{1,0:T(8,128)}, f32[512,512]{1,0:T(8,128)}, f32[4,8,128]{2,1,0:T(8,128)}) custom-call(bf16[2048,512]{1,0:T(8,128)(2,1)} %copy-done.1, bf16[1024,512]{1,0:T(8,128)(2,1)} %w_out.3, bf16[256,1024]{1,0:T(8,128)(2,1)} %get-tuple-element.44.queries, ...), custom_call_target="tpu_custom_call" | custom-call | tf_op jit(solution)/shard_map/tail_9/pallas_call | solution.py:391
  707.9 4.2 convert_element_type.84
  712.2 1.5 slice.49
  713.6 0.6 slice_bitcast_fusion
  714.2 0.3 copy-done.5
  714.5 1.3 copy.36
  715.9 1.0 copy.37
  716.8 6.9 copy.38
  723.7 2.8 copy.39
  726.6 0.3 slice-done.3
  726.8 2.7 copy.40
  (47 shorter events, 0.2 us)
Async XLA Ops:
  36.7 4.2 copy-start.9
  37.5 4.4 copy-start.14
  37.5 4.4 copy-start.11
  218.5 4.4 copy-start.16
  347.2 2.1 copy-start.2
  547.2 3.5 copy-start.4
  550.2 4.1 copy-start.1
  550.7 3.7 copy-start.3
  554.4 3.2 copy-start.8
  554.4 3.2 copy-start.13
  554.4 3.9 copy-start.7
  554.4 3.9 copy-start.12
  554.4 4.6 copy-start
  554.4 4.6 copy-start.15
  707.9 4.3 copy-start.6
  712.2 1.5 copy-start.17
  712.2 2.4 copy-start.5
  713.6 2.2 copy-start.10
  715.8 7.9 %slice-start = ((s8[6291456]{0:T(1024)(128)(4,1)}), s8[4194304]{0:T(1024)(128)(4,1)S(1)}, s32[]{:S(2)}) async-start(s8[6291456]{0:T(1024)(128)(4,1)} %bitcast.48), calls=%async_computation | async-start | bytes 8388608
  716.8 6.9 slice-start.1
  716.8 9.8 %slice-start.2 = ((s8[6291456]{0:T(1024)(128)(4,1)}), s8[4194304]{0:T(1024)(128)(4,1)S(1)}, s32[]{:S(2)}) async-start(s8[6291456]{0:T(1024)(128)(4,1)} %bitcast.50), calls=%async_computation.2 | async-start | bytes 8388608
  723.7 3.1 slice-start.3

commit v6 on v5

--- a/solution.py
+++ b/solution.py
@@ -386,13 +386,13 @@
     return [here.device(*turned(at)) for at in range(7)]
 
 
-def kernel_call(kernel, out_shape, operands, specs, scratch, cid, name):
+def kernel_call(kernel, out_shape, operands, specs, scratch, cid, name, out_specs=None):
     vm = pl.BlockSpec(memory_space=pltpu.VMEM)
     return pl.pallas_call(
         kernel,
         out_shape=out_shape,
         in_specs=specs,
-        out_specs=[vm] * len(out_shape),
+        out_specs=out_specs or [vm] * len(out_shape),
         scratch_shapes=scratch,
         compiler_params=pltpu.CompilerParams(
             collective_id=cid, has_side_effects=True, vmem_limit_bytes=VMEM_LIMIT
@@ -425,96 +425,127 @@
 
 
 class Reduce:
-    def __init__(self, here, counts, width, product, out, refs):
-        self.counts, self.width, self.product, self.out = counts, width, product, out
+    def __init__(self, here, counts, product, refs, before=None):
+        self.counts, self.product, self.before = counts, product, before
         self.held, self.sib_out, self.sib_in, self.from_x, self.from_y = refs[:5]
         self.sib_sems, self.x_sems, self.y_sems = refs[5:7], refs[7:9], refs[9:11]
         self.sib, self.xdev, self.ydev = here.device(0, 1), here.device(1, 0), here.device(2, 0)
-        self.stages = (((3, 0), (3, 1)), ((1, 0), (2, 1)), ((0, 0), (0, 1)), ((1, 1), (2, 0)))
-
-    def to_sib(self, stage, stream, at):
-        spot = (stage, stream, at)
-        return remote(self.sib_out.at[spot], self.sib_in.at[spot], self.sib_sems[0].at[spot],
-                      self.sib_sems[1].at[spot], self.sib)
-
-    def to_x(self, step, at, stage=0):
-        return remote(self.held.at[stage, 0, at], self.from_x.at[step, at], self.x_sems[0].at[step, at],
-                      self.x_sems[1].at[step, at], self.xdev)
-
-    def to_y(self, step, at, stage=0):
-        return remote(self.held.at[stage, 1, at], self.from_y.at[step, at], self.y_sems[0].at[step, at],
-                      self.y_sems[1].at[step, at], self.ydev)
-
-    def cols(self, half, at):
-        return pl.ds(pl.multiple_of((half * self.counts + at) * self.width, self.width), self.width)
-
-    def compute(self, stage, at):
-        for stream, (across, half) in enumerate(self.stages[stage]):
-            self.sib_out[stage, stream, at] = self.product(across, 1, half, at).astype(jnp.bfloat16)
+        self.steps = 4 * counts
+        self.ring = self.sib_out.shape[0]
+
+    def streams(self, stage):
+        far = stage // 3
+        x_chip = jnp.where(stage == 0, 3, jnp.where(stage == 2, 0, 1))
+        y_chip = jnp.where(stage == 0, 3, jnp.where(stage == 2, 0, 2))
+        return (x_chip, far), (y_chip, 1 - far)
+
+    def to_sib(self, step, stream):
+        stage, at = step // self.counts, step % self.counts
+        return remote(self.sib_out.at[step % self.ring, stream], self.sib_in.at[stage, stream, at],
+                      self.sib_sems[0].at[stage, stream, at], self.sib_sems[1].at[stage, stream, at], self.sib)
+
+    def to_x(self, hop, at, stage=0):
+        return remote(self.held.at[stage, 0, at], self.from_x.at[hop, at], self.x_sems[0].at[hop, at],
+                      self.x_sems[1].at[hop, at], self.xdev)
+
+    def to_y(self, hop, at, stage=0):
+        return remote(self.held.at[stage, 1, at], self.from_y.at[hop, at], self.y_sems[0].at[hop, at],
+                      self.y_sems[1].at[hop, at], self.ydev)
+
+    def compute(self, step):
+        stage, at = step // self.counts, step % self.counts
+        if self.before:
+            for stop in range(3):
+                @pl.when(step == stop * self.counts)
+                def _():
+                    self.before(stop)
+
+        @pl.when(step >= self.ring)
+        def _():
+            for stream in range(2):
+                self.to_sib(step - self.ring, stream).wait_send()
+
+        for stream, (across, half) in enumerate(self.streams(stage)):
+            self.sib_out[step % self.ring, stream] = self.product(across, 1, half, at).astype(jnp.bfloat16)
             self.held[stage, stream, at] = self.product(across, 0, half, at).astype(jnp.bfloat16)
         for stream in range(2):
-            self.to_sib(stage, stream, at).start()
-
-    def finish(self, stage, at):
+            self.to_sib(step, stream).start()
+
+    def finish(self, step):
+        stage, at = step // self.counts, step % self.counts
         for stream in range(2):
-            self.to_sib(stage, stream, at).wait_recv()
-            total = self.held[stage, stream, at].astype(jnp.float32)
-            total += self.sib_in[stage, stream, at].astype(jnp.float32)
-            if stage == 3 and stream == 0:
-                self.to_y(0, at).wait_recv()
-                total += self.from_y[0, at].astype(jnp.float32)
-            if stage == 3 and stream == 1:
-                self.to_x(0, at).wait_recv()
-                total += self.from_x[0, at].astype(jnp.float32)
-            if stage == 2:
-                self.out[:, self.cols(stream, at)] = total
-            else:
-                self.held[stage, stream, at] = total.astype(jnp.bfloat16)
-        if stage != 2:
-            step = (0, 1, None, 2)[stage]
-            self.to_x(step, at, stage).start()
-            self.to_y(step, at, stage).start()
+            self.to_sib(step, stream).wait_recv()
+
+        def total(stream):
+            return self.held[stage, stream, at].astype(jnp.float32) + self.sib_in[stage, stream, at].astype(
+                jnp.float32)
+
+        @pl.when(stage < 3)
+        def _():
+            for stream in range(2):
+                self.held[stage, stream, at] = total(stream).astype(jnp.bfloat16)
+
+        @pl.when(stage == 3)
+        def _():
+            self.to_y(0, at).wait_recv()
+            self.held[3, 0, at] = (total(0) + self.from_y[0, at].astype(jnp.float32)).astype(jnp.bfloat16)
+            self.to_x(0, at).wait_recv()
+            self.held[3, 1, at] = (total(1) + self.from_x[0, at].astype(jnp.float32)).astype(jnp.bfloat16)
+
+        @pl.when(stage != 2)
+        def _():
+            hop = stage - stage // 3
+            self.to_x(hop, at, stage).start()
+            self.to_y(hop, at, stage).start()
 
     def run(self, line=None):
-        for stage in range(4):
-            def body(at, _, stage=stage):
-                self.compute(stage, at)
-
-                @pl.when(at > 0)
-                def _():
-                    self.finish(stage, at - 1)
-
-                if line:
-                    line.step(stage * self.counts + at)
-                return 0
-
-            lax.fori_loop(0, self.counts, body, 0)
-            self.finish(stage, self.counts - 1)
-
-    def end(self):
+        def body(step, _):
+            @pl.when(step < self.steps)
+            def _():
+                self.compute(step)
+
+            @pl.when(step > 0)
+            def _():
+                self.finish(step - 1)
+
+            if line:
+                line.step(step)
+            return 0
+
+        lax.fori_loop(0, self.steps + 1, body, 0)
+        return self.steps + 1
+
+    def end(self, emit):
         def last(at, _):
+            values = []
             for half in range(2):
                 xs, ys = (1, 2) if half == 0 else (2, 1)
                 self.to_x(xs, at).wait_recv()
                 self.to_y(ys, at).wait_recv()
-                self.out[:, self.cols(half, at)] += self.from_x[xs, at].astype(
-                    jnp.float32) + self.from_y[ys, at].astype(jnp.float32)
-            for stage in range(4):
-                for stream in range(2):
-                    self.to_sib(stage, stream, at).wait_send()
-            for step in range(3):
-                self.to_x(step, at).wait_send()
-                self.to_y(step, at).wait_send()
+                values.append(self.held[2, half, at].astype(jnp.float32) + self.from_x[xs, at].astype(jnp.float32)
+                              + self.from_y[ys, at].astype(jnp.float32))
+            emit(at, *values)
+            for hop in range(3):
+                self.to_x(hop, at).wait_send()
+                self.to_y(hop, at).wait_send()
             return 0
 
         lax.fori_loop(0, self.counts, last, 0)
 
-
-def reduce_scratch(counts, rows, width):
+        def drain(at, _):
+            for stream in range(2):
+                self.to_sib(self.steps - self.ring + at, stream).wait_send()
+            return 0
+
+        lax.fori_loop(0, self.ring, drain, 0)
+
+
+def reduce_scratch(counts, rows, width, ring=4):
     low, dma = jnp.bfloat16, pltpu.SemaphoreType.DMA
     block = pltpu.VMEM((4, 2, counts, rows, width), low)
     landed = pltpu.VMEM((3, counts, rows, width), low)
-    return [block] * 3 + [landed] * 2 + [dma((4, 2, counts))] * 2 + [dma((3, counts))] * 4
+    sent = pltpu.VMEM((ring, 2, rows, width), low)
+    return [block, sent, block, landed, landed] + [dma((4, 2, counts))] * 2 + [dma((3, counts))] * 4
 
 
 class Spread:
@@ -524,84 +555,85 @@
         self.x_sems, self.y_sems, self.sib_sems = refs[1:3], refs[3:5], refs[5:7]
         self.core = here.core
         self.sib, self.xdev, self.ydev = here.device(0, 1), here.device(1, 0), here.device(2, 0)
-        self.stages = (((1, 0), (2, 1)), ((1, 1), (2, 0)), ((3, 1), (3, 0)))
 
     def slot(self, across, half, at):
         return self.got.at[across, self.core, half, at]
 
-    def x_copy(self, step, at):
-        src = self.slot(0, step, at) if step < 2 else self.slot(2, 1, at)
-        dst = self.slot(1, step, at) if step < 2 else self.slot(3, 1, at)
-        return remote(src, dst, self.x_sems[0].at[step, at], self.x_sems[1].at[step, at], self.xdev)
-
-    def y_copy(self, step, at):
-        src = self.slot(0, 1 - step, at) if step < 2 else self.slot(1, 0, at)
-        dst = self.slot(2, 1 - step, at) if step < 2 else self.slot(3, 0, at)
-        return remote(src, dst, self.y_sems[0].at[step, at], self.y_sems[1].at[step, at], self.ydev)
+    def x_copy(self, hop, at):
+        half = jnp.minimum(hop, 1)
+        src = self.slot(2 * (hop // 2), half, at)
+        dst = self.slot(1 + 2 * (hop // 2), half, at)
+        return remote(src, dst, self.x_sems[0].at[hop, at], self.x_sems[1].at[hop, at], self.xdev)
+
+    def y_copy(self, hop, at):
+        half = 1 - jnp.minimum(hop, 1)
+        src = self.slot(hop // 2, half, at)
+        dst = self.slot(2 + hop // 2, half, at)
+        return remote(src, dst, self.y_sems[0].at[hop, at], self.y_sems[1].at[hop, at], self.ydev)
+
+    def streams(self, stage):
+        some, last, late = jnp.minimum(stage, 1), stage // 3, stage // 2
+        return (some + 2 * last, late), (2 * some + last, 1 - late)
 
     def sib_copy(self, stage, stream, at):
-        across, half = (0, stream) if stage == 3 else self.stages[stage][stream]
+        across, half = self.streams(stage)[stream]
         slot = self.slot(across, half, at)
         spot = (stage, stream, at)
         return remote(slot, slot, self.sib_sems[0].at[spot], self.sib_sems[1].at[spot], self.sib)
 
     def begin(self):
-        for at in range(self.counts):
+        def first(at, _):
             self.x_copy(0, at).start()
             self.y_copy(0, at).start()
-        for at in range(self.counts):
-            self.sib_copy(3, 0, at).start()
-            self.sib_copy(3, 1, at).start()
-
-    def run(self, blocks, line=None, hook=None, between=None):
-        if hook is None:
-            def hook(stage, at):
-                if line:
-                    line.step((stage + 1) * self.counts + at)
+            return 0
 
         def own(at, _):
-            for half in range(2):
-                self.sib_copy(3, half, at).wait_recv()
-                blocks(0, half, at, True)
-            hook(-1, at)
+            self.sib_copy(0, 0, at).start()
+            self.sib_copy(0, 1, at).start()
             return 0
 
+        lax.fori_loop(0, self.counts, first, 0)
         lax.fori_loop(0, self.counts, own, 0)
-        if between:
-            between(-1)
-
-        def work(stage, at):
-            for stream, (across, half) in enumerate(self.stages[stage]):
-                self.sib_copy(stage, stream, at).wait_recv()
-                blocks(across, half, at, False)
-
-        for stage in range(3):
-            def body(at, _, stage=stage):
-                self.x_copy(stage, at).wait_recv()
+
+    def run(self, blocks, hook=None, done=None):
+        counts = self.counts
+
+        def body(step, _):
+            stage, at = step // counts, step % counts
+
+            @pl.when(jnp.logical_and(stage > 0, stage < 4))
+            def _():
+                self.x_copy(stage - 1, at).wait_recv()
                 self.sib_copy(stage, 0, at).start()
-                self.y_copy(stage, at).wait_recv()
+                self.y_copy(stage - 1, at).wait_recv()
                 self.sib_copy(stage, 1, at).start()
-                if stage < 2:
-                    self.x_copy(stage + 1, at).start()
-                    self.y_copy(stage + 1, at).start()
-
-                @pl.when(at > 0)
-                def _():
-                    work(stage, at - 1)
-
-                hook(stage, at)
-                return 0
-
-            lax.fori_loop(0, self.counts, body, 0)
-            work(stage, self.counts - 1)
-            if between:
-                between(stage)
+
+            @pl.when(jnp.logical_and(stage > 0, stage < 3))
+            def _():
+                self.x_copy(stage, at).start()
+                self.y_copy(stage, at).start()
+
+            @pl.when(step > 0)
+            def _():
+                old, spot = (step - 1) // counts, (step - 1) % counts
+                for stream, (across, half) in enumerate(self.streams(old)):
+                    self.sib_copy(old, stream, spot).wait_recv()
+                    blocks(across, half, spot)
+                if done:
+                    done(old, spot)
+
+            if hook:
+                hook(step)
+            return 0
+
+        lax.fori_loop(0, 4 * counts + 1, body, 0)
+        return 4 * counts + 1
 
     def end(self):
         def drain(at, _):
-            for step in range(3):
-                self.x_copy(step, at).wait_send()
-                self.y_copy(step, at).wait_send()
+            for hop in range(3):
+                self.x_copy(hop, at).wait_send()
+                self.y_copy(hop, at).wait_send()
             for stage in range(4):
                 self.sib_copy(stage, 0, at).wait_send()
                 self.sib_copy(stage, 1, at).wait_send()
@@ -632,162 +664,454 @@
     return jnp.dot(left, right, preferred_element_type=jnp.float32)
 
 
-def products(here, act, weight_of, nt, rows, width, half_cols, shared):
+def products(here, act, weight, nt, rows, width, counts):
     def product(across, other, half, at):
-        first = half * half_cols if shared else 0
-        cols = pl.ds(pl.multiple_of(first + at * width, width), width)
+        cols = pl.ds(pl.multiple_of((half * counts + at) * width, width), width)
         block = act[row_span(here, across, other, rows), :]
-        weight = weight_of(half)
         return dot_nt(block, weight[cols, :]) if nt else dot_nn(block, weight[:, cols])
 
     return product
 
 
-def scatter_kernel(rows, width, counts, nt, shared, line_counts, act, *refs):
-    refs = list(refs)
+def diagonal():
+    return (lax.broadcasted_iota(jnp.int32, (LANES, LANES), 0) ==
+            lax.broadcasted_iota(jnp.int32, (LANES, LANES), 1)).astype(jnp.float32)
+
+
+def to_tile(tile, first, column, eye):
+    for at in range(column.shape[0] // LANES):
+        spread = column[at * LANES : (at + 1) * LANES, :] * eye
+        tile[first + at : first + at + 1, :] = jnp.sum(spread, axis=0, keepdims=True)
+
+
+def from_tile(row, eye):
+    return jnp.sum(eye * row, axis=1, keepdims=True)
+
+
+def open_kernel(rows, width, counts, tokens, gain, w_query, kv_weight, qkv, x_low, act_t, w_qkv, rms, *refs):
     here = Place()
-    w0 = refs.pop(0)
-    w1 = w0 if shared else refs.pop(0)
-    tiny_own = refs.pop(0)
-    line_own = refs.pop(0) if line_counts else None
-    out, tiny_all = refs.pop(0), refs.pop(0)
-    line = None
-    if line_counts:
-        line = Line(here, line_counts, [line_own, refs.pop(0)] + refs[13:])
-    weights = (w0, w1)
-    product = products(here, act, lambda half: weights[half], nt, rows, width, counts * width, shared)
-    total = Reduce(here, counts, width, product, out, refs[:11])
-    tiny = Tiny(here, tiny_own, tiny_all, refs[11:13], True)
-    greet(here, tiny.peers, line is not None)
-    if line:
-        line.begin()
-    tiny.begin()
-    total.run(line)
-    if line:
-        line.end(4 * counts)
-    total.end()
-    tiny.end()
-
-
-def scatter_product(act, weights, tiny, width, nt, cid, line=None, line_counts=16):
-    total, depth = act.shape
-    rows = total // 8
-    shared = len(weights) == 1
-    half = weights[0].shape[0 if nt else 1] // (2 if shared else 1)
-    counts = half // width
+    cols = gain.shape[1]
+    act, turn_send, turn_recv, local_sems = refs[:4]
+    me = here.shard(0, 0)
+    own_rows = pl.ds(pl.multiple_of(me * rows, rows), rows)
+
+    def turn_copy(at):
+        across, other = turned(at)
+        first = pl.multiple_of(here.shard(across, other) * cols, cols)
+        return remote(tokens.at[:, pl.ds(first, cols)], x_low.at[own_rows, :], turn_send.at[at], turn_recv.at[at],
+                      here.device(across, other))
+
+    wide = w_query.shape[1]
+    local = [
+        pltpu.make_async_copy(w_query, w_qkv.at[:, :wide], local_sems.at[0]),
+        pltpu.make_async_copy(kv_weight, w_qkv.at[:, wide:], local_sems.at[1]),
+        pltpu.make_async_copy(tokens.at[:, pl.ds(pl.multiple_of(me * cols, cols), cols)], x_low.at[own_rows, :],
+                              local_sems.at[2]),
+    ]
+    for copy in local:
+        copy.start()
+    greet(here, slice_peers(here))
+    for at in range(7):
+        turn_copy(at).start()
+    for copy in local:
+        copy.wait()
+
+    def squares(at, total):
+        values = tokens[:, pl.ds(pl.multiple_of(at * cols, cols), cols)].astype(jnp.float32)
+        return total + jnp.sum(values * values, axis=-1, keepdims=True)
+
+    total = lax.fori_loop(0, 8, squares, jnp.zeros((rows, 1), jnp.float32))
+    rms[...] = jnp.broadcast_to(lax.rsqrt(total / (8 * cols) + EPS), rms.shape)
+
+    def prepare(first, count):
+        def one(step, _):
+            at = first + step
+            span = row_span(here, *turned(at), rows)
+            value = (x_low[span, :].astype(jnp.float32) * gain[...]).astype(act.dtype)
+            act[span, :] = value
+            return 0
+
+        lax.fori_loop(0, count, one, 0)
+
+    def before(stop):
+        first, count = ((0, 2), (2, 4), (6, 2))[stop]
+        for at in range(first, min(first + count, 7)):
+            turn_copy(at).wait_recv()
+        prepare(first, count)
+
+    def flip():
+        def one(shard, _):
+            span = pl.ds(pl.multiple_of(shard * rows, rows), rows)
+            act_t[:, span] = act[span, :].T
+            return 0
+
+        lax.fori_loop(0, 8, one, 0)
+
+    product = products(here, act, w_qkv, False, rows, width, counts)
+    total = Reduce(here, counts, product, refs[4:15], before)
+    total.run()
+    flip()
+
+    def emit(at, first, second):
+        for half, value in enumerate((first, second)):
+            qkv[:, pl.ds(pl.multiple_of((half * counts + at) * width, width), width)] = value
+
+    total.end(emit)
+    for at in range(7):
+        turn_copy(at).wait_send()
+
+
+def opening(tokens, gain, w_query, kv_weight, cid, width=256):
+    rows = tokens.shape[0]
+    cols, wide = w_query.shape
+    every = wide + kv_weight.shape[1]
+    counts = every // (2 * width)
+    low, f32 = jnp.bfloat16, jnp.float32
     dma = pltpu.SemaphoreType.DMA
     vm = pl.BlockSpec(memory_space=pltpu.VMEM)
+    hbm = pl.BlockSpec(memory_space=pl.ANY)
     out_shape = [
-        jax.ShapeDtypeStruct((rows, 2 * half), jnp.float32),
-        jax.ShapeDtypeStruct(tiny.shape, jnp.float32),
+        jax.ShapeDtypeStruct((rows, every), f32),
+        jax.ShapeDtypeStruct((8 * rows, cols), low),
+        jax.ShapeDtypeStruct((cols, 8 * rows), low),
+        jax.ShapeDtypeStruct((cols, every), low),
+        jax.ShapeDtypeStruct((rows, LANES), f32),
     ]
-    scratch = reduce_scratch(counts, rows, width) + [dma((7,))] * 2
-    operands = [act, *weights, tiny]
-    if line is not None:
-        operands.append(line)
-        out_shape.append(jax.ShapeDtypeStruct(line.shape, line.dtype))
-        scratch += line_scratch(line_counts, line.shape, line.dtype)
-    kernel = functools.partial(scatter_kernel, rows, width, counts, nt, shared,
-                               0 if line is None else line_counts)
-    return kernel_call(kernel, out_shape, operands, [vm] * len(operands), scratch, cid, "scatter_product")
-
-
-def gather_kernel(rows, width, counts, down, n_own, line_counts, act, *refs):
-    refs = list(refs)
+    scratch = [pltpu.VMEM((8 * rows, cols), low), dma((7,)), dma((7,)), dma((3,))]
+    scratch += reduce_scratch(counts, rows, width)
+    kernel = functools.partial(open_kernel, rows, width, counts)
+    return kernel_call(kernel, out_shape, [tokens, gain, w_query, kv_weight], [vm, vm, hbm, hbm], scratch, cid, "open")
+
+
+def scatter_kernel(rows, width, counts, line_counts, act, weight, line_own, out, line_out, *refs):
     here = Place()
-    weights = [refs.pop(0) for _ in range(n_own)]
-    payload = [refs.pop(0) for _ in range(n_own)]
-    tiny_own = refs.pop(0)
-    line_own = refs.pop(0) if line_counts else None
-    sums = refs.pop(0)
-    grads = [refs.pop(0) for _ in range(n_own)]
-    tiny_all = refs.pop(0)
-    line_out = refs.pop(0) if line_counts else None
-    spread = Spread(here, counts, refs[:7])
-    tiny = Tiny(here, tiny_own, tiny_all, refs[7:9], False)
-    own_sem = refs[9]
-    line = Line(here, line_counts, [line_own, line_out] + refs[10:]) if line_counts else None
-    got, core = spread.got, here.core
-
-    def part(half, at):
-        first = half * counts * width if n_own == 1 else 0
-        return pl.ds(pl.multiple_of(first + at * width, width), width)
-
-    def own_copy(half, at):
-        src = payload[half if n_own > 1 else 0].at[:, part(half, at)]
-        return pltpu.make_async_copy(src, got.at[0, core, half, at], own_sem.at[half, at])
-
+    line = Line(here, line_counts, [line_own, line_out] + list(refs[11:]))
+    product = products(here, act, weight, True, rows, width, counts)
+    total = Reduce(here, counts, product, refs[:11])
+    greet(here, slice_peers(here), True)
+    line.begin()
+    done = total.run(line)
+    line.end(done)
+
+    def emit(at, first, second):
+        for half, value in enumerate((first, second)):
+            out[:, pl.ds(pl.multiple_of((half * counts + at) * width, width), width)] = value
+
+    total.end(emit)
+
+
+def scatter_product(act, weight, width, cid, line, line_counts=16):
+    rows = act.shape[0] // 8
+    every = weight.shape[0]
+    counts = every // (2 * width)
+    vm = pl.BlockSpec(memory_space=pltpu.VMEM)
+    out_shape = [
+        jax.ShapeDtypeStruct((rows, every), jnp.float32),
+        jax.ShapeDtypeStruct(line.shape, line.dtype),
+    ]
+    scratch = reduce_scratch(counts, rows, width) + line_scratch(line_counts, line.shape, line.dtype)
+    kernel = functools.partial(scatter_kernel, rows, width, counts, line_counts)
+    return kernel_call(kernel, out_shape, [act, weight, line], [vm] * 3, scratch, cid, "scatter_product")
+
+
+def ffn_kernel(rows, width, counts, x_low, attn, gain, w_gate, w_up, d_hidden, hidden, d_gate, d_up, act_t, tile_out,
+               *refs):
+    here = Place()
+    cols = gain.shape[1]
+    act, weight, tiny_own, tiny_all, tiny_send, tiny_recv, dots, local_sems = refs[:8]
+    tiny = Tiny(here, tiny_own, tiny_all, (tiny_send, tiny_recv), True)
+    half_cols = counts * width
+    local = [
+        pltpu.make_async_copy(w_gate, weight.at[:, :half_cols], local_sems.at[0]),
+        pltpu.make_async_copy(w_up, weight.at[:, half_cols:], local_sems.at[1]),
+    ]
+    for copy in local:
+        copy.start()
+    eye = diagonal()
+    tiny_own[...] = jnp.zeros_like(tiny_own)
+
+    def prepare(shard, _):
+        for at in range(rows // LANES):
+            span = pl.ds(pl.multiple_of(shard * rows + at * LANES, LANES), LANES)
+            resid = x_low[span, :].astype(jnp.float32) + attn[span, :].astype(jnp.float32)
+            act[span, :] = (resid * gain[...]).astype(act.dtype)
+            square = jnp.sum(resid * resid, axis=-1, keepdims=True)
+            tiny_own[shard, at : at + 1, :] = jnp.sum(square * eye, axis=0, keepdims=True)
+        return 0
+
+    lax.fori_loop(0, 8, prepare, 0)
+    greet(here, slice_peers(here))
+    tiny.begin()
+    for copy in local:
+        copy.wait()
+    product = products(here, act, weight, False, rows, width, counts)
+    total = Reduce(here, counts, product, refs[8:19])
+    total.run()
+
+    def flip(shard, _):
+        span = pl.ds(pl.multiple_of(shard * rows, rows), rows)
+        act_t[:, span] = act[span, :].T
+        return 0
+
+    lax.fori_loop(0, 8, flip, 0)
+    tiny.end()
+    tiles = rows // LANES
+    mean = [from_tile(jnp.sum(tiny_all[:, at, :], axis=0, keepdims=True), eye) for at in range(tiles)]
+    scale = lax.rsqrt(jnp.concatenate(mean, axis=0) / (8 * cols) + EPS)
+    dots[...] = jnp.zeros_like(dots)
+    coeff = math.sqrt(2.0 / math.pi)
+
+    def emit(at, first, second):
+        span = pl.ds(pl.multiple_of(at * width, width), width)
+        gate, up = first * scale, second * scale
+        inner = jnp.tanh(coeff * (gate + 0.044715 * (gate * gate * gate)))
+        gelu = 0.5 * gate * (1.0 + inner)
+        slope = 0.5 * (1.0 + inner) + 0.5 * gate * (1.0 - inner * inner) * (
+            coeff * (1.0 + 3.0 * 0.044715 * gate * gate))
+        cot = d_hidden[:, span]
+        hidden[:, span] = (gelu * up).astype(hidden.dtype)
+        back_gate, back_up = cot * up * slope, cot * gelu
+        d_gate[:, span] = (back_gate * scale).astype(d_gate.dtype)
+        d_up[:, span] = (back_up * scale).astype(d_up.dtype)
+        dots[...] += jnp.sum(back_gate * gate + back_up * up, axis=-1, keepdims=True)
+
+    total.end(emit)
+    tile_out[...] = jnp.zeros_like(tile_out)
+    to_tile(tile_out, 0, dots[...] * (scale * scale * (1.0 / (8 * cols))), eye)
+
+
+def ffn_scatter(x_low, attn, gain, w_gate, w_up, d_hidden, cid, width=512):
+    rows, half = d_hidden.shape
+    cols = gain.shape[1]
+    counts = half // width
+    low, f32 = jnp.bfloat16, jnp.float32
+    dma = pltpu.SemaphoreType.DMA
+    vm = pl.BlockSpec(memory_space=pltpu.VMEM)
+    hbm = pl.BlockSpec(memory_space=pl.ANY)
+    out_shape = [jax.ShapeDtypeStruct((rows, half), low)] * 3 + [
+        jax.ShapeDtypeStruct((cols, 8 * rows), low),
+        jax.ShapeDtypeStruct((8, LANES), f32),
+    ]
+    scratch = [
+        pltpu.VMEM((8 * rows, cols), low),
+        pltpu.VMEM((cols, 2 * half), low),
+        pltpu.VMEM((8, 8, LANES), f32),
+        pltpu.VMEM((8, 8, LANES), f32),
+        dma((7,)), dma((7,)),
+        pltpu.VMEM((rows, 1), f32),
+        dma((2,)),
+    ] + reduce_scratch(counts, rows, width)
+    kernel = functools.partial(ffn_kernel, rows, width, counts)
+    return kernel_call(kernel, out_shape, [x_low, attn, gain, w_gate, w_up, d_hidden], [vm, vm, vm, hbm, hbm, vm],
+                       scratch, cid, "ffn")
+
+
+def load_own(spread, payload, width, counts, sems):
+    copies = []
     for half in range(2):
         for at in range(counts):
-            own_copy(half, at).start()
-    greet(here, tiny.peers, line is not None)
-    if line:
-        line.begin()
-    for at in range(counts):
-        for half in range(2):
-            own_copy(half, at).wait()
+            first = at * width + (half * counts * width if len(payload) == 1 else 0)
+            src = payload[half % len(payload)].at[:, first : first + width]
+            copies.append(pltpu.make_async_copy(src, spread.slot(0, half, at), sems.at[half, at]))
+    return copies
+
+
+def back_kernel(rows, width, counts, act_t, w_gate, w_up, d_gate, d_up, dots, x_low, attn, gain, contrib, gain_grad,
+                grad_gate, grad_up, *refs):
+    here = Place()
+    spread = Spread(here, counts, refs[:7])
+    tiny_all, tiny_send, tiny_recv, own_sems, weight, sums, grads, local_sems, out_sems = refs[7:16]
+    tiny = Tiny(here, dots, tiny_all, (tiny_send, tiny_recv), False)
+    half_cols = counts * width
+    local = [
+        pltpu.make_async_copy(w_gate, weight.at[:, :half_cols], local_sems.at[0]),
+        pltpu.make_async_copy(w_up, weight.at[:, half_cols:], local_sems.at[1]),
+    ]
+    own = load_own(spread, (d_gate, d_up), width, counts, own_sems)
+    for copy in own + local:
+        copy.start()
+    greet(here, tiny.peers)
+    for copy in own:
+        copy.wait()
     spread.begin()
     tiny.begin()
     sums[...] = jnp.zeros_like(sums)
-
-    def blocks(across, half, at, fresh):
-        gained = None
-        cols = part(half, at)
-        weight = weights[half if n_own > 1 else 0]
+    for copy in local:
+        copy.wait()
+
+    def columns(half, at):
+        return pl.ds(pl.multiple_of((half * counts + at) * width, width), width)
+
+    def clear(at, _):
+        grads[:, columns(0, at)] = jnp.zeros((grads.shape[0], width), jnp.float32)
+        return 0
+
+    lax.fori_loop(0, 2 * counts, clear, 0)
+
+    def blocks(across, half, at):
+        cols = columns(half, at)
+        gained = grads[:, cols]
         for other in range(2):
             row = row_span(here, across, other, rows)
-            block = got[across, (core + other) % 2, half, at]
-            if down:
-                sums[row, :] += dot_nn(block, weight[cols, :])
-                more = dot_tn(block, act[row, :])
-            else:
-                sums[row, :] += dot_nt(block, weight[:, cols])
-                more = dot_nn(act[:, row], block)
-            gained = more if gained is None else gained + more
-        grad = grads[half if n_own > 1 else 0]
-        where = (cols, slice(None)) if down else (slice(None), cols)
-        if fresh:
-            grad[where] = gained
-        else:
-            grad[where] += gained
-
-    spread.run(blocks, line)
-    if line:
-        line.end(4 * counts)
+            block = spread.got[across, (spread.core + other) % 2, half, at]
+            sums[row, :] += dot_nt(block, weight[:, cols])
+            gained = gained + dot_nn(act_t[:, row], block)
+        grads[:, cols] = gained
+
+    def leave(half, at):
+        spot = pl.ds(pl.multiple_of(at * width, width), width)
+        return pltpu.make_async_copy(grads.at[:, columns(half, at)], (grad_gate, grad_up)[half].at[:, spot],
+                                     out_sems.at[half, at])
+
+    def done(stage, at):
+        @pl.when(stage == 3)
+        def _():
+            leave(0, at).start()
+            leave(1, at).start()
+
+    spread.run(blocks, done=done)
+    tiny.end()
+    eye = diagonal()
+    gain_grad[...] = jnp.zeros_like(gain_grad)
+
+    def close_shard(shard, _):
+        for at in range(rows // LANES):
+            span = pl.ds(pl.multiple_of(shard * rows + at * LANES, LANES), LANES)
+            dot = from_tile(tiny_all[shard, at : at + 1, :], eye)
+            resid = x_low[span, :].astype(jnp.float32) + attn[span, :].astype(jnp.float32)
+            value = sums[span, :]
+            contrib[span, :] = (value * gain[...] - resid * dot).astype(contrib.dtype)
+            gain_grad[...] += jnp.sum(value * resid, axis=0, keepdims=True)
+        return 0
+
+    lax.fori_loop(0, 8, close_shard, 0)
     spread.end()
-    tiny.end()
-
-
-def gather_product(act, weights, payload, tiny, width, down, cid, line=None, line_counts=16):
-    total, depth = act.shape if down else act.shape[::-1]
-    rows = payload[0].shape[0]
-    half = payload[0].shape[1] // (2 if len(payload) == 1 else 1)
+
+    def drain(at, _):
+        leave(0, at).wait()
+        leave(1, at).wait()
+        return 0
+
+    lax.fori_loop(0, counts, drain, 0)
+
+
+def back_gather(act_t, w_gate, w_up, d_gate, d_up, dots, x_low, attn, gain, cid, width=512):
+    cols, total = act_t.shape
+    rows, half = d_gate.shape
     counts = half // width
-    f32 = jnp.float32
+    low, f32 = jnp.bfloat16, jnp.float32
     dma = pltpu.SemaphoreType.DMA
     vm = pl.BlockSpec(memory_space=pltpu.VMEM)
     hbm = pl.BlockSpec(memory_space=pl.ANY)
-    out_shape = [jax.ShapeDtypeStruct((total, depth), f32)]
-    out_shape += [jax.ShapeDtypeStruct(w.shape, f32) for w in weights]
-    out_shape.append(jax.ShapeDtypeStruct((8,) + tiny.shape, f32))
-    scratch = spread_scratch(counts, rows, width) + [dma((7,))] * 2 + [dma((2, counts))]
-    operands = [act, *weights, *payload, tiny]
-    specs = [vm] * (1 + len(weights)) + [hbm] * len(payload) + [vm]
-    if line is not None:
-        operands.append(line)
-        specs.append(vm)
-        out_shape.append(jax.ShapeDtypeStruct(line.shape, line.dtype))
-        scratch += line_scratch(line_counts, line.shape, line.dtype)
-    kernel = functools.partial(gather_kernel, rows, width, counts, down, len(weights),
-                               0 if line is None else line_counts)
-    return kernel_call(kernel, out_shape, operands, specs, scratch, cid, "gather_product")
-
-
-def attend_kernel(rows, heads, cols, qkv, rms, cos, sin, mask, w_out, cot, tiny_own, part, mixed_all, g_col, kv,
-                  probs, queries, tiny_pair, *refs):
+    out_shape = [
+        jax.ShapeDtypeStruct((total, cols), low),
+        jax.ShapeDtypeStruct((1, cols), f32),
+        jax.ShapeDtypeStruct((cols, half), f32),
+        jax.ShapeDtypeStruct((cols, half), f32),
+    ]
+    scratch = spread_scratch(counts, rows, width) + [
+        pltpu.VMEM((8, 8, LANES), f32), dma((7,)), dma((7,)), dma((2, counts)),
+        pltpu.VMEM((cols, 2 * half), low),
+        pltpu.VMEM((total, cols), f32),
+        pltpu.VMEM((cols, 2 * half), f32),
+        dma((2,)), dma((2, counts)),
+    ]
+    operands = [act_t, w_gate, w_up, d_gate, d_up, dots, x_low, attn, gain]
+    kernel = functools.partial(back_kernel, rows, width, counts)
+    return kernel_call(kernel, out_shape, operands, [vm] + [hbm] * 4 + [vm] * 4, scratch, cid, "back",
+                       [vm, vm, hbm, hbm])
+
+
+def down_kernel(rows, width, counts, line_counts, cot, weight, hidden, line_own, ffn, d_attn, grad, *refs):
+    here = Place()
+    spread = Spread(here, counts, refs[:7])
+    own_sems, sums, grads, out_sems, line_out = refs[7:12]
+    line = Line(here, line_counts, [line_own, line_out] + list(refs[12:]))
+    own = load_own(spread, (hidden,), width, counts, own_sems)
+    for copy in own:
+        copy.start()
+    greet(here, slice_peers(here), True)
+    line.begin()
+    for copy in own:
+        copy.wait()
+    spread.begin()
+    sums[...] = jnp.zeros_like(sums)
+    grads[...] = jnp.zeros_like(grads)
+
+    def columns(half, at):
+        return pl.ds(pl.multiple_of((half * counts + at) * width, width), width)
+
+    def blocks(across, half, at):
+        cols = columns(half, at)
+        gained = grads[cols, :]
+        for other in range(2):
+            row = row_span(here, across, other, rows)
+            block = spread.got[across, (spread.core + other) % 2, half, at]
+            sums[row, :] += dot_nn(block, weight[cols, :])
+            gained = gained + dot_tn(block, cot[row, :])
+        grads[cols, :] = gained
+
+    def leave(half, at):
+        cols = columns(half, at)
+        return pltpu.make_async_copy(grads.at[cols, :], grad.at[cols, :], out_sems.at[half, at])
+
+    def done(stage, at):
+        @pl.when(stage == 3)
+        def _():
+            leave(0, at).start()
+            leave(1, at).start()
+
+    steps = spread.run(blocks, line.step, done)
+    line.end(steps)
+
+    def close_shard(shard, _):
+        span = pl.ds(pl.multiple_of(shard * rows, rows), rows)
+        ffn[span, :] = sums[span, :].astype(ffn.dtype)
+        d_attn[span, :] = (cot[span, :].astype(jnp.float32) + line_out[span, :].astype(jnp.float32)).astype(
+            d_attn.dtype)
+        return 0
+
+    lax.fori_loop(0, 8, close_shard, 0)
+    spread.end()
+
+    def drain(at, _):
+        leave(0, at).wait()
+        leave(1, at).wait()
+        return 0
+
+    lax.fori_loop(0, counts, drain, 0)
+
+
+def down_gather(cot, weight, hidden, line, cid, width=256, line_counts=16):
+    total, cols = cot.shape
+    rows, every = hidden.shape
+    counts = every // (2 * width)
+    low, f32 = jnp.bfloat16, jnp.float32
+    dma = pltpu.SemaphoreType.DMA
+    vm = pl.BlockSpec(memory_space=pltpu.VMEM)
+    hbm = pl.BlockSpec(memory_space=pl.ANY)
+    out_shape = [
+        jax.ShapeDtypeStruct((total, cols), low),
+        jax.ShapeDtypeStruct((total, cols), low),
+        jax.ShapeDtypeStruct(weight.shape, f32),
+    ]
+    scratch = spread_scratch(counts, rows, width) + [
+        dma((2, counts)),
+        pltpu.VMEM((total, cols), f32),
+        pltpu.VMEM(weight.shape, f32),
+        dma((2, counts)),
+        pltpu.VMEM((total, cols), low),
+    ] + line_scratch(line_counts, line.shape, low)
+    kernel = functools.partial(down_kernel, rows, width, counts, line_counts)
+    return kernel_call(kernel, out_shape, [cot, weight, hidden, line], [vm, vm, hbm, vm], scratch, cid, "down",
+                       [vm, vm, hbm])
+
+
+def attend_kernel(rows, heads, cols, qkv, rms, cos, sin, mask, w_out, cot, part, mixed_all, g_col, kv, probs, queries,
+                  pair_rms, *refs):
     here = Place()
     spread = Spread(here, heads // 2, refs[:7])
-    sums, pair_sems, turn_send, turn_recv, local_sem = refs[7:12]
+    sums, pair_sems, turn_send, turn_recv, local_sem, tiny_own, tiny_pair = refs[7:14]
     got, core = spread.got, here.core
     greet(here, slice_peers(here))
     me = here.shard(0, 0)
@@ -816,9 +1140,12 @@
     for at in range(2):
         first = HD + at * half
         kv[0, :, first : first + half] = (qkv[:, wide + first : wide + first + half] * rms[...]).astype(kv.dtype)
-    tiny_pair[0] = tiny_own[...]
+    eye = diagonal()
+    tiny_own[...] = jnp.zeros_like(tiny_own)
+    to_tile(tiny_own, 0, rms[:, :1], eye)
+    pair_rms[0] = rms[...]
     pair = remote(kv.at[0], kv.at[1], pair_sems.at[0], pair_sems.at[1], spread.ydev)
-    tiny = remote(tiny_own, tiny_pair.at[1], pair_sems.at[2], pair_sems.at[3], spread.ydev)
+    tiny = remote(tiny_own, tiny_pair, pair_sems.at[2], pair_sems.at[3], spread.ydev)
     for head in range(heads):
         if head == 1:
             pair.start()
@@ -849,7 +1176,7 @@
     sums[...] = jnp.zeros_like(sums)
     spread.begin()
 
-    def blocks(across, half_at, at, fresh):
+    def blocks(across, half_at, at):
         span = pl.ds(pl.multiple_of((half_at * (heads // 2) + at) * HD, HD), HD)
         for other in range(2):
             row = row_span(here, across, other, rows)
@@ -861,12 +1188,15 @@
     part[...] = sums[...].astype(part.dtype)
     spread.end()
     tiny.wait()
+    for at in range(rows // LANES):
+        values = jnp.broadcast_to(from_tile(tiny_pair[at : at + 1, :], eye), (LANES, LANES))
+        pair_rms[1, at * LANES : (at + 1) * LANES, :] = values
     own_turn.wait()
     for at in range(7):
         turn_copy(at).wait()
 
 
-def attend(qkv, rms, cos, sin, mask, w_out, cot, tiny, cid):
+def attend(qkv, rms, cos, sin, mask, w_out, cot, cid):
     rows = qkv.shape[0]
     wide, cols = w_out.shape
     heads = wide // HD
@@ -880,17 +1210,18 @@
         jax.ShapeDtypeStruct((2, rows, 2 * HD), low),
         jax.ShapeDtypeStruct((heads, rows, 2 * rows), f32),
         jax.ShapeDtypeStruct((rows, wide), low),
-        jax.ShapeDtypeStruct((2,) + tiny.shape, f32),
+        jax.ShapeDtypeStruct((2,) + rms.shape, f32),
     ]
     scratch = spread_scratch(heads // 2, rows, HD) + [
-        pltpu.VMEM((8 * rows, cols), f32), dma((4,)), dma((7,)), dma((7,)), dma(())]
+        pltpu.VMEM((8 * rows, cols), f32), dma((4,)), dma((7,)), dma((7,)), dma(()),
+        pltpu.VMEM((8, LANES), f32), pltpu.VMEM((8, LANES), f32)]
     kernel = functools.partial(attend_kernel, rows, heads, cols)
-    return kernel_call(kernel, out_shape, [qkv, rms, cos, sin, mask, w_out, cot, tiny], [vm] * 8, scratch, cid,
+    return kernel_call(kernel, out_shape, [qkv, rms, cos, sin, mask, w_out, cot], [vm] * 7, scratch, cid,
                        "attend")
 
 
 def tail_kernel(rows, heads, per, d_attn, w_out, queries, kv, probs, rms, cos, sin, act_t, w_qkv, ffn, x_low,
-                resid, gain, gain_grad, d_tok, out, grad, kv_sum, gain_tiles, *refs):
+                attn, gain, gain_grad, d_tok, out, grad, kv_sum, gain_tiles, *refs):
     here = Place()
     width = HD
     counts, out_counts = heads // 2, (heads + 2) // 2
@@ -927,13 +1258,17 @@
     line_tok = Line(here, line_counts + extra, [contrib, summed] + take(8), place_tok)
     tiny = Tiny(here, tiny_own, tiny_all, (tiny_send, tiny_recv), False)
     got, core = spread.got, here.core
-    product = products(here, d_attn, lambda half: w_out, True, rows, width, counts * width, True)
-    total = Reduce(here, counts, width, product, d_mixed, total_refs)
+    product = products(here, d_attn, w_out, True, rows, width, counts)
+    total = Reduce(here, counts, product, total_refs)
     greet(here, tiny.peers, True)
     line.begin()
-    total.run(line)
-    done = 4 * counts
-    total.end()
+    done = total.run(line)
+
+    def land(at, first, second):
+        for half_at, value in enumerate((first, second)):
+            d_mixed[:, pl.ds(pl.multiple_of((half_at * counts + at) * width, width), width)] = value
+
+    total.end(land)
     half = HD // 2
     scale = 1.0 / math.sqrt(HD)
     depth = w_qkv.shape[0] * 8
@@ -964,8 +1299,7 @@
 
     dots = lax.fori_loop(0, heads, one_head, jnp.zeros((rows, 1), jnp.float32))
     done += heads
-    eye = (lax.broadcasted_iota(jnp.int32, (LANES, LANES), 0) ==
-           lax.broadcasted_iota(jnp.int32, (LANES, LANES), 1)).astype(jnp.float32)
+    eye = diagonal()
     tiny_own[...] = jnp.zeros_like(tiny_own)
     for side in (1, 0):
         d_key, d_value = d_kv[side, :, :HD], d_kv[side, :, HD:]
@@ -974,10 +1308,7 @@
         if side == 0:
             own = own + dots * (1.0 / scale)
         own = own * (rms[side] * rms[side] * (1.0 / depth))
-        for at in range(rows // LANES):
-            spot_values = own[at * LANES : (at + 1) * LANES, :] * eye
-            spot = side * (rows // LANES) + at
-            tiny_own[spot : spot + 1, :] = jnp.sum(spot_values, axis=0, keepdims=True)
+        to_tile(tiny_own, side * (rows // LANES), own, eye)
         lead, trail = d_key[:, :half], d_key[:, half:]
         parts = [(lead * cos[side] + trail * sin[side]) * rms[side],
                  (trail * cos[side] - lead * sin[side]) * rms[side],
@@ -999,22 +1330,17 @@
     spread.begin()
     gain_sum[...] = jnp.zeros_like(gain_sum)
 
-    def blocks(across, half_at, at, fresh):
+    grad[...] = jnp.zeros_like(grad)
+
+    def blocks(across, half_at, at):
         span = pl.ds(pl.multiple_of((half_at * out_counts + at) * width, width), width)
-        gained = None
+        gained = grad[:, span]
         for other in range(2):
             row = row_span(here, across, other, rows)
             block = got[across, (core + other) % 2, half_at, at]
             sums[row, :] += dot_nt(block, w_qkv[:, span])
-            more = dot_nn(act_t[:, row], block)
-            gained = more if gained is None else gained + more
-        if fresh:
-            grad[:, span] = gained
-        else:
-            grad[:, span] += gained
-
-    def column(values):
-        return jnp.sum(eye * values, axis=1, keepdims=True)
+            gained = gained + dot_nn(act_t[:, row], block)
+        grad[:, span] = gained
 
     def contribute(chip):
         def shard_rows(other, _):
@@ -1022,7 +1348,7 @@
             for at in range(rows // LANES):
                 row = pl.ds(pl.multiple_of(shard * rows + at * LANES, LANES), LANES)
                 kept = rows // LANES + at
-                dot = column(tiny_all[shard, at : at + 1, :] + tiny_all[partner, kept : kept + 1, :])
+                dot = from_tile(tiny_all[shard, at : at + 1, :] + tiny_all[partner, kept : kept + 1, :], eye)
                 value, x_rows = sums[row, :], x_low[row, :].astype(jnp.float32)
                 contrib[row, :] = (value * gain[...] - x_rows * dot).astype(contrib.dtype)
                 gain_sum[...] += jnp.sum(value * x_rows, axis=0, keepdims=True)
@@ -1032,28 +1358,35 @@
         line_tok.launch(2 * per * chip, 2 * per)
 
     first_part = 2 * per
-
-    def hook(stage, at):
-        if stage < 0:
-            line.step(done + at)
-        elif stage < 2:
-            line_tok.step(stage * out_counts + at, 0, first_part)
-        else:
-            line_tok.step(at, first_part, line_counts + extra - first_part)
-
-    def between(stage):
-        if stage < 0:
-            tiny.end()
+    left = line_counts + extra - first_part
+    line.steps(done, line_counts + 2)
+    tiny.end()
+
+    def hook(step):
+        stage, at = step // out_counts, step % out_counts
+
+        @pl.when(jnp.logical_and(stage > 0, stage < 3))
+        def _():
+            line_tok.step((stage - 1) * out_counts + at, 0, first_part)
+
+        @pl.when(stage == 3)
+        def _():
+            line_tok.step(at, first_part, left)
+
+    def complete(stage, at):
+        @pl.when(jnp.logical_and(at == out_counts - 1, stage == 0))
+        def _():
             contribute(0)
-            line.steps(min(done + out_counts, line_counts + 2), line_counts + 2)
-        elif stage == 1:
-            line_tok.steps(2 * out_counts, first_part + 2, 0, first_part)
-            contribute(1)
-            contribute(2)
-        elif stage == 2:
+
+        @pl.when(jnp.logical_and(at == out_counts - 1, stage == 2))
+        def _():
+            lax.fori_loop(1, 3, lambda chip, _: (contribute(chip), 0)[1], 0)
+
+        @pl.when(jnp.logical_and(at == out_counts - 1, stage == 3))
+        def _():
             contribute(3)
 
-    spread.run(blocks, hook=hook, between=between)
+    spread.run(blocks, hook, complete)
     for half_at in range(cols // (rows // per)):
         span = pl.ds(line_counts * (rows // per) + half_at * (rows // per), rows // per)
         source = slice(half_at * (rows // per), (half_at + 1) * (rows // per))
@@ -1082,7 +1415,9 @@
     def emit(which, at):
         kind = (line, line_tok)[which]
         row = kind.rows(at)
-        base = (resid, d_attn)[which][row, :].astype(jnp.float32)
+        base = (attn, d_attn)[which][row, :].astype(jnp.float32)
+        if which == 0:
+            base = base + x_low[row, :].astype(jnp.float32)
         kind.from_end[at] = (base + kind.out[row, :].astype(jnp.float32)).astype(out.dtype)
 
     def is_own(which, at):
@@ -1103,7 +1438,6 @@
     for step in range(3):
         tile_copy(step).start()
     gain_tiles[here.z] = tile[...]
-    left = line_counts + extra - first_part
 
     @pl.when(line.inner == 1)
     def _():
@@ -1187,7 +1521,7 @@
         tile_copy(step).wait()
 
 
-def tail(d_attn, w_out, queries, kv, probs, rms, cos, sin, act_t, w_qkv, ffn, x_low, resid, gain, gain_grad, cid,
+def tail(d_attn, w_out, queries, kv, probs, rms, cos, sin, act_t, w_qkv, ffn, x_low, attn, gain, gain_grad, cid,
          per=2):
     total, cols = d_attn.shape
     rows = total // 8
@@ -1223,71 +1557,18 @@
         pltpu.VMEM((total, cols), low),
     ] + line_scratch(counts, (total, cols), low)
     scratch += [pltpu.VMEM(long, low), pltpu.VMEM(long, low)] + line_scratch(counts + extra, long, low)
-    operands = [d_attn, w_out, queries, kv, probs, rms, cos, sin, act_t, w_qkv, ffn, x_low, resid, gain, gain_grad]
+    operands = [d_attn, w_out, queries, kv, probs, rms, cos, sin, act_t, w_qkv, ffn, x_low, attn, gain, gain_grad]
     kernel = functools.partial(tail_kernel, rows, heads, per)
     return kernel_call(kernel, out_shape, operands, [vm] * len(operands), scratch, cid, "tail")
 
 
-def turn_kernel(rows, cols, back, src, out, own_sem, send, recv):
-    here = Place()
-    peers = [(a, o) for a in (3, 1, 2, 0) for o in range(2) if a + o > 0]
-    greet(here, [here.device(a, o) for a, o in peers])
-
-    def by_row(ref, shard):
-        return ref.at[pl.ds(pl.multiple_of(shard * rows, rows), rows), :]
-
-    def by_col(ref, shard):
-        return ref.at[:, pl.ds(pl.multiple_of(shard * cols, cols), cols)]
-
-    take, put = (by_row, by_col) if back else (by_col, by_row)
-    me = here.shard(0, 0)
-
-    def copy(at):
-        across, other = peers[at]
-        return remote(take(src, here.shard(across, other)), put(out, me), send.at[at], recv.at[at],
-                      here.device(across, other))
-
-    for at in range(7):
-        copy(at).start()
-    own = pltpu.make_async_copy(take(src, me), put(out, me), own_sem)
-    own.start()
-    own.wait()
-    for at in range(7):
-        copy(at).wait()
-
-
-def turn(src, back, cid):
-    rows, cols = (src.shape[0] // 8, src.shape[1]) if back else (src.shape[0], src.shape[1] // 8)
-    shape = (rows, 8 * cols) if back else (8 * rows, cols)
-    dma = pltpu.SemaphoreType.DMA
-    vm = pl.BlockSpec(memory_space=pltpu.VMEM)
-    return pl.pallas_call(
-        functools.partial(turn_kernel, rows, cols, back),
-        out_shape=jax.ShapeDtypeStruct(shape, src.dtype),
-        in_specs=[vm],
-        out_specs=vm,
-        scratch_shapes=[dma(()), dma((7,)), dma((7,))],
-        compiler_params=pltpu.CompilerParams(collective_id=cid, has_side_effects=True,
-                                             vmem_limit_bytes=VMEM_LIMIT),
-        name=f"turn_{cid}",
-    )(src)
-
-
 LANES = 128
-
-
-def pack_rows(values):
-    parts = values.reshape(8, -1, LANES)
-    return jnp.pad(parts, ((0, 0), (0, 8 - parts.shape[1]), (0, 0)))
 
 
 def acts_move(
     tokens, seg_ids, gain_attn, w_query, kv_weight, w_out, gain_ffn, w_gate, w_up, w_down, d_out
 ):
-    low = jnp.bfloat16
-    rows, width = tokens.shape
-    seqs = lax.axis_size("seq")
-    parts = lax.axis_size("dp") * seqs
+    rows = tokens.shape[0]
     offset = lax.axis_index("seq") * rows
     places, cos_table, sin_table = place_tables(seg_ids)
     away = rows - offset
@@ -1307,74 +1588,21 @@
     allowed = (pair_segs[0][:, None] == pair_segs.reshape(1, -1)) & (
         pair_places[0][:, None] >= pair_places.reshape(1, -1)
     )
-    gain_one = gain_attn.astype(jnp.float32)
-    gain_two = gain_ffn.astype(jnp.float32)
-    qw = w_query.shape[1]
-    ff = w_gate.shape[1]
-
-    none = jnp.zeros((8, 8, LANES), jnp.float32)
-    x_low = turn(tokens, False, 1)
-    x_col = x_low.astype(jnp.float32)
-    own_x = tokens.astype(jnp.float32)
-    rms_one = lax.rsqrt(jnp.mean(own_x * own_x, axis=-1, keepdims=True) + EPS)
-    act_one = (x_col * gain_one).astype(low)
-    w_qkv = jnp.concatenate([w_query, kv_weight], axis=1)
-    qkv = scatter_product(act_one, (w_qkv,), none, 256, False, 2)[0]
-    tiles = rows // LANES
-    attn_part, mixed_all, g_low, kv, probs, queries, rms_tiles = attend(
-        qkv,
-        jnp.broadcast_to(rms_one, (rows, LANES)),
-        pair_cos[0],
-        pair_sin[0],
-        allowed.astype(jnp.float32),
-        w_out,
-        d_out,
-        jnp.pad(rms_one.reshape(tiles, LANES), ((0, 8 - tiles), (0, 0))),
-        3,
-    )
-    pair_rms = jnp.broadcast_to(rms_tiles[:, :tiles].reshape(2, rows, 1), (2, rows, LANES))
-    d_hidden, _, attn = scatter_product(g_low, (w_down,), none, 512, True, 4, line=attn_part)
-    resid = x_col + attn.astype(jnp.float32)
-    act_two = (resid * gain_two).astype(low)
-    squares = pack_rows(jnp.sum(resid * resid, axis=-1))
-    both, squares_all = scatter_product(act_two, (w_gate, w_up), squares, 512, False, 6)
-    mean_two = jnp.sum(squares_all[:, : rows // LANES], axis=0).reshape(rows, 1) / width
-    rms_two = lax.rsqrt(mean_two + EPS)
-    gate = both[:, :ff] * rms_two
-    up_val = both[:, ff : 2 * ff] * rms_two
-    gelu_val, gelu_pull = jax.vjp(gelu_tanh, gate)
-    hidden = (gelu_val * up_val).astype(low)
-    d_gate = gelu_pull(d_hidden * up_val)[0]
-    d_up = d_hidden * gelu_val
-    dots_two = jnp.sum(d_gate * gate + d_up * up_val, axis=-1, keepdims=True) * (
-        rms_two * rms_two / width
-    )
-    dots_own = jnp.pad(dots_two.reshape(-1, LANES), ((0, 8 - rows // LANES), (0, 0)))
-    d_act_two, grad_gate, grad_up, dots_all = gather_product(
-        act_two.T,
-        (w_gate, w_up),
-        ((d_gate * rms_two).astype(low), (d_up * rms_two).astype(low)),
-        dots_own,
-        512,
-        False,
-        7,
-    )
-    dot_two = dots_all[:, : rows // LANES].reshape(parts * rows, 1)
-    grad_gain_two = jnp.sum(d_act_two * resid, axis=0)
-    ffn, grad_down, _, d_norm = gather_product(
-        g_low,
-        (w_down,),
-        (hidden,),
-        none[0],
-        256,
-        True,
-        8,
-        line=(d_act_two * gain_two - resid * dot_two).astype(low),
-    )
-    d_resid = g_low.astype(jnp.float32) + d_norm.astype(jnp.float32)
-    d_attn = d_resid.astype(low)
+    gain_one = gain_attn.astype(jnp.float32)[None, :]
+    gain_two = gain_ffn.astype(jnp.float32)[None, :]
+    wide = w_query.shape[1]
+
+    qkv, x_low, act_one_t, w_qkv, rms = opening(tokens, gain_one, w_query, kv_weight, 1)
+    attn_part, mixed_all, g_low, kv, probs, queries, pair_rms = attend(
+        qkv, rms, pair_cos[0], pair_sin[0], allowed.astype(jnp.float32), w_out, d_out, 2
+    )
+    d_hidden, attn = scatter_product(g_low, w_down, 512, 3, attn_part)
+    hidden, d_gate, d_up, act_two_t, dots = ffn_scatter(x_low, attn, gain_two, w_gate, w_up, d_hidden, 4)
+    contrib, grad_gain_two, grad_gate, grad_up = back_gather(
+        act_two_t, w_gate, w_up, d_gate, d_up, dots, x_low, attn, gain_two, 5
+    )
+    ffn, d_attn, grad_down = down_gather(g_low, w_down, hidden, contrib, 6)
     grad_out = matmul_tn(mixed_all, d_attn)
-
     d_tokens, out, grad_qkv, grad_kv, gain_tiles = tail(
         d_attn,
         w_out,
@@ -1384,22 +1612,21 @@
         pair_rms,
         pair_cos,
         pair_sin,
-        act_one.T,
+        act_one_t,
         w_qkv,
-        ffn.astype(low),
+        ffn,
         x_low,
-        resid.astype(low),
-        gain_one[None, :],
-        grad_gain_two[None, :],
-        9,
-    )
-    grad_query = grad_qkv[:, :qw]
+        attn,
+        gain_one,
+        grad_gain_two,
+        7,
+    )
     gains = jnp.sum(gain_tiles, axis=0).reshape(2, -1)
     return (
         out,
         d_tokens.astype(jnp.float32),
         gains[0],
-        grad_query,
+        grad_qkv[:, :wide],
         grad_kv,
         grad_out,
         gains[1],

time: 741 us -> 676 us (0.912)
  other arithmetic: 40.9 us -> 10.7 us
  Pallas kernels: 652 us -> 631 us
  local copies, waits for them, and re-layouts: 32.4 us -> 20.7 us
    pallas_call x8 -> x7, Pallas kernels: 652 us -> 631 us  [kernel_call(): pl.pallas_call(kernel, out_shape=out_shape, in_specs=specs, out_specs=out...]
    reduce_sum x5 -> x0, other arithmetic: 20.6 us -> none  [the longest x1 7.39 us: acts_move(): jnp.sum(d_gate * gate + d_up * up_val, axis=-1, keepdims=True)]
    convert_element_type x6 -> x0, other arithmetic: 10.9 us -> none  [the longest x1 3.37 us: acts_move(): act_one = (x_col * gain_one).astype(low)]
    unnamed x54 -> x29, local copies, waits for them, and re-layouts: 17.6 us -> 15.7 us
where the time goes in v6:
time: 676 us; the launch traced here: 670 us
  Pallas kernels  631 us (93%)
  local copies, waits for them, and re-layouts  20.7 us (3%)
  other arithmetic  10.7 us (2%)
    pallas_call x7, Pallas kernels, kernel_call(): pl.pallas_call(kernel, out_shape=out_shape, in_specs=specs, out_specs=out...  631 us
    unnamed x29, local copies, waits for them, and re-layouts  15.7 us

profile of v6, /device:TPU:0, one launch (start us, length us, event | category | flops | bytes accessed | tf_op | source)
XLA Modules:
  0.0 669.7 jit_solution(13368204351644196622)
XLA Ops:
  0.6 0.8 slice_compare_fusion
  1.5 0.1 add_select_fusion
  1.6 0.3 reduce-window.9
  1.9 0.1 slice.26
  2.0 0.1 slice_reduce_fusion
  2.1 0.1 fusion
  2.2 1.3 broadcast_in_dim.20
  3.4 1.3 broadcast_in_dim.21
  4.7 0.8 fusion.1
  5.6 0.9 and_convert_fusion.mask
  6.5 1.0 multiply_sine_fusion
  7.6 0.0 copy-start.2
  7.6 0.0 copy-start.3
  7.6 0.6 copy-done.2
  8.2 0.7 pad_maximum_fusion.1.sin
  8.9 0.0 copy-done.3
  8.9 0.7 pad_maximum_fusion.cos
  9.7 58.9 %open_1.1 = (f32[256,1536]{1,0:T(8,128)}, bf16[2048,512]{1,0:T(8,128)(2,1)}, bf16[512,2048]{1,0:T(8,128)(2,1)}, bf16[512,1536]{1,0:T(8,128)(2,1)}, f32[256,128]{1,0:T(8,128)}) custom-call(bf16[256,4096]{1,0:T(8,128)(2,1)} %tokens.1, f32[1,512]{1,0:T(1,128)} %bitcast.39, bf16[512,1024]{1,0:T(8,128)(2,1)} %w_query.1, bf16[512,512]{1,0:T(8,128)(2,1)} %kv_weight.1), custom_call_target="tpu_custom_call" | custom-call | tf_op jit(solution)/shard_map/open_1/pallas_call | solution.py:391
  68.6 59.5 %attend_2.1 = (bf16[2048,512]{1,0:T(8,128)(2,1)}, bf16[2048,1024]{1,0:T(8,128)(2,1)}, bf16[2048,512]{1,0:T(8,128)(2,1)}, bf16[2,256,512]{2,1,0:T(8,128)(2,1)}, f...) custom-call(f32[256,1536]{1,0:T(8,128)} %get-tuple-element.41.qkv, ...), custom_call_target="tpu_custom_call" | custom-call | tf_op jit(solution)/shard_map/attend_2/pallas_call | solution.py:391
  128.1 68.9 %scatter_product_3.1 = (f32[256,3072]{1,0:T(8,128)}, bf16[2048,512]{1,0:T(8,128)(2,1)}) custom-call(bf16[2048,512]{1,0:T(8,128)(2,1)} %get-tuple-element.43.act.cot, bf16[3072,512]{1,0:T(8,128)(2,1)} %weight.3, bf16[2048,512]{1,0:T(8,128)(2,1)} %get-tuple-element.45.line_own), custom_call_target="tpu_custom_call" | custom-call | tf_op jit(solution)/shard_map/scatter_product_3/pallas_call | solution.py:391
  197.0 117.8 %ffn_4.1 = (bf16[256,3072]{1,0:T(8,128)(2,1)}, bf16[256,3072]{1,0:T(8,128)(2,1)}, bf16[256,3072]{1,0:T(8,128)(2,1)}, bf16[512,2048]{1,0:T(8,128)(2,1)}, f32[8,128]{1,0:T(8,128)}) custom-call(bf16[2048,512]{1,0:T(8,128)(2,1)} %get-tuple-element.44.x_low, bf16[2048,512]{1,0:T(8,128)(2,1)} %get-tuple-element.46.attn, f32[1,512]{1,0:T(1,128)} %bitcast.41, ...), custom_call_target="tpu_custom_call" | custom-call | tf_op jit(solution)/shard_map/ffn_4/pallas_call | solution.py:391
  314.8 116.4 %back_5.1 = (bf16[2048,512]{1,0:T(8,128)(2,1)}, f32[1,512]{1,0:T(1,128)}, f32[512,3072]{1,0:T(8,128)}, f32[512,3072]{1,0:T(8,128)}) custom-call(bf16[512,2048]{1,0:T(8,128)(2,1)} %get-tuple-element.49.act_t, bf16[512,3072]{1,0:T(8,128)(2,1)} %w_gate.3, bf16[512,3072]{1,0:T(8,128)(2,1)} %w_up.3, bf16[256,3072]{1,0:T(8,128)(2,1)} %get-tuple-element.50.d_gate, ...), custom_call_target="tpu_custom_call" | custom-call | tf_op jit(solution)/shard_map/back_5/pallas_call | solution.py:391
  431.2 67.5 %down_6.1 = (bf16[2048,512]{1,0:T(8,128)(2,1)}, bf16[2048,512]{1,0:T(8,128)(2,1)}, f32[3072,512]{1,0:T(8,128)}) custom-call(bf16[2048,512]{1,0:T(8,128)(2,1)} %get-tuple-element.43.act.cot, bf16[3072,512]{1,0:T(8,128)(2,1)} %weight.3, bf16[256,3072]{1,0:T(8,128)(2,1)} %get-tuple-element.48.hidden, bf16[2048,512]{1,0:T(8,128)(2,1)} %get-tuple-element.53.line_own), custom_call_target="tpu_custom_call" | custom-call | tf_op jit(solution)/shard_map/down_6/pallas_call | solution.py:391
  498.6 6.5 fusion.3
  505.2 141.9 %tail_7.1 = (bf16[256,4096]{1,0:T(8,128)(2,1)}, bf16[256,4096]{1,0:T(8,128)(2,1)}, f32[512,1536]{1,0:T(8,128)}, f32[512,512]{1,0:T(8,128)}, f32[4,8,128]{2,1,0:T(8,128)}) custom-call(bf16[2048,512]{1,0:T(8,128)(2,1)} %get-tuple-element.54.d_attn, bf16[1024,512]{1,0:T(8,128)(2,1)} %w_out.3, bf16[256,1024]{1,0:T(8,128)(2,1)} %get-tuple-element.55.queries, ...), custom_call_target="tpu_custom_call" | custom-call | tf_op jit(solution)/shard_map/tail_7/pallas_call | solution.py:391
  647.1 0.0 copy-start
  647.1 0.9 reduce_sum.9
  648.0 0.6 slice_bitcast_fusion
  648.6 0.0 slice-start.2
  648.6 3.3 slice.29
  651.9 0.0 copy-done
  651.9 0.0 copy-start.1
  651.9 0.0 slice-start.3
  651.9 2.6 convert_element_type.17
  654.5 0.0 copy-done.1
  654.5 0.0 copy-start.4
  654.5 1.3 copy.28
  655.9 0.8 copy-done.4
  656.7 0.0 slice-start
  656.7 1.0 copy.29
  657.6 0.0 slice-done.2
  657.6 0.0 slice-done.3
  657.7 0.0 slice-start.1
  657.7 0.0 slice-start.4
  657.7 3.2 copy.30
  660.9 0.0 slice-done
  660.9 1.5 slice-done.1
  662.3 0.0 slice-start.5
  662.3 3.2 copy.31
  665.5 0.0 slice-done.4
  665.5 1.4 slice-done.5
  667.0 2.7 copy.32
  (10 shorter events, 0.1 us)
Async XLA Ops:
  7.6 0.7 copy-start.2
  7.6 1.4 copy-start.3
  647.1 4.8 copy-start
  648.6 9.0 %slice-start.2 = ((s8[6291456]{0:T(1024)(128)(4,1)}), s8[4194304]{0:T(1024)(128)(4,1)S(1)}, s32[]{:S(2)}) async-start(s8[6291456]{0:T(1024)(128)(4,1)} %bitcast.33), calls=%async_computation.2 | async-start | bytes 8388608
  651.9 2.6 copy-start.1
  651.9 5.7 slice-start.3
  654.5 2.1 copy-start.4
  656.7 4.2 slice-start
  657.7 4.7 slice-start.1
  657.7 7.9 %slice-start.4 = ((s8[6291456]{0:T(1024)(128)(4,1)}), s8[2097152]{0:T(1024)(128)(4,1)S(1)}, s32[]{:S(2)}) async-start(s8[6291456]{0:T(1024)(128)(4,1)} %bitcast.35), calls=%async_computation.4 | async-start | bytes 4194304
  662.3 4.6 slice-start.5

commit v7 on v6

--- a/solution.py
+++ b/solution.py
@@ -498,7 +498,7 @@
             self.to_x(hop, at, stage).start()
             self.to_y(hop, at, stage).start()
 
-    def run(self, line=None):
+    def run(self, hook=None):
         def body(step, _):
             @pl.when(step < self.steps)
             def _():
@@ -508,8 +508,8 @@
             def _():
                 self.finish(step - 1)
 
-            if line:
-                line.step(step)
+            if hook:
+                hook(step)
             return 0
 
         lax.fori_loop(0, self.steps + 1, body, 0)
@@ -688,7 +688,41 @@
     return jnp.sum(eye * row, axis=1, keepdims=True)
 
 
-def open_kernel(rows, width, counts, tokens, gain, w_query, kv_weight, qkv, x_low, act_t, w_qkv, rms, *refs):
+def make_tables(here, rows, segs, cos, sin, mask):
+    eye = diagonal()
+    tiles = rows // LANES
+    freqs = jnp.exp(lax.broadcasted_iota(jnp.int32, (1, LANES), 1).astype(jnp.float32) * (-math.log(10000.0) / LANES))
+    lane = lax.broadcasted_iota(jnp.int32, (1, LANES), 1)
+    line = lax.broadcasted_iota(jnp.int32, (LANES, 1), 0)
+
+    def row_of(side, at):
+        return ((here.seq + side) % 2) * tiles + at
+
+    for side in range(2):
+        for at in range(tiles):
+            row = row_of(side, at)
+            ids = from_tile(segs[pl.ds(row, 1), :], eye)
+            before = jnp.zeros((LANES, 1), jnp.float32)
+            for other in range(2 * tiles):
+                smaller = segs[other : other + 1, :] < ids
+                before += jnp.sum(smaller.astype(jnp.float32), axis=-1, keepdims=True)
+            index = row * LANES + line
+            angles = (index.astype(jnp.float32) - before) * freqs
+            span = slice(at * LANES, (at + 1) * LANES)
+            cos[side, span, :] = jnp.cos(angles)
+            sin[side, span, :] = jnp.sin(angles)
+            if side == 0:
+                for key_side in range(2):
+                    for key_at in range(tiles):
+                        key_row = row_of(key_side, key_at)
+                        same = segs[pl.ds(key_row, 1), :] == ids
+                        allowed = jnp.logical_and(same, key_row * LANES + lane <= index)
+                        first = key_side * rows + key_at * LANES
+                        mask[span, first : first + LANES] = allowed.astype(jnp.float32)
+
+
+def open_kernel(rows, width, counts, tokens, gain, w_query, kv_weight, segs, qkv, x_low, act_t, w_qkv, rms, cos, sin,
+                mask, *refs):
     here = Place()
     cols = gain.shape[1]
     act, turn_send, turn_recv, local_sems = refs[:4]
@@ -722,6 +756,7 @@
 
     total = lax.fori_loop(0, 8, squares, jnp.zeros((rows, 1), jnp.float32))
     rms[...] = jnp.broadcast_to(lax.rsqrt(total / (8 * cols) + EPS), rms.shape)
+    make_tables(here, rows, segs, cos, sin, mask)
 
     def prepare(first, count):
         def one(step, _):
@@ -761,7 +796,7 @@
         turn_copy(at).wait_send()
 
 
-def opening(tokens, gain, w_query, kv_weight, cid, width=256):
+def opening(tokens, gain, w_query, kv_weight, segs, cid, width=256):
     rows = tokens.shape[0]
     cols, wide = w_query.shape
     every = wide + kv_weight.shape[1]
@@ -776,11 +811,15 @@
         jax.ShapeDtypeStruct((cols, 8 * rows), low),
         jax.ShapeDtypeStruct((cols, every), low),
         jax.ShapeDtypeStruct((rows, LANES), f32),
+        jax.ShapeDtypeStruct((2, rows, LANES), f32),
+        jax.ShapeDtypeStruct((2, rows, LANES), f32),
+        jax.ShapeDtypeStruct((rows, 2 * rows), f32),
     ]
     scratch = [pltpu.VMEM((8 * rows, cols), low), dma((7,)), dma((7,)), dma((3,))]
     scratch += reduce_scratch(counts, rows, width)
     kernel = functools.partial(open_kernel, rows, width, counts)
-    return kernel_call(kernel, out_shape, [tokens, gain, w_query, kv_weight], [vm, vm, hbm, hbm], scratch, cid, "open")
+    return kernel_call(kernel, out_shape, [tokens, gain, w_query, kv_weight, segs],
+                       [vm, vm, hbm, hbm, vm], scratch, cid, "open")
 
 
 def scatter_kernel(rows, width, counts, line_counts, act, weight, line_own, out, line_out, *refs):
@@ -790,7 +829,7 @@
     total = Reduce(here, counts, product, refs[:11])
     greet(here, slice_peers(here), True)
     line.begin()
-    done = total.run(line)
+    done = total.run(line.step)
     line.end(done)
 
     def emit(at, first, second):
@@ -920,7 +959,7 @@
                 grad_gate, grad_up, *refs):
     here = Place()
     spread = Spread(here, counts, refs[:7])
-    tiny_all, tiny_send, tiny_recv, own_sems, weight, sums, grads, local_sems, out_sems = refs[7:16]
+    tiny_all, tiny_send, tiny_recv, own_sems, weight, sums, grads, staged, local_sems, out_sems = refs[7:17]
     tiny = Tiny(here, dots, tiny_all, (tiny_send, tiny_recv), False)
     half_cols = counts * width
     local = [
@@ -960,12 +999,19 @@
 
     def leave(half, at):
         spot = pl.ds(pl.multiple_of(at * width, width), width)
-        return pltpu.make_async_copy(grads.at[:, columns(half, at)], (grad_gate, grad_up)[half].at[:, spot],
+        return pltpu.make_async_copy(staged.at[at % 2, half], (grad_gate, grad_up)[half].at[:, spot],
                                      out_sems.at[half, at])
 
     def done(stage, at):
+        @pl.when(jnp.logical_and(stage == 3, at > 1))
+        def _():
+            leave(0, at - 2).wait()
+            leave(1, at - 2).wait()
+
         @pl.when(stage == 3)
         def _():
+            for half in range(2):
+                staged[at % 2, half] = grads[:, columns(half, at)].astype(staged.dtype)
             leave(0, at).start()
             leave(1, at).start()
 
@@ -992,7 +1038,7 @@
         leave(1, at).wait()
         return 0
 
-    lax.fori_loop(0, counts, drain, 0)
+    lax.fori_loop(counts - 2, counts, drain, 0)
 
 
 def back_gather(act_t, w_gate, w_up, d_gate, d_up, dots, x_low, attn, gain, cid, width=512):
@@ -1006,14 +1052,15 @@
     out_shape = [
         jax.ShapeDtypeStruct((total, cols), low),
         jax.ShapeDtypeStruct((1, cols), f32),
-        jax.ShapeDtypeStruct((cols, half), f32),
-        jax.ShapeDtypeStruct((cols, half), f32),
+        jax.ShapeDtypeStruct((cols, half), low),
+        jax.ShapeDtypeStruct((cols, half), low),
     ]
     scratch = spread_scratch(counts, rows, width) + [
         pltpu.VMEM((8, 8, LANES), f32), dma((7,)), dma((7,)), dma((2, counts)),
         pltpu.VMEM((cols, 2 * half), low),
         pltpu.VMEM((total, cols), f32),
         pltpu.VMEM((cols, 2 * half), f32),
+        pltpu.VMEM((2, 2, cols, width), low),
         dma((2,)), dma((2, counts)),
     ]
     operands = [act_t, w_gate, w_up, d_gate, d_up, dots, x_low, attn, gain]
@@ -1025,8 +1072,8 @@
 def down_kernel(rows, width, counts, line_counts, cot, weight, hidden, line_own, ffn, d_attn, grad, *refs):
     here = Place()
     spread = Spread(here, counts, refs[:7])
-    own_sems, sums, grads, out_sems, line_out = refs[7:12]
-    line = Line(here, line_counts, [line_own, line_out] + list(refs[12:]))
+    own_sems, sums, grads, staged, out_sems, line_out = refs[7:13]
+    line = Line(here, line_counts, [line_own, line_out] + list(refs[13:]))
     own = load_own(spread, (hidden,), width, counts, own_sems)
     for copy in own:
         copy.start()
@@ -1052,12 +1099,18 @@
         grads[cols, :] = gained
 
     def leave(half, at):
-        cols = columns(half, at)
-        return pltpu.make_async_copy(grads.at[cols, :], grad.at[cols, :], out_sems.at[half, at])
+        return pltpu.make_async_copy(staged.at[at % 2, half], grad.at[columns(half, at), :], out_sems.at[half, at])
 
     def done(stage, at):
+        @pl.when(jnp.logical_and(stage == 3, at > 1))
+        def _():
+            leave(0, at - 2).wait()
+            leave(1, at - 2).wait()
+
         @pl.when(stage == 3)
         def _():
+            for half in range(2):
+                staged[at % 2, half] = grads[columns(half, at), :].astype(staged.dtype)
             leave(0, at).start()
             leave(1, at).start()
 
@@ -1079,7 +1132,7 @@
         leave(1, at).wait()
         return 0
 
-    lax.fori_loop(0, counts, drain, 0)
+    lax.fori_loop(counts - 2, counts, drain, 0)
 
 
 def down_gather(cot, weight, hidden, line, cid, width=256, line_counts=16):
@@ -1093,12 +1146,13 @@
     out_shape = [
         jax.ShapeDtypeStruct((total, cols), low),
         jax.ShapeDtypeStruct((total, cols), low),
-        jax.ShapeDtypeStruct(weight.shape, f32),
+        jax.ShapeDtypeStruct(weight.shape, low),
     ]
     scratch = spread_scratch(counts, rows, width) + [
         dma((2, counts)),
         pltpu.VMEM((total, cols), f32),
         pltpu.VMEM(weight.shape, f32),
+        pltpu.VMEM((2, 2, width, cols), low),
         dma((2, counts)),
         pltpu.VMEM((total, cols), low),
     ] + line_scratch(line_counts, line.shape, low)
@@ -1132,7 +1186,7 @@
     def rotated(first):
         lead = qkv[:, first : first + half] * rms[...]
         trail = qkv[:, first + half : first + HD] * rms[...]
-        return lead * cos[...] - trail * sin[...], trail * cos[...] + lead * sin[...]
+        return lead * cos[0] - trail * sin[0], trail * cos[0] + lead * sin[0]
 
     low_k, high_k = rotated(wide)
     kv[0, :, :half] = low_k.astype(kv.dtype)
@@ -1221,10 +1275,11 @@
 
 
 def tail_kernel(rows, heads, per, d_attn, w_out, queries, kv, probs, rms, cos, sin, act_t, w_qkv, ffn, x_low,
-                attn, gain, gain_grad, d_tok, out, grad, kv_sum, gain_tiles, *refs):
+                attn, gain, gain_grad, mixed_all, d_tok, out, grad_query, grad_out, kv_sum, gain_tiles, *refs):
     here = Place()
     width = HD
-    counts, out_counts = heads // 2, (heads + 2) // 2
+    counts = heads // 2
+    part = rows // 2
     refs = list(refs)
     line_counts = 8 * per
     cols = d_attn.shape[1]
@@ -1236,21 +1291,27 @@
         return taken_refs
 
     total_refs = take(11)
-    spread = Spread(here, out_counts, take(7))
+    spread = Spread(here, 1, take(7))
     d_mixed, tiny_own, tiny_all, d_kv, give, taken, give_sems, tiny_send, tiny_recv = take(9)
-    sums, gain_sum, tile, tile_send, tile_recv, put_sems, local_sems = take(7)
+    grad, grad_mixed, gain_sum, tile, tile_send, tile_recv, put_sems, local_sems, mixed_two, mixed_sems = take(10)
 
     def far(at):
         return turned(at // per)
 
     def near(at):
-        return at // (2 * per), at // per % 2
+        at = jnp.minimum(at, line_counts - 1)
+        x_stream, y_stream = spread.streams(at // 4)
+        second = at // 2 % 2
+        across = x_stream[0] + second * (y_stream[0] - x_stream[0])
+        half_at = x_stream[1] + second * (y_stream[1] - x_stream[1])
+        return across, at % 2, half_at
 
     def place_ffn(at):
         return here.shard(*far(at)) * per + at % per
 
     def place_tok(at):
-        return jnp.where(at < line_counts, here.shard(*near(jnp.minimum(at, line_counts - 1))) * per + at % per, at)
+        across, other, half_at = near(at)
+        return jnp.where(at < line_counts, here.shard(across, other) * per + half_at, at)
 
     ffn_sum = take(1)[0]
     line = Line(here, line_counts, [ffn, ffn_sum] + take(8), place_ffn)
@@ -1262,11 +1323,35 @@
     total = Reduce(here, counts, product, total_refs)
     greet(here, tiny.peers, True)
     line.begin()
-    done = total.run(line)
+    grad_mixed[...] = jnp.zeros_like(grad_mixed)
+
+    def mixed_copy(step):
+        span = pl.ds(pl.multiple_of(step * rows, rows), rows)
+        return pltpu.make_async_copy(mixed_all.at[span, :], mixed_two.at[step % 2], mixed_sems.at[step % 2])
+
+    mixed_copy(0).start()
+
+    def beside(step):
+        line.step(step)
+
+        @pl.when(step < 8)
+        def _():
+            span = pl.ds(pl.multiple_of(step * rows, rows), rows)
+            mixed_copy(step).wait()
+
+            @pl.when(step < 7)
+            def _():
+                mixed_copy(step + 1).start()
+
+            grad_mixed[...] += dot_tn(mixed_two[step % 2], d_attn[span, :])
+
+    done = total.run(beside)
+    grad_out[...] = grad_mixed[...].astype(grad_out.dtype)
 
     def land(at, first, second):
         for half_at, value in enumerate((first, second)):
-            d_mixed[:, pl.ds(pl.multiple_of((half_at * counts + at) * width, width), width)] = value
+            d_mixed[:, pl.ds(pl.multiple_of((half_at * counts + at) * width, width), width)] = value.astype(
+                d_mixed.dtype)
 
     total.end(land)
     half = HD // 2
@@ -1277,7 +1362,7 @@
     def one_head(head, dots):
         span = pl.ds(pl.multiple_of(head * HD, HD), HD)
         query = queries[:, span]
-        cot = d_mixed[:, span].astype(jnp.bfloat16)
+        cot = d_mixed[:, span]
         prob = probs[head]
         d_prob = jnp.concatenate([dot_nt(cot, kv[0, :, HD:]), dot_nt(cot, kv[1, :, HD:])], axis=1)
         delta = jnp.sum(prob * d_prob, axis=-1, keepdims=True)
@@ -1290,9 +1375,12 @@
             d_kv[side, :, HD:] += dot_tn(prob_low[:, keys], cot)
         dots = dots + jnp.sum(d_query * query.astype(jnp.float32), axis=-1, keepdims=True)
         lead, trail = d_query[:, :half], d_query[:, half:]
-        slot = got.at[0, core, head // out_counts, head % out_counts]
-        slot[:, :half] = ((lead * cos[0] + trail * sin[0]) * rms[0]).astype(got.dtype)
-        slot[:, half:] = ((trail * cos[0] - lead * sin[0]) * rms[0]).astype(got.dtype)
+        first = ((lead * cos[0] + trail * sin[0]) * rms[0]).astype(got.dtype)
+        second = ((trail * cos[0] - lead * sin[0]) * rms[0]).astype(got.dtype)
+        for rows_at in range(2):
+            piece = slice(rows_at * part, (rows_at + 1) * part)
+            got[0, core, rows_at, 0, :, pl.ds(pl.multiple_of(head * HD, HD), half)] = first[piece, :]
+            got[0, core, rows_at, 0, :, pl.ds(pl.multiple_of(head * HD + half, half), half)] = second[piece, :]
 
         line.step(done + head)
         return dots
@@ -1320,78 +1408,78 @@
                 d_kv[0, :, at * half : (at + 1) * half] = value
     given = remote(give, taken, give_sems.at[0], give_sems.at[1], spread.ydev)
     given.start()
-    sums[...] = jnp.zeros_like(sums)
+    grad[...] = jnp.zeros_like(grad)
     given.wait()
-    for at in range(2):
-        span = slice(at * HD, (at + 1) * HD)
-        value = d_kv[0, :, span] + taken[:, span].astype(jnp.float32)
-        got[0, core, 1, out_counts - 2 + at] = value.astype(got.dtype)
+    for rows_at in range(2):
+        piece = slice(rows_at * part, (rows_at + 1) * part)
+        value = d_kv[0, piece, :] + taken[piece, :].astype(jnp.float32)
+        got[0, core, rows_at, 0, :, heads * HD :] = value.astype(got.dtype)
     tiny.begin()
-    spread.begin()
+    for hop in range(2):
+        spread.x_copy(hop, 0).start()
+        spread.y_copy(hop, 0).start()
+    for stream in range(2):
+        spread.sib_copy(0, stream, 0).start()
     gain_sum[...] = jnp.zeros_like(gain_sum)
-
-    grad[...] = jnp.zeros_like(grad)
-
-    def blocks(across, half_at, at):
-        span = pl.ds(pl.multiple_of((half_at * out_counts + at) * width, width), width)
-        gained = grad[:, span]
-        for other in range(2):
-            row = row_span(here, across, other, rows)
-            block = got[across, (core + other) % 2, half_at, at]
-            sums[row, :] += dot_nt(block, w_qkv[:, span])
-            gained = gained + dot_nn(act_t[:, row], block)
-        grad[:, span] = gained
-
-    def contribute(chip):
-        def shard_rows(other, _):
-            shard, partner = here.shard(chip, other), here.shard((chip + 2) % 4, other)
-            for at in range(rows // LANES):
-                row = pl.ds(pl.multiple_of(shard * rows + at * LANES, LANES), LANES)
-                kept = rows // LANES + at
-                dot = from_tile(tiny_all[shard, at : at + 1, :] + tiny_all[partner, kept : kept + 1, :], eye)
-                value, x_rows = sums[row, :], x_low[row, :].astype(jnp.float32)
-                contrib[row, :] = (value * gain[...] - x_rows * dot).astype(contrib.dtype)
-                gain_sum[...] += jnp.sum(value * x_rows, axis=0, keepdims=True)
-            return 0
-
-        lax.fori_loop(0, 2, shard_rows, 0)
-        line_tok.launch(2 * per * chip, 2 * per)
-
-    first_part = 2 * per
-    left = line_counts + extra - first_part
     line.steps(done, line_counts + 2)
     tiny.end()
 
-    def hook(step):
-        stage, at = step // out_counts, step % out_counts
-
-        @pl.when(jnp.logical_and(stage > 0, stage < 3))
-        def _():
-            line_tok.step((stage - 1) * out_counts + at, 0, first_part)
-
-        @pl.when(stage == 3)
-        def _():
-            line_tok.step(at, first_part, left)
-
-    def complete(stage, at):
-        @pl.when(jnp.logical_and(at == out_counts - 1, stage == 0))
-        def _():
-            contribute(0)
-
-        @pl.when(jnp.logical_and(at == out_counts - 1, stage == 2))
-        def _():
-            lax.fori_loop(1, 3, lambda chip, _: (contribute(chip), 0)[1], 0)
-
-        @pl.when(jnp.logical_and(at == out_counts - 1, stage == 3))
-        def _():
-            contribute(3)
-
-    spread.run(blocks, hook, complete)
+    def block_of(at):
+        across, other, half_at = near(at)
+        shard, partner = here.shard(across, other), here.shard((across + 2) % 4, other)
+        block = got[across, (core + other) % 2, half_at, 0]
+        first = pl.multiple_of(shard * rows + half_at * part, part)
+        for tile_at in range(part // LANES):
+            row = pl.ds(pl.multiple_of(first + tile_at * LANES, LANES), LANES)
+            low_at = half_at * (part // LANES) + tile_at
+            kept = rows // LANES + low_at
+            dot = from_tile(tiny_all[shard, pl.ds(low_at, 1), :] + tiny_all[partner, pl.ds(kept, 1), :], eye)
+            value = dot_nt(block[tile_at * LANES : (tile_at + 1) * LANES, :], w_qkv[...])
+            x_rows = x_low[row, :].astype(jnp.float32)
+            contrib[row, :] = (value * gain[...] - x_rows * dot).astype(contrib.dtype)
+            gain_sum[...] += jnp.sum(value * x_rows, axis=0, keepdims=True)
+        line_tok.launch(at, 1)
+        rows_t = act_t[:, pl.ds(first, part)]
+        for at_col in range((heads + 2) * HD // 512):
+            span = slice(at_col * 512, (at_col + 1) * 512)
+            grad[:, span] += dot_nn(rows_t, block[:, span])
+
+    def stage_step(step, _):
+        stage = step // 4
+
+        @pl.when(jnp.logical_and(step % 4 == 0, jnp.logical_and(stage > 0, stage < 4)))
+        def _():
+            spread.x_copy(stage - 1, 0).wait_recv()
+            spread.sib_copy(stage, 0, 0).start()
+            spread.y_copy(stage - 1, 0).wait_recv()
+            spread.sib_copy(stage, 1, 0).start()
+
+        @pl.when(step == 4)
+        def _():
+            spread.x_copy(2, 0).start()
+            spread.y_copy(2, 0).start()
+
+        @pl.when(step < line_counts)
+        def _():
+            for stream in range(2):
+                @pl.when(step % 4 == 2 * stream)
+                def _(stream=stream):
+                    spread.sib_copy(stage, stream, 0).wait_recv()
+
+            block_of(step)
+
+        @pl.when(step >= 4)
+        def _():
+            line_tok.step(step - 4)
+        return 0
+
+    lax.fori_loop(0, line_counts, stage_step, 0)
     for half_at in range(cols // (rows // per)):
         span = pl.ds(line_counts * (rows // per) + half_at * (rows // per), rows // per)
         source = slice(half_at * (rows // per), (half_at + 1) * (rows // per))
         contrib[span, :] = grad[source, heads * HD :].astype(contrib.dtype)
     line_tok.launch(line_counts, extra)
+    grad_query[...] = grad[:, : heads * HD].astype(grad_query.dtype)
     for at in range(cols // LANES):
         tile[at : at + 1, :] = gain_sum[:, at * LANES : (at + 1) * LANES]
         spot = cols // LANES + at
@@ -1406,11 +1494,20 @@
     columns = pl.ds(pl.multiple_of(me * cols, cols), cols)
     chunk = line.chunk
 
+    def landing(which, at):
+        sub = at % per if which == 0 else near(at)[2]
+        return (out, d_tok)[which].at[pl.ds(pl.multiple_of(sub * chunk, chunk), chunk), columns]
+
     def put(which, at):
         kind = (line, line_tok)[which]
-        goal = here.device(*(far, near)[which](at))
-        dst = (out, d_tok)[which].at[pl.ds(pl.multiple_of(at % per * chunk, chunk), chunk), columns]
-        return remote(kind.from_end.at[at], dst, put_sems.at[which, 0, at], put_sems.at[which, 1, at], goal)
+        goal = here.device(*(far(at) if which == 0 else near(at)[:2]))
+        return remote(kind.from_end.at[at], landing(which, at), put_sems.at[which, 0, at], put_sems.at[which, 1, at],
+                      goal)
+
+    def keep(which, at):
+        spot = at % per if which == 0 else near(at)[2]
+        return pltpu.make_async_copy((line, line_tok)[which].from_end.at[at], landing(which, at),
+                                     local_sems.at[which, spot])
 
     def emit(which, at):
         kind = (line, line_tok)[which]
@@ -1421,15 +1518,14 @@
         kind.from_end[at] = (base + kind.out[row, :].astype(jnp.float32)).astype(out.dtype)
 
     def is_own(which, at):
-        return at >= 7 * per if which == 0 else at < per
+        return at >= 7 * per if which == 0 else jnp.logical_and(at < 4, at % 2 == 0)
 
     def send(which, at):
         own = is_own(which, at)
 
         @pl.when(own)
         def _():
-            dst = (out, d_tok)[which].at[pl.ds(pl.multiple_of(at % per * chunk, chunk), chunk), columns]
-            pltpu.make_async_copy((line, line_tok)[which].from_end.at[at], dst, local_sems.at[which, at % per]).start()
+            keep(which, at).start()
 
         @pl.when(jnp.logical_not(own))
         def _():
@@ -1441,40 +1537,26 @@
 
     @pl.when(line.inner == 1)
     def _():
-        def early(at, _):
-            emit(1, at)
+        start = line_counts - 4
+
+        def both(at, _):
+            line_tok.step(at)
+            spot = at - start
+
+            @pl.when(jnp.logical_and(spot > 0, spot <= line_counts // 2))
+            def _():
+                for which in range(2):
+                    for last in range(2):
+                        send(which, 2 * spot - 2 + last)
+
+            @pl.when(spot < line_counts // 2)
+            def _():
+                for which in range(2):
+                    for last in range(2):
+                        emit(which, 2 * spot + last)
             return 0
 
-        lax.fori_loop(0, first_part, early, 0)
-
-        def both(at, _):
-            line_tok.step(at, first_part, left)
-            spot = at - out_counts
-            ready = first_part + at - out_counts
-
-            @pl.when(jnp.logical_and(spot > 0, spot <= line_counts))
-            def _():
-                send(0, spot - 1)
-
-            @pl.when(jnp.logical_and(spot > 0, spot <= first_part))
-            def _():
-                send(1, spot - 1)
-
-            @pl.when(jnp.logical_and(ready > first_part, ready <= line_counts))
-            def _():
-                send(1, ready - 1)
-
-            @pl.when(spot < line_counts)
-            def _():
-                emit(0, spot)
-
-            @pl.when(ready < line_counts)
-            def _():
-                emit(1, ready)
-            return 0
-
-        lax.fori_loop(out_counts, out_counts + line_counts + 1, both, 0)
-        line_tok.steps(out_counts + line_counts + 1, left + 2, first_part, left)
+        lax.fori_loop(start, line_counts + extra + 2, both, 0)
 
         def drain(at, _):
             line_tok.down(at).wait_send()
@@ -1503,26 +1585,35 @@
 
     for half_at in range(extra):
         span = pl.ds((line_counts + half_at) * chunk, chunk)
-        kv_sum[half_at * chunk : (half_at + 1) * chunk, :] = summed[span, :].astype(jnp.float32)
-    spread.end()
-    for which in range(2):
-        def finish(at, _, which=which):
-            @pl.when(jnp.logical_not(is_own(which, at)))
+        kv_sum[half_at * chunk : (half_at + 1) * chunk, :] = summed[span, :]
+    for hop in range(3):
+        spread.x_copy(hop, 0).wait_send()
+        spread.y_copy(hop, 0).wait_send()
+    for stage in range(4):
+        spread.sib_copy(stage, 0, 0).wait_send()
+        spread.sib_copy(stage, 1, 0).wait_send()
+
+    def finish(at, _):
+        for which in range(2):
+            own = is_own(which, at)
+
+            @pl.when(own)
+            def _():
+                keep(which, at).wait()
+
+            @pl.when(jnp.logical_not(own))
             def _():
                 put(which, at).wait()
-            return 0
-
-        lax.fori_loop(0, line_counts, finish, 0)
-        for at in range(per):
-            dst = (out, d_tok)[which].at[at * chunk : (at + 1) * chunk, columns]
-            spot = (7 * per if which == 0 else 0) + at
-            pltpu.make_async_copy((line, line_tok)[which].from_end.at[spot], dst, local_sems.at[which, at]).wait()
+        return 0
+
+    lax.fori_loop(0, line_counts, finish, 0)
     for step in range(3):
         tile_copy(step).wait()
 
 
-def tail(d_attn, w_out, queries, kv, probs, rms, cos, sin, act_t, w_qkv, ffn, x_low, attn, gain, gain_grad, cid,
-         per=2):
+def tail(d_attn, w_out, queries, kv, probs, rms, cos, sin, act_t, w_qkv, ffn, x_low, attn, gain, gain_grad,
+         mixed_all, cid,
+ per=2):
     total, cols = d_attn.shape
     rows = total // 8
     wide = w_out.shape[0]
@@ -1537,29 +1628,34 @@
     out_shape = [
         jax.ShapeDtypeStruct((rows, 8 * cols), low),
         jax.ShapeDtypeStruct((rows, 8 * cols), low),
-        jax.ShapeDtypeStruct(w_qkv.shape, f32),
-        jax.ShapeDtypeStruct((cols, 2 * HD), f32),
+        jax.ShapeDtypeStruct((cols, wide), low),
+        jax.ShapeDtypeStruct(w_out.shape, low),
+        jax.ShapeDtypeStruct((cols, 2 * HD), low),
         jax.ShapeDtypeStruct((4, 8, LANES), f32),
     ]
-    scratch = reduce_scratch(heads // 2, rows, HD) + spread_scratch((heads + 2) // 2, rows, HD)
+    scratch = reduce_scratch(heads // 2, rows, HD, 2) + spread_scratch(1, rows // 2, wide + 2 * HD)
     scratch += [
-        pltpu.VMEM((rows, wide), f32),
+        pltpu.VMEM((rows, wide), low),
         pltpu.VMEM((8, LANES), f32),
         pltpu.VMEM((8, 8, LANES), f32),
         pltpu.VMEM((2, rows, 2 * HD), f32),
         pltpu.VMEM((rows, 2 * HD), low),
         pltpu.VMEM((rows, 2 * HD), low),
         dma((2,)), dma((7,)), dma((7,)),
-        pltpu.VMEM((total, cols), f32),
+        pltpu.VMEM(w_qkv.shape, f32),
+        pltpu.VMEM(w_out.shape, f32),
         pltpu.VMEM((1, cols), f32),
         pltpu.VMEM((8, LANES), f32),
         dma((3,)), dma((3,)), dma((2, 2, counts)), dma((2, per)),
+        pltpu.VMEM((2, rows, wide), low), dma((2,)),
         pltpu.VMEM((total, cols), low),
     ] + line_scratch(counts, (total, cols), low)
     scratch += [pltpu.VMEM(long, low), pltpu.VMEM(long, low)] + line_scratch(counts + extra, long, low)
-    operands = [d_attn, w_out, queries, kv, probs, rms, cos, sin, act_t, w_qkv, ffn, x_low, attn, gain, gain_grad]
+    operands = [d_attn, w_out, queries, kv, probs, rms, cos, sin, act_t, w_qkv, ffn, x_low, attn, gain,
+                gain_grad, mixed_all]
     kernel = functools.partial(tail_kernel, rows, heads, per)
-    return kernel_call(kernel, out_shape, operands, [vm] * len(operands), scratch, cid, "tail")
+    specs = [vm] * (len(operands) - 1) + [pl.BlockSpec(memory_space=pl.ANY)]
+    return kernel_call(kernel, out_shape, operands, specs, scratch, cid, "tail")
 
 
 LANES = 128
@@ -1569,32 +1665,17 @@
     tokens, seg_ids, gain_attn, w_query, kv_weight, w_out, gain_ffn, w_gate, w_up, w_down, d_out
 ):
     rows = tokens.shape[0]
-    offset = lax.axis_index("seq") * rows
-    places, cos_table, sin_table = place_tables(seg_ids)
-    away = rows - offset
-
-    def own_first(table):
-        return jnp.stack(
-            [
-                lax.dynamic_slice_in_dim(table, offset, rows, 0),
-                lax.dynamic_slice_in_dim(table, away, rows, 0),
-            ]
-        )
-
-    pair_places = own_first(places)
-    pair_segs = own_first(seg_ids)
-    pair_cos = own_first(cos_table)
-    pair_sin = own_first(sin_table)
-    allowed = (pair_segs[0][:, None] == pair_segs.reshape(1, -1)) & (
-        pair_places[0][:, None] >= pair_places.reshape(1, -1)
-    )
+    segs = seg_ids.astype(jnp.float32).reshape(2 * rows // LANES, LANES)
+    segs = jnp.pad(segs, ((0, 8 - 2 * rows // LANES), (0, 0)))
     gain_one = gain_attn.astype(jnp.float32)[None, :]
     gain_two = gain_ffn.astype(jnp.float32)[None, :]
-    wide = w_query.shape[1]
-
-    qkv, x_low, act_one_t, w_qkv, rms = opening(tokens, gain_one, w_query, kv_weight, 1)
+    wider = jnp.float32
+
+    qkv, x_low, act_one_t, w_qkv, rms, cos, sin, mask = opening(
+        tokens, gain_one, w_query, kv_weight, segs, 1
+    )
     attn_part, mixed_all, g_low, kv, probs, queries, pair_rms = attend(
-        qkv, rms, pair_cos[0], pair_sin[0], allowed.astype(jnp.float32), w_out, d_out, 2
+        qkv, rms, cos, sin, mask, w_out, d_out, 2
     )
     d_hidden, attn = scatter_product(g_low, w_down, 512, 3, attn_part)
     hidden, d_gate, d_up, act_two_t, dots = ffn_scatter(x_low, attn, gain_two, w_gate, w_up, d_hidden, 4)
@@ -1602,16 +1683,15 @@
         act_two_t, w_gate, w_up, d_gate, d_up, dots, x_low, attn, gain_two, 5
     )
     ffn, d_attn, grad_down = down_gather(g_low, w_down, hidden, contrib, 6)
-    grad_out = matmul_tn(mixed_all, d_attn)
-    d_tokens, out, grad_qkv, grad_kv, gain_tiles = tail(
+    d_tokens, out, grad_query, grad_out, grad_kv, gain_tiles = tail(
         d_attn,
         w_out,
         queries,
         kv,
         probs,
         pair_rms,
-        pair_cos,
-        pair_sin,
+        cos,
+        sin,
         act_one_t,
         w_qkv,
         ffn,
@@ -1619,20 +1699,21 @@
         attn,
         gain_one,
         grad_gain_two,
+        mixed_all,
         7,
     )
     gains = jnp.sum(gain_tiles, axis=0).reshape(2, -1)
     return (
         out,
-        d_tokens.astype(jnp.float32),
+        d_tokens.astype(wider),
         gains[0],
-        grad_qkv[:, :wide],
-        grad_kv,
-        grad_out,
+        grad_query.astype(wider),
+        grad_kv.astype(wider),
+        grad_out.astype(wider),
         gains[1],
-        grad_gate,
-        grad_up,
-        grad_down,
+        grad_gate.astype(wider),
+        grad_up.astype(wider),
+        grad_down.astype(wider),
     )
 
 

time: 676 us -> 675 us (level)
  the two profiles are of different devices: /device:TPU:0 before, /device:TPU:9 now
where the time goes in v7:
time: 675 us
  Pallas kernels  648 us (96%)
  other arithmetic  22.5 us (3%)
    pallas_call x7, Pallas kernels, kernel_call(): pl.pallas_call(kernel, out_shape=out_shape, in_specs=specs, out_specs=out...  648 us

profile of v7, /device:TPU:9, one launch (start us, length us, event | category | flops | bytes accessed | tf_op | source)
XLA Modules:
  0.0 674.8 jit_solution(14598246323494065734)
XLA Ops:
  0.6 0.7 convert_bitcast_fusion
  1.3 0.6 pad.4.segs
  1.9 1.3 broadcast_in_dim.14
  3.2 1.3 broadcast_in_dim.15
  4.4 58.0 %open_1.1 = (f32[256,1536]{1,0:T(8,128)}, bf16[2048,512]{1,0:T(8,128)(2,1)}, bf16[512,2048]{1,0:T(8,128)(2,1)}, bf16[512,1536]{1,0:T(8,128)(2,1)}, f32[256,128]{...) custom-call(bf16[256,4096]{1,0:T(8,128)(2,1)} %tokens.1, f32[1,512]{1,0:T(1,128)} %bitcast.8, ...), custom_call_target="tpu_custom_call" | custom-call | tf_op jit(solution)/shard_map/open_1/pallas_call | solution.py:391
  62.5 60.1 %attend_2.1 = (bf16[2048,512]{1,0:T(8,128)(2,1)}, bf16[2048,1024]{1,0:T(8,128)(2,1)}, bf16[2048,512]{1,0:T(8,128)(2,1)}, bf16[2,256,512]{2,1,0:T(8,128)(2,1)}, f...) custom-call(f32[256,1536]{1,0:T(8,128)} %get-tuple-element.45.qkv, ...), custom_call_target="tpu_custom_call" | custom-call | tf_op jit(solution)/shard_map/attend_2/pallas_call | solution.py:391
  122.6 66.2 %scatter_product_3.1 = (f32[256,3072]{1,0:T(8,128)}, bf16[2048,512]{1,0:T(8,128)(2,1)}) custom-call(bf16[2048,512]{1,0:T(8,128)(2,1)} %get-tuple-element.50.act.cot, bf16[3072,512]{1,0:T(8,128)(2,1)} %weight.3, bf16[2048,512]{1,0:T(8,128)(2,1)} %get-tuple-element.52.line_own), custom_call_target="tpu_custom_call" | custom-call | tf_op jit(solution)/shard_map/scatter_product_3/pallas_call | solution.py:391
  188.8 119.1 %ffn_4.1 = (bf16[256,3072]{1,0:T(8,128)(2,1)}, bf16[256,3072]{1,0:T(8,128)(2,1)}, bf16[256,3072]{1,0:T(8,128)(2,1)}, bf16[512,2048]{1,0:T(8,128)(2,1)}, f32[8,128]{1,0:T(8,128)}) custom-call(bf16[2048,512]{1,0:T(8,128)(2,1)} %get-tuple-element.51.x_low, bf16[2048,512]{1,0:T(8,128)(2,1)} %get-tuple-element.53.attn, f32[1,512]{1,0:T(1,128)} %bitcast.10, ...), custom_call_target="tpu_custom_call" | custom-call | tf_op jit(solution)/shard_map/ffn_4/pallas_call | solution.py:391
  307.9 116.9 %back_5.1 = (bf16[2048,512]{1,0:T(8,128)(2,1)}, f32[1,512]{1,0:T(1,128)}, bf16[512,3072]{1,0:T(8,128)(2,1)}, bf16[512,3072]{1,0:T(8,128)(2,1)}) custom-call(bf16[512,2048]{1,0:T(8,128)(2,1)} %get-tuple-element.56.act_t, bf16[512,3072]{1,0:T(8,128)(2,1)} %w_gate.3, bf16[512,3072]{1,0:T(8,128)(2,1)} %w_up.3, bf16[256,3072]{1,0:T(8,128)(2,1)} %get-tuple-element.57.d_gate, ...), custom_call_target="tpu_custom_call" | custom-call | tf_op jit(solution)/shard_map/back_5/pallas_call | solution.py:391
  424.8 69.8 %down_6.1 = (bf16[2048,512]{1,0:T(8,128)(2,1)}, bf16[2048,512]{1,0:T(8,128)(2,1)}, bf16[3072,512]{1,0:T(8,128)(2,1)}) custom-call(bf16[2048,512]{1,0:T(8,128)(2,1)} %get-tuple-element.50.act.cot, bf16[3072,512]{1,0:T(8,128)(2,1)} %weight.3, bf16[256,3072]{1,0:T(8,128)(2,1)} %get-tuple-element.55.hidden, bf16[2048,512]{1,0:T(8,128)(2,1)} %get-tuple-element.60.line_own), custom_call_target="tpu_custom_call" | custom-call | tf_op jit(solution)/shard_map/down_6/pallas_call | solution.py:391
  494.6 157.7 %tail_7.1 = (bf16[256,4096]{1,0:T(8,128)(2,1)}, bf16[256,4096]{1,0:T(8,128)(2,1)}, bf16[512,1024]{1,0:T(8,128)(2,1)}, bf16[1024,512]{1,0:T(8,128)(2,1)}, bf16[512,512]{1,0:T(8,128)(2,1)}, /*index=5*/f32[4,8,128]{2,1,0:T(8,128)}) custom-call(bf16[2048,512]{1,0:T(8,128)(2,1)} %get-tuple-element.61.d_attn, bf16[1024,512]{1,0:T(8,128)(2,1)} %w_out.3, ...), custom_call_target="tpu_custom_call" | custom-call | tf_op jit(solution)/shard_map/tail_7/pallas_call | solution.py:391
  652.3 0.0 copy-start.6
  652.3 0.8 reduce_sum.9
  653.2 0.6 slice_bitcast_fusion
  653.7 0.0 copy-start.5
  653.7 2.2 convert_element_type.31
  656.0 0.0 copy-done.6
  656.0 1.6 convert_element_type.30
  657.5 0.0 copy-done.5
  657.6 0.0 copy-start.3
  657.6 1.6 convert_element_type.32
  659.2 0.7 copy-done.3
  659.9 0.0 copy-start.2
  659.9 2.5 convert_element_type.29
  662.4 0.5 copy-done.2
  662.9 0.0 copy-start.1
  662.9 3.6 convert_element_type.35
  666.5 0.0 copy-done.1
  666.5 0.0 copy-start
  666.5 3.5 convert_element_type.33
  670.0 0.0 copy-done
  670.0 0.0 copy-start.4
  670.0 3.5 convert_element_type.34
  673.5 0.0 copy-done.4
  673.5 1.3 copy.22
Async XLA Ops:
  652.3 3.6 copy-start.6
  653.7 3.8 copy-start.5
  657.6 2.3 copy-start.3
  659.9 3.0 copy-start.2
  662.9 3.6 copy-start.1
  666.5 3.5 copy-start
  670.0 3.5 copy-start.4

commit v8 on v7

--- a/solution.py
+++ b/solution.py
@@ -360,6 +360,9 @@
 
             lax.fori_loop(0, self.counts, take, 0)
 
+        self.drain()
+
+    def drain(self):
         @pl.when(self.inner == 1)
         def _():
             def drain(at, _):
@@ -1444,6 +1447,47 @@
             span = slice(at_col * 512, (at_col + 1) * 512)
             grad[:, span] += dot_nn(rows_t, block[:, span])
 
+    me = here.shard(0, 0)
+    columns = pl.ds(pl.multiple_of(me * cols, cols), cols)
+    chunk = line.chunk
+
+    def landing(which, at):
+        sub = at % per if which == 0 else near(at)[2]
+        return (out, d_tok)[which].at[pl.ds(pl.multiple_of(sub * chunk, chunk), chunk), columns]
+
+    def put(which, at):
+        kind = (line, line_tok)[which]
+        goal = here.device(*(far(at) if which == 0 else near(at)[:2]))
+        return remote(kind.from_end.at[at], landing(which, at), put_sems.at[which, 0, at], put_sems.at[which, 1, at],
+                      goal)
+
+    def keep(which, at):
+        spot = at % per if which == 0 else near(at)[2]
+        return pltpu.make_async_copy((line, line_tok)[which].from_end.at[at], landing(which, at),
+                                     local_sems.at[which, spot])
+
+    def emit(which, at):
+        kind = (line, line_tok)[which]
+        row = kind.rows(at)
+        base = (attn, d_attn)[which][row, :].astype(jnp.float32)
+        if which == 0:
+            base = base + x_low[row, :].astype(jnp.float32)
+        kind.from_end[at] = (base + kind.out[row, :].astype(jnp.float32)).astype(out.dtype)
+
+    def is_own(which, at):
+        return at >= 7 * per if which == 0 else jnp.logical_and(at < 4, at % 2 == 0)
+
+    def send(which, at):
+        own = is_own(which, at)
+
+        @pl.when(own)
+        def _():
+            keep(which, at).start()
+
+        @pl.when(jnp.logical_not(own))
+        def _():
+            put(which, at).start()
+
     def stage_step(step, _):
         stage = step // 4
 
@@ -1471,6 +1515,25 @@
         @pl.when(step >= 4)
         def _():
             line_tok.step(step - 4)
+
+        @pl.when(step > 0)
+        def _():
+            send(0, step - 1)
+
+        @pl.when(line.inner == 0)
+        def _():
+            line.up(step).wait_send()
+            line.down(step).wait_recv()
+
+        emit(0, step)
+
+        @pl.when(jnp.logical_and(line.inner == 1, step > 7))
+        def _():
+            send(1, step - 8)
+
+        @pl.when(jnp.logical_and(line.inner == 1, step > 6))
+        def _():
+            emit(1, step - 7)
         return 0
 
     lax.fori_loop(0, line_counts, stage_step, 0)
@@ -1489,48 +1552,8 @@
         return remote(tile, gain_tiles.at[here.z], tile_send.at[step], tile_recv.at[step],
                       (here.dp, here.seq, (here.z + step + 1) % 4))
 
-    line.settle()
-    me = here.shard(0, 0)
-    columns = pl.ds(pl.multiple_of(me * cols, cols), cols)
-    chunk = line.chunk
-
-    def landing(which, at):
-        sub = at % per if which == 0 else near(at)[2]
-        return (out, d_tok)[which].at[pl.ds(pl.multiple_of(sub * chunk, chunk), chunk), columns]
-
-    def put(which, at):
-        kind = (line, line_tok)[which]
-        goal = here.device(*(far(at) if which == 0 else near(at)[:2]))
-        return remote(kind.from_end.at[at], landing(which, at), put_sems.at[which, 0, at], put_sems.at[which, 1, at],
-                      goal)
-
-    def keep(which, at):
-        spot = at % per if which == 0 else near(at)[2]
-        return pltpu.make_async_copy((line, line_tok)[which].from_end.at[at], landing(which, at),
-                                     local_sems.at[which, spot])
-
-    def emit(which, at):
-        kind = (line, line_tok)[which]
-        row = kind.rows(at)
-        base = (attn, d_attn)[which][row, :].astype(jnp.float32)
-        if which == 0:
-            base = base + x_low[row, :].astype(jnp.float32)
-        kind.from_end[at] = (base + kind.out[row, :].astype(jnp.float32)).astype(out.dtype)
-
-    def is_own(which, at):
-        return at >= 7 * per if which == 0 else jnp.logical_and(at < 4, at % 2 == 0)
-
-    def send(which, at):
-        own = is_own(which, at)
-
-        @pl.when(own)
-        def _():
-            keep(which, at).start()
-
-        @pl.when(jnp.logical_not(own))
-        def _():
-            put(which, at).start()
-
+    send(0, line_counts - 1)
+    line.drain()
     for step in range(3):
         tile_copy(step).start()
     gain_tiles[here.z] = tile[...]
@@ -1541,19 +1564,14 @@
 
         def both(at, _):
             line_tok.step(at)
-            spot = at - start
-
-            @pl.when(jnp.logical_and(spot > 0, spot <= line_counts // 2))
+
+            @pl.when(at < line_counts + 4)
             def _():
-                for which in range(2):
-                    for last in range(2):
-                        send(which, 2 * spot - 2 + last)
-
-            @pl.when(spot < line_counts // 2)
+                send(1, at - 4)
+
+            @pl.when(at < line_counts + 3)
             def _():
-                for which in range(2):
-                    for last in range(2):
-                        emit(which, 2 * spot + last)
+                emit(1, at - 3)
             return 0
 
         lax.fori_loop(start, line_counts + extra + 2, both, 0)
@@ -1572,12 +1590,10 @@
 
             @pl.when(jnp.logical_and(at > 0, at <= line_counts))
             def _():
-                send(0, at - 1)
                 send(1, at - 1)
 
             @pl.when(at < line_counts)
             def _():
-                emit(0, at)
                 emit(1, at)
             return 0
 

time: 675 us -> 660 us (0.978)
  the two profiles are of different devices: /device:TPU:9 before, /device:TPU:0 now
where the time goes in v8:
time: 660 us
  Pallas kernels  633 us (96%)
  other arithmetic  22.5 us (3%)
    pallas_call x7, Pallas kernels, kernel_call(): pl.pallas_call(kernel, out_shape=out_shape, in_specs=specs, out_specs=out...  633 us

profile of v8, /device:TPU:0, one launch (start us, length us, event | category | flops | bytes accessed | tf_op | source)
XLA Modules:
  0.0 659.9 jit_solution(7353712586177697481)
XLA Ops:
  0.6 0.7 convert_bitcast_fusion
  1.3 0.6 pad.4.segs
  1.9 1.3 broadcast_in_dim.14
  3.2 1.3 broadcast_in_dim.15
  4.4 59.3 %open_1.1 = (f32[256,1536]{1,0:T(8,128)}, bf16[2048,512]{1,0:T(8,128)(2,1)}, bf16[512,2048]{1,0:T(8,128)(2,1)}, bf16[512,1536]{1,0:T(8,128)(2,1)}, f32[256,128]{...) custom-call(bf16[256,4096]{1,0:T(8,128)(2,1)} %tokens.1, f32[1,512]{1,0:T(1,128)} %bitcast.8, ...), custom_call_target="tpu_custom_call" | custom-call | tf_op jit(solution)/shard_map/open_1/pallas_call | solution.py:394
  63.7 59.5 %attend_2.1 = (bf16[2048,512]{1,0:T(8,128)(2,1)}, bf16[2048,1024]{1,0:T(8,128)(2,1)}, bf16[2048,512]{1,0:T(8,128)(2,1)}, bf16[2,256,512]{2,1,0:T(8,128)(2,1)}, f...) custom-call(f32[256,1536]{1,0:T(8,128)} %get-tuple-element.45.qkv, ...), custom_call_target="tpu_custom_call" | custom-call | tf_op jit(solution)/shard_map/attend_2/pallas_call | solution.py:394
  123.3 68.9 %scatter_product_3.1 = (f32[256,3072]{1,0:T(8,128)}, bf16[2048,512]{1,0:T(8,128)(2,1)}) custom-call(bf16[2048,512]{1,0:T(8,128)(2,1)} %get-tuple-element.50.act.cot, bf16[3072,512]{1,0:T(8,128)(2,1)} %weight.3, bf16[2048,512]{1,0:T(8,128)(2,1)} %get-tuple-element.52.line_own), custom_call_target="tpu_custom_call" | custom-call | tf_op jit(solution)/shard_map/scatter_product_3/pallas_call | solution.py:394
  192.2 117.8 %ffn_4.1 = (bf16[256,3072]{1,0:T(8,128)(2,1)}, bf16[256,3072]{1,0:T(8,128)(2,1)}, bf16[256,3072]{1,0:T(8,128)(2,1)}, bf16[512,2048]{1,0:T(8,128)(2,1)}, f32[8,128]{1,0:T(8,128)}) custom-call(bf16[2048,512]{1,0:T(8,128)(2,1)} %get-tuple-element.51.x_low, bf16[2048,512]{1,0:T(8,128)(2,1)} %get-tuple-element.53.attn, f32[1,512]{1,0:T(1,128)} %bitcast.10, ...), custom_call_target="tpu_custom_call" | custom-call | tf_op jit(solution)/shard_map/ffn_4/pallas_call | solution.py:394
  310.0 116.7 %back_5.1 = (bf16[2048,512]{1,0:T(8,128)(2,1)}, f32[1,512]{1,0:T(1,128)}, bf16[512,3072]{1,0:T(8,128)(2,1)}, bf16[512,3072]{1,0:T(8,128)(2,1)}) custom-call(bf16[512,2048]{1,0:T(8,128)(2,1)} %get-tuple-element.56.act_t, bf16[512,3072]{1,0:T(8,128)(2,1)} %w_gate.3, bf16[512,3072]{1,0:T(8,128)(2,1)} %w_up.3, bf16[256,3072]{1,0:T(8,128)(2,1)} %get-tuple-element.57.d_gate, ...), custom_call_target="tpu_custom_call" | custom-call | tf_op jit(solution)/shard_map/back_5/pallas_call | solution.py:394
  426.7 67.4 %down_6.1 = (bf16[2048,512]{1,0:T(8,128)(2,1)}, bf16[2048,512]{1,0:T(8,128)(2,1)}, bf16[3072,512]{1,0:T(8,128)(2,1)}) custom-call(bf16[2048,512]{1,0:T(8,128)(2,1)} %get-tuple-element.50.act.cot, bf16[3072,512]{1,0:T(8,128)(2,1)} %weight.3, bf16[256,3072]{1,0:T(8,128)(2,1)} %get-tuple-element.55.hidden, bf16[2048,512]{1,0:T(8,128)(2,1)} %get-tuple-element.60.line_own), custom_call_target="tpu_custom_call" | custom-call | tf_op jit(solution)/shard_map/down_6/pallas_call | solution.py:394
  494.1 143.2 %tail_7.1 = (bf16[256,4096]{1,0:T(8,128)(2,1)}, bf16[256,4096]{1,0:T(8,128)(2,1)}, bf16[512,1024]{1,0:T(8,128)(2,1)}, bf16[1024,512]{1,0:T(8,128)(2,1)}, bf16[512,512]{1,0:T(8,128)(2,1)}, /*index=5*/f32[4,8,128]{2,1,0:T(8,128)}) custom-call(bf16[2048,512]{1,0:T(8,128)(2,1)} %get-tuple-element.61.d_attn, bf16[1024,512]{1,0:T(8,128)(2,1)} %w_out.3, ...), custom_call_target="tpu_custom_call" | custom-call | tf_op jit(solution)/shard_map/tail_7/pallas_call | solution.py:394
  637.4 0.0 copy-start.6
  637.4 0.8 reduce_sum.9
  638.2 0.6 slice_bitcast_fusion
  638.8 0.0 copy-start.5
  638.8 2.2 convert_element_type.31
  641.0 0.0 copy-done.6
  641.0 1.6 convert_element_type.30
  642.6 0.0 copy-done.5
  642.6 0.0 copy-start.3
  642.6 1.6 convert_element_type.32
  644.2 0.7 copy-done.3
  644.9 0.0 copy-start.2
  644.9 2.5 convert_element_type.29
  647.4 0.5 copy-done.2
  647.9 0.0 copy-start.1
  647.9 3.6 convert_element_type.35
  651.5 0.0 copy-done.1
  651.5 0.0 copy-start
  651.5 3.5 convert_element_type.33
  655.0 0.0 copy-done
  655.0 0.0 copy-start.4
  655.0 3.5 convert_element_type.34
  658.5 0.0 copy-done.4
  658.5 1.3 copy.22
Async XLA Ops:
  637.4 3.6 copy-start.6
  638.8 3.8 copy-start.5
  642.6 2.3 copy-start.3
  644.9 3.0 copy-start.2
  647.9 3.6 copy-start.1
  651.5 3.5 copy-start
  655.0 3.5 copy-start.4

commit v9 on v8

--- a/solution.py
+++ b/solution.py
@@ -282,7 +282,7 @@
         self.own, self.out, self.from_end, self.from_mid = refs[:4]
         self.sems = refs[4:10]
         self.counts = counts
-        self.chunk = self.own.shape[0] // counts
+        self.chunk = self.from_end.shape[1]
         self.place = place
         z = here.z
         self.inner = ((z + 1) // 2) % 2
@@ -958,11 +958,33 @@
     return copies
 
 
-def back_kernel(rows, width, counts, act_t, w_gate, w_up, d_gate, d_up, dots, x_low, attn, gain, contrib, gain_grad,
+def chip_place(here, per):
+    def place(at):
+        return here.shard(at // (2 * per), at // per % 2) * per + at % per
+
+    return place
+
+
+def chip_steps(line, counts):
+    def hook(step):
+        @pl.when(jnp.logical_and(step >= counts, step < 2 * counts))
+        def _():
+            line.step(step - counts, 0, 4)
+
+        @pl.when(step >= 3 * counts)
+        def _():
+            line.step(step - 3 * counts, 4, 8)
+
+    return hook
+
+
+def back_kernel(rows, width, counts, act_t, w_gate, w_up, d_gate, d_up, dots, x_low, attn, gain, d_norm, gain_grad,
                 grad_gate, grad_up, *refs):
     here = Place()
     spread = Spread(here, counts, refs[:7])
     tiny_all, tiny_send, tiny_recv, own_sems, weight, sums, grads, staged, local_sems, out_sems = refs[7:17]
+    contrib, rest, rest_sems = refs[17:20]
+    line = Line(here, 12, [contrib, d_norm] + list(refs[20:]), chip_place(here, 2))
     tiny = Tiny(here, dots, tiny_all, (tiny_send, tiny_recv), False)
     half_cols = counts * width
     local = [
@@ -972,11 +994,11 @@
     own = load_own(spread, (d_gate, d_up), width, counts, own_sems)
     for copy in own + local:
         copy.start()
-    greet(here, tiny.peers)
+    greet(here, tiny.peers, True)
     for copy in own:
         copy.wait()
+    tiny.begin()
     spread.begin()
-    tiny.begin()
     sums[...] = jnp.zeros_like(sums)
     for copy in local:
         copy.wait()
@@ -1002,38 +1024,61 @@
 
     def leave(half, at):
         spot = pl.ds(pl.multiple_of(at * width, width), width)
-        return pltpu.make_async_copy(staged.at[at % 2, half], (grad_gate, grad_up)[half].at[:, spot],
+        return pltpu.make_async_copy(staged.at[half], (grad_gate, grad_up)[half].at[:, spot],
                                      out_sems.at[half, at])
 
+    eye = diagonal()
+    gain_grad[...] = jnp.zeros_like(gain_grad)
+
+    def close_chip(chip, target):
+        def close_shard(other, _):
+            shard = here.shard(chip, other)
+            span = pl.ds(pl.multiple_of(shard * rows, rows), rows)
+            loads = [pltpu.make_async_copy(src.at[span, :], rest.at[at], rest_sems.at[at])
+                     for at, src in enumerate((x_low, attn))]
+            for copy in loads:
+                copy.start()
+            for copy in loads:
+                copy.wait()
+            for at in range(rows // LANES):
+                span = pl.ds(pl.multiple_of(shard * rows + at * LANES, LANES), LANES)
+                piece = slice(at * LANES, (at + 1) * LANES)
+                dot = from_tile(tiny_all[shard, at : at + 1, :], eye)
+                resid = rest[0, piece, :].astype(jnp.float32) + rest[1, piece, :].astype(jnp.float32)
+                value = sums[span, :]
+                target[span, :] = (value * gain[...] - resid * dot).astype(target.dtype)
+                gain_grad[...] += jnp.sum(value * resid, axis=0, keepdims=True)
+            return 0
+
+        lax.fori_loop(0, 2, close_shard, 0)
+
     def done(stage, at):
-        @pl.when(jnp.logical_and(stage == 3, at > 1))
-        def _():
-            leave(0, at - 2).wait()
-            leave(1, at - 2).wait()
+        @pl.when(jnp.logical_and(stage == 3, at > 0))
+        def _():
+            leave(0, at - 1).wait()
+            leave(1, at - 1).wait()
 
         @pl.when(stage == 3)
         def _():
             for half in range(2):
-                staged[at % 2, half] = grads[:, columns(half, at)].astype(staged.dtype)
+                staged[half] = grads[:, columns(half, at)].astype(staged.dtype)
             leave(0, at).start()
             leave(1, at).start()
 
-    spread.run(blocks, done=done)
+        @pl.when(jnp.logical_and(at == counts - 1, stage % 2 == 0))
+        def _():
+            def close(chip, _):
+                close_chip(chip, contrib)
+                line.launch(4 * chip, 4)
+                return 0
+
+            lax.fori_loop(stage // 2, stage // 2 * 2 + 1, close, 0)
+
     tiny.end()
-    eye = diagonal()
-    gain_grad[...] = jnp.zeros_like(gain_grad)
-
-    def close_shard(shard, _):
-        for at in range(rows // LANES):
-            span = pl.ds(pl.multiple_of(shard * rows + at * LANES, LANES), LANES)
-            dot = from_tile(tiny_all[shard, at : at + 1, :], eye)
-            resid = x_low[span, :].astype(jnp.float32) + attn[span, :].astype(jnp.float32)
-            value = sums[span, :]
-            contrib[span, :] = (value * gain[...] - resid * dot).astype(contrib.dtype)
-            gain_grad[...] += jnp.sum(value * resid, axis=0, keepdims=True)
-        return 0
-
-    lax.fori_loop(0, 8, close_shard, 0)
+    spread.run(blocks, chip_steps(line, counts), done)
+    close_chip(3, d_norm)
+    line.steps(counts + 1, 10, 4, 8)
+    line.settle()
     spread.end()
 
     def drain(at, _):
@@ -1041,7 +1086,7 @@
         leave(1, at).wait()
         return 0
 
-    lax.fori_loop(counts - 2, counts, drain, 0)
+    lax.fori_loop(counts - 1, counts, drain, 0)
 
 
 def back_gather(act_t, w_gate, w_up, d_gate, d_up, dots, x_low, attn, gain, cid, width=512):
@@ -1063,25 +1108,30 @@
         pltpu.VMEM((cols, 2 * half), low),
         pltpu.VMEM((total, cols), f32),
         pltpu.VMEM((cols, 2 * half), f32),
-        pltpu.VMEM((2, 2, cols, width), low),
+        pltpu.VMEM((2, cols, width), low),
         dma((2,)), dma((2, counts)),
-    ]
+        pltpu.VMEM((total, cols), low),
+        pltpu.VMEM((2, rows, cols), low),
+        dma((2,)),
+    ] + line_scratch(12, (12 * rows // 2, cols), low)
     operands = [act_t, w_gate, w_up, d_gate, d_up, dots, x_low, attn, gain]
     kernel = functools.partial(back_kernel, rows, width, counts)
-    return kernel_call(kernel, out_shape, operands, [vm] + [hbm] * 4 + [vm] * 4, scratch, cid, "back",
+    return kernel_call(kernel, out_shape, operands, [vm] + [hbm] * 4 + [vm, hbm, hbm, vm], scratch, cid, "back",
                        [vm, vm, hbm, hbm])
 
 
-def down_kernel(rows, width, counts, line_counts, cot, weight, hidden, line_own, ffn, d_attn, grad, *refs):
+def down_kernel(rows, width, counts, cot, weight, hidden, d_norm, ffn, d_attn, grad, *refs):
     here = Place()
     spread = Spread(here, counts, refs[:7])
-    own_sems, sums, grads, staged, out_sems, line_out = refs[7:13]
-    line = Line(here, line_counts, [line_own, line_out] + list(refs[13:]))
+    own_sems, sums, grads, staged, out_sems, norm_out, part = refs[7:14]
+    place = chip_place(here, 2)
+    norm_line = Line(here, 4, [d_norm, norm_out] + list(refs[14:22]), lambda at: place(at + 12))
+    line = Line(here, 12, [part, ffn] + list(refs[22:]), place)
     own = load_own(spread, (hidden,), width, counts, own_sems)
     for copy in own:
         copy.start()
     greet(here, slice_peers(here), True)
-    line.begin()
+    norm_line.begin()
     for copy in own:
         copy.wait()
     spread.begin()
@@ -1117,17 +1167,54 @@
             leave(0, at).start()
             leave(1, at).start()
 
-    steps = spread.run(blocks, line.step, done)
-    line.end(steps)
-
-    def close_shard(shard, _):
-        span = pl.ds(pl.multiple_of(shard * rows, rows), rows)
-        ffn[span, :] = sums[span, :].astype(ffn.dtype)
-        d_attn[span, :] = (cot[span, :].astype(jnp.float32) + line_out[span, :].astype(jnp.float32)).astype(
-            d_attn.dtype)
+        @pl.when(jnp.logical_and(at == counts - 1, stage % 2 == 0))
+        def _():
+            def close(chip, _):
+                close_chip(chip, part)
+                line.launch(4 * chip, 4)
+                return 0
+
+            lax.fori_loop(stage // 2, stage // 2 * 2 + 1, close, 0)
+
+    def close_chip(chip, target):
+        def close_shard(other, _):
+            span = row_span(here, chip, other, rows)
+            target[span, :] = sums[span, :].astype(target.dtype)
+            return 0
+
+        lax.fori_loop(0, 2, close_shard, 0)
+
+    steps = chip_steps(line, counts)
+
+    def hook(step):
+        steps(step)
+
+        @pl.when(step < counts)
+        def _():
+            norm_line.step(step)
+
+    spread.run(blocks, hook, done)
+    close_chip(3, ffn)
+    line.steps(counts + 1, 10, 4, 8)
+    norm_line.settle()
+
+    def add_norm(at, _):
+        def add(source):
+            span = row_span(here, at // 2, at % 2, rows)
+            d_attn[span, :] = (cot[span, :].astype(jnp.float32) + source[span, :].astype(jnp.float32)).astype(
+                d_attn.dtype)
+
+        @pl.when(at < 6)
+        def _():
+            add(d_norm)
+
+        @pl.when(at >= 6)
+        def _():
+            add(norm_out)
         return 0
 
-    lax.fori_loop(0, 8, close_shard, 0)
+    lax.fori_loop(0, 8, add_norm, 0)
+    line.settle()
     spread.end()
 
     def drain(at, _):
@@ -1138,7 +1225,7 @@
     lax.fori_loop(counts - 2, counts, drain, 0)
 
 
-def down_gather(cot, weight, hidden, line, cid, width=256, line_counts=16):
+def down_gather(cot, weight, hidden, d_norm, cid, width=256):
     total, cols = cot.shape
     rows, every = hidden.shape
     counts = every // (2 * width)
@@ -1158,9 +1245,10 @@
         pltpu.VMEM((2, 2, width, cols), low),
         dma((2, counts)),
         pltpu.VMEM((total, cols), low),
-    ] + line_scratch(line_counts, line.shape, low)
-    kernel = functools.partial(down_kernel, rows, width, counts, line_counts)
-    return kernel_call(kernel, out_shape, [cot, weight, hidden, line], [vm, vm, hbm, vm], scratch, cid, "down",
+        pltpu.VMEM((total, cols), low),
+    ] + line_scratch(4, (4 * rows // 2, cols), low) + line_scratch(12, (12 * rows // 2, cols), low)
+    kernel = functools.partial(down_kernel, rows, width, counts)
+    return kernel_call(kernel, out_shape, [cot, weight, hidden, d_norm], [vm, vm, hbm, vm], scratch, cid, "down",
                        [vm, vm, hbm])
 
 
@@ -1316,8 +1404,9 @@
         across, other, half_at = near(at)
         return jnp.where(at < line_counts, here.shard(across, other) * per + half_at, at)
 
-    ffn_sum = take(1)[0]
-    line = Line(here, line_counts, [ffn, ffn_sum] + take(8), place_ffn)
+    ffn_sum, leaving = take(2)
+    by_chip = chip_place(here, per)
+    line = Line(here, 2 * per, [ffn, ffn_sum] + take(8), lambda at: by_chip(at + 6 * per))
     contrib, summed = take(2)
     line_tok = Line(here, line_counts + extra, [contrib, summed] + take(8), place_tok)
     tiny = Tiny(here, tiny_own, tiny_all, (tiny_send, tiny_recv), False)
@@ -1348,7 +1437,7 @@
 
             grad_mixed[...] += dot_tn(mixed_two[step % 2], d_attn[span, :])
 
-    done = total.run(beside)
+    line.end(total.run(beside))
     grad_out[...] = grad_mixed[...].astype(grad_out.dtype)
 
     def land(at, first, second):
@@ -1385,11 +1474,9 @@
             got[0, core, rows_at, 0, :, pl.ds(pl.multiple_of(head * HD, HD), half)] = first[piece, :]
             got[0, core, rows_at, 0, :, pl.ds(pl.multiple_of(head * HD + half, half), half)] = second[piece, :]
 
-        line.step(done + head)
         return dots
 
     dots = lax.fori_loop(0, heads, one_head, jnp.zeros((rows, 1), jnp.float32))
-    done += heads
     eye = diagonal()
     tiny_own[...] = jnp.zeros_like(tiny_own)
     for side in (1, 0):
@@ -1424,7 +1511,6 @@
     for stream in range(2):
         spread.sib_copy(0, stream, 0).start()
     gain_sum[...] = jnp.zeros_like(gain_sum)
-    line.steps(done, line_counts + 2)
     tiny.end()
 
     def block_of(at):
@@ -1455,24 +1541,37 @@
         sub = at % per if which == 0 else near(at)[2]
         return (out, d_tok)[which].at[pl.ds(pl.multiple_of(sub * chunk, chunk), chunk), columns]
 
+    def leaver(which, at):
+        return (leaving, line_tok.from_end)[which].at[at]
+
     def put(which, at):
-        kind = (line, line_tok)[which]
         goal = here.device(*(far(at) if which == 0 else near(at)[:2]))
-        return remote(kind.from_end.at[at], landing(which, at), put_sems.at[which, 0, at], put_sems.at[which, 1, at],
+        return remote(leaver(which, at), landing(which, at), put_sems.at[which, 0, at], put_sems.at[which, 1, at],
                       goal)
 
     def keep(which, at):
         spot = at % per if which == 0 else near(at)[2]
-        return pltpu.make_async_copy((line, line_tok)[which].from_end.at[at], landing(which, at),
-                                     local_sems.at[which, spot])
+        return pltpu.make_async_copy(leaver(which, at), landing(which, at), local_sems.at[which, spot])
 
     def emit(which, at):
-        kind = (line, line_tok)[which]
-        row = kind.rows(at)
-        base = (attn, d_attn)[which][row, :].astype(jnp.float32)
-        if which == 0:
-            base = base + x_low[row, :].astype(jnp.float32)
-        kind.from_end[at] = (base + kind.out[row, :].astype(jnp.float32)).astype(out.dtype)
+        if which == 1:
+            row = line_tok.rows(at)
+            value = d_attn[row, :].astype(jnp.float32) + summed[row, :].astype(jnp.float32)
+            line_tok.from_end[at] = value.astype(out.dtype)
+            return
+        row = pl.ds(pl.multiple_of(place_ffn(at) * chunk, chunk), chunk)
+
+        def leave(source):
+            value = x_low[row, :].astype(jnp.float32) + attn[row, :].astype(jnp.float32)
+            leaving[at] = (value + source[row, :].astype(jnp.float32)).astype(out.dtype)
+
+        @pl.when(at < 2 * per)
+        def _():
+            leave(ffn_sum)
+
+        @pl.when(at >= 2 * per)
+        def _():
+            leave(ffn)
 
     def is_own(which, at):
         return at >= 7 * per if which == 0 else jnp.logical_and(at < 4, at % 2 == 0)
@@ -1519,11 +1618,6 @@
         @pl.when(step > 0)
         def _():
             send(0, step - 1)
-
-        @pl.when(line.inner == 0)
-        def _():
-            line.up(step).wait_send()
-            line.down(step).wait_recv()
 
         emit(0, step)
 
@@ -1553,7 +1647,6 @@
                       (here.dp, here.seq, (here.z + step + 1) % 4))
 
     send(0, line_counts - 1)
-    line.drain()
     for step in range(3):
         tile_copy(step).start()
     gain_tiles[here.z] = tile[...]
@@ -1665,7 +1758,8 @@
         dma((3,)), dma((3,)), dma((2, 2, counts)), dma((2, per)),
         pltpu.VMEM((2, rows, wide), low), dma((2,)),
         pltpu.VMEM((total, cols), low),
-    ] + line_scratch(counts, (total, cols), low)
+        pltpu.VMEM((counts, chunk, cols), low),
+    ] + line_scratch(2 * per, (2 * per * chunk, cols), low)
     scratch += [pltpu.VMEM(long, low), pltpu.VMEM(long, low)] + line_scratch(counts + extra, long, low)
     operands = [d_attn, w_out, queries, kv, probs, rms, cos, sin, act_t, w_qkv, ffn, x_low, attn, gain,
                 gain_grad, mixed_all]
@@ -1695,10 +1789,10 @@
     )
     d_hidden, attn = scatter_product(g_low, w_down, 512, 3, attn_part)
     hidden, d_gate, d_up, act_two_t, dots = ffn_scatter(x_low, attn, gain_two, w_gate, w_up, d_hidden, 4)
-    contrib, grad_gain_two, grad_gate, grad_up = back_gather(
+    d_norm, grad_gain_two, grad_gate, grad_up = back_gather(
         act_two_t, w_gate, w_up, d_gate, d_up, dots, x_low, attn, gain_two, 5
     )
-    ffn, d_attn, grad_down = down_gather(g_low, w_down, hidden, contrib, 6)
+    ffn, d_attn, grad_down = down_gather(g_low, w_down, hidden, d_norm, 6)
     d_tokens, out, grad_query, grad_out, grad_kv, gain_tiles = tail(
         d_attn,
         w_out,

time: 660 us -> 679 us (1.029)
  Pallas kernels: 633 us -> 652 us
    pallas_call x7, Pallas kernels: 633 us -> 652 us  [kernel_call(): pl.pallas_call(kernel, out_shape=out_shape, in_specs=specs, out_specs=out...]
where the time goes in v9:
time: 679 us
  Pallas kernels  652 us (96%)
  other arithmetic  22.5 us (3%)
    pallas_call x7, Pallas kernels, kernel_call(): pl.pallas_call(kernel, out_shape=out_shape, in_specs=specs, out_specs=out...  652 us

profile of v9, /device:TPU:0, one launch (start us, length us, event | category | flops | bytes accessed | tf_op | source)
XLA Modules:
  0.0 678.6 jit_solution(4188425986602793379)
XLA Ops:
  0.6 0.7 convert_bitcast_fusion
  1.3 0.6 pad.4.segs
  1.9 1.3 broadcast_in_dim.14
  3.2 1.3 broadcast_in_dim.15
  4.4 59.3 %open_1.1 = (f32[256,1536]{1,0:T(8,128)}, bf16[2048,512]{1,0:T(8,128)(2,1)}, bf16[512,2048]{1,0:T(8,128)(2,1)}, bf16[512,1536]{1,0:T(8,128)(2,1)}, f32[256,128]{...) custom-call(bf16[256,4096]{1,0:T(8,128)(2,1)} %tokens.1, f32[1,512]{1,0:T(1,128)} %bitcast.8, ...), custom_call_target="tpu_custom_call" | custom-call | tf_op jit(solution)/shard_map/open_1/pallas_call | solution.py:394
  63.7 59.5 %attend_2.1 = (bf16[2048,512]{1,0:T(8,128)(2,1)}, bf16[2048,1024]{1,0:T(8,128)(2,1)}, bf16[2048,512]{1,0:T(8,128)(2,1)}, bf16[2,256,512]{2,1,0:T(8,128)(2,1)}, f...) custom-call(f32[256,1536]{1,0:T(8,128)} %get-tuple-element.45.qkv, ...), custom_call_target="tpu_custom_call" | custom-call | tf_op jit(solution)/shard_map/attend_2/pallas_call | solution.py:394
  123.3 68.9 %scatter_product_3.1 = (f32[256,3072]{1,0:T(8,128)}, bf16[2048,512]{1,0:T(8,128)(2,1)}) custom-call(bf16[2048,512]{1,0:T(8,128)(2,1)} %get-tuple-element.50.act.cot, bf16[3072,512]{1,0:T(8,128)(2,1)} %weight.3, bf16[2048,512]{1,0:T(8,128)(2,1)} %get-tuple-element.52.line_own), custom_call_target="tpu_custom_call" | custom-call | tf_op jit(solution)/shard_map/scatter_product_3/pallas_call | solution.py:394
  192.2 117.8 %ffn_4.1 = (bf16[256,3072]{1,0:T(8,128)(2,1)}, bf16[256,3072]{1,0:T(8,128)(2,1)}, bf16[256,3072]{1,0:T(8,128)(2,1)}, bf16[512,2048]{1,0:T(8,128)(2,1)}, f32[8,128]{1,0:T(8,128)}) custom-call(bf16[2048,512]{1,0:T(8,128)(2,1)} %get-tuple-element.51.x_low, bf16[2048,512]{1,0:T(8,128)(2,1)} %get-tuple-element.53.attn, f32[1,512]{1,0:T(1,128)} %bitcast.10, ...), custom_call_target="tpu_custom_call" | custom-call | tf_op jit(solution)/shard_map/ffn_4/pallas_call | solution.py:394
  310.0 128.5 %back_5.1 = (bf16[2048,512]{1,0:T(8,128)(2,1)}, f32[1,512]{1,0:T(1,128)}, bf16[512,3072]{1,0:T(8,128)(2,1)}, bf16[512,3072]{1,0:T(8,128)(2,1)}) custom-call(bf16[512,2048]{1,0:T(8,128)(2,1)} %get-tuple-element.56.act_t, bf16[512,3072]{1,0:T(8,128)(2,1)} %w_gate.3, bf16[512,3072]{1,0:T(8,128)(2,1)} %w_up.3, bf16[256,3072]{1,0:T(8,128)(2,1)} %get-tuple-element.57.d_gate, ...), custom_call_target="tpu_custom_call" | custom-call | tf_op jit(solution)/shard_map/back_5/pallas_call | solution.py:394
  438.5 83.3 %down_6.1 = (bf16[2048,512]{1,0:T(8,128)(2,1)}, bf16[2048,512]{1,0:T(8,128)(2,1)}, bf16[3072,512]{1,0:T(8,128)(2,1)}) custom-call(bf16[2048,512]{1,0:T(8,128)(2,1)} %get-tuple-element.50.act.cot, bf16[3072,512]{1,0:T(8,128)(2,1)} %weight.3, bf16[256,3072]{1,0:T(8,128)(2,1)} %get-tuple-element.55.hidden, bf16[2048,512]{1,0:T(8,128)(2,1)} %get-tuple-element.60.d_norm), custom_call_target="tpu_custom_call" | custom-call | tf_op jit(solution)/shard_map/down_6/pallas_call | solution.py:394
  521.9 134.2 %tail_7.1 = (bf16[256,4096]{1,0:T(8,128)(2,1)}, bf16[256,4096]{1,0:T(8,128)(2,1)}, bf16[512,1024]{1,0:T(8,128)(2,1)}, bf16[1024,512]{1,0:T(8,128)(2,1)}, bf16[512,512]{1,0:T(8,128)(2,1)}, /*index=5*/f32[4,8,128]{2,1,0:T(8,128)}) custom-call(bf16[2048,512]{1,0:T(8,128)(2,1)} %get-tuple-element.61.d_attn, bf16[1024,512]{1,0:T(8,128)(2,1)} %w_out.3, ...), custom_call_target="tpu_custom_call" | custom-call | tf_op jit(solution)/shard_map/tail_7/pallas_call | solution.py:394
  656.1 0.0 copy-start.6
  656.1 0.8 reduce_sum.9
  656.9 0.6 slice_bitcast_fusion
  657.5 0.0 copy-start.5
  657.5 2.2 convert_element_type.31
  659.7 0.0 copy-done.6
  659.7 1.6 convert_element_type.30
  661.3 0.0 copy-done.5
  661.3 0.0 copy-start.3
  661.3 1.6 convert_element_type.32
  662.9 0.7 copy-done.3
  663.7 0.0 copy-start.2
  663.7 2.5 convert_element_type.29
  666.2 0.5 copy-done.2
  666.6 0.0 copy-start.1
  666.6 3.6 convert_element_type.35
  670.2 0.0 copy-done.1
  670.2 0.0 copy-start
  670.2 3.5 convert_element_type.33
  673.8 0.0 copy-done
  673.8 0.0 copy-start.4
  673.8 3.5 convert_element_type.34
  677.3 0.0 copy-done.4
  677.3 1.3 copy.22
Async XLA Ops:
  656.1 3.6 copy-start.6
  657.5 3.8 copy-start.5
  661.3 2.3 copy-start.3
  663.7 3.0 copy-start.2
  666.6 3.6 copy-start.1
  670.2 3.5 copy-start
  673.8 3.5 copy-start.4

commit v10 on v9

--- a/solution.py
+++ b/solution.py
@@ -965,26 +965,13 @@
     return place
 
 
-def chip_steps(line, counts):
-    def hook(step):
-        @pl.when(jnp.logical_and(step >= counts, step < 2 * counts))
-        def _():
-            line.step(step - counts, 0, 4)
-
-        @pl.when(step >= 3 * counts)
-        def _():
-            line.step(step - 3 * counts, 4, 8)
-
-    return hook
-
-
 def back_kernel(rows, width, counts, act_t, w_gate, w_up, d_gate, d_up, dots, x_low, attn, gain, d_norm, gain_grad,
                 grad_gate, grad_up, *refs):
     here = Place()
     spread = Spread(here, counts, refs[:7])
     tiny_all, tiny_send, tiny_recv, own_sems, weight, sums, grads, staged, local_sems, out_sems = refs[7:17]
     contrib, rest, rest_sems = refs[17:20]
-    line = Line(here, 12, [contrib, d_norm] + list(refs[20:]), chip_place(here, 2))
+    line = Line(here, 4, [contrib, d_norm] + list(refs[20:]), chip_place(here, 2))
     tiny = Tiny(here, dots, tiny_all, (tiny_send, tiny_recv), False)
     half_cols = counts * width
     local = [
@@ -1065,19 +1052,23 @@
             leave(0, at).start()
             leave(1, at).start()
 
-        @pl.when(jnp.logical_and(at == counts - 1, stage % 2 == 0))
-        def _():
-            def close(chip, _):
-                close_chip(chip, contrib)
-                line.launch(4 * chip, 4)
-                return 0
-
-            lax.fori_loop(stage // 2, stage // 2 * 2 + 1, close, 0)
+        @pl.when(jnp.logical_and(at == counts - 1, stage == 0))
+        def _():
+            close_chip(0, contrib)
+            line.launch(0, 4)
+
+        @pl.when(jnp.logical_and(at == counts - 1, stage == 2))
+        def _():
+            lax.fori_loop(1, 3, lambda chip, _: (close_chip(chip, d_norm), 0)[1], 0)
+
+    def hook(step):
+        @pl.when(jnp.logical_and(step >= counts, step < counts + 6))
+        def _():
+            line.step(step - counts)
 
     tiny.end()
-    spread.run(blocks, chip_steps(line, counts), done)
+    spread.run(blocks, hook, done)
     close_chip(3, d_norm)
-    line.steps(counts + 1, 10, 4, 8)
     line.settle()
     spread.end()
 
@@ -1113,7 +1104,7 @@
         pltpu.VMEM((total, cols), low),
         pltpu.VMEM((2, rows, cols), low),
         dma((2,)),
-    ] + line_scratch(12, (12 * rows // 2, cols), low)
+    ] + line_scratch(4, (4 * rows // 2, cols), low)
     operands = [act_t, w_gate, w_up, d_gate, d_up, dots, x_low, attn, gain]
     kernel = functools.partial(back_kernel, rows, width, counts)
     return kernel_call(kernel, out_shape, operands, [vm] + [hbm] * 4 + [vm, hbm, hbm, vm], scratch, cid, "back",
@@ -1125,8 +1116,8 @@
     spread = Spread(here, counts, refs[:7])
     own_sems, sums, grads, staged, out_sems, norm_out, part = refs[7:14]
     place = chip_place(here, 2)
-    norm_line = Line(here, 4, [d_norm, norm_out] + list(refs[14:22]), lambda at: place(at + 12))
-    line = Line(here, 12, [part, ffn] + list(refs[22:]), place)
+    norm_line = Line(here, 12, [d_norm, norm_out] + list(refs[14:22]), lambda at: place(at + 4))
+    line = Line(here, 4, [part, ffn] + list(refs[22:]), place)
     own = load_own(spread, (hidden,), width, counts, own_sems)
     for copy in own:
         copy.start()
@@ -1167,14 +1158,10 @@
             leave(0, at).start()
             leave(1, at).start()
 
-        @pl.when(jnp.logical_and(at == counts - 1, stage % 2 == 0))
-        def _():
-            def close(chip, _):
-                close_chip(chip, part)
-                line.launch(4 * chip, 4)
-                return 0
-
-            lax.fori_loop(stage // 2, stage // 2 * 2 + 1, close, 0)
+        @pl.when(jnp.logical_and(at == counts - 1, stage == 0))
+        def _():
+            close_chip(0, part)
+            line.launch(0, 4)
 
     def close_chip(chip, target):
         def close_shard(other, _):
@@ -1184,18 +1171,19 @@
 
         lax.fori_loop(0, 2, close_shard, 0)
 
-    steps = chip_steps(line, counts)
+    last_steps = 4 * counts - 5
 
     def hook(step):
-        steps(step)
-
-        @pl.when(step < counts)
-        def _():
-            norm_line.step(step)
+        @pl.when(jnp.logical_and(step % 3 < 2, step <= last_steps))
+        def _():
+            norm_line.step(step // 3 * 2 + step % 3)
+
+        @pl.when(step >= last_steps)
+        def _():
+            line.step(step - last_steps)
 
     spread.run(blocks, hook, done)
-    close_chip(3, ffn)
-    line.steps(counts + 1, 10, 4, 8)
+    lax.fori_loop(1, 4, lambda chip, _: (close_chip(chip, ffn), 0)[1], 0)
     norm_line.settle()
 
     def add_norm(at, _):
@@ -1204,11 +1192,11 @@
             d_attn[span, :] = (cot[span, :].astype(jnp.float32) + source[span, :].astype(jnp.float32)).astype(
                 d_attn.dtype)
 
-        @pl.when(at < 6)
+        @pl.when(at < 2)
         def _():
             add(d_norm)
 
-        @pl.when(at >= 6)
+        @pl.when(at >= 2)
         def _():
             add(norm_out)
         return 0
@@ -1246,7 +1234,8 @@
         dma((2, counts)),
         pltpu.VMEM((total, cols), low),
         pltpu.VMEM((total, cols), low),
-    ] + line_scratch(4, (4 * rows // 2, cols), low) + line_scratch(12, (12 * rows // 2, cols), low)
+    ] + line_scratch(12, (12 * rows // 2, cols), low) + line_scratch(
+        4, (4 * rows // 2, cols), low)
     kernel = functools.partial(down_kernel, rows, width, counts)
     return kernel_call(kernel, out_shape, [cot, weight, hidden, d_norm], [vm, vm, hbm, vm], scratch, cid, "down",
                        [vm, vm, hbm])
@@ -1406,7 +1395,7 @@
 
     ffn_sum, leaving = take(2)
     by_chip = chip_place(here, per)
-    line = Line(here, 2 * per, [ffn, ffn_sum] + take(8), lambda at: by_chip(at + 6 * per))
+    line = Line(here, 6 * per, [ffn, ffn_sum] + take(8), lambda at: by_chip(at + 2 * per))
     contrib, summed = take(2)
     line_tok = Line(here, line_counts + extra, [contrib, summed] + take(8), place_tok)
     tiny = Tiny(here, tiny_own, tiny_all, (tiny_send, tiny_recv), False)
@@ -1437,7 +1426,7 @@
 
             grad_mixed[...] += dot_tn(mixed_two[step % 2], d_attn[span, :])
 
-    line.end(total.run(beside))
+    done = total.run(beside)
     grad_out[...] = grad_mixed[...].astype(grad_out.dtype)
 
     def land(at, first, second):
@@ -1469,6 +1458,7 @@
         lead, trail = d_query[:, :half], d_query[:, half:]
         first = ((lead * cos[0] + trail * sin[0]) * rms[0]).astype(got.dtype)
         second = ((trail * cos[0] - lead * sin[0]) * rms[0]).astype(got.dtype)
+        line.step(done + head)
         for rows_at in range(2):
             piece = slice(rows_at * part, (rows_at + 1) * part)
             got[0, core, rows_at, 0, :, pl.ds(pl.multiple_of(head * HD, HD), half)] = first[piece, :]
@@ -1511,6 +1501,7 @@
     for stream in range(2):
         spread.sib_copy(0, stream, 0).start()
     gain_sum[...] = jnp.zeros_like(gain_sum)
+    line.end(done + heads)
     tiny.end()
 
     def block_of(at):
@@ -1565,11 +1556,11 @@
             value = x_low[row, :].astype(jnp.float32) + attn[row, :].astype(jnp.float32)
             leaving[at] = (value + source[row, :].astype(jnp.float32)).astype(out.dtype)
 
-        @pl.when(at < 2 * per)
+        @pl.when(at < 6 * per)
         def _():
             leave(ffn_sum)
 
-        @pl.when(at >= 2 * per)
+        @pl.when(at >= 6 * per)
         def _():
             leave(ffn)
 
@@ -1759,7 +1750,7 @@
         pltpu.VMEM((2, rows, wide), low), dma((2,)),
         pltpu.VMEM((total, cols), low),
         pltpu.VMEM((counts, chunk, cols), low),
-    ] + line_scratch(2 * per, (2 * per * chunk, cols), low)
+    ] + line_scratch(6 * per, (6 * per * chunk, cols), low)
     scratch += [pltpu.VMEM(long, low), pltpu.VMEM(long, low)] + line_scratch(counts + extra, long, low)
     operands = [d_attn, w_out, queries, kv, probs, rms, cos, sin, act_t, w_qkv, ffn, x_low, attn, gain,
                 gain_grad, mixed_all]

time: 679 us -> 665 us (0.979)
  Pallas kernels: 652 us -> 637 us
    pallas_call x7, Pallas kernels: 652 us -> 637 us  [kernel_call(): pl.pallas_call(kernel, out_shape=out_shape, in_specs=specs, out_specs=out...]
where the time goes in v10:
time: 665 us; the launch traced here: 664 us
  Pallas kernels  637 us (96%)
  other arithmetic  22.5 us (3%)
    pallas_call x7, Pallas kernels, kernel_call(): pl.pallas_call(kernel, out_shape=out_shape, in_specs=specs, out_specs=out...  637 us

profile of v10, /device:TPU:0, one launch (start us, length us, event | category | flops | bytes accessed | tf_op | source)
XLA Modules:
  0.0 664.1 jit_solution(16091271233780796432)
XLA Ops:
  0.6 0.7 convert_bitcast_fusion
  1.3 0.6 pad.4.segs
  1.9 1.3 broadcast_in_dim.14
  3.2 1.3 broadcast_in_dim.15
  4.4 59.3 %open_1.1 = (f32[256,1536]{1,0:T(8,128)}, bf16[2048,512]{1,0:T(8,128)(2,1)}, bf16[512,2048]{1,0:T(8,128)(2,1)}, bf16[512,1536]{1,0:T(8,128)(2,1)}, f32[256,128]{...) custom-call(bf16[256,4096]{1,0:T(8,128)(2,1)} %tokens.1, f32[1,512]{1,0:T(1,128)} %bitcast.8, ...), custom_call_target="tpu_custom_call" | custom-call | tf_op jit(solution)/shard_map/open_1/pallas_call | solution.py:394
  63.7 59.5 %attend_2.1 = (bf16[2048,512]{1,0:T(8,128)(2,1)}, bf16[2048,1024]{1,0:T(8,128)(2,1)}, bf16[2048,512]{1,0:T(8,128)(2,1)}, bf16[2,256,512]{2,1,0:T(8,128)(2,1)}, f...) custom-call(f32[256,1536]{1,0:T(8,128)} %get-tuple-element.45.qkv, ...), custom_call_target="tpu_custom_call" | custom-call | tf_op jit(solution)/shard_map/attend_2/pallas_call | solution.py:394
  123.3 68.9 %scatter_product_3.1 = (f32[256,3072]{1,0:T(8,128)}, bf16[2048,512]{1,0:T(8,128)(2,1)}) custom-call(bf16[2048,512]{1,0:T(8,128)(2,1)} %get-tuple-element.50.act.cot, bf16[3072,512]{1,0:T(8,128)(2,1)} %weight.3, bf16[2048,512]{1,0:T(8,128)(2,1)} %get-tuple-element.52.line_own), custom_call_target="tpu_custom_call" | custom-call | tf_op jit(solution)/shard_map/scatter_product_3/pallas_call | solution.py:394
  192.2 117.8 %ffn_4.1 = (bf16[256,3072]{1,0:T(8,128)(2,1)}, bf16[256,3072]{1,0:T(8,128)(2,1)}, bf16[256,3072]{1,0:T(8,128)(2,1)}, bf16[512,2048]{1,0:T(8,128)(2,1)}, f32[8,128]{1,0:T(8,128)}) custom-call(bf16[2048,512]{1,0:T(8,128)(2,1)} %get-tuple-element.51.x_low, bf16[2048,512]{1,0:T(8,128)(2,1)} %get-tuple-element.53.attn, f32[1,512]{1,0:T(1,128)} %bitcast.10, ...), custom_call_target="tpu_custom_call" | custom-call | tf_op jit(solution)/shard_map/ffn_4/pallas_call | solution.py:394
  310.0 117.0 %back_5.1 = (bf16[2048,512]{1,0:T(8,128)(2,1)}, f32[1,512]{1,0:T(1,128)}, bf16[512,3072]{1,0:T(8,128)(2,1)}, bf16[512,3072]{1,0:T(8,128)(2,1)}) custom-call(bf16[512,2048]{1,0:T(8,128)(2,1)} %get-tuple-element.56.act_t, bf16[512,3072]{1,0:T(8,128)(2,1)} %w_gate.3, bf16[512,3072]{1,0:T(8,128)(2,1)} %w_up.3, bf16[256,3072]{1,0:T(8,128)(2,1)} %get-tuple-element.57.d_gate, ...), custom_call_target="tpu_custom_call" | custom-call | tf_op jit(solution)/shard_map/back_5/pallas_call | solution.py:394
  427.1 70.8 %down_6.1 = (bf16[2048,512]{1,0:T(8,128)(2,1)}, bf16[2048,512]{1,0:T(8,128)(2,1)}, bf16[3072,512]{1,0:T(8,128)(2,1)}) custom-call(bf16[2048,512]{1,0:T(8,128)(2,1)} %get-tuple-element.50.act.cot, bf16[3072,512]{1,0:T(8,128)(2,1)} %weight.3, bf16[256,3072]{1,0:T(8,128)(2,1)} %get-tuple-element.55.hidden, bf16[2048,512]{1,0:T(8,128)(2,1)} %get-tuple-element.60.d_norm), custom_call_target="tpu_custom_call" | custom-call | tf_op jit(solution)/shard_map/down_6/pallas_call | solution.py:394
  497.8 143.7 %tail_7.1 = (bf16[256,4096]{1,0:T(8,128)(2,1)}, bf16[256,4096]{1,0:T(8,128)(2,1)}, bf16[512,1024]{1,0:T(8,128)(2,1)}, bf16[1024,512]{1,0:T(8,128)(2,1)}, bf16[512,512]{1,0:T(8,128)(2,1)}, /*index=5*/f32[4,8,128]{2,1,0:T(8,128)}) custom-call(bf16[2048,512]{1,0:T(8,128)(2,1)} %get-tuple-element.61.d_attn, bf16[1024,512]{1,0:T(8,128)(2,1)} %w_out.3, ...), custom_call_target="tpu_custom_call" | custom-call | tf_op jit(solution)/shard_map/tail_7/pallas_call | solution.py:394
  641.6 0.0 copy-start.6
  641.6 0.8 reduce_sum.9
  642.4 0.6 slice_bitcast_fusion
  643.0 0.0 copy-start.5
  643.0 2.2 convert_element_type.31
  645.2 0.0 copy-done.6
  645.2 1.6 convert_element_type.30
  646.8 0.0 copy-done.5
  646.8 0.0 copy-start.3
  646.8 1.6 convert_element_type.32
  648.4 0.7 copy-done.3
  649.2 0.0 copy-start.2
  649.2 2.5 convert_element_type.29
  651.7 0.5 copy-done.2
  652.1 0.0 copy-start.1
  652.1 3.6 convert_element_type.35
  655.7 0.0 copy-done.1
  655.7 0.0 copy-start
  655.7 3.5 convert_element_type.33
  659.2 0.0 copy-done
  659.2 0.0 copy-start.4
  659.3 3.5 convert_element_type.34
  662.8 0.0 copy-done.4
  662.8 1.3 copy.22
Async XLA Ops:
  641.6 3.6 copy-start.6
  643.0 3.8 copy-start.5
  646.8 2.3 copy-start.3
  649.2 3.0 copy-start.2
  652.1 3.6 copy-start.1
  655.7 3.5 copy-start
  659.2 3.5 copy-start.4

commit v11 on v10

--- a/solution.py
+++ b/solution.py
@@ -389,14 +389,32 @@
     return [here.device(*turned(at)) for at in range(7)]
 
 
-def kernel_call(kernel, out_shape, operands, specs, scratch, cid, name, out_specs=None):
+def kernel_call(kernel, out_shape, operands, specs, scratch, cid, name, out_specs=None, late=()):
     vm = pl.BlockSpec(memory_space=pltpu.VMEM)
+    specs = [pl.BlockSpec(memory_space=pl.ANY) if at in late else spec for at, spec in enumerate(specs)]
+    inside = [pltpu.VMEM(operands[at].shape, operands[at].dtype) for at in late]
+    if late:
+        inside.append(pltpu.SemaphoreType.DMA((len(late),)))
+
+    def body(*refs):
+        if not late:
+            kernel(*refs)
+            return
+        ins, rest, own = list(refs[: len(operands)]), refs[len(operands) : -len(inside)], refs[-len(inside) :]
+        copies = []
+        for spot, at in enumerate(late):
+            copy = pltpu.make_async_copy(ins[at], own[spot], own[-1].at[spot])
+            copy.start()
+            copies.append(copy)
+            ins[at] = own[spot]
+        kernel(*ins, *rest, late=copies)
+
     return pl.pallas_call(
-        kernel,
+        body,
         out_shape=out_shape,
         in_specs=specs,
         out_specs=out_specs or [vm] * len(out_shape),
-        scratch_shapes=scratch,
+        scratch_shapes=scratch + inside,
         compiler_params=pltpu.CompilerParams(
             collective_id=cid, has_side_effects=True, vmem_limit_bytes=VMEM_LIMIT
         ),
@@ -765,7 +783,7 @@
         def one(step, _):
             at = first + step
             span = row_span(here, *turned(at), rows)
-            value = (x_low[span, :].astype(jnp.float32) * gain[...]).astype(act.dtype)
+            value = (x_low[span, :].astype(jnp.float32) * gain[0:1, :]).astype(act.dtype)
             act[span, :] = value
             return 0
 
@@ -832,8 +850,11 @@
     total = Reduce(here, counts, product, refs[:11])
     greet(here, slice_peers(here), True)
     line.begin()
-    done = total.run(line.step)
-    line.end(done)
+    def beside(step):
+        line.step(2 * step)
+        line.step(2 * step + 1)
+
+    line.end(2 * total.run(beside))
 
     def emit(at, first, second):
         for half, value in enumerate((first, second)):
@@ -842,7 +863,7 @@
     total.end(emit)
 
 
-def scatter_product(act, weight, width, cid, line, line_counts=16):
+def scatter_product(act, weight, width, cid, line, line_counts=32):
     rows = act.shape[0] // 8
     every = weight.shape[0]
     counts = every // (2 * width)
@@ -857,7 +878,7 @@
 
 
 def ffn_kernel(rows, width, counts, x_low, attn, gain, w_gate, w_up, d_hidden, hidden, d_gate, d_up, act_t, tile_out,
-               *refs):
+               *refs, late):
     here = Place()
     cols = gain.shape[1]
     act, weight, tiny_own, tiny_all, tiny_send, tiny_recv, dots, local_sems = refs[:8]
@@ -876,7 +897,7 @@
         for at in range(rows // LANES):
             span = pl.ds(pl.multiple_of(shard * rows + at * LANES, LANES), LANES)
             resid = x_low[span, :].astype(jnp.float32) + attn[span, :].astype(jnp.float32)
-            act[span, :] = (resid * gain[...]).astype(act.dtype)
+            act[span, :] = (resid * gain[0:1, :]).astype(act.dtype)
             square = jnp.sum(resid * resid, axis=-1, keepdims=True)
             tiny_own[shard, at : at + 1, :] = jnp.sum(square * eye, axis=0, keepdims=True)
         return 0
@@ -901,6 +922,7 @@
     mean = [from_tile(jnp.sum(tiny_all[:, at, :], axis=0, keepdims=True), eye) for at in range(tiles)]
     scale = lax.rsqrt(jnp.concatenate(mean, axis=0) / (8 * cols) + EPS)
     dots[...] = jnp.zeros_like(dots)
+    late[0].wait()
     coeff = math.sqrt(2.0 / math.pi)
 
     def emit(at, first, second):
@@ -945,7 +967,7 @@
     ] + reduce_scratch(counts, rows, width)
     kernel = functools.partial(ffn_kernel, rows, width, counts)
     return kernel_call(kernel, out_shape, [x_low, attn, gain, w_gate, w_up, d_hidden], [vm, vm, vm, hbm, hbm, vm],
-                       scratch, cid, "ffn")
+                       scratch, cid, "ffn", late=(5,))
 
 
 def load_own(spread, payload, width, counts, sems):
@@ -966,7 +988,7 @@
 
 
 def back_kernel(rows, width, counts, act_t, w_gate, w_up, d_gate, d_up, dots, x_low, attn, gain, d_norm, gain_grad,
-                grad_gate, grad_up, *refs):
+                grad_gate, grad_up, *refs, late):
     here = Place()
     spread = Spread(here, counts, refs[:7])
     tiny_all, tiny_send, tiny_recv, own_sems, weight, sums, grads, staged, local_sems, out_sems = refs[7:17]
@@ -987,7 +1009,7 @@
     tiny.begin()
     spread.begin()
     sums[...] = jnp.zeros_like(sums)
-    for copy in local:
+    for copy in local + late:
         copy.wait()
 
     def columns(half, at):
@@ -1033,7 +1055,7 @@
                 dot = from_tile(tiny_all[shard, at : at + 1, :], eye)
                 resid = rest[0, piece, :].astype(jnp.float32) + rest[1, piece, :].astype(jnp.float32)
                 value = sums[span, :]
-                target[span, :] = (value * gain[...] - resid * dot).astype(target.dtype)
+                target[span, :] = (value * gain[0:1, :] - resid * dot).astype(target.dtype)
                 gain_grad[...] += jnp.sum(value * resid, axis=0, keepdims=True)
             return 0
 
@@ -1108,16 +1130,15 @@
     operands = [act_t, w_gate, w_up, d_gate, d_up, dots, x_low, attn, gain]
     kernel = functools.partial(back_kernel, rows, width, counts)
     return kernel_call(kernel, out_shape, operands, [vm] + [hbm] * 4 + [vm, hbm, hbm, vm], scratch, cid, "back",
-                       [vm, vm, hbm, hbm])
-
-
-def down_kernel(rows, width, counts, cot, weight, hidden, d_norm, ffn, d_attn, grad, *refs):
+                       [vm, vm, hbm, hbm], (0,))
+
+
+def down_kernel(rows, width, counts, cot, weight, hidden, d_norm, ffn, d_attn, grad, *refs, late):
     here = Place()
     spread = Spread(here, counts, refs[:7])
-    own_sems, sums, grads, staged, out_sems, norm_out, part = refs[7:14]
-    place = chip_place(here, 2)
-    norm_line = Line(here, 12, [d_norm, norm_out] + list(refs[14:22]), lambda at: place(at + 4))
-    line = Line(here, 4, [part, ffn] + list(refs[22:]), place)
+    own_sems, sums, grads, staged, out_sems, norm_out = refs[7:13]
+    place = chip_place(here, 4)
+    norm_line = Line(here, 24, [d_norm, norm_out] + list(refs[13:]), lambda at: place(at + 8))
     own = load_own(spread, (hidden,), width, counts, own_sems)
     for copy in own:
         copy.start()
@@ -1128,6 +1149,8 @@
     spread.begin()
     sums[...] = jnp.zeros_like(sums)
     grads[...] = jnp.zeros_like(grads)
+    for copy in late:
+        copy.wait()
 
     def columns(half, at):
         return pl.ds(pl.multiple_of((half * counts + at) * width, width), width)
@@ -1158,32 +1181,8 @@
             leave(0, at).start()
             leave(1, at).start()
 
-        @pl.when(jnp.logical_and(at == counts - 1, stage == 0))
-        def _():
-            close_chip(0, part)
-            line.launch(0, 4)
-
-    def close_chip(chip, target):
-        def close_shard(other, _):
-            span = row_span(here, chip, other, rows)
-            target[span, :] = sums[span, :].astype(target.dtype)
-            return 0
-
-        lax.fori_loop(0, 2, close_shard, 0)
-
-    last_steps = 4 * counts - 5
-
-    def hook(step):
-        @pl.when(jnp.logical_and(step % 3 < 2, step <= last_steps))
-        def _():
-            norm_line.step(step // 3 * 2 + step % 3)
-
-        @pl.when(step >= last_steps)
-        def _():
-            line.step(step - last_steps)
-
-    spread.run(blocks, hook, done)
-    lax.fori_loop(1, 4, lambda chip, _: (close_chip(chip, ffn), 0)[1], 0)
+    norm_line.steps(spread.run(blocks, norm_line.step, done), 26)
+    ffn[...] = sums[...].astype(ffn.dtype)
     norm_line.settle()
 
     def add_norm(at, _):
@@ -1202,7 +1201,6 @@
         return 0
 
     lax.fori_loop(0, 8, add_norm, 0)
-    line.settle()
     spread.end()
 
     def drain(at, _):
@@ -1233,16 +1231,14 @@
         pltpu.VMEM((2, 2, width, cols), low),
         dma((2, counts)),
         pltpu.VMEM((total, cols), low),
-        pltpu.VMEM((total, cols), low),
-    ] + line_scratch(12, (12 * rows // 2, cols), low) + line_scratch(
-        4, (4 * rows // 2, cols), low)
+    ] + line_scratch(24, (24 * rows // 4, cols), low)
     kernel = functools.partial(down_kernel, rows, width, counts)
     return kernel_call(kernel, out_shape, [cot, weight, hidden, d_norm], [vm, vm, hbm, vm], scratch, cid, "down",
-                       [vm, vm, hbm])
+                       [vm, vm, hbm], (0, 1))
 
 
 def attend_kernel(rows, heads, cols, qkv, rms, cos, sin, mask, w_out, cot, part, mixed_all, g_col, kv, probs, queries,
-                  pair_rms, *refs):
+                  pair_rms, *refs, late):
     here = Place()
     spread = Spread(here, heads // 2, refs[:7])
     sums, pair_sems, turn_send, turn_recv, local_sem, tiny_own, tiny_pair = refs[7:14]
@@ -1290,6 +1286,8 @@
         queries[:, head * HD : head * HD + half] = (lead * scale).astype(queries.dtype)
         queries[:, head * HD + half : (head + 1) * HD] = (trail * scale).astype(queries.dtype)
     pair.wait()
+    for copy in late:
+        copy.wait()
     for at in range(7):
         if at // 2 != 2:
             turn_copy(at).start()
@@ -1351,11 +1349,11 @@
         pltpu.VMEM((8, LANES), f32), pltpu.VMEM((8, LANES), f32)]
     kernel = functools.partial(attend_kernel, rows, heads, cols)
     return kernel_call(kernel, out_shape, [qkv, rms, cos, sin, mask, w_out, cot], [vm] * 7, scratch, cid,
-                       "attend")
+                       "attend", late=(4, 5))
 
 
 def tail_kernel(rows, heads, per, d_attn, w_out, queries, kv, probs, rms, cos, sin, act_t, w_qkv, ffn, x_low,
-                attn, gain, gain_grad, mixed_all, d_tok, out, grad_query, grad_out, kv_sum, gain_tiles, *refs):
+                attn, gain, gain_grad, mixed_all, d_tok, out, grad_query, grad_out, kv_sum, gain_tiles, *refs, late):
     here = Place()
     width = HD
     counts = heads // 2
@@ -1395,7 +1393,7 @@
 
     ffn_sum, leaving = take(2)
     by_chip = chip_place(here, per)
-    line = Line(here, 6 * per, [ffn, ffn_sum] + take(8), lambda at: by_chip(at + 2 * per))
+    line = Line(here, line_counts, [ffn, ffn_sum] + take(8), by_chip)
     contrib, summed = take(2)
     line_tok = Line(here, line_counts + extra, [contrib, summed] + take(8), place_tok)
     tiny = Tiny(here, tiny_own, tiny_all, (tiny_send, tiny_recv), False)
@@ -1439,6 +1437,8 @@
     scale = 1.0 / math.sqrt(HD)
     depth = w_qkv.shape[0] * 8
     d_kv[...] = jnp.zeros_like(d_kv)
+    for copy in late:
+        copy.wait()
 
     def one_head(head, dots):
         span = pl.ds(pl.multiple_of(head * HD, HD), HD)
@@ -1516,7 +1516,7 @@
             dot = from_tile(tiny_all[shard, pl.ds(low_at, 1), :] + tiny_all[partner, pl.ds(kept, 1), :], eye)
             value = dot_nt(block[tile_at * LANES : (tile_at + 1) * LANES, :], w_qkv[...])
             x_rows = x_low[row, :].astype(jnp.float32)
-            contrib[row, :] = (value * gain[...] - x_rows * dot).astype(contrib.dtype)
+            contrib[row, :] = (value * gain[0:1, :] - x_rows * dot).astype(contrib.dtype)
             gain_sum[...] += jnp.sum(value * x_rows, axis=0, keepdims=True)
         line_tok.launch(at, 1)
         rows_t = act_t[:, pl.ds(first, part)]
@@ -1556,13 +1556,7 @@
             value = x_low[row, :].astype(jnp.float32) + attn[row, :].astype(jnp.float32)
             leaving[at] = (value + source[row, :].astype(jnp.float32)).astype(out.dtype)
 
-        @pl.when(at < 6 * per)
-        def _():
-            leave(ffn_sum)
-
-        @pl.when(at >= 6 * per)
-        def _():
-            leave(ffn)
+        leave(ffn_sum)
 
     def is_own(which, at):
         return at >= 7 * per if which == 0 else jnp.logical_and(at < 4, at % 2 == 0)
@@ -1750,13 +1744,14 @@
         pltpu.VMEM((2, rows, wide), low), dma((2,)),
         pltpu.VMEM((total, cols), low),
         pltpu.VMEM((counts, chunk, cols), low),
-    ] + line_scratch(6 * per, (6 * per * chunk, cols), low)
+    ] + line_scratch(counts, (total, cols), low)
     scratch += [pltpu.VMEM(long, low), pltpu.VMEM(long, low)] + line_scratch(counts + extra, long, low)
     operands = [d_attn, w_out, queries, kv, probs, rms, cos, sin, act_t, w_qkv, ffn, x_low, attn, gain,
                 gain_grad, mixed_all]
     kernel = functools.partial(tail_kernel, rows, heads, per)
     specs = [vm] * (len(operands) - 1) + [pl.BlockSpec(memory_space=pl.ANY)]
-    return kernel_call(kernel, out_shape, operands, specs, scratch, cid, "tail")
+    return kernel_call(kernel, out_shape, operands, specs, scratch, cid, "tail",
+                       late=(2, 3, 4, 8, 9, 11, 12))
 
 
 LANES = 128
@@ -1768,8 +1763,8 @@
     rows = tokens.shape[0]
     segs = seg_ids.astype(jnp.float32).reshape(2 * rows // LANES, LANES)
     segs = jnp.pad(segs, ((0, 8 - 2 * rows // LANES), (0, 0)))
-    gain_one = gain_attn.astype(jnp.float32)[None, :]
-    gain_two = gain_ffn.astype(jnp.float32)[None, :]
+    both = jnp.stack([gain_attn, gain_ffn, gain_ffn, gain_attn]).astype(jnp.float32)
+    gain_one, gain_two = both[:2], both[2:]
     wider = jnp.float32
 
     qkv, x_low, act_one_t, w_qkv, rms, cos, sin, mask = opening(

time: 665 us -> 661 us (level)
  no operation moved by 1% of the time
where the time goes in v11:
time: 661 us; the launch traced here: 660 us
  Pallas kernels  634 us (96%)
  other arithmetic  20 us (3%)
    pallas_call x7, Pallas kernels, kernel_call(): pl.pallas_call(body, out_shape=out_shape, in_specs=specs, out_specs=out_s...  634 us

profile of v11, /device:TPU:0, one launch (start us, length us, event | category | flops | bytes accessed | tf_op | source)
XLA Modules:
  0.0 660.5 jit_solution(1744278883281958618)
XLA Ops:
  0.6 0.7 convert_bitcast_fusion
  1.3 0.6 pad.4.refs_4_
  1.9 0.7 stack.11
  2.6 0.7 stack.12
  3.3 0.6 fusion
  3.9 59.3 %open_1.1 = (f32[256,1536]{1,0:T(8,128)}, bf16[2048,512]{1,0:T(8,128)(2,1)}, bf16[512,2048]{1,0:T(8,128)(2,1)}, bf16[512,1536]{1,0:T(8,128)(2,1)}, f32[256,128]{...) custom-call(bf16[256,4096]{1,0:T(8,128)(2,1)} %refs_0_.1, ...), custom_call_target="tpu_custom_call" | custom-call | tf_op jit(solution)/shard_map/open_1/pallas_call | solution.py:412
  63.2 59.1 %attend_2.1 = (bf16[2048,512]{1,0:T(8,128)(2,1)}, bf16[2048,1024]{1,0:T(8,128)(2,1)}, bf16[2048,512]{1,0:T(8,128)(2,1)}, bf16[2,256,512]{2,1,0:T(8,128)(2,1)}, f...) custom-call(f32[256,1536]{1,0:T(8,128)} %get-tuple-element.45.refs_0_, ...), custom_call_target="tpu_custom_call" | custom-call | tf_op jit(solution)/shard_map/attend_2/pallas_call | solution.py:412
  122.3 67.8 %scatter_product_3.1 = (f32[256,3072]{1,0:T(8,128)}, bf16[2048,512]{1,0:T(8,128)(2,1)}) custom-call(bf16[2048,512]{1,0:T(8,128)(2,1)} %get-tuple-element.50.refs_0_, bf16[3072,512]{1,0:T(8,128)(2,1)} %refs_1_.6, bf16[2048,512]{1,0:T(8,128)(2,1)} %get-tuple-element.52.refs_2_), custom_call_target="tpu_custom_call" | custom-call | tf_op jit(solution)/shard_map/scatter_product_3/pallas_call | solution.py:412
  190.1 116.4 %ffn_4.1 = (bf16[256,3072]{1,0:T(8,128)(2,1)}, bf16[256,3072]{1,0:T(8,128)(2,1)}, bf16[256,3072]{1,0:T(8,128)(2,1)}, bf16[512,2048]{1,0:T(8,128)(2,1)}, f32[8,128]{1,0:T(8,128)}) custom-call(bf16[2048,512]{1,0:T(8,128)(2,1)} %get-tuple-element.51.refs_0_.refs_6_.refs_11_, bf16[2048,512]{1,0:T(8,128)(2,1)} %get-tuple-element.53.refs_1_.refs_7_.refs_12_, ...), custom_call_target="tpu_custom_call" | custom-call | tf_op jit(solution)/shard_map/ffn_4/pallas_call | solution.py:412
  306.5 118.2 %back_5.1 = (bf16[2048,512]{1,0:T(8,128)(2,1)}, f32[1,512]{1,0:T(1,128)}, bf16[512,3072]{1,0:T(8,128)(2,1)}, bf16[512,3072]{1,0:T(8,128)(2,1)}) custom-call(bf16[512,2048]{1,0:T(8,128)(2,1)} %get-tuple-element.56.refs_0_, bf16[512,3072]{1,0:T(8,128)(2,1)} %refs_1_.5, bf16[512,3072]{1,0:T(8,128)(2,1)} %refs_2_.3, ...), custom_call_target="tpu_custom_call" | custom-call | tf_op jit(solution)/shard_map/back_5/pallas_call | solution.py:412
  424.7 71.5 %down_6.1 = (bf16[2048,512]{1,0:T(8,128)(2,1)}, bf16[2048,512]{1,0:T(8,128)(2,1)}, bf16[3072,512]{1,0:T(8,128)(2,1)}) custom-call(bf16[2048,512]{1,0:T(8,128)(2,1)} %get-tuple-element.50.refs_0_, bf16[3072,512]{1,0:T(8,128)(2,1)} %refs_1_.6, bf16[256,3072]{1,0:T(8,128)(2,1)} %get-tuple-element.55.refs_2_, bf16[2048,512]{1,0:T(8,128)(2,1)} %get-tuple-element.60.refs_3_), custom_call_target="tpu_custom_call" | custom-call | tf_op jit(solution)/shard_map/down_6/pallas_call | solution.py:412
  496.2 141.8 %tail_7.1 = (bf16[256,4096]{1,0:T(8,128)(2,1)}, bf16[256,4096]{1,0:T(8,128)(2,1)}, bf16[512,1024]{1,0:T(8,128)(2,1)}, bf16[1024,512]{1,0:T(8,128)(2,1)}, bf16[512,512]{1,0:T(8,128)(2,1)}, /*index=5*/f32[4,8,128]{2,1,0:T(8,128)}) custom-call(bf16[2048,512]{1,0:T(8,128)(2,1)} %get-tuple-element.61.refs_0_, bf16[1024,512]{1,0:T(8,128)(2,1)} %refs_1_.7, ...), custom_call_target="tpu_custom_call" | custom-call | tf_op jit(solution)/shard_map/tail_7/pallas_call | solution.py:412
  638.0 0.0 copy-start.6
  638.0 0.8 reduce_sum.9
  638.8 0.6 slice_bitcast_fusion
  639.4 0.0 copy-start.5
  639.4 2.2 convert_element_type.33
  641.6 0.0 copy-done.6
  641.7 1.6 convert_element_type.32
  643.2 0.0 copy-done.5
  643.2 0.0 copy-start.3
  643.2 1.6 convert_element_type.34
  644.8 0.7 copy-done.3
  645.6 0.0 copy-start.2
  645.6 2.5 convert_element_type.31
  648.1 0.5 copy-done.2
  648.5 0.0 copy-start.1
  648.5 3.6 convert_element_type.37
  652.2 0.0 copy-done.1
  652.2 0.0 copy-start
  652.2 3.5 convert_element_type.35
  655.7 0.0 copy-done
  655.7 0.0 copy-start.4
  655.7 3.5 convert_element_type.36
  659.2 0.0 copy-done.4
  659.2 1.3 copy.22
  (1 shorter events, 0.0 us)
Async XLA Ops:
  638.0 3.6 copy-start.6
  639.4 3.8 copy-start.5
  643.2 2.3 copy-start.3
  645.6 3.0 copy-start.2
  648.5 3.6 copy-start.1
  652.2 3.5 copy-start
  655.7 3.5 copy-start.4

commit v12 on v11

--- a/solution.py
+++ b/solution.py
@@ -519,15 +519,18 @@
             self.to_x(hop, at, stage).start()
             self.to_y(hop, at, stage).start()
 
+    def advance(self, step):
+        @pl.when(step < self.steps)
+        def _():
+            self.compute(step)
+
+        @pl.when(jnp.logical_and(step > 0, step <= self.steps))
+        def _():
+            self.finish(step - 1)
+
     def run(self, hook=None):
         def body(step, _):
-            @pl.when(step < self.steps)
-            def _():
-                self.compute(step)
-
-            @pl.when(step > 0)
-            def _():
-                self.finish(step - 1)
+            self.advance(step)
 
             if hook:
                 hook(step)
@@ -595,6 +598,40 @@
     def streams(self, stage):
         some, last, late = jnp.minimum(stage, 1), stage // 3, stage // 2
         return (some + 2 * last, late), (2 * some + last, 1 - late)
+
+    def block(self, at):
+        x_stream, y_stream = self.streams(at // 4)
+        second = at // 2 % 2
+        across = x_stream[0] + second * (y_stream[0] - x_stream[0])
+        half = x_stream[1] + second * (y_stream[1] - x_stream[1])
+        return across, at % 2, half
+
+    def begin_rows(self):
+        for hop in range(2):
+            self.x_copy(hop, 0).start()
+            self.y_copy(hop, 0).start()
+        for stream in range(2):
+            self.sib_copy(0, stream, 0).start()
+
+    def receive_rows(self, step):
+        stage = step // 4
+
+        @pl.when(jnp.logical_and(step % 4 == 0, jnp.logical_and(stage > 0, stage < 4)))
+        def _():
+            self.x_copy(stage - 1, 0).wait_recv()
+            self.sib_copy(stage, 0, 0).start()
+            self.y_copy(stage - 1, 0).wait_recv()
+            self.sib_copy(stage, 1, 0).start()
+
+        @pl.when(step == 4)
+        def _():
+            self.x_copy(2, 0).start()
+            self.y_copy(2, 0).start()
+
+        for stream in range(2):
+            @pl.when(jnp.logical_and(step % 4 == 2 * stream, step < 16))
+            def _(stream=stream):
+                self.sib_copy(stage, stream, 0).wait_recv()
 
     def sib_copy(self, stage, stream, at):
         across, half = self.streams(stage)[stream]
@@ -841,40 +878,6 @@
     kernel = functools.partial(open_kernel, rows, width, counts)
     return kernel_call(kernel, out_shape, [tokens, gain, w_query, kv_weight, segs],
                        [vm, vm, hbm, hbm, vm], scratch, cid, "open")
-
-
-def scatter_kernel(rows, width, counts, line_counts, act, weight, line_own, out, line_out, *refs):
-    here = Place()
-    line = Line(here, line_counts, [line_own, line_out] + list(refs[11:]))
-    product = products(here, act, weight, True, rows, width, counts)
-    total = Reduce(here, counts, product, refs[:11])
-    greet(here, slice_peers(here), True)
-    line.begin()
-    def beside(step):
-        line.step(2 * step)
-        line.step(2 * step + 1)
-
-    line.end(2 * total.run(beside))
-
-    def emit(at, first, second):
-        for half, value in enumerate((first, second)):
-            out[:, pl.ds(pl.multiple_of((half * counts + at) * width, width), width)] = value
-
-    total.end(emit)
-
-
-def scatter_product(act, weight, width, cid, line, line_counts=32):
-    rows = act.shape[0] // 8
-    every = weight.shape[0]
-    counts = every // (2 * width)
-    vm = pl.BlockSpec(memory_space=pltpu.VMEM)
-    out_shape = [
-        jax.ShapeDtypeStruct((rows, every), jnp.float32),
-        jax.ShapeDtypeStruct(line.shape, line.dtype),
-    ]
-    scratch = reduce_scratch(counts, rows, width) + line_scratch(line_counts, line.shape, line.dtype)
-    kernel = functools.partial(scatter_kernel, rows, width, counts, line_counts)
-    return kernel_call(kernel, out_shape, [act, weight, line], [vm] * 3, scratch, cid, "scatter_product")
 
 
 def ffn_kernel(rows, width, counts, x_low, attn, gain, w_gate, w_up, d_hidden, hidden, d_gate, d_up, act_t, tile_out,
@@ -1237,13 +1240,22 @@
                        [vm, vm, hbm], (0, 1))
 
 
-def attend_kernel(rows, heads, cols, qkv, rms, cos, sin, mask, w_out, cot, part, mixed_all, g_col, kv, probs, queries,
-                  pair_rms, *refs, late):
+def attend_kernel(rows, heads, cols, width, counts, qkv, rms, cos, sin, mask, w_out, cot, w_down, attn, mixed_all, g_col,
+                  kv, probs, queries, pair_rms, d_hidden, *refs, late):
     here = Place()
-    spread = Spread(here, heads // 2, refs[:7])
-    sums, pair_sems, turn_send, turn_recv, local_sem, tiny_own, tiny_pair = refs[7:14]
+    spread = Spread(here, 1, refs[:7])
+    part, pair_sems, turn_send, turn_recv, local_sem, tiny_own, tiny_pair, mixed_sems = refs[7:15]
+    product = products(here, g_col, w_down, True, rows, width, counts)
+    total = Reduce(here, counts, product, refs[15:26])
+    piece = rows // 2
+
+    def place(at):
+        across, other, half_at = spread.block(at)
+        return here.shard(across, other) * 2 + half_at
+
+    line = Line(here, 16, [part, attn] + list(refs[26:]), place)
     got, core = spread.got, here.core
-    greet(here, slice_peers(here))
+    greet(here, slice_peers(here), True)
     me = here.shard(0, 0)
 
     def turn_copy(at):
@@ -1301,37 +1313,73 @@
         probs[head] = prob
         prob_low = prob.astype(jnp.bfloat16)
         mixed = dot_nn(prob_low[:, :rows], kv[0, :, HD:]) + dot_nn(prob_low[:, rows:], kv[1, :, HD:])
-        got[0, core, head // (heads // 2), head % (heads // 2)] = mixed.astype(got.dtype)
+        span = pl.ds(pl.multiple_of(head * HD, HD), HD)
+        for half_at in range(2):
+            low_mixed = mixed[half_at * piece : (half_at + 1) * piece, :].astype(got.dtype)
+            got[0, core, half_at, 0, :, span] = low_mixed
         return 0
 
     lax.fori_loop(0, heads, one_head, 0)
-    sums[...] = jnp.zeros_like(sums)
-    spread.begin()
-
-    def blocks(across, half_at, at):
-        span = pl.ds(pl.multiple_of((half_at * (heads // 2) + at) * HD, HD), HD)
-        for other in range(2):
-            row = row_span(here, across, other, rows)
-            block = got[across, (core + other) % 2, half_at, at]
-            mixed_all[row, span] = block
-            sums[row, :] += dot_nn(block, w_out[span, :])
-
-    spread.run(blocks)
-    part[...] = sums[...].astype(part.dtype)
-    spread.end()
+    spread.begin_rows()
+
+    def mixed_copy(at):
+        across, other, half_at = spread.block(at)
+        span = pl.ds(pl.multiple_of(place(at) * piece, piece), piece)
+        return pltpu.make_async_copy(got.at[across, (core + other) % 2, half_at, 0], mixed_all.at[span, :],
+                                     mixed_sems.at[at])
+
+    def one_step(step, _):
+        spread.receive_rows(step)
+
+        @pl.when(step < 16)
+        def _():
+            across, other, half_at = spread.block(step)
+            value = dot_nn(got[across, (core + other) % 2, half_at, 0], w_out[...])
+            part[pl.ds(pl.multiple_of(place(step) * piece, piece), piece), :] = value.astype(part.dtype)
+            mixed_copy(step).start()
+            line.launch(step, 1)
+
+        @pl.when(step == 4)
+        def _():
+            own_turn.wait()
+            for at in range(7):
+                turn_copy(at).wait_recv()
+
+        @pl.when(step >= 4)
+        def _():
+            total.advance(step - 4)
+            line.step(step - 4)
+        return 0
+
+    lax.fori_loop(0, 4 + max(16, total.steps + 1), one_step, 0)
+    line.end(max(16, total.steps + 1))
+
+    def emit(at, first, second):
+        for half_at, value in enumerate((first, second)):
+            d_hidden[:, pl.ds(pl.multiple_of((half_at * counts + at) * width, width), width)] = value
+
+    total.end(emit)
+    for hop in range(3):
+        spread.x_copy(hop, 0).wait_send()
+        spread.y_copy(hop, 0).wait_send()
+    for stage in range(4):
+        for stream in range(2):
+            spread.sib_copy(stage, stream, 0).wait_send()
+    for at in range(16):
+        mixed_copy(at).wait()
     tiny.wait()
     for at in range(rows // LANES):
         values = jnp.broadcast_to(from_tile(tiny_pair[at : at + 1, :], eye), (LANES, LANES))
         pair_rms[1, at * LANES : (at + 1) * LANES, :] = values
-    own_turn.wait()
     for at in range(7):
-        turn_copy(at).wait()
-
-
-def attend(qkv, rms, cos, sin, mask, w_out, cot, cid):
+        turn_copy(at).wait_send()
+
+
+def attend(qkv, rms, cos, sin, mask, w_out, cot, w_down, cid, width=512):
     rows = qkv.shape[0]
     wide, cols = w_out.shape
     heads = wide // HD
+    counts = w_down.shape[0] // (2 * width)
     low, f32 = jnp.bfloat16, jnp.float32
     dma = pltpu.SemaphoreType.DMA
     vm = pl.BlockSpec(memory_space=pltpu.VMEM)
@@ -1343,13 +1391,16 @@
         jax.ShapeDtypeStruct((heads, rows, 2 * rows), f32),
         jax.ShapeDtypeStruct((rows, wide), low),
         jax.ShapeDtypeStruct((2,) + rms.shape, f32),
+        jax.ShapeDtypeStruct((rows, w_down.shape[0]), f32),
     ]
-    scratch = spread_scratch(heads // 2, rows, HD) + [
-        pltpu.VMEM((8 * rows, cols), f32), dma((4,)), dma((7,)), dma((7,)), dma(()),
-        pltpu.VMEM((8, LANES), f32), pltpu.VMEM((8, LANES), f32)]
-    kernel = functools.partial(attend_kernel, rows, heads, cols)
-    return kernel_call(kernel, out_shape, [qkv, rms, cos, sin, mask, w_out, cot], [vm] * 7, scratch, cid,
-                       "attend", late=(4, 5))
+    scratch = spread_scratch(1, rows // 2, wide) + [
+        pltpu.VMEM((8 * rows, cols), low), dma((4,)), dma((7,)), dma((7,)), dma(()),
+        pltpu.VMEM((8, LANES), f32), pltpu.VMEM((8, LANES), f32), dma((16,)),
+    ] + reduce_scratch(counts, rows, width) + line_scratch(16, (8 * rows, cols), low)
+    kernel = functools.partial(attend_kernel, rows, heads, cols, width, counts)
+    operands = [qkv, rms, cos, sin, mask, w_out, cot, w_down]
+    out_specs = [vm, pl.BlockSpec(memory_space=pl.ANY)] + [vm] * 6
+    return kernel_call(kernel, out_shape, operands, [vm] * 8, scratch, cid, "attend", out_specs, (4, 5, 7))
 
 
 def tail_kernel(rows, heads, per, d_attn, w_out, queries, kv, probs, rms, cos, sin, act_t, w_qkv, ffn, x_low,
@@ -1374,15 +1425,10 @@
     grad, grad_mixed, gain_sum, tile, tile_send, tile_recv, put_sems, local_sems, mixed_two, mixed_sems = take(10)
 
     def far(at):
-        return turned(at // per)
+        return at // (2 * per), at // per % 2
 
     def near(at):
-        at = jnp.minimum(at, line_counts - 1)
-        x_stream, y_stream = spread.streams(at // 4)
-        second = at // 2 % 2
-        across = x_stream[0] + second * (y_stream[0] - x_stream[0])
-        half_at = x_stream[1] + second * (y_stream[1] - x_stream[1])
-        return across, at % 2, half_at
+        return spread.block(jnp.minimum(at, line_counts - 1))
 
     def place_ffn(at):
         return here.shard(*far(at)) * per + at % per
@@ -1495,13 +1541,8 @@
         value = d_kv[0, piece, :] + taken[piece, :].astype(jnp.float32)
         got[0, core, rows_at, 0, :, heads * HD :] = value.astype(got.dtype)
     tiny.begin()
-    for hop in range(2):
-        spread.x_copy(hop, 0).start()
-        spread.y_copy(hop, 0).start()
-    for stream in range(2):
-        spread.sib_copy(0, stream, 0).start()
+    spread.begin_rows()
     gain_sum[...] = jnp.zeros_like(gain_sum)
-    line.end(done + heads)
     tiny.end()
 
     def block_of(at):
@@ -1559,7 +1600,7 @@
         leave(ffn_sum)
 
     def is_own(which, at):
-        return at >= 7 * per if which == 0 else jnp.logical_and(at < 4, at % 2 == 0)
+        return at < per if which == 0 else jnp.logical_and(at < 4, at % 2 == 0)
 
     def send(which, at):
         own = is_own(which, at)
@@ -1573,29 +1614,16 @@
             put(which, at).start()
 
     def stage_step(step, _):
-        stage = step // 4
-
-        @pl.when(jnp.logical_and(step % 4 == 0, jnp.logical_and(stage > 0, stage < 4)))
-        def _():
-            spread.x_copy(stage - 1, 0).wait_recv()
-            spread.sib_copy(stage, 0, 0).start()
-            spread.y_copy(stage - 1, 0).wait_recv()
-            spread.sib_copy(stage, 1, 0).start()
-
-        @pl.when(step == 4)
-        def _():
-            spread.x_copy(2, 0).start()
-            spread.y_copy(2, 0).start()
+        spread.receive_rows(step)
 
         @pl.when(step < line_counts)
         def _():
-            for stream in range(2):
-                @pl.when(step % 4 == 2 * stream)
-                def _(stream=stream):
-                    spread.sib_copy(stage, stream, 0).wait_recv()
-
             block_of(step)
 
+        @pl.when(step < 5)
+        def _():
+            line.step(done + heads + step)
+
         @pl.when(step >= 4)
         def _():
             line_tok.step(step - 4)
@@ -1603,6 +1631,11 @@
         @pl.when(step > 0)
         def _():
             send(0, step - 1)
+
+        @pl.when(line.inner == 0)
+        def _():
+            line.up(step).wait_send()
+            line.down(step).wait_recv()
 
         emit(0, step)
 
@@ -1632,6 +1665,7 @@
                       (here.dp, here.seq, (here.z + step + 1) % 4))
 
     send(0, line_counts - 1)
+    line.drain()
     for step in range(3):
         tile_copy(step).start()
     gain_tiles[here.z] = tile[...]
@@ -1770,10 +1804,9 @@
     qkv, x_low, act_one_t, w_qkv, rms, cos, sin, mask = opening(
         tokens, gain_one, w_query, kv_weight, segs, 1
     )
-    attn_part, mixed_all, g_low, kv, probs, queries, pair_rms = attend(
-        qkv, rms, cos, sin, mask, w_out, d_out, 2
-    )
-    d_hidden, attn = scatter_product(g_low, w_down, 512, 3, attn_part)
+    attn, mixed_all, g_low, kv, probs, queries, pair_rms, d_hidden = attend(
+        qkv, rms, cos, sin, mask, w_out, d_out, w_down, 2
+    )
     hidden, d_gate, d_up, act_two_t, dots = ffn_scatter(x_low, attn, gain_two, w_gate, w_up, d_hidden, 4)
     d_norm, grad_gain_two, grad_gate, grad_up = back_gather(
         act_two_t, w_gate, w_up, d_gate, d_up, dots, x_low, attn, gain_two, 5

time: 661 us -> 639 us (0.967)
  Pallas kernels: 634 us -> 612 us
    pallas_call x7 -> x6, Pallas kernels: 634 us -> 612 us  [kernel_call(): pl.pallas_call(body, out_shape=out_shape, in_specs=specs, out_specs=out_s...]
where the time goes in v12:
time: 639 us; the launch traced here: 638 us
  Pallas kernels  612 us (96%)
  other arithmetic  20 us (3%)
    pallas_call x6, Pallas kernels, kernel_call(): pl.pallas_call(body, out_shape=out_shape, in_specs=specs, out_specs=out_s...  612 us

profile of v12, /device:TPU:0, one launch (start us, length us, event | category | flops | bytes accessed | tf_op | source)
XLA Modules:
  0.0 638.5 jit_solution(24097171969929512)
XLA Ops:
  0.6 0.7 convert_bitcast_fusion
  1.3 0.6 pad.4.refs_4_
  1.9 0.7 stack.11
  2.6 0.7 stack.12
  3.3 0.6 fusion
  3.9 59.3 %open_1.1 = (f32[256,1536]{1,0:T(8,128)}, bf16[2048,512]{1,0:T(8,128)(2,1)}, bf16[512,2048]{1,0:T(8,128)(2,1)}, bf16[512,1536]{1,0:T(8,128)(2,1)}, f32[256,128]{...) custom-call(bf16[256,4096]{1,0:T(8,128)(2,1)} %refs_0_.1, ...), custom_call_target="tpu_custom_call" | custom-call | tf_op jit(solution)/shard_map/open_1/pallas_call | solution.py:412
  63.2 111.1 %attend_2.1 = (bf16[2048,512]{1,0:T(8,128)(2,1)}, bf16[2048,1024]{1,0:T(8,128)(2,1)}, bf16[2048,512]{1,0:T(8,128)(2,1)}, bf16[2,256,512]{2,1,0:T(8,128)(2,1)}, f...) custom-call(f32[256,1536]{1,0:T(8,128)} %get-tuple-element.44.refs_0_, ...), custom_call_target="tpu_custom_call" | custom-call | tf_op jit(solution)/shard_map/attend_2/pallas_call | solution.py:412
  174.3 116.7 %ffn_4.1 = (bf16[256,3072]{1,0:T(8,128)(2,1)}, bf16[256,3072]{1,0:T(8,128)(2,1)}, bf16[256,3072]{1,0:T(8,128)(2,1)}, bf16[512,2048]{1,0:T(8,128)(2,1)}, f32[8,128]{1,0:T(8,128)}) custom-call(bf16[2048,512]{1,0:T(8,128)(2,1)} %get-tuple-element.50.refs_0_.refs_6_.refs_11_, bf16[2048,512]{1,0:T(8,128)(2,1)} %get-tuple-element.51.refs_1_.refs_7_.refs_12_, ...), custom_call_target="tpu_custom_call" | custom-call | tf_op jit(solution)/shard_map/ffn_4/pallas_call | solution.py:412
  291.0 117.2 %back_5.1 = (bf16[2048,512]{1,0:T(8,128)(2,1)}, f32[1,512]{1,0:T(1,128)}, bf16[512,3072]{1,0:T(8,128)(2,1)}, bf16[512,3072]{1,0:T(8,128)(2,1)}) custom-call(bf16[512,2048]{1,0:T(8,128)(2,1)} %get-tuple-element.54.refs_0_, bf16[512,3072]{1,0:T(8,128)(2,1)} %refs_1_.3, bf16[512,3072]{1,0:T(8,128)(2,1)} %refs_2_.3, ...), custom_call_target="tpu_custom_call" | custom-call | tf_op jit(solution)/shard_map/back_5/pallas_call | solution.py:412
  408.2 70.3 %down_6.1 = (bf16[2048,512]{1,0:T(8,128)(2,1)}, bf16[2048,512]{1,0:T(8,128)(2,1)}, bf16[3072,512]{1,0:T(8,128)(2,1)}) custom-call(bf16[2048,512]{1,0:T(8,128)(2,1)} %get-tuple-element.49.refs_0_, bf16[3072,512]{1,0:T(8,128)(2,1)} %refs_1_.4, bf16[256,3072]{1,0:T(8,128)(2,1)} %get-tuple-element.53.refs_2_, bf16[2048,512]{1,0:T(8,128)(2,1)} %get-tuple-element.58.refs_3_), custom_call_target="tpu_custom_call" | custom-call | tf_op jit(solution)/shard_map/down_6/pallas_call | solution.py:412
  478.5 137.4 %tail_7.1 = (bf16[256,4096]{1,0:T(8,128)(2,1)}, bf16[256,4096]{1,0:T(8,128)(2,1)}, bf16[512,1024]{1,0:T(8,128)(2,1)}, bf16[1024,512]{1,0:T(8,128)(2,1)}, bf16[512,512]{1,0:T(8,128)(2,1)}, /*index=5*/f32[4,8,128]{2,1,0:T(8,128)}) custom-call(bf16[2048,512]{1,0:T(8,128)(2,1)} %get-tuple-element.59.refs_0_, bf16[1024,512]{1,0:T(8,128)(2,1)} %refs_1_.5, ...), custom_call_target="tpu_custom_call" | custom-call | tf_op jit(solution)/shard_map/tail_7/pallas_call | solution.py:412
  616.0 0.0 copy-start.6
  616.0 0.8 reduce_sum.9
  616.8 0.6 slice_bitcast_fusion
  617.4 0.0 copy-start.5
  617.4 2.2 convert_element_type.33
  619.6 0.0 copy-done.6
  619.6 1.6 convert_element_type.32
  621.2 0.0 copy-done.5
  621.2 0.0 copy-start.3
  621.2 1.6 convert_element_type.34
  622.8 0.7 copy-done.3
  623.5 0.0 copy-start.2
  623.5 2.5 convert_element_type.31
  626.0 0.5 copy-done.2
  626.5 0.0 copy-start.1
  626.5 3.6 convert_element_type.37
  630.1 0.0 copy-done.1
  630.1 0.0 copy-start
  630.1 3.5 convert_element_type.35
  633.6 0.0 copy-done
  633.6 0.0 copy-start.4
  633.6 3.5 convert_element_type.36
  637.1 0.0 copy-done.4
  637.1 1.3 copy.22
  (1 shorter events, 0.0 us)
Async XLA Ops:
  616.0 3.6 copy-start.6
  617.4 3.8 copy-start.5
  621.2 2.3 copy-start.3
  623.5 3.0 copy-start.2
  626.5 3.6 copy-start.1
  630.1 3.5 copy-start
  633.6 3.5 copy-start.4

commit v13 on v12

--- a/solution.py
+++ b/solution.py
@@ -779,11 +779,12 @@
                         mask[span, first : first + LANES] = allowed.astype(jnp.float32)
 
 
-def open_kernel(rows, width, counts, tokens, gain, w_query, kv_weight, segs, qkv, x_low, act_t, w_qkv, rms, cos, sin,
-                mask, *refs):
+def open_kernel(rows, width, counts, tokens, gain, w_query, kv_weight, segs, cot, qkv, x_low, act_t, w_qkv, rms, cos, sin,
+                mask, g_col, *refs):
     here = Place()
     cols = gain.shape[1]
-    act, turn_send, turn_recv, local_sems = refs[:4]
+    act, turn_send, turn_recv, local_sems, cot_part, g_send, g_recv, z_send, z_recv = refs[:9]
+    share = rows // 4
     me = here.shard(0, 0)
     own_rows = pl.ds(pl.multiple_of(me * rows, rows), rows)
 
@@ -800,9 +801,49 @@
         pltpu.make_async_copy(tokens.at[:, pl.ds(pl.multiple_of(me * cols, cols), cols)], x_low.at[own_rows, :],
                               local_sems.at[2]),
     ]
+    load = pltpu.make_async_copy(cot.at[pl.ds(pl.multiple_of(here.z * share, share), share), :], cot_part,
+                                 local_sems.at[3])
+    load.start()
     for copy in local:
         copy.start()
-    greet(here, slice_peers(here))
+
+    def g_copy(at):
+        across, other = turned(at)
+        first = pl.multiple_of(here.shard(across, other) * cols, cols)
+        return remote(cot_part.at[:, pl.ds(first, cols)], g_col.at[me, here.z], g_send.at[at], g_recv.at[at],
+                      here.device(across, other))
+
+    def own_part():
+        return pltpu.make_async_copy(cot_part.at[:, pl.ds(pl.multiple_of(me * cols, cols), cols)],
+                                     g_col.at[me, here.z], local_sems.at[4])
+
+    def quarter(way, at, step, peer):
+        spot = g_col.at[:, at]
+        return remote(spot, spot, z_send.at[way, step], z_recv.at[way, step], (here.dp, here.seq, here.z + peer))
+
+    def pass_on(step):
+        @pl.when(jnp.logical_and(here.z < 3, here.z >= step))
+        def _():
+            quarter(0, here.z - step, step, 1).start()
+
+        @pl.when(jnp.logical_and(here.z > 0, here.z <= 3 - step))
+        def _():
+            quarter(1, here.z + step, step, -1).start()
+
+    def take_quarters(step):
+        @pl.when(here.z > step)
+        def _():
+            quarter(0, here.z - 1 - step, step, -1).wait_recv()
+
+        @pl.when(here.z < 3 - step)
+        def _():
+            quarter(1, here.z + 1 + step, step, 1).wait_recv()
+
+    greet(here, slice_peers(here), True)
+    load.wait()
+    own_part().start()
+    for at in range(7):
+        g_copy(at).start()
     for at in range(7):
         turn_copy(at).start()
     for copy in local:
@@ -828,6 +869,13 @@
 
     def before(stop):
         first, count = ((0, 2), (2, 4), (6, 2))[stop]
+        if stop == 0:
+            own_part().wait()
+            for at in range(7):
+                g_copy(at).wait_recv()
+        else:
+            take_quarters(stop - 1)
+        pass_on(stop)
         for at in range(first, min(first + count, 7)):
             turn_copy(at).wait_recv()
         prepare(first, count)
@@ -841,7 +889,7 @@
         lax.fori_loop(0, 8, one, 0)
 
     product = products(here, act, w_qkv, False, rows, width, counts)
-    total = Reduce(here, counts, product, refs[4:15], before)
+    total = Reduce(here, counts, product, refs[9:20], before)
     total.run()
     flip()
 
@@ -850,11 +898,21 @@
             qkv[:, pl.ds(pl.multiple_of((half * counts + at) * width, width), width)] = value
 
     total.end(emit)
+    take_quarters(2)
     for at in range(7):
         turn_copy(at).wait_send()
-
-
-def opening(tokens, gain, w_query, kv_weight, segs, cid, width=256):
+        g_copy(at).wait_send()
+    for step in range(3):
+        @pl.when(jnp.logical_and(here.z < 3, here.z >= step))
+        def _(step=step):
+            quarter(0, here.z - step, step, 1).wait_send()
+
+        @pl.when(jnp.logical_and(here.z > 0, here.z <= 3 - step))
+        def _(step=step):
+            quarter(1, here.z + step, step, -1).wait_send()
+
+
+def opening(tokens, gain, w_query, kv_weight, segs, cot, cid, width=256):
     rows = tokens.shape[0]
     cols, wide = w_query.shape
     every = wide + kv_weight.shape[1]
@@ -872,12 +930,16 @@
         jax.ShapeDtypeStruct((2, rows, LANES), f32),
         jax.ShapeDtypeStruct((2, rows, LANES), f32),
         jax.ShapeDtypeStruct((rows, 2 * rows), f32),
+        jax.ShapeDtypeStruct((8, 4, rows // 4, cols), low),
     ]
-    scratch = [pltpu.VMEM((8 * rows, cols), low), dma((7,)), dma((7,)), dma((3,))]
+    scratch = [
+        pltpu.VMEM((8 * rows, cols), low), dma((7,)), dma((7,)), dma((5,)),
+        pltpu.VMEM((rows // 4, 8 * cols), low), dma((7,)), dma((7,)), dma((2, 3)), dma((2, 3)),
+    ]
     scratch += reduce_scratch(counts, rows, width)
     kernel = functools.partial(open_kernel, rows, width, counts)
-    return kernel_call(kernel, out_shape, [tokens, gain, w_query, kv_weight, segs],
-                       [vm, vm, hbm, hbm, vm], scratch, cid, "open")
+    return kernel_call(kernel, out_shape, [tokens, gain, w_query, kv_weight, segs, cot],
+                       [vm, vm, hbm, hbm, vm, hbm], scratch, cid, "open")
 
 
 def ffn_kernel(rows, width, counts, x_low, attn, gain, w_gate, w_up, d_hidden, hidden, d_gate, d_up, act_t, tile_out,
@@ -1139,9 +1201,10 @@
 def down_kernel(rows, width, counts, cot, weight, hidden, d_norm, ffn, d_attn, grad, *refs, late):
     here = Place()
     spread = Spread(here, counts, refs[:7])
-    own_sems, sums, grads, staged, out_sems, norm_out = refs[7:13]
+    own_sems, sums, grads, staged, out_sems, norm_out, part = refs[7:14]
     place = chip_place(here, 4)
-    norm_line = Line(here, 24, [d_norm, norm_out] + list(refs[13:]), lambda at: place(at + 8))
+    norm_line = Line(here, 24, [d_norm, norm_out] + list(refs[14:22]), lambda at: place(at + 8))
+    line = Line(here, 4, [part, ffn] + list(refs[22:]), chip_place(here, 2))
     own = load_own(spread, (hidden,), width, counts, own_sems)
     for copy in own:
         copy.start()
@@ -1184,8 +1247,28 @@
             leave(0, at).start()
             leave(1, at).start()
 
-    norm_line.steps(spread.run(blocks, norm_line.step, done), 26)
-    ffn[...] = sums[...].astype(ffn.dtype)
+        @pl.when(jnp.logical_and(at == counts - 1, stage == 0))
+        def _():
+            close_chip(0, part)
+            line.launch(0, 4)
+
+    def close_chip(chip, target):
+        def close_shard(other, _):
+            span = row_span(here, chip, other, rows)
+            target[span, :] = sums[span, :].astype(target.dtype)
+            return 0
+
+        lax.fori_loop(0, 2, close_shard, 0)
+
+    def hook(step):
+        norm_line.step(step)
+
+        @pl.when(step >= 4 * counts - 5)
+        def _():
+            line.step(step - (4 * counts - 5))
+
+    norm_line.steps(spread.run(blocks, hook, done), 26)
+    lax.fori_loop(1, 4, lambda chip, _: (close_chip(chip, ffn), 0)[1], 0)
     norm_line.settle()
 
     def add_norm(at, _):
@@ -1204,6 +1287,7 @@
         return 0
 
     lax.fori_loop(0, 8, add_norm, 0)
+    line.settle()
     spread.end()
 
     def drain(at, _):
@@ -1234,39 +1318,29 @@
         pltpu.VMEM((2, 2, width, cols), low),
         dma((2, counts)),
         pltpu.VMEM((total, cols), low),
-    ] + line_scratch(24, (24 * rows // 4, cols), low)
+        pltpu.VMEM((total, cols), low),
+    ] + line_scratch(24, (24 * rows // 4, cols), low) + line_scratch(4, (4 * rows // 2, cols), low)
     kernel = functools.partial(down_kernel, rows, width, counts)
     return kernel_call(kernel, out_shape, [cot, weight, hidden, d_norm], [vm, vm, hbm, vm], scratch, cid, "down",
                        [vm, vm, hbm], (0, 1))
 
 
-def attend_kernel(rows, heads, cols, width, counts, qkv, rms, cos, sin, mask, w_out, cot, w_down, attn, mixed_all, g_col,
+def attend_kernel(rows, heads, cols, width, counts, qkv, rms, cos, sin, mask, w_out, g_col, w_down, attn, mixed_all,
                   kv, probs, queries, pair_rms, d_hidden, *refs, late):
     here = Place()
     spread = Spread(here, 1, refs[:7])
-    part, pair_sems, turn_send, turn_recv, local_sem, tiny_own, tiny_pair, mixed_sems = refs[7:15]
+    part, pair_sems, tiny_own, tiny_pair, mixed_sems = refs[7:12]
     product = products(here, g_col, w_down, True, rows, width, counts)
-    total = Reduce(here, counts, product, refs[15:26])
+    total = Reduce(here, counts, product, refs[12:23])
     piece = rows // 2
 
     def place(at):
         across, other, half_at = spread.block(at)
         return here.shard(across, other) * 2 + half_at
 
-    line = Line(here, 16, [part, attn] + list(refs[26:]), place)
+    line = Line(here, 16, [part, attn] + list(refs[23:]), place)
     got, core = spread.got, here.core
     greet(here, slice_peers(here), True)
-    me = here.shard(0, 0)
-
-    def turn_copy(at):
-        across, other = turned(at)
-        first = pl.multiple_of(here.shard(across, other) * cols, cols)
-        return remote(cot.at[:, pl.ds(first, cols)], g_col.at[pl.ds(pl.multiple_of(me * rows, rows), rows), :],
-                      turn_send.at[at], turn_recv.at[at], here.device(across, other))
-
-    own_turn = pltpu.make_async_copy(cot.at[:, pl.ds(pl.multiple_of(me * cols, cols), cols)],
-                                     g_col.at[pl.ds(pl.multiple_of(me * rows, rows), rows), :], local_sem)
-    own_turn.start()
     half = HD // 2
     scale = 1.0 / math.sqrt(HD)
     wide = heads * HD
@@ -1292,17 +1366,12 @@
         if head == 1:
             pair.start()
             tiny.start()
-            turn_copy(2 * (3 - 1)).start()
-            turn_copy(2 * (3 - 1) + 1).start()
         lead, trail = rotated(head * HD)
         queries[:, head * HD : head * HD + half] = (lead * scale).astype(queries.dtype)
         queries[:, head * HD + half : (head + 1) * HD] = (trail * scale).astype(queries.dtype)
     pair.wait()
     for copy in late:
         copy.wait()
-    for at in range(7):
-        if at // 2 != 2:
-            turn_copy(at).start()
 
     def one_head(head, _):
         query = queries[:, pl.ds(pl.multiple_of(head * HD, HD), HD)]
@@ -1339,15 +1408,12 @@
             mixed_copy(step).start()
             line.launch(step, 1)
 
-        @pl.when(step == 4)
-        def _():
-            own_turn.wait()
-            for at in range(7):
-                turn_copy(at).wait_recv()
+        @pl.when(step >= 2)
+        def _():
+            total.advance(step - 2)
 
         @pl.when(step >= 4)
         def _():
-            total.advance(step - 4)
             line.step(step - 4)
         return 0
 
@@ -1371,11 +1437,9 @@
     for at in range(rows // LANES):
         values = jnp.broadcast_to(from_tile(tiny_pair[at : at + 1, :], eye), (LANES, LANES))
         pair_rms[1, at * LANES : (at + 1) * LANES, :] = values
-    for at in range(7):
-        turn_copy(at).wait_send()
-
-
-def attend(qkv, rms, cos, sin, mask, w_out, cot, w_down, cid, width=512):
+
+
+def attend(qkv, rms, cos, sin, mask, w_out, g_col, w_down, cid, width=512):
     rows = qkv.shape[0]
     wide, cols = w_out.shape
     heads = wide // HD
@@ -1386,7 +1450,6 @@
     out_shape = [
         jax.ShapeDtypeStruct((8 * rows, cols), low),
         jax.ShapeDtypeStruct((8 * rows, wide), low),
-        jax.ShapeDtypeStruct((8 * rows, cols), low),
         jax.ShapeDtypeStruct((2, rows, 2 * HD), low),
         jax.ShapeDtypeStruct((heads, rows, 2 * rows), f32),
         jax.ShapeDtypeStruct((rows, wide), low),
@@ -1394,13 +1457,13 @@
         jax.ShapeDtypeStruct((rows, w_down.shape[0]), f32),
     ]
     scratch = spread_scratch(1, rows // 2, wide) + [
-        pltpu.VMEM((8 * rows, cols), low), dma((4,)), dma((7,)), dma((7,)), dma(()),
+        pltpu.VMEM((8 * rows, cols), low), dma((4,)),
         pltpu.VMEM((8, LANES), f32), pltpu.VMEM((8, LANES), f32), dma((16,)),
     ] + reduce_scratch(counts, rows, width) + line_scratch(16, (8 * rows, cols), low)
     kernel = functools.partial(attend_kernel, rows, heads, cols, width, counts)
-    operands = [qkv, rms, cos, sin, mask, w_out, cot, w_down]
-    out_specs = [vm, pl.BlockSpec(memory_space=pl.ANY)] + [vm] * 6
-    return kernel_call(kernel, out_shape, operands, [vm] * 8, scratch, cid, "attend", out_specs, (4, 5, 7))
+    operands = [qkv, rms, cos, sin, mask, w_out, g_col, w_down]
+    out_specs = [vm, pl.BlockSpec(memory_space=pl.ANY)] + [vm] * 5
+    return kernel_call(kernel, out_shape, operands, [vm] * 8, scratch, cid, "attend", out_specs, (4, 5, 6, 7))
 
 
 def tail_kernel(rows, heads, per, d_attn, w_out, queries, kv, probs, rms, cos, sin, act_t, w_qkv, ffn, x_low,
@@ -1439,7 +1502,7 @@
 
     ffn_sum, leaving = take(2)
     by_chip = chip_place(here, per)
-    line = Line(here, line_counts, [ffn, ffn_sum] + take(8), by_chip)
+    line = Line(here, 6 * per, [ffn, ffn_sum] + take(8), lambda at: by_chip(at + 2 * per))
     contrib, summed = take(2)
     line_tok = Line(here, line_counts + extra, [contrib, summed] + take(8), place_tok)
     tiny = Tiny(here, tiny_own, tiny_all, (tiny_send, tiny_recv), False)
@@ -1597,7 +1660,13 @@
             value = x_low[row, :].astype(jnp.float32) + attn[row, :].astype(jnp.float32)
             leaving[at] = (value + source[row, :].astype(jnp.float32)).astype(out.dtype)
 
-        leave(ffn_sum)
+        @pl.when(at < 2 * per)
+        def _():
+            leave(ffn)
+
+        @pl.when(at >= 2 * per)
+        def _():
+            leave(ffn_sum)
 
     def is_own(which, at):
         return at < per if which == 0 else jnp.logical_and(at < 4, at % 2 == 0)
@@ -1632,10 +1701,10 @@
         def _():
             send(0, step - 1)
 
-        @pl.when(line.inner == 0)
-        def _():
-            line.up(step).wait_send()
-            line.down(step).wait_recv()
+        @pl.when(jnp.logical_and(line.inner == 0, step >= 2 * per))
+        def _():
+            line.up(step - 2 * per).wait_send()
+            line.down(step - 2 * per).wait_recv()
 
         emit(0, step)
 
@@ -1778,7 +1847,7 @@
         pltpu.VMEM((2, rows, wide), low), dma((2,)),
         pltpu.VMEM((total, cols), low),
         pltpu.VMEM((counts, chunk, cols), low),
-    ] + line_scratch(counts, (total, cols), low)
+    ] + line_scratch(6 * per, (6 * per * chunk, cols), low)
     scratch += [pltpu.VMEM(long, low), pltpu.VMEM(long, low)] + line_scratch(counts + extra, long, low)
     operands = [d_attn, w_out, queries, kv, probs, rms, cos, sin, act_t, w_qkv, ffn, x_low, attn, gain,
                 gain_grad, mixed_all]
@@ -1801,11 +1870,12 @@
     gain_one, gain_two = both[:2], both[2:]
     wider = jnp.float32
 
-    qkv, x_low, act_one_t, w_qkv, rms, cos, sin, mask = opening(
-        tokens, gain_one, w_query, kv_weight, segs, 1
-    )
-    attn, mixed_all, g_low, kv, probs, queries, pair_rms, d_hidden = attend(
-        qkv, rms, cos, sin, mask, w_out, d_out, w_down, 2
+    qkv, x_low, act_one_t, w_qkv, rms, cos, sin, mask, g_parts = opening(
+        tokens, gain_one, w_query, kv_weight, segs, d_out, 1
+    )
+    g_low = g_parts.reshape(x_low.shape)
+    attn, mixed_all, kv, probs, queries, pair_rms, d_hidden = attend(
+        qkv, rms, cos, sin, mask, w_out, g_low, w_down, 2
     )
     hidden, d_gate, d_up, act_two_t, dots = ffn_scatter(x_low, attn, gain_two, w_gate, w_up, d_hidden, 4)
     d_norm, grad_gain_two, grad_gate, grad_up = back_gather(

time: 639 us -> 629 us (0.984)
  Pallas kernels: 612 us -> 602 us
    pallas_call x6, Pallas kernels: 612 us -> 602 us  [kernel_call(): pl.pallas_call(body, out_shape=out_shape, in_specs=specs, out_specs=out_s...]
where the time goes in v13:
time: 629 us; the launch traced here: 628 us
  Pallas kernels  602 us (96%)
  other arithmetic  20 us (3%)
    pallas_call x6, Pallas kernels, kernel_call(): pl.pallas_call(body, out_shape=out_shape, in_specs=specs, out_specs=out_s...  602 us

profile of v13, /device:TPU:0, one launch (start us, length us, event | category | flops | bytes accessed | tf_op | source)
XLA Modules:
  0.0 628.4 jit_solution(13435644821569527632)
XLA Ops:
  0.6 0.7 convert_bitcast_fusion
  1.3 0.6 pad.4.refs_4_
  1.9 0.7 stack.11
  2.6 0.7 stack.12
  3.3 0.6 fusion
  3.9 67.5 %open_1.1 = (f32[256,1536]{1,0:T(8,128)}, bf16[2048,512]{1,0:T(8,128)(2,1)}, bf16[512,2048]{1,0:T(8,128)(2,1)}, bf16[512,1536]{1,0:T(8,128)(2,1)}, f32[256,128]{...) custom-call(bf16[256,4096]{1,0:T(8,128)(2,1)} %refs_0_.1, ...), custom_call_target="tpu_custom_call" | custom-call | tf_op jit(solution)/shard_map/open_1/pallas_call | solution.py:412
  71.4 88.1 %attend_2.1 = (bf16[2048,512]{1,0:T(8,128)(2,1)}, bf16[2048,1024]{1,0:T(8,128)(2,1)}, bf16[2,256,512]{2,1,0:T(8,128)(2,1)}, f32[4,256,512]{2,1,0:T(8,128)}, bf16...) custom-call(f32[256,1536]{1,0:T(8,128)} %get-tuple-element.46.refs_0_, ...), custom_call_target="tpu_custom_call" | custom-call | tf_op jit(solution)/shard_map/attend_2/pallas_call | solution.py:412
  159.5 117.0 %ffn_4.1 = (bf16[256,3072]{1,0:T(8,128)(2,1)}, bf16[256,3072]{1,0:T(8,128)(2,1)}, bf16[256,3072]{1,0:T(8,128)(2,1)}, bf16[512,2048]{1,0:T(8,128)(2,1)}, f32[8,128]{1,0:T(8,128)}) custom-call(bf16[2048,512]{1,0:T(8,128)(2,1)} %get-tuple-element.45.refs_0_.refs_6_.refs_11_, bf16[2048,512]{1,0:T(8,128)(2,1)} %get-tuple-element.51.refs_1_.refs_7_.refs_12_, ...), custom_call_target="tpu_custom_call" | custom-call | tf_op jit(solution)/shard_map/ffn_4/pallas_call | solution.py:412
  276.5 117.3 %back_5.1 = (bf16[2048,512]{1,0:T(8,128)(2,1)}, f32[1,512]{1,0:T(1,128)}, bf16[512,3072]{1,0:T(8,128)(2,1)}, bf16[512,3072]{1,0:T(8,128)(2,1)}) custom-call(bf16[512,2048]{1,0:T(8,128)(2,1)} %get-tuple-element.54.refs_0_, bf16[512,3072]{1,0:T(8,128)(2,1)} %refs_1_.3, bf16[512,3072]{1,0:T(8,128)(2,1)} %refs_2_.3, ...), custom_call_target="tpu_custom_call" | custom-call | tf_op jit(solution)/shard_map/back_5/pallas_call | solution.py:412
  393.8 77.9 %down_6.1 = (bf16[2048,512]{1,0:T(8,128)(2,1)}, bf16[2048,512]{1,0:T(8,128)(2,1)}, bf16[3072,512]{1,0:T(8,128)(2,1)}) custom-call(bf16[2048,512]{1,0:T(8,128)(2,1)} %bitcast.8, bf16[3072,512]{1,0:T(8,128)(2,1)} %refs_1_.4, bf16[256,3072]{1,0:T(8,128)(2,1)} %get-tuple-element.53.refs_2_, bf16[2048,512]{1,0:T(8,128)(2,1)} %get-tuple-element.58.refs_3_), custom_call_target="tpu_custom_call" | custom-call | tf_op jit(solution)/shard_map/down_6/pallas_call | solution.py:412
  471.7 134.2 %tail_7.1 = (bf16[256,4096]{1,0:T(8,128)(2,1)}, bf16[256,4096]{1,0:T(8,128)(2,1)}, bf16[512,1024]{1,0:T(8,128)(2,1)}, bf16[1024,512]{1,0:T(8,128)(2,1)}, bf16[512,512]{1,0:T(8,128)(2,1)}, /*index=5*/f32[4,8,128]{2,1,0:T(8,128)}) custom-call(bf16[2048,512]{1,0:T(8,128)(2,1)} %get-tuple-element.59.refs_0_, bf16[1024,512]{1,0:T(8,128)(2,1)} %refs_1_.5, ...), custom_call_target="tpu_custom_call" | custom-call | tf_op jit(solution)/shard_map/tail_7/pallas_call | solution.py:412
  605.9 0.0 copy-start.6
  606.0 0.8 reduce_sum.9
  606.8 0.6 slice_bitcast_fusion
  607.4 0.0 copy-start.5
  607.4 2.2 convert_element_type.33
  609.6 0.0 copy-done.6
  609.6 1.6 convert_element_type.32
  611.2 0.0 copy-done.5
  611.2 0.0 copy-start.3
  611.2 1.6 convert_element_type.34
  612.8 0.7 copy-done.3
  613.5 0.0 copy-start.2
  613.5 2.5 convert_element_type.31
  616.0 0.5 copy-done.2
  616.5 0.0 copy-start.1
  616.5 3.6 convert_element_type.37
  620.1 0.0 copy-done.1
  620.1 0.0 copy-start
  620.1 3.5 convert_element_type.35
  623.6 0.0 copy-done
  623.6 0.0 copy-start.4
  623.6 3.5 convert_element_type.36
  627.1 0.0 copy-done.4
  627.1 1.3 copy.22
  (1 shorter events, 0.0 us)
Async XLA Ops:
  605.9 3.6 copy-start.6
  607.4 3.8 copy-start.5
  611.2 2.3 copy-start.3
  613.5 3.0 copy-start.2
  616.5 3.6 copy-start.1
  620.1 3.5 copy-start
  623.6 3.5 copy-start.4

commit v14 on v13

--- a/solution.py
+++ b/solution.py
@@ -753,16 +753,19 @@
     lane = lax.broadcasted_iota(jnp.int32, (1, LANES), 1)
     line = lax.broadcasted_iota(jnp.int32, (LANES, 1), 0)
 
+    def ids_of(row):
+        return segs[2:3, pl.ds(pl.multiple_of(row * LANES, LANES), LANES)]
+
     def row_of(side, at):
         return ((here.seq + side) % 2) * tiles + at
 
     for side in range(2):
         for at in range(tiles):
             row = row_of(side, at)
-            ids = from_tile(segs[pl.ds(row, 1), :], eye)
+            ids = from_tile(ids_of(row), eye)
             before = jnp.zeros((LANES, 1), jnp.float32)
             for other in range(2 * tiles):
-                smaller = segs[other : other + 1, :] < ids
+                smaller = ids_of(other) < ids
                 before += jnp.sum(smaller.astype(jnp.float32), axis=-1, keepdims=True)
             index = row * LANES + line
             angles = (index.astype(jnp.float32) - before) * freqs
@@ -773,16 +776,16 @@
                 for key_side in range(2):
                     for key_at in range(tiles):
                         key_row = row_of(key_side, key_at)
-                        same = segs[pl.ds(key_row, 1), :] == ids
+                        same = ids_of(key_row) == ids
                         allowed = jnp.logical_and(same, key_row * LANES + lane <= index)
                         first = key_side * rows + key_at * LANES
                         mask[span, first : first + LANES] = allowed.astype(jnp.float32)
 
 
-def open_kernel(rows, width, counts, tokens, gain, w_query, kv_weight, segs, cot, qkv, x_low, act_t, w_qkv, rms, cos, sin,
+def open_kernel(rows, width, counts, tokens, gain, w_query, kv_weight, cot, qkv, x_low, act_t, w_qkv, rms, cos, sin,
                 mask, g_col, *refs):
     here = Place()
-    cols = gain.shape[1]
+    cols, segs = gain.shape[1], gain
     act, turn_send, turn_recv, local_sems, cot_part, g_send, g_recv, z_send, z_recv = refs[:9]
     share = rows // 4
     me = here.shard(0, 0)
@@ -912,7 +915,7 @@
             quarter(1, here.z + step, step, -1).wait_send()
 
 
-def opening(tokens, gain, w_query, kv_weight, segs, cot, cid, width=256):
+def opening(tokens, gain, w_query, kv_weight, cot, cid, width=256):
     rows = tokens.shape[0]
     cols, wide = w_query.shape
     every = wide + kv_weight.shape[1]
@@ -938,8 +941,8 @@
     ]
     scratch += reduce_scratch(counts, rows, width)
     kernel = functools.partial(open_kernel, rows, width, counts)
-    return kernel_call(kernel, out_shape, [tokens, gain, w_query, kv_weight, segs, cot],
-                       [vm, vm, hbm, hbm, vm, hbm], scratch, cid, "open")
+    return kernel_call(kernel, out_shape, [tokens, gain, w_query, kv_weight, cot],
+                       [vm, vm, hbm, hbm, hbm], scratch, cid, "open")
 
 
 def ffn_kernel(rows, width, counts, x_low, attn, gain, w_gate, w_up, d_hidden, hidden, d_gate, d_up, act_t, tile_out,
@@ -962,7 +965,7 @@
         for at in range(rows // LANES):
             span = pl.ds(pl.multiple_of(shard * rows + at * LANES, LANES), LANES)
             resid = x_low[span, :].astype(jnp.float32) + attn[span, :].astype(jnp.float32)
-            act[span, :] = (resid * gain[0:1, :]).astype(act.dtype)
+            act[span, :] = (resid * gain[1:2, :]).astype(act.dtype)
             square = jnp.sum(resid * resid, axis=-1, keepdims=True)
             tiny_own[shard, at : at + 1, :] = jnp.sum(square * eye, axis=0, keepdims=True)
         return 0
@@ -1120,7 +1123,7 @@
                 dot = from_tile(tiny_all[shard, at : at + 1, :], eye)
                 resid = rest[0, piece, :].astype(jnp.float32) + rest[1, piece, :].astype(jnp.float32)
                 value = sums[span, :]
-                target[span, :] = (value * gain[0:1, :] - resid * dot).astype(target.dtype)
+                target[span, :] = (value * gain[1:2, :] - resid * dot).astype(target.dtype)
                 gain_grad[...] += jnp.sum(value * resid, axis=0, keepdims=True)
             return 0
 
@@ -1201,10 +1204,9 @@
 def down_kernel(rows, width, counts, cot, weight, hidden, d_norm, ffn, d_attn, grad, *refs, late):
     here = Place()
     spread = Spread(here, counts, refs[:7])
-    own_sems, sums, grads, staged, out_sems, norm_out, part = refs[7:14]
+    own_sems, sums, grads, staged, out_sems, norm_out = refs[7:13]
     place = chip_place(here, 4)
-    norm_line = Line(here, 24, [d_norm, norm_out] + list(refs[14:22]), lambda at: place(at + 8))
-    line = Line(here, 4, [part, ffn] + list(refs[22:]), chip_place(here, 2))
+    norm_line = Line(here, 24, [d_norm, norm_out] + list(refs[13:]), lambda at: place(at + 8))
     own = load_own(spread, (hidden,), width, counts, own_sems)
     for copy in own:
         copy.start()
@@ -1247,28 +1249,8 @@
             leave(0, at).start()
             leave(1, at).start()
 
-        @pl.when(jnp.logical_and(at == counts - 1, stage == 0))
-        def _():
-            close_chip(0, part)
-            line.launch(0, 4)
-
-    def close_chip(chip, target):
-        def close_shard(other, _):
-            span = row_span(here, chip, other, rows)
-            target[span, :] = sums[span, :].astype(target.dtype)
-            return 0
-
-        lax.fori_loop(0, 2, close_shard, 0)
-
-    def hook(step):
-        norm_line.step(step)
-
-        @pl.when(step >= 4 * counts - 5)
-        def _():
-            line.step(step - (4 * counts - 5))
-
-    norm_line.steps(spread.run(blocks, hook, done), 26)
-    lax.fori_loop(1, 4, lambda chip, _: (close_chip(chip, ffn), 0)[1], 0)
+    norm_line.steps(spread.run(blocks, norm_line.step, done), 26)
+    ffn[...] = sums[...].astype(ffn.dtype)
     norm_line.settle()
 
     def add_norm(at, _):
@@ -1287,7 +1269,6 @@
         return 0
 
     lax.fori_loop(0, 8, add_norm, 0)
-    line.settle()
     spread.end()
 
     def drain(at, _):
@@ -1318,8 +1299,7 @@
         pltpu.VMEM((2, 2, width, cols), low),
         dma((2, counts)),
         pltpu.VMEM((total, cols), low),
-        pltpu.VMEM((total, cols), low),
-    ] + line_scratch(24, (24 * rows // 4, cols), low) + line_scratch(4, (4 * rows // 2, cols), low)
+    ] + line_scratch(24, (24 * rows // 4, cols), low)
     kernel = functools.partial(down_kernel, rows, width, counts)
     return kernel_call(kernel, out_shape, [cot, weight, hidden, d_norm], [vm, vm, hbm, vm], scratch, cid, "down",
                        [vm, vm, hbm], (0, 1))
@@ -1338,7 +1318,7 @@
         across, other, half_at = spread.block(at)
         return here.shard(across, other) * 2 + half_at
 
-    line = Line(here, 16, [part, attn] + list(refs[23:]), place)
+    line = Line(here, 32, [part, attn] + list(refs[23:]), lambda at: place(at // 2) * 2 + at % 2)
     got, core = spread.got, here.core
     greet(here, slice_peers(here), True)
     half = HD // 2
@@ -1406,7 +1386,7 @@
             value = dot_nn(got[across, (core + other) % 2, half_at, 0], w_out[...])
             part[pl.ds(pl.multiple_of(place(step) * piece, piece), piece), :] = value.astype(part.dtype)
             mixed_copy(step).start()
-            line.launch(step, 1)
+            line.launch(2 * step, 2)
 
         @pl.when(step >= 2)
         def _():
@@ -1414,11 +1394,12 @@
 
         @pl.when(step >= 4)
         def _():
-            line.step(step - 4)
+            line.step(2 * step - 8)
+            line.step(2 * step - 7)
         return 0
 
-    lax.fori_loop(0, 4 + max(16, total.steps + 1), one_step, 0)
-    line.end(max(16, total.steps + 1))
+    lax.fori_loop(0, 20, one_step, 0)
+    line.end(32)
 
     def emit(at, first, second):
         for half_at, value in enumerate((first, second)):
@@ -1459,7 +1440,7 @@
     scratch = spread_scratch(1, rows // 2, wide) + [
         pltpu.VMEM((8 * rows, cols), low), dma((4,)),
         pltpu.VMEM((8, LANES), f32), pltpu.VMEM((8, LANES), f32), dma((16,)),
-    ] + reduce_scratch(counts, rows, width) + line_scratch(16, (8 * rows, cols), low)
+    ] + reduce_scratch(counts, rows, width) + line_scratch(32, (8 * rows, cols), low)
     kernel = functools.partial(attend_kernel, rows, heads, cols, width, counts)
     operands = [qkv, rms, cos, sin, mask, w_out, g_col, w_down]
     out_specs = [vm, pl.BlockSpec(memory_space=pl.ANY)] + [vm] * 5
@@ -1502,7 +1483,7 @@
 
     ffn_sum, leaving = take(2)
     by_chip = chip_place(here, per)
-    line = Line(here, 6 * per, [ffn, ffn_sum] + take(8), lambda at: by_chip(at + 2 * per))
+    line = Line(here, line_counts, [ffn, ffn_sum] + take(8), by_chip)
     contrib, summed = take(2)
     line_tok = Line(here, line_counts + extra, [contrib, summed] + take(8), place_tok)
     tiny = Tiny(here, tiny_own, tiny_all, (tiny_send, tiny_recv), False)
@@ -1660,13 +1641,7 @@
             value = x_low[row, :].astype(jnp.float32) + attn[row, :].astype(jnp.float32)
             leaving[at] = (value + source[row, :].astype(jnp.float32)).astype(out.dtype)
 
-        @pl.when(at < 2 * per)
-        def _():
-            leave(ffn)
-
-        @pl.when(at >= 2 * per)
-        def _():
-            leave(ffn_sum)
+        leave(ffn_sum)
 
     def is_own(which, at):
         return at < per if which == 0 else jnp.logical_and(at < 4, at % 2 == 0)
@@ -1701,10 +1676,10 @@
         def _():
             send(0, step - 1)
 
-        @pl.when(jnp.logical_and(line.inner == 0, step >= 2 * per))
-        def _():
-            line.up(step - 2 * per).wait_send()
-            line.down(step - 2 * per).wait_recv()
+        @pl.when(line.inner == 0)
+        def _():
+            line.up(step).wait_send()
+            line.down(step).wait_recv()
 
         emit(0, step)
 
@@ -1847,7 +1822,7 @@
         pltpu.VMEM((2, rows, wide), low), dma((2,)),
         pltpu.VMEM((total, cols), low),
         pltpu.VMEM((counts, chunk, cols), low),
-    ] + line_scratch(6 * per, (6 * per * chunk, cols), low)
+    ] + line_scratch(counts, (total, cols), low)
     scratch += [pltpu.VMEM(long, low), pltpu.VMEM(long, low)] + line_scratch(counts + extra, long, low)
     operands = [d_attn, w_out, queries, kv, probs, rms, cos, sin, act_t, w_qkv, ffn, x_low, attn, gain,
                 gain_grad, mixed_all]
@@ -1857,29 +1832,90 @@
                        late=(2, 3, 4, 8, 9, 11, 12))
 
 
+def widen_kernel(plan, *refs):
+    count = len(plan)
+    sources, results, scratch = refs[:count], refs[count : 2 * count], refs[2 * count :]
+
+    def part(ref, at, step):
+        span = plan[at][0]
+        return ref.at[pl.ds(pl.multiple_of(step * span, span), span), :]
+
+    def load(at, step):
+        taken, sems = scratch[4 * at], scratch[4 * at + 2]
+        return pltpu.make_async_copy(part(sources[at], at, step), taken.at[step % 3], sems.at[step % 3])
+
+    def store(at, step):
+        given, sems = scratch[4 * at + 1], scratch[4 * at + 3]
+        return pltpu.make_async_copy(given.at[step % 3], part(results[at], at, step), sems.at[step % 3])
+
+    for at, (_, steps) in enumerate(plan):
+        for step in range(min(3, steps)):
+            load(at, step).start()
+    for at, (_, steps) in enumerate(plan):
+        taken, given = scratch[4 * at], scratch[4 * at + 1]
+
+        def one(step, _, at=at, steps=steps, taken=taken, given=given):
+            load(at, step).wait()
+
+            @pl.when(step >= 3)
+            def _():
+                store(at, step - 3).wait()
+
+            given[step % 3] = taken[step % 3].astype(given.dtype)
+            store(at, step).start()
+
+            @pl.when(step + 3 < steps)
+            def _():
+                load(at, step + 3).start()
+            return 0
+
+        lax.fori_loop(0, steps, one, 0)
+    for at, (_, steps) in enumerate(plan):
+        for step in range(max(0, steps - 3), steps):
+            store(at, step).wait()
+
+
+def widen(arrays, block=2 ** 17):
+    plan, scratch = [], []
+    dma = pltpu.SemaphoreType.DMA
+    for array in arrays:
+        height, width = array.shape
+        span = min(height, max(8, block // width))
+        while height % span:
+            span //= 2
+        plan.append((span, height // span))
+        scratch += [pltpu.VMEM((3, span, width), array.dtype), pltpu.VMEM((3, span, width), jnp.float32),
+                    dma((3,)), dma((3,))]
+    hbm = pl.BlockSpec(memory_space=pl.ANY)
+    return pl.pallas_call(
+        functools.partial(widen_kernel, tuple(plan)),
+        out_shape=[jax.ShapeDtypeStruct(array.shape, jnp.float32) for array in arrays],
+        in_specs=[hbm] * len(arrays),
+        out_specs=[hbm] * len(arrays),
+        scratch_shapes=scratch,
+        compiler_params=pltpu.CompilerParams(vmem_limit_bytes=VMEM_LIMIT),
+        name="widen",
+    )(*arrays)
+
+
 LANES = 128
 
 
 def acts_move(
     tokens, seg_ids, gain_attn, w_query, kv_weight, w_out, gain_ffn, w_gate, w_up, w_down, d_out
 ):
-    rows = tokens.shape[0]
-    segs = seg_ids.astype(jnp.float32).reshape(2 * rows // LANES, LANES)
-    segs = jnp.pad(segs, ((0, 8 - 2 * rows // LANES), (0, 0)))
-    both = jnp.stack([gain_attn, gain_ffn, gain_ffn, gain_attn]).astype(jnp.float32)
-    gain_one, gain_two = both[:2], both[2:]
-    wider = jnp.float32
+    small = jnp.stack([gain_attn, gain_ffn, seg_ids.astype(gain_ffn.dtype), gain_attn]).astype(jnp.float32)
 
     qkv, x_low, act_one_t, w_qkv, rms, cos, sin, mask, g_parts = opening(
-        tokens, gain_one, w_query, kv_weight, segs, d_out, 1
+        tokens, small, w_query, kv_weight, d_out, 1
     )
     g_low = g_parts.reshape(x_low.shape)
     attn, mixed_all, kv, probs, queries, pair_rms, d_hidden = attend(
         qkv, rms, cos, sin, mask, w_out, g_low, w_down, 2
     )
-    hidden, d_gate, d_up, act_two_t, dots = ffn_scatter(x_low, attn, gain_two, w_gate, w_up, d_hidden, 4)
+    hidden, d_gate, d_up, act_two_t, dots = ffn_scatter(x_low, attn, small, w_gate, w_up, d_hidden, 4)
     d_norm, grad_gain_two, grad_gate, grad_up = back_gather(
-        act_two_t, w_gate, w_up, d_gate, d_up, dots, x_low, attn, gain_two, 5
+        act_two_t, w_gate, w_up, d_gate, d_up, dots, x_low, attn, small, 5
     )
     ffn, d_attn, grad_down = down_gather(g_low, w_down, hidden, d_norm, 6)
     d_tokens, out, grad_query, grad_out, grad_kv, gain_tiles = tail(
@@ -1896,23 +1932,26 @@
         ffn,
         x_low,
         attn,
-        gain_one,
+        small,
         grad_gain_two,
         mixed_all,
         7,
     )
     gains = jnp.sum(gain_tiles, axis=0).reshape(2, -1)
+    d_tokens, grad_query, grad_kv, grad_out, grad_gate, grad_up, grad_down = widen(
+        [d_tokens, grad_query, grad_kv, grad_out, grad_gate, grad_up, grad_down]
+    )
     return (
         out,
-        d_tokens.astype(wider),
+        d_tokens,
         gains[0],
-        grad_query.astype(wider),
-        grad_kv.astype(wider),
-        grad_out.astype(wider),
+        grad_query,
+        grad_kv,
+        grad_out,
         gains[1],
-        grad_gate.astype(wider),
-        grad_up.astype(wider),
-        grad_down.astype(wider),
+        grad_gate,
+        grad_up,
+        grad_down,
     )
 
 

time: 629 us -> 752 us (1.20); the launches traced: 628 us -> 740 us
  Pallas kernels: 602 us -> 732 us
  other arithmetic: 20 us -> 2.03 us
    pallas_call x0 -> x1, Pallas kernels: none -> 134 us  [widen(): pl.pallas_call(functools.partial(widen_kernel, tuple(plan)), out_shape=[j...]
    convert_element_type x8 -> x2, other arithmetic: 18.5 us -> 1.3 us  [the longest x1 0.69 us: acts_move(): seg_ids.astype(gain_ffn.dtype)]
where the time goes in v14:
time: 752 us; the launch traced here: 740 us
  Pallas kernels  732 us (97%)
    pallas_call x6, Pallas kernels, kernel_call(): pl.pallas_call(body, out_shape=out_shape, in_specs=specs, out_specs=out_s...  598 us
    pallas_call x1, Pallas kernels, widen(): pl.pallas_call(functools.partial(widen_kernel, tuple(plan)), out_shape=[j...  134 us

profile of v14, /device:TPU:0, one launch (start us, length us, event | category | flops | bytes accessed | tf_op | source)
XLA Modules:
  0.0 740.3 jit_solution(12365117091448862072)
XLA Ops:
  0.6 0.7 convert_element_type.6
  1.3 0.7 stack.13
  2.0 0.7 stack.14
  2.7 0.6 maximum_convert_fusion.refs_1_.refs_2_.refs_8_.refs_13_
  3.3 67.5 %open_1.1 = (f32[256,1536]{1,0:T(8,128)}, bf16[2048,512]{1,0:T(8,128)(2,1)}, bf16[512,2048]{1,0:T(8,128)(2,1)}, bf16[512,1536]{1,0:T(8,128)(2,1)}, f32[256,128]{...) custom-call(bf16[256,4096]{1,0:T(8,128)(2,1)} %refs_0_.1, ...), custom_call_target="tpu_custom_call" | custom-call | tf_op jit(solution)/shard_map/open_1/pallas_call | solution.py:412
  70.8 89.0 %attend_2.1 = (bf16[2048,512]{1,0:T(8,128)(2,1)}, bf16[2048,1024]{1,0:T(8,128)(2,1)}, bf16[2,256,512]{2,1,0:T(8,128)(2,1)}, f32[4,256,512]{2,1,0:T(8,128)}, bf16...) custom-call(f32[256,1536]{1,0:T(8,128)} %get-tuple-element.53.refs_0_, ...), custom_call_target="tpu_custom_call" | custom-call | tf_op jit(solution)/shard_map/attend_2/pallas_call | solution.py:412
  159.8 117.0 %ffn_4.1 = (bf16[256,3072]{1,0:T(8,128)(2,1)}, bf16[256,3072]{1,0:T(8,128)(2,1)}, bf16[256,3072]{1,0:T(8,128)(2,1)}, bf16[512,2048]{1,0:T(8,128)(2,1)}, f32[8,128]{1,0:T(8,128)}) custom-call(bf16[2048,512]{1,0:T(8,128)(2,1)} %get-tuple-element.52.refs_0_.refs_6_.refs_11_, bf16[2048,512]{1,0:T(8,128)(2,1)} %get-tuple-element.58.refs_1_.refs_7_.refs_12_, ...), custom_call_target="tpu_custom_call" | custom-call | tf_op jit(solution)/shard_map/ffn_4/pallas_call | solution.py:412
  276.8 117.2 %back_5.1 = (bf16[2048,512]{1,0:T(8,128)(2,1)}, f32[1,512]{1,0:T(1,128)}, bf16[512,3072]{1,0:T(8,128)(2,1)}, bf16[512,3072]{1,0:T(8,128)(2,1)}) custom-call(bf16[512,2048]{1,0:T(8,128)(2,1)} %get-tuple-element.61.refs_0_, bf16[512,3072]{1,0:T(8,128)(2,1)} %refs_1_.3, bf16[512,3072]{1,0:T(8,128)(2,1)} %refs_2_.3, ...), custom_call_target="tpu_custom_call" | custom-call | tf_op jit(solution)/shard_map/back_5/pallas_call | solution.py:412
  394.0 70.1 %down_6.1 = (bf16[2048,512]{1,0:T(8,128)(2,1)}, bf16[2048,512]{1,0:T(8,128)(2,1)}, bf16[3072,512]{1,0:T(8,128)(2,1)}) custom-call(bf16[2048,512]{1,0:T(8,128)(2,1)} %bitcast.6, bf16[3072,512]{1,0:T(8,128)(2,1)} %refs_1_.4, bf16[256,3072]{1,0:T(8,128)(2,1)} %get-tuple-element.60.refs_2_, bf16[2048,512]{1,0:T(8,128)(2,1)} %get-tuple-element.65.refs_3_), custom_call_target="tpu_custom_call" | custom-call | tf_op jit(solution)/shard_map/down_6/pallas_call | solution.py:412
  464.1 137.3 %tail_7.1 = (bf16[256,4096]{1,0:T(8,128)(2,1)}, bf16[256,4096]{1,0:T(8,128)(2,1)}, bf16[512,1024]{1,0:T(8,128)(2,1)}, bf16[1024,512]{1,0:T(8,128)(2,1)}, bf16[512,512]{1,0:T(8,128)(2,1)}, /*index=5*/f32[4,8,128]{2,1,0:T(8,128)}) custom-call(bf16[2048,512]{1,0:T(8,128)(2,1)} %get-tuple-element.66.refs_0_, bf16[1024,512]{1,0:T(8,128)(2,1)} %refs_1_.5, ...), custom_call_target="tpu_custom_call" | custom-call | tf_op jit(solution)/shard_map/tail_7/pallas_call | solution.py:412
  601.4 0.7 reduce_sum.9
  602.1 0.6 slice_bitcast_fusion
  602.7 134.4 %widen.1 = (f32[256,4096]{1,0:T(8,128)}, f32[512,1024]{1,0:T(8,128)}, f32[512,512]{1,0:T(8,128)}, f32[1024,512]{1,0:T(8,128)}, f32[512,3072]{1,0:T(8,128)}, /*index=5*/f32[512,3072]{1,0:T(8,128)}, f32[3072,512]{1,0:T(8,128)}) custom-call(bf16[256,4096]{1,0:T(8,128)(2,1)} %get-tuple-element.77.refs_0_, bf16[512,1024]{1,0:T(8,128)(2,1)} %get-tuple-element.78.refs_1_, ...), custom_call_target="tpu_custom_call" | custom-call | tf_op jit(solution)/shard_map/widen/pallas_call | solution.py:1890
  737.1 3.1 copy.22
  (1 shorter events, 0.0 us)

commit v15 on v14

--- a/solution.py
+++ b/solution.py
@@ -282,7 +282,8 @@
         self.own, self.out, self.from_end, self.from_mid = refs[:4]
         self.sems = refs[4:10]
         self.counts = counts
-        self.chunk = self.from_end.shape[1]
+        self.chunk = self.from_mid.shape[1]
+        self.fold = self.from_end.shape[1] // self.chunk
         self.place = place
         z = here.z
         self.inner = ((z + 1) // 2) % 2
@@ -293,8 +294,12 @@
         at = at if self.place is None else self.place(at)
         return pl.ds(pl.multiple_of(at * self.chunk, self.chunk), self.chunk)
 
+    def inbox(self, at):
+        span = pl.ds(pl.multiple_of(at % self.fold * self.chunk, self.chunk), self.chunk)
+        return self.from_end.at[at // self.fold, span, :]
+
     def up(self, at):
-        return remote(self.own.at[self.rows(at), :], self.from_end.at[at], self.sems[0].at[at],
+        return remote(self.own.at[self.rows(at), :], self.inbox(at), self.sems[0].at[at],
                       self.sems[1].at[at], self.mate)
 
     def over(self, at):
@@ -321,7 +326,7 @@
     def first(self, at):
         rows = self.rows(at)
         self.up(at).wait_recv()
-        total = self.own[rows, :].astype(jnp.float32) + self.from_end[at].astype(jnp.float32)
+        total = self.own[rows, :].astype(jnp.float32) + self.inbox(at)[...].astype(jnp.float32)
         self.out[rows, :] = total.astype(self.out.dtype)
         self.over(at).start()
 
@@ -376,9 +381,10 @@
         self.settle()
 
 
-def line_scratch(counts, shape, low):
-    buf = pltpu.VMEM((counts, shape[0] // counts, shape[1]), low)
-    return [buf, buf] + [pltpu.SemaphoreType.DMA((counts,))] * 6
+def line_scratch(counts, shape, low, fold=1):
+    chunk = shape[0] // counts
+    inbox = pltpu.VMEM((counts // fold, chunk * fold, shape[1]), low)
+    return [inbox, pltpu.VMEM((counts, chunk, shape[1]), low)] + [pltpu.SemaphoreType.DMA((counts,))] * 6
 
 
 def turned(at):
@@ -961,7 +967,8 @@
     eye = diagonal()
     tiny_own[...] = jnp.zeros_like(tiny_own)
 
-    def prepare(shard, _):
+    def prepare(number, _):
+        shard = here.shard(*turned(number))
         for at in range(rows // LANES):
             span = pl.ds(pl.multiple_of(shard * rows + at * LANES, LANES), LANES)
             resid = x_low[span, :].astype(jnp.float32) + attn[span, :].astype(jnp.float32)
@@ -970,13 +977,19 @@
             tiny_own[shard, at : at + 1, :] = jnp.sum(square * eye, axis=0, keepdims=True)
         return 0
 
-    lax.fori_loop(0, 8, prepare, 0)
+    def before(stop):
+        if stop == 1:
+            lax.fori_loop(2, 6, prepare, 0)
+        if stop == 2:
+            lax.fori_loop(6, 8, prepare, 0)
+            tiny.begin()
+
+    lax.fori_loop(0, 2, prepare, 0)
     greet(here, slice_peers(here))
-    tiny.begin()
     for copy in local:
         copy.wait()
     product = products(here, act, weight, False, rows, width, counts)
-    total = Reduce(here, counts, product, refs[8:19])
+    total = Reduce(here, counts, product, refs[8:19], before)
     total.run()
 
     def flip(shard, _):
@@ -1479,13 +1492,15 @@
 
     def place_tok(at):
         across, other, half_at = near(at)
-        return jnp.where(at < line_counts, here.shard(across, other) * per + half_at, at)
+        return here.shard(across, other) * per + half_at
+
+    def place_half(at):
+        return jnp.where(at < 2 * line_counts, 2 * place_tok(at // 2) + at % 2, at)
 
     ffn_sum, leaving = take(2)
-    by_chip = chip_place(here, per)
-    line = Line(here, line_counts, [ffn, ffn_sum] + take(8), by_chip)
+    line = Line(here, 2 * line_counts, [ffn, ffn_sum] + take(8), chip_place(here, 2 * per))
     contrib, summed = take(2)
-    line_tok = Line(here, line_counts + extra, [contrib, summed] + take(8), place_tok)
+    line_tok = Line(here, 2 * (line_counts + extra), [contrib, summed] + take(8), place_half)
     tiny = Tiny(here, tiny_own, tiny_all, (tiny_send, tiny_recv), False)
     got, core = spread.got, here.core
     product = products(here, d_attn, w_out, True, rows, width, counts)
@@ -1500,8 +1515,12 @@
 
     mixed_copy(0).start()
 
+    def both_steps(which, at):
+        which.step(2 * at)
+        which.step(2 * at + 1)
+
     def beside(step):
-        line.step(step)
+        both_steps(line, step)
 
         @pl.when(step < 8)
         def _():
@@ -1548,7 +1567,7 @@
         lead, trail = d_query[:, :half], d_query[:, half:]
         first = ((lead * cos[0] + trail * sin[0]) * rms[0]).astype(got.dtype)
         second = ((trail * cos[0] - lead * sin[0]) * rms[0]).astype(got.dtype)
-        line.step(done + head)
+        both_steps(line, done + head)
         for rows_at in range(2):
             piece = slice(rows_at * part, (rows_at + 1) * part)
             got[0, core, rows_at, 0, :, pl.ds(pl.multiple_of(head * HD, HD), half)] = first[piece, :]
@@ -1603,7 +1622,7 @@
             x_rows = x_low[row, :].astype(jnp.float32)
             contrib[row, :] = (value * gain[0:1, :] - x_rows * dot).astype(contrib.dtype)
             gain_sum[...] += jnp.sum(value * x_rows, axis=0, keepdims=True)
-        line_tok.launch(at, 1)
+        line_tok.launch(2 * at, 2)
         rows_t = act_t[:, pl.ds(first, part)]
         for at_col in range((heads + 2) * HD // 512):
             span = slice(at_col * 512, (at_col + 1) * 512)
@@ -1611,7 +1630,7 @@
 
     me = here.shard(0, 0)
     columns = pl.ds(pl.multiple_of(me * cols, cols), cols)
-    chunk = line.chunk
+    chunk = rows // per
 
     def landing(which, at):
         sub = at % per if which == 0 else near(at)[2]
@@ -1631,7 +1650,7 @@
 
     def emit(which, at):
         if which == 1:
-            row = line_tok.rows(at)
+            row = pl.ds(pl.multiple_of(place_tok(at) * chunk, chunk), chunk)
             value = d_attn[row, :].astype(jnp.float32) + summed[row, :].astype(jnp.float32)
             line_tok.from_end[at] = value.astype(out.dtype)
             return
@@ -1666,11 +1685,11 @@
 
         @pl.when(step < 5)
         def _():
-            line.step(done + heads + step)
+            both_steps(line, done + heads + step)
 
         @pl.when(step >= 4)
         def _():
-            line_tok.step(step - 4)
+            both_steps(line_tok, step - 4)
 
         @pl.when(step > 0)
         def _():
@@ -1678,8 +1697,9 @@
 
         @pl.when(line.inner == 0)
         def _():
-            line.up(step).wait_send()
-            line.down(step).wait_recv()
+            for last in range(2):
+                line.up(2 * step + last).wait_send()
+                line.down(2 * step + last).wait_recv()
 
         emit(0, step)
 
@@ -1697,7 +1717,7 @@
         span = pl.ds(line_counts * (rows // per) + half_at * (rows // per), rows // per)
         source = slice(half_at * (rows // per), (half_at + 1) * (rows // per))
         contrib[span, :] = grad[source, heads * HD :].astype(contrib.dtype)
-    line_tok.launch(line_counts, extra)
+    line_tok.launch(2 * line_counts, 2 * extra)
     grad_query[...] = grad[:, : heads * HD].astype(grad_query.dtype)
     for at in range(cols // LANES):
         tile[at : at + 1, :] = gain_sum[:, at * LANES : (at + 1) * LANES]
@@ -1719,7 +1739,7 @@
         start = line_counts - 4
 
         def both(at, _):
-            line_tok.step(at)
+            both_steps(line_tok, at)
 
             @pl.when(at < line_counts + 4)
             def _():
@@ -1736,13 +1756,14 @@
             line_tok.down(at).wait_send()
             return 0
 
-        lax.fori_loop(0, line_counts + extra, drain, 0)
+        lax.fori_loop(0, 2 * (line_counts + extra), drain, 0)
 
     @pl.when(line.inner == 0)
     def _():
         def arrive(at, _):
-            line_tok.up(at).wait_send()
-            line_tok.down(at).wait_recv()
+            for last in range(2):
+                line_tok.up(2 * at + last).wait_send()
+                line_tok.down(2 * at + last).wait_recv()
 
             @pl.when(jnp.logical_and(at > 0, at <= line_counts))
             def _():
@@ -1822,80 +1843,14 @@
         pltpu.VMEM((2, rows, wide), low), dma((2,)),
         pltpu.VMEM((total, cols), low),
         pltpu.VMEM((counts, chunk, cols), low),
-    ] + line_scratch(counts, (total, cols), low)
-    scratch += [pltpu.VMEM(long, low), pltpu.VMEM(long, low)] + line_scratch(counts + extra, long, low)
+    ] + line_scratch(2 * counts, (total, cols), low)
+    scratch += [pltpu.VMEM(long, low), pltpu.VMEM(long, low)] + line_scratch(2 * (counts + extra), long, low, 2)
     operands = [d_attn, w_out, queries, kv, probs, rms, cos, sin, act_t, w_qkv, ffn, x_low, attn, gain,
                 gain_grad, mixed_all]
     kernel = functools.partial(tail_kernel, rows, heads, per)
     specs = [vm] * (len(operands) - 1) + [pl.BlockSpec(memory_space=pl.ANY)]
     return kernel_call(kernel, out_shape, operands, specs, scratch, cid, "tail",
                        late=(2, 3, 4, 8, 9, 11, 12))
-
-
-def widen_kernel(plan, *refs):
-    count = len(plan)
-    sources, results, scratch = refs[:count], refs[count : 2 * count], refs[2 * count :]
-
-    def part(ref, at, step):
-        span = plan[at][0]
-        return ref.at[pl.ds(pl.multiple_of(step * span, span), span), :]
-
-    def load(at, step):
-        taken, sems = scratch[4 * at], scratch[4 * at + 2]
-        return pltpu.make_async_copy(part(sources[at], at, step), taken.at[step % 3], sems.at[step % 3])
-
-    def store(at, step):
-        given, sems = scratch[4 * at + 1], scratch[4 * at + 3]
-        return pltpu.make_async_copy(given.at[step % 3], part(results[at], at, step), sems.at[step % 3])
-
-    for at, (_, steps) in enumerate(plan):
-        for step in range(min(3, steps)):
-            load(at, step).start()
-    for at, (_, steps) in enumerate(plan):
-        taken, given = scratch[4 * at], scratch[4 * at + 1]
-
-        def one(step, _, at=at, steps=steps, taken=taken, given=given):
-            load(at, step).wait()
-
-            @pl.when(step >= 3)
-            def _():
-                store(at, step - 3).wait()
-
-            given[step % 3] = taken[step % 3].astype(given.dtype)
-            store(at, step).start()
-
-            @pl.when(step + 3 < steps)
-            def _():
-                load(at, step + 3).start()
-            return 0
-
-        lax.fori_loop(0, steps, one, 0)
-    for at, (_, steps) in enumerate(plan):
-        for step in range(max(0, steps - 3), steps):
-            store(at, step).wait()
-
-
-def widen(arrays, block=2 ** 17):
-    plan, scratch = [], []
-    dma = pltpu.SemaphoreType.DMA
-    for array in arrays:
-        height, width = array.shape
-        span = min(height, max(8, block // width))
-        while height % span:
-            span //= 2
-        plan.append((span, height // span))
-        scratch += [pltpu.VMEM((3, span, width), array.dtype), pltpu.VMEM((3, span, width), jnp.float32),
-                    dma((3,)), dma((3,))]
-    hbm = pl.BlockSpec(memory_space=pl.ANY)
-    return pl.pallas_call(
-        functools.partial(widen_kernel, tuple(plan)),
-        out_shape=[jax.ShapeDtypeStruct(array.shape, jnp.float32) for array in arrays],
-        in_specs=[hbm] * len(arrays),
-        out_specs=[hbm] * len(arrays),
-        scratch_shapes=scratch,
-        compiler_params=pltpu.CompilerParams(vmem_limit_bytes=VMEM_LIMIT),
-        name="widen",
-    )(*arrays)
 
 
 LANES = 128
@@ -1938,20 +1893,18 @@
         7,
     )
     gains = jnp.sum(gain_tiles, axis=0).reshape(2, -1)
-    d_tokens, grad_query, grad_kv, grad_out, grad_gate, grad_up, grad_down = widen(
-        [d_tokens, grad_query, grad_kv, grad_out, grad_gate, grad_up, grad_down]
-    )
+    wider = jnp.float32
     return (
         out,
-        d_tokens,
+        d_tokens.astype(wider),
         gains[0],
-        grad_query,
-        grad_kv,
-        grad_out,
+        grad_query.astype(wider),
+        grad_kv.astype(wider),
+        grad_out.astype(wider),
         gains[1],
-        grad_gate,
-        grad_up,
-        grad_down,
+        grad_gate.astype(wider),
+        grad_up.astype(wider),
+        grad_down.astype(wider),
     )
 
 

time: 752 us -> 636 us (0.85); the launches traced: 740 us -> 635 us
  Pallas kernels: 732 us -> 609 us
  other arithmetic: 2.03 us -> 20.6 us
    pallas_call x1 -> x0, Pallas kernels: 134 us -> none  [widen(): pl.pallas_call(functools.partial(widen_kernel, tuple(plan)), out_shape=[j...]
    convert_element_type x0 -> x7, other arithmetic: none -> 18.5 us  [the longest x1 3.6 us: acts_move(): grad_down.astype(wider)]
    pallas_call x6, Pallas kernels: 598 us -> 609 us  [kernel_call(): pl.pallas_call(body, out_shape=out_shape, in_specs=specs, out_specs=out_s...]
where the time goes in v15:
time: 636 us; the launch traced here: 635 us
  Pallas kernels  609 us (96%)
  other arithmetic  20.6 us (3%)
    pallas_call x6, Pallas kernels, kernel_call(): pl.pallas_call(body, out_shape=out_shape, in_specs=specs, out_specs=out_s...  609 us

profile of v15, /device:TPU:0, one launch (start us, length us, event | category | flops | bytes accessed | tf_op | source)
XLA Modules:
  0.0 635.1 jit_solution(17193737269271316011)
XLA Ops:
  0.6 0.7 convert_element_type.27
  1.3 0.7 stack.13
  2.0 0.7 stack.14
  2.7 0.6 maximum_convert_fusion.refs_1_.refs_2_.refs_8_.refs_13_
  3.3 67.4 %open_1.1 = (f32[256,1536]{1,0:T(8,128)}, bf16[2048,512]{1,0:T(8,128)(2,1)}, bf16[512,2048]{1,0:T(8,128)(2,1)}, bf16[512,1536]{1,0:T(8,128)(2,1)}, f32[256,128]{...) custom-call(bf16[256,4096]{1,0:T(8,128)(2,1)} %refs_0_.1, ...), custom_call_target="tpu_custom_call" | custom-call | tf_op jit(solution)/shard_map/open_1/pallas_call | solution.py:418
  70.8 88.9 %attend_2.1 = (bf16[2048,512]{1,0:T(8,128)(2,1)}, bf16[2048,1024]{1,0:T(8,128)(2,1)}, bf16[2,256,512]{2,1,0:T(8,128)(2,1)}, f32[4,256,512]{2,1,0:T(8,128)}, bf16...) custom-call(f32[256,1536]{1,0:T(8,128)} %get-tuple-element.46.refs_0_, ...), custom_call_target="tpu_custom_call" | custom-call | tf_op jit(solution)/shard_map/attend_2/pallas_call | solution.py:418
  159.7 117.3 %ffn_4.1 = (bf16[256,3072]{1,0:T(8,128)(2,1)}, bf16[256,3072]{1,0:T(8,128)(2,1)}, bf16[256,3072]{1,0:T(8,128)(2,1)}, bf16[512,2048]{1,0:T(8,128)(2,1)}, f32[8,128]{1,0:T(8,128)}) custom-call(bf16[2048,512]{1,0:T(8,128)(2,1)} %get-tuple-element.45.refs_0_.refs_6_.refs_11_, bf16[2048,512]{1,0:T(8,128)(2,1)} %get-tuple-element.51.refs_1_.refs_7_.refs_12_, ...), custom_call_target="tpu_custom_call" | custom-call | tf_op jit(solution)/shard_map/ffn_4/pallas_call | solution.py:418
  277.0 116.9 %back_5.1 = (bf16[2048,512]{1,0:T(8,128)(2,1)}, f32[1,512]{1,0:T(1,128)}, bf16[512,3072]{1,0:T(8,128)(2,1)}, bf16[512,3072]{1,0:T(8,128)(2,1)}) custom-call(bf16[512,2048]{1,0:T(8,128)(2,1)} %get-tuple-element.54.refs_0_, bf16[512,3072]{1,0:T(8,128)(2,1)} %refs_1_.3, bf16[512,3072]{1,0:T(8,128)(2,1)} %refs_2_.3, ...), custom_call_target="tpu_custom_call" | custom-call | tf_op jit(solution)/shard_map/back_5/pallas_call | solution.py:418
  393.9 70.4 %down_6.1 = (bf16[2048,512]{1,0:T(8,128)(2,1)}, bf16[2048,512]{1,0:T(8,128)(2,1)}, bf16[3072,512]{1,0:T(8,128)(2,1)}) custom-call(bf16[2048,512]{1,0:T(8,128)(2,1)} %bitcast.6, bf16[3072,512]{1,0:T(8,128)(2,1)} %refs_1_.4, bf16[256,3072]{1,0:T(8,128)(2,1)} %get-tuple-element.53.refs_2_, bf16[2048,512]{1,0:T(8,128)(2,1)} %get-tuple-element.58.refs_3_), custom_call_target="tpu_custom_call" | custom-call | tf_op jit(solution)/shard_map/down_6/pallas_call | solution.py:418
  464.3 148.2 %tail_7.1 = (bf16[256,4096]{1,0:T(8,128)(2,1)}, bf16[256,4096]{1,0:T(8,128)(2,1)}, bf16[512,1024]{1,0:T(8,128)(2,1)}, bf16[1024,512]{1,0:T(8,128)(2,1)}, bf16[512,512]{1,0:T(8,128)(2,1)}, /*index=5*/f32[4,8,128]{2,1,0:T(8,128)}) custom-call(bf16[2048,512]{1,0:T(8,128)(2,1)} %get-tuple-element.59.refs_0_, bf16[1024,512]{1,0:T(8,128)(2,1)} %refs_1_.5, ...), custom_call_target="tpu_custom_call" | custom-call | tf_op jit(solution)/shard_map/tail_7/pallas_call | solution.py:418
  612.6 0.0 copy-start.6
  612.6 0.8 reduce_sum.9
  613.4 0.6 slice_bitcast_fusion
  614.0 0.0 copy-start.5
  614.0 2.2 convert_element_type.31
  616.2 0.0 copy-done.6
  616.2 1.6 convert_element_type.30
  617.8 0.0 copy-done.5
  617.8 0.0 copy-start.3
  617.8 1.6 convert_element_type.32
  619.4 0.7 copy-done.3
  620.1 0.0 copy-start.2
  620.1 2.5 convert_element_type.29
  622.6 0.5 copy-done.2
  623.1 0.0 copy-start.1
  623.1 3.6 convert_element_type.35
  626.7 0.0 copy-done.1
  626.7 0.0 copy-start
  626.7 3.5 convert_element_type.33
  630.2 0.0 copy-done
  630.2 0.0 copy-start.4
  630.2 3.5 convert_element_type.34
  633.7 0.0 copy-done.4
  633.7 1.3 copy.22
  (1 shorter events, 0.0 us)
Async XLA Ops:
  612.6 3.6 copy-start.6
  614.0 3.8 copy-start.5
  617.8 2.3 copy-start.3
  620.1 3.0 copy-start.2
  623.1 3.6 copy-start.1
  626.7 3.5 copy-start
  630.2 3.5 copy-start.4

commit v16 on v15

--- a/solution.py
+++ b/solution.py
@@ -1492,15 +1492,13 @@
 
     def place_tok(at):
         across, other, half_at = near(at)
-        return here.shard(across, other) * per + half_at
-
-    def place_half(at):
-        return jnp.where(at < 2 * line_counts, 2 * place_tok(at // 2) + at % 2, at)
+        return jnp.where(at < line_counts, here.shard(across, other) * per + half_at, at)
 
     ffn_sum, leaving = take(2)
-    line = Line(here, 2 * line_counts, [ffn, ffn_sum] + take(8), chip_place(here, 2 * per))
+    by_chip = chip_place(here, per)
+    line = Line(here, line_counts, [ffn, ffn_sum] + take(8), by_chip)
     contrib, summed = take(2)
-    line_tok = Line(here, 2 * (line_counts + extra), [contrib, summed] + take(8), place_half)
+    line_tok = Line(here, line_counts + extra, [contrib, summed] + take(8), place_tok)
     tiny = Tiny(here, tiny_own, tiny_all, (tiny_send, tiny_recv), False)
     got, core = spread.got, here.core
     product = products(here, d_attn, w_out, True, rows, width, counts)
@@ -1515,12 +1513,8 @@
 
     mixed_copy(0).start()
 
-    def both_steps(which, at):
-        which.step(2 * at)
-        which.step(2 * at + 1)
-
     def beside(step):
-        both_steps(line, step)
+        line.step(step)
 
         @pl.when(step < 8)
         def _():
@@ -1567,7 +1561,7 @@
         lead, trail = d_query[:, :half], d_query[:, half:]
         first = ((lead * cos[0] + trail * sin[0]) * rms[0]).astype(got.dtype)
         second = ((trail * cos[0] - lead * sin[0]) * rms[0]).astype(got.dtype)
-        both_steps(line, done + head)
+        line.step(done + head)
         for rows_at in range(2):
             piece = slice(rows_at * part, (rows_at + 1) * part)
             got[0, core, rows_at, 0, :, pl.ds(pl.multiple_of(head * HD, HD), half)] = first[piece, :]
@@ -1622,15 +1616,20 @@
             x_rows = x_low[row, :].astype(jnp.float32)
             contrib[row, :] = (value * gain[0:1, :] - x_rows * dot).astype(contrib.dtype)
             gain_sum[...] += jnp.sum(value * x_rows, axis=0, keepdims=True)
-        line_tok.launch(2 * at, 2)
-        rows_t = act_t[:, pl.ds(first, part)]
-        for at_col in range((heads + 2) * HD // 512):
-            span = slice(at_col * 512, (at_col + 1) * 512)
-            grad[:, span] += dot_nn(rows_t, block[:, span])
+        line_tok.launch(at, 1)
+
+        @pl.when(other == 1)
+        def _():
+            twin = got[across, core, half_at, 0]
+            twin_first = pl.multiple_of(here.shard(across, 0) * rows + half_at * part, part)
+            rows_t, twin_t = act_t[:, pl.ds(first, part)], act_t[:, pl.ds(twin_first, part)]
+            for at_col in range((heads + 2) * HD // 512):
+                span = slice(at_col * 512, (at_col + 1) * 512)
+                grad[:, span] += dot_nn(rows_t, block[:, span]) + dot_nn(twin_t, twin[:, span])
 
     me = here.shard(0, 0)
     columns = pl.ds(pl.multiple_of(me * cols, cols), cols)
-    chunk = rows // per
+    chunk = line.chunk
 
     def landing(which, at):
         sub = at % per if which == 0 else near(at)[2]
@@ -1650,7 +1649,7 @@
 
     def emit(which, at):
         if which == 1:
-            row = pl.ds(pl.multiple_of(place_tok(at) * chunk, chunk), chunk)
+            row = line_tok.rows(at)
             value = d_attn[row, :].astype(jnp.float32) + summed[row, :].astype(jnp.float32)
             line_tok.from_end[at] = value.astype(out.dtype)
             return
@@ -1685,11 +1684,11 @@
 
         @pl.when(step < 5)
         def _():
-            both_steps(line, done + heads + step)
+            line.step(done + heads + step)
 
         @pl.when(step >= 4)
         def _():
-            both_steps(line_tok, step - 4)
+            line_tok.step(step - 4)
 
         @pl.when(step > 0)
         def _():
@@ -1697,9 +1696,8 @@
 
         @pl.when(line.inner == 0)
         def _():
-            for last in range(2):
-                line.up(2 * step + last).wait_send()
-                line.down(2 * step + last).wait_recv()
+            line.up(step).wait_send()
+            line.down(step).wait_recv()
 
         emit(0, step)
 
@@ -1717,7 +1715,7 @@
         span = pl.ds(line_counts * (rows // per) + half_at * (rows // per), rows // per)
         source = slice(half_at * (rows // per), (half_at + 1) * (rows // per))
         contrib[span, :] = grad[source, heads * HD :].astype(contrib.dtype)
-    line_tok.launch(2 * line_counts, 2 * extra)
+    line_tok.launch(line_counts, extra)
     grad_query[...] = grad[:, : heads * HD].astype(grad_query.dtype)
     for at in range(cols // LANES):
         tile[at : at + 1, :] = gain_sum[:, at * LANES : (at + 1) * LANES]
@@ -1739,7 +1737,7 @@
         start = line_counts - 4
 
         def both(at, _):
-            both_steps(line_tok, at)
+            line_tok.step(at)
 
             @pl.when(at < line_counts + 4)
             def _():
@@ -1756,14 +1754,13 @@
             line_tok.down(at).wait_send()
             return 0
 
-        lax.fori_loop(0, 2 * (line_counts + extra), drain, 0)
+        lax.fori_loop(0, line_counts + extra, drain, 0)
 
     @pl.when(line.inner == 0)
     def _():
         def arrive(at, _):
-            for last in range(2):
-                line_tok.up(2 * at + last).wait_send()
-                line_tok.down(2 * at + last).wait_recv()
+            line_tok.up(at).wait_send()
+            line_tok.down(at).wait_recv()
 
             @pl.when(jnp.logical_and(at > 0, at <= line_counts))
             def _():
@@ -1843,8 +1840,8 @@
         pltpu.VMEM((2, rows, wide), low), dma((2,)),
         pltpu.VMEM((total, cols), low),
         pltpu.VMEM((counts, chunk, cols), low),
-    ] + line_scratch(2 * counts, (total, cols), low)
-    scratch += [pltpu.VMEM(long, low), pltpu.VMEM(long, low)] + line_scratch(2 * (counts + extra), long, low, 2)
+    ] + line_scratch(counts, (total, cols), low)
+    scratch += [pltpu.VMEM(long, low), pltpu.VMEM(long, low)] + line_scratch(counts + extra, long, low)
     operands = [d_attn, w_out, queries, kv, probs, rms, cos, sin, act_t, w_qkv, ffn, x_low, attn, gain,
                 gain_grad, mixed_all]
     kernel = functools.partial(tail_kernel, rows, heads, per)

time: 636 us -> 624 us (0.981)
  Pallas kernels: 609 us -> 597 us
    pallas_call x6, Pallas kernels: 609 us -> 597 us  [kernel_call(): pl.pallas_call(body, out_shape=out_shape, in_specs=specs, out_specs=out_s...]
where the time goes in v16:
time: 624 us; the launch traced here: 623 us
  Pallas kernels  597 us (96%)
  other arithmetic  20.6 us (3%)
    pallas_call x6, Pallas kernels, kernel_call(): pl.pallas_call(body, out_shape=out_shape, in_specs=specs, out_specs=out_s...  597 us

profile of v16, /device:TPU:0, one launch (start us, length us, event | category | flops | bytes accessed | tf_op | source)
XLA Modules:
  0.0 622.9 jit_solution(13590382936139739345)
XLA Ops:
  0.6 0.7 convert_element_type.27
  1.3 0.7 stack.13
  2.0 0.7 stack.14
  2.7 0.6 maximum_convert_fusion.refs_1_.refs_2_.refs_8_.refs_13_
  3.3 67.4 %open_1.1 = (f32[256,1536]{1,0:T(8,128)}, bf16[2048,512]{1,0:T(8,128)(2,1)}, bf16[512,2048]{1,0:T(8,128)(2,1)}, bf16[512,1536]{1,0:T(8,128)(2,1)}, f32[256,128]{...) custom-call(bf16[256,4096]{1,0:T(8,128)(2,1)} %refs_0_.1, ...), custom_call_target="tpu_custom_call" | custom-call | tf_op jit(solution)/shard_map/open_1/pallas_call | solution.py:418
  70.8 88.9 %attend_2.1 = (bf16[2048,512]{1,0:T(8,128)(2,1)}, bf16[2048,1024]{1,0:T(8,128)(2,1)}, bf16[2,256,512]{2,1,0:T(8,128)(2,1)}, f32[4,256,512]{2,1,0:T(8,128)}, bf16...) custom-call(f32[256,1536]{1,0:T(8,128)} %get-tuple-element.46.refs_0_, ...), custom_call_target="tpu_custom_call" | custom-call | tf_op jit(solution)/shard_map/attend_2/pallas_call | solution.py:418
  159.7 117.3 %ffn_4.1 = (bf16[256,3072]{1,0:T(8,128)(2,1)}, bf16[256,3072]{1,0:T(8,128)(2,1)}, bf16[256,3072]{1,0:T(8,128)(2,1)}, bf16[512,2048]{1,0:T(8,128)(2,1)}, f32[8,128]{1,0:T(8,128)}) custom-call(bf16[2048,512]{1,0:T(8,128)(2,1)} %get-tuple-element.45.refs_0_.refs_6_.refs_11_, bf16[2048,512]{1,0:T(8,128)(2,1)} %get-tuple-element.51.refs_1_.refs_7_.refs_12_, ...), custom_call_target="tpu_custom_call" | custom-call | tf_op jit(solution)/shard_map/ffn_4/pallas_call | solution.py:418
  277.0 116.9 %back_5.1 = (bf16[2048,512]{1,0:T(8,128)(2,1)}, f32[1,512]{1,0:T(1,128)}, bf16[512,3072]{1,0:T(8,128)(2,1)}, bf16[512,3072]{1,0:T(8,128)(2,1)}) custom-call(bf16[512,2048]{1,0:T(8,128)(2,1)} %get-tuple-element.54.refs_0_, bf16[512,3072]{1,0:T(8,128)(2,1)} %refs_1_.3, bf16[512,3072]{1,0:T(8,128)(2,1)} %refs_2_.3, ...), custom_call_target="tpu_custom_call" | custom-call | tf_op jit(solution)/shard_map/back_5/pallas_call | solution.py:418
  393.9 70.4 %down_6.1 = (bf16[2048,512]{1,0:T(8,128)(2,1)}, bf16[2048,512]{1,0:T(8,128)(2,1)}, bf16[3072,512]{1,0:T(8,128)(2,1)}) custom-call(bf16[2048,512]{1,0:T(8,128)(2,1)} %bitcast.6, bf16[3072,512]{1,0:T(8,128)(2,1)} %refs_1_.4, bf16[256,3072]{1,0:T(8,128)(2,1)} %get-tuple-element.53.refs_2_, bf16[2048,512]{1,0:T(8,128)(2,1)} %get-tuple-element.58.refs_3_), custom_call_target="tpu_custom_call" | custom-call | tf_op jit(solution)/shard_map/down_6/pallas_call | solution.py:418
  464.3 136.1 %tail_7.1 = (bf16[256,4096]{1,0:T(8,128)(2,1)}, bf16[256,4096]{1,0:T(8,128)(2,1)}, bf16[512,1024]{1,0:T(8,128)(2,1)}, bf16[1024,512]{1,0:T(8,128)(2,1)}, bf16[512,512]{1,0:T(8,128)(2,1)}, /*index=5*/f32[4,8,128]{2,1,0:T(8,128)}) custom-call(bf16[2048,512]{1,0:T(8,128)(2,1)} %get-tuple-element.59.refs_0_, bf16[1024,512]{1,0:T(8,128)(2,1)} %refs_1_.5, ...), custom_call_target="tpu_custom_call" | custom-call | tf_op jit(solution)/shard_map/tail_7/pallas_call | solution.py:418
  600.4 0.0 copy-start.6
  600.5 0.8 reduce_sum.9
  601.3 0.6 slice_bitcast_fusion
  601.9 0.0 copy-start.5
  601.9 2.2 convert_element_type.31
  604.1 0.0 copy-done.6
  604.1 1.6 convert_element_type.30
  605.7 0.0 copy-done.5
  605.7 0.0 copy-start.3
  605.7 1.6 convert_element_type.32
  607.3 0.7 copy-done.3
  608.0 0.0 copy-start.2
  608.0 2.5 convert_element_type.29
  610.5 0.5 copy-done.2
  611.0 0.0 copy-start.1
  611.0 3.6 convert_element_type.35
  614.6 0.0 copy-done.1
  614.6 0.0 copy-start
  614.6 3.5 convert_element_type.33
  618.1 0.0 copy-done
  618.1 0.0 copy-start.4
  618.1 3.5 convert_element_type.34
  621.6 0.0 copy-done.4
  621.6 1.3 copy.22
  (1 shorter events, 0.0 us)
Async XLA Ops:
  600.4 3.6 copy-start.6
  601.9 3.8 copy-start.5
  605.7 2.3 copy-start.3
  608.0 3.0 copy-start.2
  611.0 3.6 copy-start.1
  614.6 3.5 copy-start
  618.1 3.5 copy-start.4

commit v17 on v16

--- a/solution.py
+++ b/solution.py
@@ -395,31 +395,43 @@
     return [here.device(*turned(at)) for at in range(7)]
 
 
-def kernel_call(kernel, out_shape, operands, specs, scratch, cid, name, out_specs=None, late=()):
+def kernel_call(kernel, out_shape, operands, specs, scratch, cid, name, out_specs=None, late=(), early=()):
     vm = pl.BlockSpec(memory_space=pltpu.VMEM)
-    specs = [pl.BlockSpec(memory_space=pl.ANY) if at in late else spec for at, spec in enumerate(specs)]
+    hbm = pl.BlockSpec(memory_space=pl.ANY)
+    specs = [hbm if at in late else spec for at, spec in enumerate(specs)]
+    out_specs = [hbm if at in early else spec for at, spec in enumerate(out_specs or [vm] * len(out_shape))]
     inside = [pltpu.VMEM(operands[at].shape, operands[at].dtype) for at in late]
-    if late:
-        inside.append(pltpu.SemaphoreType.DMA((len(late),)))
+    inside += [pltpu.VMEM(out_shape[at].shape, out_shape[at].dtype) for at in early]
+    inside.append(pltpu.SemaphoreType.DMA((max(1, len(late) + len(early)),)))
+    n_in, n_out = len(operands), len(out_shape)
 
     def body(*refs):
-        if not late:
-            kernel(*refs)
-            return
-        ins, rest, own = list(refs[: len(operands)]), refs[len(operands) : -len(inside)], refs[-len(inside) :]
-        copies = []
+        ins, outs = list(refs[:n_in]), list(refs[n_in : n_in + n_out])
+        rest, own = refs[n_in + n_out : -len(inside)], refs[-len(inside) :]
+        loads, stores = [], []
         for spot, at in enumerate(late):
             copy = pltpu.make_async_copy(ins[at], own[spot], own[-1].at[spot])
             copy.start()
-            copies.append(copy)
+            loads.append(copy)
             ins[at] = own[spot]
-        kernel(*ins, *rest, late=copies)
+        for number, at in enumerate(early):
+            spot = len(late) + number
+            stores.append(pltpu.make_async_copy(own[spot], outs[at], own[-1].at[spot]))
+            outs[at] = own[spot]
+        more = {}
+        if late:
+            more["late"] = loads
+        if early:
+            more["early"] = stores
+        kernel(*ins, *outs, *rest, **more)
+        for copy in stores:
+            copy.wait()
 
     return pl.pallas_call(
         body,
         out_shape=out_shape,
         in_specs=specs,
-        out_specs=out_specs or [vm] * len(out_shape),
+        out_specs=out_specs,
         scratch_shapes=scratch + inside,
         compiler_params=pltpu.CompilerParams(
             collective_id=cid, has_side_effects=True, vmem_limit_bytes=VMEM_LIMIT
@@ -789,7 +801,7 @@
 
 
 def open_kernel(rows, width, counts, tokens, gain, w_query, kv_weight, cot, qkv, x_low, act_t, w_qkv, rms, cos, sin,
-                mask, g_col, *refs):
+                mask, g_col, *refs, early):
     here = Place()
     cols, segs = gain.shape[1], gain
     act, turn_send, turn_recv, local_sems, cot_part, g_send, g_recv, z_send, z_recv = refs[:9]
@@ -857,6 +869,7 @@
         turn_copy(at).start()
     for copy in local:
         copy.wait()
+    early[2].start()
 
     def squares(at, total):
         values = tokens[:, pl.ds(pl.multiple_of(at * cols, cols), cols)].astype(jnp.float32)
@@ -865,6 +878,8 @@
     total = lax.fori_loop(0, 8, squares, jnp.zeros((rows, 1), jnp.float32))
     rms[...] = jnp.broadcast_to(lax.rsqrt(total / (8 * cols) + EPS), rms.shape)
     make_tables(here, rows, segs, cos, sin, mask)
+    for at in (3, 4, 5):
+        early[at].start()
 
     def prepare(first, count):
         def one(step, _):
@@ -888,6 +903,8 @@
         for at in range(first, min(first + count, 7)):
             turn_copy(at).wait_recv()
         prepare(first, count)
+        if stop == 2:
+            early[0].start()
 
     def flip():
         def one(shard, _):
@@ -901,6 +918,7 @@
     total = Reduce(here, counts, product, refs[9:20], before)
     total.run()
     flip()
+    early[1].start()
 
     def emit(at, first, second):
         for half, value in enumerate((first, second)):
@@ -908,6 +926,7 @@
 
     total.end(emit)
     take_quarters(2)
+    early[6].start()
     for at in range(7):
         turn_copy(at).wait_send()
         g_copy(at).wait_send()
@@ -948,11 +967,12 @@
     scratch += reduce_scratch(counts, rows, width)
     kernel = functools.partial(open_kernel, rows, width, counts)
     return kernel_call(kernel, out_shape, [tokens, gain, w_query, kv_weight, cot],
-                       [vm, vm, hbm, hbm, hbm], scratch, cid, "open")
+                       [vm, vm, hbm, hbm, hbm], scratch, cid, "open",
+                       early=(1, 2, 3, 5, 6, 7, 8))
 
 
 def ffn_kernel(rows, width, counts, x_low, attn, gain, w_gate, w_up, d_hidden, hidden, d_gate, d_up, act_t, tile_out,
-               *refs, late):
+               *refs, late, early):
     here = Place()
     cols = gain.shape[1]
     act, weight, tiny_own, tiny_all, tiny_send, tiny_recv, dots, local_sems = refs[:8]
@@ -998,6 +1018,7 @@
         return 0
 
     lax.fori_loop(0, 8, flip, 0)
+    early[0].start()
     tiny.end()
     tiles = rows // LANES
     mean = [from_tile(jnp.sum(tiny_all[:, at, :], axis=0, keepdims=True), eye) for at in range(tiles)]
@@ -1048,7 +1069,7 @@
     ] + reduce_scratch(counts, rows, width)
     kernel = functools.partial(ffn_kernel, rows, width, counts)
     return kernel_call(kernel, out_shape, [x_low, attn, gain, w_gate, w_up, d_hidden], [vm, vm, vm, hbm, hbm, vm],
-                       scratch, cid, "ffn", late=(5,))
+                       scratch, cid, "ffn", late=(5,), early=(3,))
 
 
 def load_own(spread, payload, width, counts, sems):
@@ -1218,8 +1239,8 @@
     here = Place()
     spread = Spread(here, counts, refs[:7])
     own_sems, sums, grads, staged, out_sems, norm_out = refs[7:13]
-    place = chip_place(here, 4)
-    norm_line = Line(here, 24, [d_norm, norm_out] + list(refs[13:]), lambda at: place(at + 8))
+    place = chip_place(here, 2)
+    norm_line = Line(here, 12, [d_norm, norm_out] + list(refs[13:]), lambda at: place(at + 4))
     own = load_own(spread, (hidden,), width, counts, own_sems)
     for copy in own:
         copy.start()
@@ -1262,7 +1283,13 @@
             leave(0, at).start()
             leave(1, at).start()
 
-    norm_line.steps(spread.run(blocks, norm_line.step, done), 26)
+
+    def hook(step):
+        @pl.when(step % 3 < 2)
+        def _():
+            norm_line.step(step // 3 * 2 + step % 3)
+
+    spread.run(blocks, hook, done)
     ffn[...] = sums[...].astype(ffn.dtype)
     norm_line.settle()
 
@@ -1312,14 +1339,14 @@
         pltpu.VMEM((2, 2, width, cols), low),
         dma((2, counts)),
         pltpu.VMEM((total, cols), low),
-    ] + line_scratch(24, (24 * rows // 4, cols), low)
+    ] + line_scratch(12, (12 * rows // 2, cols), low)
     kernel = functools.partial(down_kernel, rows, width, counts)
     return kernel_call(kernel, out_shape, [cot, weight, hidden, d_norm], [vm, vm, hbm, vm], scratch, cid, "down",
                        [vm, vm, hbm], (0, 1))
 
 
 def attend_kernel(rows, heads, cols, width, counts, qkv, rms, cos, sin, mask, w_out, g_col, w_down, attn, mixed_all,
-                  kv, probs, queries, pair_rms, d_hidden, *refs, late):
+                  kv, probs, queries, pair_rms, d_hidden, *refs, late, early):
     here = Place()
     spread = Spread(here, 1, refs[:7])
     part, pair_sems, tiny_own, tiny_pair, mixed_sems = refs[7:12]
@@ -1331,7 +1358,7 @@
         across, other, half_at = spread.block(at)
         return here.shard(across, other) * 2 + half_at
 
-    line = Line(here, 32, [part, attn] + list(refs[23:]), lambda at: place(at // 2) * 2 + at % 2)
+    line = Line(here, 16, [part, attn] + list(refs[23:]), place)
     got, core = spread.got, here.core
     greet(here, slice_peers(here), True)
     half = HD // 2
@@ -1362,7 +1389,9 @@
         lead, trail = rotated(head * HD)
         queries[:, head * HD : head * HD + half] = (lead * scale).astype(queries.dtype)
         queries[:, head * HD + half : (head + 1) * HD] = (trail * scale).astype(queries.dtype)
+    early[2].start()
     pair.wait()
+    early[0].start()
     for copy in late:
         copy.wait()
 
@@ -1382,6 +1411,7 @@
         return 0
 
     lax.fori_loop(0, heads, one_head, 0)
+    early[1].start()
     spread.begin_rows()
 
     def mixed_copy(at):
@@ -1399,7 +1429,7 @@
             value = dot_nn(got[across, (core + other) % 2, half_at, 0], w_out[...])
             part[pl.ds(pl.multiple_of(place(step) * piece, piece), piece), :] = value.astype(part.dtype)
             mixed_copy(step).start()
-            line.launch(2 * step, 2)
+            line.launch(step, 1)
 
         @pl.when(step >= 2)
         def _():
@@ -1407,12 +1437,11 @@
 
         @pl.when(step >= 4)
         def _():
-            line.step(2 * step - 8)
-            line.step(2 * step - 7)
+            line.step(step - 4)
         return 0
 
     lax.fori_loop(0, 20, one_step, 0)
-    line.end(32)
+    line.end(16)
 
     def emit(at, first, second):
         for half_at, value in enumerate((first, second)):
@@ -1453,15 +1482,15 @@
     scratch = spread_scratch(1, rows // 2, wide) + [
         pltpu.VMEM((8 * rows, cols), low), dma((4,)),
         pltpu.VMEM((8, LANES), f32), pltpu.VMEM((8, LANES), f32), dma((16,)),
-    ] + reduce_scratch(counts, rows, width) + line_scratch(32, (8 * rows, cols), low)
+    ] + reduce_scratch(counts, rows, width) + line_scratch(16, (8 * rows, cols), low)
     kernel = functools.partial(attend_kernel, rows, heads, cols, width, counts)
     operands = [qkv, rms, cos, sin, mask, w_out, g_col, w_down]
     out_specs = [vm, pl.BlockSpec(memory_space=pl.ANY)] + [vm] * 5
-    return kernel_call(kernel, out_shape, operands, [vm] * 8, scratch, cid, "attend", out_specs, (4, 5, 6, 7))
+    return kernel_call(kernel, out_shape, operands, [vm] * 8, scratch, cid, "attend", out_specs, (4, 5, 6, 7), (2, 3, 4))
 
 
 def tail_kernel(rows, heads, per, d_attn, w_out, queries, kv, probs, rms, cos, sin, act_t, w_qkv, ffn, x_low,
-                attn, gain, gain_grad, mixed_all, d_tok, out, grad_query, grad_out, kv_sum, gain_tiles, *refs, late):
+                attn, gain, gain_grad, mixed_all, d_tok, out, grad_query, grad_out, kv_sum, gain_tiles, *refs, late, early):
     here = Place()
     width = HD
     counts = heads // 2
@@ -1529,6 +1558,7 @@
 
     done = total.run(beside)
     grad_out[...] = grad_mixed[...].astype(grad_out.dtype)
+    early[1].start()
 
     def land(at, first, second):
         for half_at, value in enumerate((first, second)):
@@ -1717,6 +1747,7 @@
         contrib[span, :] = grad[source, heads * HD :].astype(contrib.dtype)
     line_tok.launch(line_counts, extra)
     grad_query[...] = grad[:, : heads * HD].astype(grad_query.dtype)
+    early[0].start()
     for at in range(cols // LANES):
         tile[at : at + 1, :] = gain_sum[:, at * LANES : (at + 1) * LANES]
         spot = cols // LANES + at
@@ -1847,7 +1878,7 @@
     kernel = functools.partial(tail_kernel, rows, heads, per)
     specs = [vm] * (len(operands) - 1) + [pl.BlockSpec(memory_space=pl.ANY)]
     return kernel_call(kernel, out_shape, operands, specs, scratch, cid, "tail",
-                       late=(2, 3, 4, 8, 9, 11, 12))
+                       late=(2, 3, 4, 8, 9, 11, 12), early=(2, 3))
 
 
 LANES = 128

time: 624 us -> 615 us (0.986)
  Pallas kernels: 597 us -> 588 us
    pallas_call x6, Pallas kernels: 597 us -> 588 us  [kernel_call(): pl.pallas_call(body, out_shape=out_shape, in_specs=specs, out_specs=out_s...]
where the time goes in v17:
time: 615 us; the launch traced here: 614 us
  Pallas kernels  588 us (96%)
  other arithmetic  20.6 us (3%)
    pallas_call x6, Pallas kernels, kernel_call(): pl.pallas_call(body, out_shape=out_shape, in_specs=specs, out_specs=out_s...  588 us

profile of v17, /device:TPU:0, one launch (start us, length us, event | category | flops | bytes accessed | tf_op | source)
XLA Modules:
  0.0 614.0 jit_solution(13929687916093480078)
XLA Ops:
  0.6 0.7 convert_element_type.27
  1.3 0.7 stack.13
  2.0 0.7 stack.14
  2.7 0.6 maximum_convert_fusion.refs_1_.refs_2_.refs_8_.refs_13_
  3.3 66.2 %open_1.1 = (f32[256,1536]{1,0:T(8,128)}, bf16[2048,512]{1,0:T(8,128)(2,1)}, bf16[512,2048]{1,0:T(8,128)(2,1)}, bf16[512,1536]{1,0:T(8,128)(2,1)}, f32[256,128]{...) custom-call(bf16[256,4096]{1,0:T(8,128)(2,1)} %refs_0_.1, ...), custom_call_target="tpu_custom_call" | custom-call | tf_op jit(solution)/shard_map/open_1/pallas_call | solution.py:430
  69.5 87.2 %attend_2.1 = (bf16[2048,512]{1,0:T(8,128)(2,1)}, bf16[2048,1024]{1,0:T(8,128)(2,1)}, bf16[2,256,512]{2,1,0:T(8,128)(2,1)}, f32[4,256,512]{2,1,0:T(8,128)}, bf16...) custom-call(f32[256,1536]{1,0:T(8,128)} %get-tuple-element.46.refs_0_, ...), custom_call_target="tpu_custom_call" | custom-call | tf_op jit(solution)/shard_map/attend_2/pallas_call | solution.py:430
  156.7 116.9 %ffn_4.1 = (bf16[256,3072]{1,0:T(8,128)(2,1)}, bf16[256,3072]{1,0:T(8,128)(2,1)}, bf16[256,3072]{1,0:T(8,128)(2,1)}, bf16[512,2048]{1,0:T(8,128)(2,1)}, f32[8,128]{1,0:T(8,128)}) custom-call(bf16[2048,512]{1,0:T(8,128)(2,1)} %get-tuple-element.45.refs_0_.refs_6_.refs_11_, bf16[2048,512]{1,0:T(8,128)(2,1)} %get-tuple-element.51.refs_1_.refs_7_.refs_12_, ...), custom_call_target="tpu_custom_call" | custom-call | tf_op jit(solution)/shard_map/ffn_4/pallas_call | solution.py:430
  273.6 116.9 %back_5.1 = (bf16[2048,512]{1,0:T(8,128)(2,1)}, f32[1,512]{1,0:T(1,128)}, bf16[512,3072]{1,0:T(8,128)(2,1)}, bf16[512,3072]{1,0:T(8,128)(2,1)}) custom-call(bf16[512,2048]{1,0:T(8,128)(2,1)} %get-tuple-element.54.refs_0_, bf16[512,3072]{1,0:T(8,128)(2,1)} %refs_1_.3, bf16[512,3072]{1,0:T(8,128)(2,1)} %refs_2_.3, ...), custom_call_target="tpu_custom_call" | custom-call | tf_op jit(solution)/shard_map/back_5/pallas_call | solution.py:430
  390.5 65.1 %down_6.1 = (bf16[2048,512]{1,0:T(8,128)(2,1)}, bf16[2048,512]{1,0:T(8,128)(2,1)}, bf16[3072,512]{1,0:T(8,128)(2,1)}) custom-call(bf16[2048,512]{1,0:T(8,128)(2,1)} %bitcast.6, bf16[3072,512]{1,0:T(8,128)(2,1)} %refs_1_.4, bf16[256,3072]{1,0:T(8,128)(2,1)} %get-tuple-element.53.refs_2_, bf16[2048,512]{1,0:T(8,128)(2,1)} %get-tuple-element.58.refs_3_), custom_call_target="tpu_custom_call" | custom-call | tf_op jit(solution)/shard_map/down_6/pallas_call | solution.py:430
  455.6 135.8 %tail_7.1 = (bf16[256,4096]{1,0:T(8,128)(2,1)}, bf16[256,4096]{1,0:T(8,128)(2,1)}, bf16[512,1024]{1,0:T(8,128)(2,1)}, bf16[1024,512]{1,0:T(8,128)(2,1)}, bf16[512,512]{1,0:T(8,128)(2,1)}, /*index=5*/f32[4,8,128]{2,1,0:T(8,128)}) custom-call(bf16[2048,512]{1,0:T(8,128)(2,1)} %get-tuple-element.59.refs_0_, bf16[1024,512]{1,0:T(8,128)(2,1)} %refs_1_.5, ...), custom_call_target="tpu_custom_call" | custom-call | tf_op jit(solution)/shard_map/tail_7/pallas_call | solution.py:430
  591.5 0.0 copy-start.6
  591.5 0.8 reduce_sum.9
  592.3 0.6 slice_bitcast_fusion
  592.9 0.0 copy-start.5
  592.9 2.2 convert_element_type.31
  595.1 0.0 copy-done.6
  595.1 1.6 convert_element_type.30
  596.7 0.0 copy-done.5
  596.7 0.0 copy-start.3
  596.7 1.6 convert_element_type.32
  598.3 0.7 copy-done.3
  599.0 0.0 copy-start.2
  599.0 2.5 convert_element_type.29
  601.5 0.5 copy-done.2
  602.0 0.0 copy-start.1
  602.0 3.6 convert_element_type.35
  605.6 0.0 copy-done.1
  605.6 0.0 copy-start
  605.6 3.5 convert_element_type.33
  609.1 0.0 copy-done
  609.1 0.0 copy-start.4
  609.1 3.5 convert_element_type.34
  612.6 0.0 copy-done.4
  612.6 1.3 copy.22
  (1 shorter events, 0.0 us)
Async XLA Ops:
  591.5 3.6 copy-start.6
  592.9 3.8 copy-start.5
  596.7 2.3 copy-start.3
  599.0 3.0 copy-start.2
  602.0 3.6 copy-start.1
  605.6 3.5 copy-start
  609.1 3.5 copy-start.4

commit v18 on v17

--- a/solution.py
+++ b/solution.py
@@ -800,9 +800,14 @@
                         mask[span, first : first + LANES] = allowed.astype(jnp.float32)
 
 
-def open_kernel(rows, width, counts, tokens, gain, w_query, kv_weight, cot, qkv, x_low, act_t, w_qkv, rms, cos, sin,
-                mask, g_col, *refs, early):
+def open_kernel(rows, width, counts, tokens, gain_one, gain_two, ids, w_query, kv_weight, cot, qkv, x_low, act_t, w_qkv, rms, cos, sin,
+                mask, g_col, gain, *refs, early):
     here = Place()
+    gain[...] = jnp.zeros_like(gain)
+    gain[0:1, :] = gain_one[...].astype(jnp.float32).reshape(1, -1)
+    gain[1:2, :] = gain_two[...].astype(jnp.float32).reshape(1, -1)
+    gain[2:3, :] = ids[...].astype(jnp.float32).reshape(1, -1)
+    early[7].start()
     cols, segs = gain.shape[1], gain
     act, turn_send, turn_recv, local_sems, cot_part, g_send, g_recv, z_send, z_recv = refs[:9]
     share = rows // 4
@@ -940,7 +945,7 @@
             quarter(1, here.z + step, step, -1).wait_send()
 
 
-def opening(tokens, gain, w_query, kv_weight, cot, cid, width=256):
+def opening(tokens, gain_one, gain_two, ids, w_query, kv_weight, cot, cid, width=256):
     rows = tokens.shape[0]
     cols, wide = w_query.shape
     every = wide + kv_weight.shape[1]
@@ -959,6 +964,7 @@
         jax.ShapeDtypeStruct((2, rows, LANES), f32),
         jax.ShapeDtypeStruct((rows, 2 * rows), f32),
         jax.ShapeDtypeStruct((8, 4, rows // 4, cols), low),
+        jax.ShapeDtypeStruct((8, cols), f32),
     ]
     scratch = [
         pltpu.VMEM((8 * rows, cols), low), dma((7,)), dma((7,)), dma((5,)),
@@ -966,9 +972,9 @@
     ]
     scratch += reduce_scratch(counts, rows, width)
     kernel = functools.partial(open_kernel, rows, width, counts)
-    return kernel_call(kernel, out_shape, [tokens, gain, w_query, kv_weight, cot],
-                       [vm, vm, hbm, hbm, hbm], scratch, cid, "open",
-                       early=(1, 2, 3, 5, 6, 7, 8))
+    return kernel_call(kernel, out_shape, [tokens, gain_one, gain_two, ids, w_query, kv_weight, cot],
+                       [vm, vm, vm, vm, hbm, hbm, hbm], scratch, cid, "open",
+                       early=(1, 2, 3, 5, 6, 7, 8, 9))
 
 
 def ffn_kernel(rows, width, counts, x_low, attn, gain, w_gate, w_up, d_hidden, hidden, d_gate, d_up, act_t, tile_out,
@@ -1490,7 +1496,7 @@
 
 
 def tail_kernel(rows, heads, per, d_attn, w_out, queries, kv, probs, rms, cos, sin, act_t, w_qkv, ffn, x_low,
-                attn, gain, gain_grad, mixed_all, d_tok, out, grad_query, grad_out, kv_sum, gain_tiles, *refs, late, early):
+                attn, gain, gain_grad, mixed_all, d_tok, out, grad_query, grad_out, kv_sum, gains, *refs, late, early):
     here = Place()
     width = HD
     counts = heads // 2
@@ -1523,7 +1529,7 @@
         across, other, half_at = near(at)
         return jnp.where(at < line_counts, here.shard(across, other) * per + half_at, at)
 
-    ffn_sum, leaving = take(2)
+    gain_tiles, ffn_sum, leaving = take(3)
     by_chip = chip_place(here, per)
     line = Line(here, line_counts, [ffn, ffn_sum] + take(8), by_chip)
     contrib, summed = take(2)
@@ -1622,6 +1628,7 @@
     given = remote(give, taken, give_sems.at[0], give_sems.at[1], spread.ydev)
     given.start()
     grad[...] = jnp.zeros_like(grad)
+    line.steps(done + heads, done + heads + 2)
     given.wait()
     for rows_at in range(2):
         piece = slice(rows_at * part, (rows_at + 1) * part)
@@ -1712,9 +1719,9 @@
         def _():
             block_of(step)
 
-        @pl.when(step < 5)
-        def _():
-            line.step(done + heads + step)
+        @pl.when(step < 3)
+        def _():
+            line.step(done + heads + 2 + step)
 
         @pl.when(step >= 4)
         def _():
@@ -1830,6 +1837,7 @@
     lax.fori_loop(0, line_counts, finish, 0)
     for step in range(3):
         tile_copy(step).wait()
+    gains[...] = gain_tiles[0] + gain_tiles[1] + gain_tiles[2] + gain_tiles[3]
 
 
 def tail(d_attn, w_out, queries, kv, probs, rms, cos, sin, act_t, w_qkv, ffn, x_low, attn, gain, gain_grad,
@@ -1852,7 +1860,7 @@
         jax.ShapeDtypeStruct((cols, wide), low),
         jax.ShapeDtypeStruct(w_out.shape, low),
         jax.ShapeDtypeStruct((cols, 2 * HD), low),
-        jax.ShapeDtypeStruct((4, 8, LANES), f32),
+        jax.ShapeDtypeStruct((8, LANES), f32),
     ]
     scratch = reduce_scratch(heads // 2, rows, HD, 2) + spread_scratch(1, rows // 2, wide + 2 * HD)
     scratch += [
@@ -1869,6 +1877,7 @@
         pltpu.VMEM((8, LANES), f32),
         dma((3,)), dma((3,)), dma((2, 2, counts)), dma((2, per)),
         pltpu.VMEM((2, rows, wide), low), dma((2,)),
+        pltpu.VMEM((4, 8, LANES), f32),
         pltpu.VMEM((total, cols), low),
         pltpu.VMEM((counts, chunk, cols), low),
     ] + line_scratch(counts, (total, cols), low)
@@ -1887,10 +1896,8 @@
 def acts_move(
     tokens, seg_ids, gain_attn, w_query, kv_weight, w_out, gain_ffn, w_gate, w_up, w_down, d_out
 ):
-    small = jnp.stack([gain_attn, gain_ffn, seg_ids.astype(gain_ffn.dtype), gain_attn]).astype(jnp.float32)
-
-    qkv, x_low, act_one_t, w_qkv, rms, cos, sin, mask, g_parts = opening(
-        tokens, small, w_query, kv_weight, d_out, 1
+    qkv, x_low, act_one_t, w_qkv, rms, cos, sin, mask, g_parts, small = opening(
+        tokens, gain_attn, gain_ffn, seg_ids, w_query, kv_weight, d_out, 1
     )
     g_low = g_parts.reshape(x_low.shape)
     attn, mixed_all, kv, probs, queries, pair_rms, d_hidden = attend(
@@ -1901,7 +1908,7 @@
         act_two_t, w_gate, w_up, d_gate, d_up, dots, x_low, attn, small, 5
     )
     ffn, d_attn, grad_down = down_gather(g_low, w_down, hidden, d_norm, 6)
-    d_tokens, out, grad_query, grad_out, grad_kv, gain_tiles = tail(
+    d_tokens, out, grad_query, grad_out, grad_kv, gain_sums = tail(
         d_attn,
         w_out,
         queries,
@@ -1920,7 +1927,7 @@
         mixed_all,
         7,
     )
-    gains = jnp.sum(gain_tiles, axis=0).reshape(2, -1)
+    gains = gain_sums.reshape(2, -1)
     wider = jnp.float32
     return (
         out,

time: 615 us -> 610 us (level)
  no operation moved by 1% of the time
where the time goes in v18:
time: 610 us; the launch traced here: 609 us
  Pallas kernels  586 us (96%)
  other arithmetic  18.5 us (3%)
    pallas_call x6, Pallas kernels, kernel_call(): pl.pallas_call(body, out_shape=out_shape, in_specs=specs, out_specs=out_s...  586 us

profile of v18, /device:TPU:0, one launch (start us, length us, event | category | flops | bytes accessed | tf_op | source)
XLA Modules:
  0.0 609.3 jit_solution(6295690813953616288)
XLA Ops:
  0.6 66.3 %open_1.1 = (f32[256,1536]{1,0:T(8,128)}, bf16[2048,512]{1,0:T(8,128)(2,1)}, bf16[512,2048]{1,0:T(8,128)(2,1)}, bf16[512,1536]{1,0:T(8,128)(2,1)}, f32[256,128]{...) custom-call(bf16[256,4096]{1,0:T(8,128)(2,1)} %refs_0_.1, ...), custom_call_target="tpu_custom_call" | custom-call | tf_op jit(solution)/shard_map/open_1/pallas_call | solution.py:430
  66.9 87.2 %attend_2.1 = (bf16[2048,512]{1,0:T(8,128)(2,1)}, bf16[2048,1024]{1,0:T(8,128)(2,1)}, bf16[2,256,512]{2,1,0:T(8,128)(2,1)}, f32[4,256,512]{2,1,0:T(8,128)}, bf16...) custom-call(f32[256,1536]{1,0:T(8,128)} %get-tuple-element.47.refs_0_, ...), custom_call_target="tpu_custom_call" | custom-call | tf_op jit(solution)/shard_map/attend_2/pallas_call | solution.py:430
  154.2 116.9 %ffn_4.1 = (bf16[256,3072]{1,0:T(8,128)(2,1)}, bf16[256,3072]{1,0:T(8,128)(2,1)}, bf16[256,3072]{1,0:T(8,128)(2,1)}, bf16[512,2048]{1,0:T(8,128)(2,1)}, f32[8,128]{1,0:T(8,128)}) custom-call(bf16[2048,512]{1,0:T(8,128)(2,1)} %get-tuple-element.46.refs_0_.refs_6_.refs_11_, bf16[2048,512]{1,0:T(8,128)(2,1)} %get-tuple-element.52.refs_1_.refs_7_.refs_12_, ...), custom_call_target="tpu_custom_call" | custom-call | tf_op jit(solution)/shard_map/ffn_4/pallas_call | solution.py:430
  271.0 116.9 %back_5.1 = (bf16[2048,512]{1,0:T(8,128)(2,1)}, f32[1,512]{1,0:T(1,128)}, bf16[512,3072]{1,0:T(8,128)(2,1)}, bf16[512,3072]{1,0:T(8,128)(2,1)}) custom-call(bf16[512,2048]{1,0:T(8,128)(2,1)} %get-tuple-element.56.refs_0_, bf16[512,3072]{1,0:T(8,128)(2,1)} %refs_1_.5, bf16[512,3072]{1,0:T(8,128)(2,1)} %refs_2_.3, ...), custom_call_target="tpu_custom_call" | custom-call | tf_op jit(solution)/shard_map/back_5/pallas_call | solution.py:430
  388.0 65.1 %down_6.1 = (bf16[2048,512]{1,0:T(8,128)(2,1)}, bf16[2048,512]{1,0:T(8,128)(2,1)}, bf16[3072,512]{1,0:T(8,128)(2,1)}) custom-call(bf16[2048,512]{1,0:T(8,128)(2,1)} %bitcast.6, bf16[3072,512]{1,0:T(8,128)(2,1)} %refs_1_.6, bf16[256,3072]{1,0:T(8,128)(2,1)} %get-tuple-element.55.refs_2_, bf16[2048,512]{1,0:T(8,128)(2,1)} %get-tuple-element.60.refs_3_), custom_call_target="tpu_custom_call" | custom-call | tf_op jit(solution)/shard_map/down_6/pallas_call | solution.py:430
  453.1 133.8 %tail_7.1 = (bf16[256,4096]{1,0:T(8,128)(2,1)}, bf16[256,4096]{1,0:T(8,128)(2,1)}, bf16[512,1024]{1,0:T(8,128)(2,1)}, bf16[1024,512]{1,0:T(8,128)(2,1)}, bf16[512,512]{1,0:T(8,128)(2,1)}, /*index=5*/f32[8,128]{1,0:T(8,128)}) custom-call(bf16[2048,512]{1,0:T(8,128)(2,1)} %get-tuple-element.61.refs_0_, bf16[1024,512]{1,0:T(8,128)(2,1)} %refs_1_.7, ...), custom_call_target="tpu_custom_call" | custom-call | tf_op jit(solution)/shard_map/tail_7/pallas_call | solution.py:430
  586.9 0.0 copy-start.6
  586.9 1.4 slice_bitcast_fusion
  588.2 0.0 copy-start.5
  588.2 2.2 convert_element_type.23
  590.5 0.0 copy-done.6
  590.5 1.6 convert_element_type.22
  592.0 0.0 copy-done.5
  592.0 0.0 copy-start.3
  592.0 1.6 convert_element_type.24
  593.6 0.7 copy-done.3
  594.4 0.0 copy-start.2
  594.4 2.5 convert_element_type.21
  596.9 0.5 copy-done.2
  597.4 0.0 copy-start.1
  597.4 3.6 convert_element_type.27
  601.0 0.0 copy-done.1
  601.0 0.0 copy-start
  601.0 3.5 convert_element_type.25
  604.5 0.0 copy-done
  604.5 0.0 copy-start.4
  604.5 3.5 convert_element_type.26
  608.0 0.0 copy-done.4
  608.0 1.3 copy.22
Async XLA Ops:
  586.9 3.6 copy-start.6
  588.2 3.8 copy-start.5
  592.0 2.3 copy-start.3
  594.4 3.0 copy-start.2
  597.4 3.6 copy-start.1
  601.0 3.5 copy-start
  604.5 3.5 copy-start.4

commit v19 on v18

--- a/solution.py
+++ b/solution.py
@@ -1241,7 +1241,7 @@
                        [vm, vm, hbm, hbm], (0,))
 
 
-def down_kernel(rows, width, counts, cot, weight, hidden, d_norm, ffn, d_attn, grad, *refs, late):
+def down_kernel(rows, width, counts, cot, weight, hidden, d_norm, ffn, d_attn, grad, *refs, late, early):
     here = Place()
     spread = Spread(here, counts, refs[:7])
     own_sems, sums, grads, staged, out_sems, norm_out = refs[7:13]
@@ -1297,6 +1297,7 @@
 
     spread.run(blocks, hook, done)
     ffn[...] = sums[...].astype(ffn.dtype)
+    early[0].start()
     norm_line.settle()
 
     def add_norm(at, _):
@@ -1348,7 +1349,7 @@
     ] + line_scratch(12, (12 * rows // 2, cols), low)
     kernel = functools.partial(down_kernel, rows, width, counts)
     return kernel_call(kernel, out_shape, [cot, weight, hidden, d_norm], [vm, vm, hbm, vm], scratch, cid, "down",
-                       [vm, vm, hbm], (0, 1))
+                       [vm, vm, hbm], (0, 1), (0,))
 
 
 def attend_kernel(rows, heads, cols, width, counts, qkv, rms, cos, sin, mask, w_out, g_col, w_down, attn, mixed_all,
@@ -1448,6 +1449,7 @@
 
     lax.fori_loop(0, 20, one_step, 0)
     line.end(16)
+    early[3].start()
 
     def emit(at, first, second):
         for half_at, value in enumerate((first, second)):
@@ -1492,7 +1494,7 @@
     kernel = functools.partial(attend_kernel, rows, heads, cols, width, counts)
     operands = [qkv, rms, cos, sin, mask, w_out, g_col, w_down]
     out_specs = [vm, pl.BlockSpec(memory_space=pl.ANY)] + [vm] * 5
-    return kernel_call(kernel, out_shape, operands, [vm] * 8, scratch, cid, "attend", out_specs, (4, 5, 6, 7), (2, 3, 4))
+    return kernel_call(kernel, out_shape, operands, [vm] * 8, scratch, cid, "attend", out_specs, (4, 5, 6, 7), (2, 3, 4, 0))
 
 
 def tail_kernel(rows, heads, per, d_attn, w_out, queries, kv, probs, rms, cos, sin, act_t, w_qkv, ffn, x_low,
@@ -1821,8 +1823,8 @@
         spread.sib_copy(stage, 0, 0).wait_send()
         spread.sib_copy(stage, 1, 0).wait_send()
 
-    def finish(at, _):
-        for which in range(2):
+    for which in range(2):
+        def finish(at, _, which=which):
             own = is_own(which, at)
 
             @pl.when(own)
@@ -1832,9 +1834,11 @@
             @pl.when(jnp.logical_not(own))
             def _():
                 put(which, at).wait()
-        return 0
-
-    lax.fori_loop(0, line_counts, finish, 0)
+            return 0
+
+        lax.fori_loop(0, line_counts, finish, 0)
+        if which == 0:
+            early[2].start()
     for step in range(3):
         tile_copy(step).wait()
     gains[...] = gain_tiles[0] + gain_tiles[1] + gain_tiles[2] + gain_tiles[3]
@@ -1887,7 +1891,7 @@
     kernel = functools.partial(tail_kernel, rows, heads, per)
     specs = [vm] * (len(operands) - 1) + [pl.BlockSpec(memory_space=pl.ANY)]
     return kernel_call(kernel, out_shape, operands, specs, scratch, cid, "tail",
-                       late=(2, 3, 4, 8, 9, 11, 12), early=(2, 3))
+                       late=(2, 3, 4, 8, 9, 11, 12), early=(2, 3, 1))
 
 
 LANES = 128

time: 610 us -> 609 us (level)
  no operation moved by 1% of the time
where the time goes in v19:
time: 609 us
  Pallas kernels  586 us (96%)
  other arithmetic  18.5 us (3%)
    pallas_call x6, Pallas kernels, kernel_call(): pl.pallas_call(body, out_shape=out_shape, in_specs=specs, out_specs=out_s...  586 us

profile of v19, /device:TPU:0, one launch (start us, length us, event | category | flops | bytes accessed | tf_op | source)
XLA Modules:
  0.0 608.7 jit_solution(591713354105816341)
XLA Ops:
  0.6 66.3 %open_1.1 = (f32[256,1536]{1,0:T(8,128)}, bf16[2048,512]{1,0:T(8,128)(2,1)}, bf16[512,2048]{1,0:T(8,128)(2,1)}, bf16[512,1536]{1,0:T(8,128)(2,1)}, f32[256,128]{...) custom-call(bf16[256,4096]{1,0:T(8,128)(2,1)} %refs_0_.1, ...), custom_call_target="tpu_custom_call" | custom-call | tf_op jit(solution)/shard_map/open_1/pallas_call | solution.py:430
  66.9 86.6 %attend_2.1 = (bf16[2048,512]{1,0:T(8,128)(2,1)}, bf16[2048,1024]{1,0:T(8,128)(2,1)}, bf16[2,256,512]{2,1,0:T(8,128)(2,1)}, f32[4,256,512]{2,1,0:T(8,128)}, bf16...) custom-call(f32[256,1536]{1,0:T(8,128)} %get-tuple-element.47.refs_0_, ...), custom_call_target="tpu_custom_call" | custom-call | tf_op jit(solution)/shard_map/attend_2/pallas_call | solution.py:430
  153.5 116.9 %ffn_4.1 = (bf16[256,3072]{1,0:T(8,128)(2,1)}, bf16[256,3072]{1,0:T(8,128)(2,1)}, bf16[256,3072]{1,0:T(8,128)(2,1)}, bf16[512,2048]{1,0:T(8,128)(2,1)}, f32[8,128]{1,0:T(8,128)}) custom-call(bf16[2048,512]{1,0:T(8,128)(2,1)} %get-tuple-element.46.refs_0_.refs_6_.refs_11_, bf16[2048,512]{1,0:T(8,128)(2,1)} %get-tuple-element.52.refs_1_.refs_7_.refs_12_, ...), custom_call_target="tpu_custom_call" | custom-call | tf_op jit(solution)/shard_map/ffn_4/pallas_call | solution.py:430
  270.4 116.9 %back_5.1 = (bf16[2048,512]{1,0:T(8,128)(2,1)}, f32[1,512]{1,0:T(1,128)}, bf16[512,3072]{1,0:T(8,128)(2,1)}, bf16[512,3072]{1,0:T(8,128)(2,1)}) custom-call(bf16[512,2048]{1,0:T(8,128)(2,1)} %get-tuple-element.56.refs_0_, bf16[512,3072]{1,0:T(8,128)(2,1)} %refs_1_.5, bf16[512,3072]{1,0:T(8,128)(2,1)} %refs_2_.3, ...), custom_call_target="tpu_custom_call" | custom-call | tf_op jit(solution)/shard_map/back_5/pallas_call | solution.py:430
  387.4 64.8 %down_6.1 = (bf16[2048,512]{1,0:T(8,128)(2,1)}, bf16[2048,512]{1,0:T(8,128)(2,1)}, bf16[3072,512]{1,0:T(8,128)(2,1)}) custom-call(bf16[2048,512]{1,0:T(8,128)(2,1)} %bitcast.6, bf16[3072,512]{1,0:T(8,128)(2,1)} %refs_1_.6, bf16[256,3072]{1,0:T(8,128)(2,1)} %get-tuple-element.55.refs_2_, bf16[2048,512]{1,0:T(8,128)(2,1)} %get-tuple-element.60.refs_3_), custom_call_target="tpu_custom_call" | custom-call | tf_op jit(solution)/shard_map/down_6/pallas_call | solution.py:430
  452.1 134.1 %tail_7.1 = (bf16[256,4096]{1,0:T(8,128)(2,1)}, bf16[256,4096]{1,0:T(8,128)(2,1)}, bf16[512,1024]{1,0:T(8,128)(2,1)}, bf16[1024,512]{1,0:T(8,128)(2,1)}, bf16[512,512]{1,0:T(8,128)(2,1)}, /*index=5*/f32[8,128]{1,0:T(8,128)}) custom-call(bf16[2048,512]{1,0:T(8,128)(2,1)} %get-tuple-element.61.refs_0_, bf16[1024,512]{1,0:T(8,128)(2,1)} %refs_1_.7, ...), custom_call_target="tpu_custom_call" | custom-call | tf_op jit(solution)/shard_map/tail_7/pallas_call | solution.py:430
  586.2 0.0 copy-start.6
  586.3 1.4 slice_bitcast_fusion
  587.6 0.0 copy-start.5
  587.6 2.2 convert_element_type.23
  589.8 0.0 copy-done.6
  589.8 1.6 convert_element_type.22
  591.4 0.0 copy-done.5
  591.4 0.0 copy-start.3
  591.4 1.6 convert_element_type.24
  593.0 0.7 copy-done.3
  593.8 0.0 copy-start.2
  593.8 2.5 convert_element_type.21
  596.3 0.5 copy-done.2
  596.7 0.0 copy-start.1
  596.7 3.6 convert_element_type.27
  600.3 0.0 copy-done.1
  600.3 0.0 copy-start
  600.4 3.5 convert_element_type.25
  603.9 0.0 copy-done
  603.9 0.0 copy-start.4
  603.9 3.5 convert_element_type.26
  607.4 0.0 copy-done.4
  607.4 1.3 copy.22
Async XLA Ops:
  586.2 3.6 copy-start.6
  587.6 3.8 copy-start.5
  591.4 2.3 copy-start.3
  593.8 3.0 copy-start.2
  596.7 3.6 copy-start.1
  600.3 3.5 copy-start
  603.9 3.5 copy-start.4

commit v20 on v19

--- a/solution.py
+++ b/solution.py
@@ -395,13 +395,14 @@
     return [here.device(*turned(at)) for at in range(7)]
 
 
-def kernel_call(kernel, out_shape, operands, specs, scratch, cid, name, out_specs=None, late=(), early=()):
+def kernel_call(kernel, out_shape, operands, specs, scratch, cid, name, out_specs=None, late=(), early=(),
+                pieces=()):
     vm = pl.BlockSpec(memory_space=pltpu.VMEM)
     hbm = pl.BlockSpec(memory_space=pl.ANY)
     specs = [hbm if at in late else spec for at, spec in enumerate(specs)]
-    out_specs = [hbm if at in early else spec for at, spec in enumerate(out_specs or [vm] * len(out_shape))]
+    out_specs = [hbm if at in early or at in pieces else spec for at, spec in enumerate(out_specs or [vm] * len(out_shape))]
     inside = [pltpu.VMEM(operands[at].shape, operands[at].dtype) for at in late]
-    inside += [pltpu.VMEM(out_shape[at].shape, out_shape[at].dtype) for at in early]
+    inside += [pltpu.VMEM(out_shape[at].shape, out_shape[at].dtype) for at in (*early, *pieces)]
     inside.append(pltpu.SemaphoreType.DMA((max(1, len(late) + len(early)),)))
     n_in, n_out = len(operands), len(out_shape)
 
@@ -418,7 +419,13 @@
             spot = len(late) + number
             stores.append(pltpu.make_async_copy(own[spot], outs[at], own[-1].at[spot]))
             outs[at] = own[spot]
+        raw = []
+        for number, at in enumerate(pieces):
+            raw.append(outs[at])
+            outs[at] = own[len(late) + len(early) + number]
         more = {}
+        if pieces:
+            more["raw"] = raw
         if late:
             more["late"] = loads
         if early:
@@ -978,7 +985,7 @@
 
 
 def ffn_kernel(rows, width, counts, x_low, attn, gain, w_gate, w_up, d_hidden, hidden, d_gate, d_up, act_t, tile_out,
-               *refs, late, early):
+               *refs, late, early, raw):
     here = Place()
     cols = gain.shape[1]
     act, weight, tiny_own, tiny_all, tiny_send, tiny_recv, dots, local_sems = refs[:8]
@@ -1016,6 +1023,7 @@
         copy.wait()
     product = products(here, act, weight, False, rows, width, counts)
     total = Reduce(here, counts, product, refs[8:19], before)
+    leave_sems = refs[19]
     total.run()
 
     def flip(shard, _):
@@ -1032,6 +1040,11 @@
     dots[...] = jnp.zeros_like(dots)
     late[0].wait()
     coeff = math.sqrt(2.0 / math.pi)
+
+    def leave(which, at):
+        span = pl.ds(pl.multiple_of(at * width, width), width)
+        return pltpu.make_async_copy((hidden, d_gate, d_up)[which].at[:, span], raw[which].at[:, span],
+                                     leave_sems.at[which, at])
 
     def emit(at, first, second):
         span = pl.ds(pl.multiple_of(at * width, width), width)
@@ -1046,9 +1059,14 @@
         d_gate[:, span] = (back_gate * scale).astype(d_gate.dtype)
         d_up[:, span] = (back_up * scale).astype(d_up.dtype)
         dots[...] += jnp.sum(back_gate * gate + back_up * up, axis=-1, keepdims=True)
+        for which in range(3):
+            leave(which, at).start()
 
     total.end(emit)
     tile_out[...] = jnp.zeros_like(tile_out)
+    for at in range(counts):
+        for which in range(3):
+            leave(which, at).wait()
     to_tile(tile_out, 0, dots[...] * (scale * scale * (1.0 / (8 * cols))), eye)
 
 
@@ -1072,10 +1090,11 @@
         dma((7,)), dma((7,)),
         pltpu.VMEM((rows, 1), f32),
         dma((2,)),
-    ] + reduce_scratch(counts, rows, width)
+    ] + reduce_scratch(counts, rows, width) + [dma((3, counts))]
     kernel = functools.partial(ffn_kernel, rows, width, counts)
     return kernel_call(kernel, out_shape, [x_low, attn, gain, w_gate, w_up, d_hidden], [vm, vm, vm, hbm, hbm, vm],
-                       scratch, cid, "ffn", late=(5,), early=(3,))
+                       scratch, cid, "ffn", late=(5,), early=(3,),
+                       pieces=(0, 1, 2))
 
 
 def load_own(spread, payload, width, counts, sems):
@@ -1353,7 +1372,7 @@
 
 
 def attend_kernel(rows, heads, cols, width, counts, qkv, rms, cos, sin, mask, w_out, g_col, w_down, attn, mixed_all,
-                  kv, probs, queries, pair_rms, d_hidden, *refs, late, early):
+                  kv, probs, queries, pair_rms, d_hidden, *refs, late, early, raw):
     here = Place()
     spread = Spread(here, 1, refs[:7])
     part, pair_sems, tiny_own, tiny_pair, mixed_sems = refs[7:12]
@@ -1365,7 +1384,7 @@
         across, other, half_at = spread.block(at)
         return here.shard(across, other) * 2 + half_at
 
-    line = Line(here, 16, [part, attn] + list(refs[23:]), place)
+    line = Line(here, 16, [part, attn] + list(refs[23:31]), place)
     got, core = spread.got, here.core
     greet(here, slice_peers(here), True)
     half = HD // 2
@@ -1451,9 +1470,16 @@
     line.end(16)
     early[3].start()
 
+    leave_sems = refs[31]
+
+    def leave(half_at, at):
+        span = pl.ds(pl.multiple_of((half_at * counts + at) * width, width), width)
+        return pltpu.make_async_copy(d_hidden.at[:, span], raw[0].at[:, span], leave_sems.at[half_at, at])
+
     def emit(at, first, second):
         for half_at, value in enumerate((first, second)):
             d_hidden[:, pl.ds(pl.multiple_of((half_at * counts + at) * width, width), width)] = value
+            leave(half_at, at).start()
 
     total.end(emit)
     for hop in range(3):
@@ -1464,6 +1490,9 @@
             spread.sib_copy(stage, stream, 0).wait_send()
     for at in range(16):
         mixed_copy(at).wait()
+    for at in range(counts):
+        for half_at in range(2):
+            leave(half_at, at).wait()
     tiny.wait()
     for at in range(rows // LANES):
         values = jnp.broadcast_to(from_tile(tiny_pair[at : at + 1, :], eye), (LANES, LANES))
@@ -1490,11 +1519,11 @@
     scratch = spread_scratch(1, rows // 2, wide) + [
         pltpu.VMEM((8 * rows, cols), low), dma((4,)),
         pltpu.VMEM((8, LANES), f32), pltpu.VMEM((8, LANES), f32), dma((16,)),
-    ] + reduce_scratch(counts, rows, width) + line_scratch(16, (8 * rows, cols), low)
+    ] + reduce_scratch(counts, rows, width) + line_scratch(16, (8 * rows, cols), low) + [dma((2, counts))]
     kernel = functools.partial(attend_kernel, rows, heads, cols, width, counts)
     operands = [qkv, rms, cos, sin, mask, w_out, g_col, w_down]
     out_specs = [vm, pl.BlockSpec(memory_space=pl.ANY)] + [vm] * 5
-    return kernel_call(kernel, out_shape, operands, [vm] * 8, scratch, cid, "attend", out_specs, (4, 5, 6, 7), (2, 3, 4, 0))
+    return kernel_call(kernel, out_shape, operands, [vm] * 8, scratch, cid, "attend", out_specs, (4, 5, 6, 7), (2, 3, 4, 0), (6,))
 
 
 def tail_kernel(rows, heads, per, d_attn, w_out, queries, kv, probs, rms, cos, sin, act_t, w_qkv, ffn, x_low,

time: 609 us -> 608 us (level)
  no operation moved by 1% of the time
where the time goes in v20:
time: 608 us
  Pallas kernels  585 us (96%)
  other arithmetic  18.5 us (3%)
    pallas_call x6, Pallas kernels, kernel_call(): pl.pallas_call(body, out_shape=out_shape, in_specs=specs, out_specs=out_s...  585 us

profile of v20, /device:TPU:0, one launch (start us, length us, event | category | flops | bytes accessed | tf_op | source)
XLA Modules:
  0.0 607.8 jit_solution(18215271055442862170)
XLA Ops:
  0.6 66.3 %open_1.1 = (f32[256,1536]{1,0:T(8,128)}, bf16[2048,512]{1,0:T(8,128)(2,1)}, bf16[512,2048]{1,0:T(8,128)(2,1)}, bf16[512,1536]{1,0:T(8,128)(2,1)}, f32[256,128]{...) custom-call(bf16[256,4096]{1,0:T(8,128)(2,1)} %refs_0_.1, ...), custom_call_target="tpu_custom_call" | custom-call | tf_op jit(solution)/shard_map/open_1/pallas_call | solution.py:437
  66.9 86.4 %attend_2.1 = (bf16[2048,512]{1,0:T(8,128)(2,1)}, bf16[2048,1024]{1,0:T(8,128)(2,1)}, bf16[2,256,512]{2,1,0:T(8,128)(2,1)}, f32[4,256,512]{2,1,0:T(8,128)}, bf16...) custom-call(f32[256,1536]{1,0:T(8,128)} %get-tuple-element.47.refs_0_, ...), custom_call_target="tpu_custom_call" | custom-call | tf_op jit(solution)/shard_map/attend_2/pallas_call | solution.py:437
  153.3 116.2 %ffn_4.1 = (bf16[256,3072]{1,0:T(8,128)(2,1)}, bf16[256,3072]{1,0:T(8,128)(2,1)}, bf16[256,3072]{1,0:T(8,128)(2,1)}, bf16[512,2048]{1,0:T(8,128)(2,1)}, f32[8,128]{1,0:T(8,128)}) custom-call(bf16[2048,512]{1,0:T(8,128)(2,1)} %get-tuple-element.46.refs_0_.refs_6_.refs_11_, bf16[2048,512]{1,0:T(8,128)(2,1)} %get-tuple-element.52.refs_1_.refs_7_.refs_12_, ...), custom_call_target="tpu_custom_call" | custom-call | tf_op jit(solution)/shard_map/ffn_4/pallas_call | solution.py:437
  269.5 116.9 %back_5.1 = (bf16[2048,512]{1,0:T(8,128)(2,1)}, f32[1,512]{1,0:T(1,128)}, bf16[512,3072]{1,0:T(8,128)(2,1)}, bf16[512,3072]{1,0:T(8,128)(2,1)}) custom-call(bf16[512,2048]{1,0:T(8,128)(2,1)} %get-tuple-element.56.refs_0_, bf16[512,3072]{1,0:T(8,128)(2,1)} %refs_1_.5, bf16[512,3072]{1,0:T(8,128)(2,1)} %refs_2_.3, ...), custom_call_target="tpu_custom_call" | custom-call | tf_op jit(solution)/shard_map/back_5/pallas_call | solution.py:437
  386.4 64.8 %down_6.1 = (bf16[2048,512]{1,0:T(8,128)(2,1)}, bf16[2048,512]{1,0:T(8,128)(2,1)}, bf16[3072,512]{1,0:T(8,128)(2,1)}) custom-call(bf16[2048,512]{1,0:T(8,128)(2,1)} %bitcast.6, bf16[3072,512]{1,0:T(8,128)(2,1)} %refs_1_.6, bf16[256,3072]{1,0:T(8,128)(2,1)} %get-tuple-element.55.refs_2_, bf16[2048,512]{1,0:T(8,128)(2,1)} %get-tuple-element.60.refs_3_), custom_call_target="tpu_custom_call" | custom-call | tf_op jit(solution)/shard_map/down_6/pallas_call | solution.py:437
  451.2 134.1 %tail_7.1 = (bf16[256,4096]{1,0:T(8,128)(2,1)}, bf16[256,4096]{1,0:T(8,128)(2,1)}, bf16[512,1024]{1,0:T(8,128)(2,1)}, bf16[1024,512]{1,0:T(8,128)(2,1)}, bf16[512,512]{1,0:T(8,128)(2,1)}, /*index=5*/f32[8,128]{1,0:T(8,128)}) custom-call(bf16[2048,512]{1,0:T(8,128)(2,1)} %get-tuple-element.61.refs_0_, bf16[1024,512]{1,0:T(8,128)(2,1)} %refs_1_.7, ...), custom_call_target="tpu_custom_call" | custom-call | tf_op jit(solution)/shard_map/tail_7/pallas_call | solution.py:437
  585.3 0.0 copy-start.6
  585.3 1.4 slice_bitcast_fusion
  586.7 0.0 copy-start.5
  586.7 2.2 convert_element_type.23
  588.9 0.0 copy-done.6
  588.9 1.6 convert_element_type.22
  590.5 0.0 copy-done.5
  590.5 0.0 copy-start.3
  590.5 1.6 convert_element_type.24
  592.1 0.7 copy-done.3
  592.8 0.0 copy-start.2
  592.8 2.5 convert_element_type.21
  595.3 0.5 copy-done.2
  595.8 0.0 copy-start.1
  595.8 3.6 convert_element_type.27
  599.4 0.0 copy-done.1
  599.4 0.0 copy-start
  599.4 3.5 convert_element_type.25
  602.9 0.0 copy-done
  602.9 0.0 copy-start.4
  602.9 3.5 convert_element_type.26
  606.4 0.0 copy-done.4
  606.5 1.3 copy.22
Async XLA Ops:
  585.3 3.6 copy-start.6
  586.7 3.8 copy-start.5
  590.5 2.3 copy-start.3
  592.8 3.0 copy-start.2
  595.8 3.6 copy-start.1
  599.4 3.5 copy-start
  602.9 3.5 copy-start.4

commit v21 on v19

--- a/solution.py
+++ b/solution.py
@@ -1442,13 +1442,13 @@
         def _():
             total.advance(step - 2)
 
-        @pl.when(step >= 4)
-        def _():
-            line.step(step - 4)
+        @pl.when(step >= 2)
+        def _():
+            line.step(step - 2)
         return 0
 
     lax.fori_loop(0, 20, one_step, 0)
-    line.end(16)
+    line.end(18)
     early[3].start()
 
     def emit(at, first, second):

time: 609 us -> 609 us (level)
  no operation moved by 1% of the time
where the time goes in v21:
time: 609 us
  Pallas kernels  586 us (96%)
  other arithmetic  18.5 us (3%)
    pallas_call x6, Pallas kernels, kernel_call(): pl.pallas_call(body, out_shape=out_shape, in_specs=specs, out_specs=out_s...  586 us

profile of v21, /device:TPU:0, one launch (start us, length us, event | category | flops | bytes accessed | tf_op | source)
XLA Modules:
  0.0 608.7 jit_solution(254282827074253346)
XLA Ops:
  0.6 66.3 %open_1.1 = (f32[256,1536]{1,0:T(8,128)}, bf16[2048,512]{1,0:T(8,128)(2,1)}, bf16[512,2048]{1,0:T(8,128)(2,1)}, bf16[512,1536]{1,0:T(8,128)(2,1)}, f32[256,128]{...) custom-call(bf16[256,4096]{1,0:T(8,128)(2,1)} %refs_0_.1, ...), custom_call_target="tpu_custom_call" | custom-call | tf_op jit(solution)/shard_map/open_1/pallas_call | solution.py:430
  66.9 86.6 %attend_2.1 = (bf16[2048,512]{1,0:T(8,128)(2,1)}, bf16[2048,1024]{1,0:T(8,128)(2,1)}, bf16[2,256,512]{2,1,0:T(8,128)(2,1)}, f32[4,256,512]{2,1,0:T(8,128)}, bf16...) custom-call(f32[256,1536]{1,0:T(8,128)} %get-tuple-element.47.refs_0_, ...), custom_call_target="tpu_custom_call" | custom-call | tf_op jit(solution)/shard_map/attend_2/pallas_call | solution.py:430
  153.5 116.9 %ffn_4.1 = (bf16[256,3072]{1,0:T(8,128)(2,1)}, bf16[256,3072]{1,0:T(8,128)(2,1)}, bf16[256,3072]{1,0:T(8,128)(2,1)}, bf16[512,2048]{1,0:T(8,128)(2,1)}, f32[8,128]{1,0:T(8,128)}) custom-call(bf16[2048,512]{1,0:T(8,128)(2,1)} %get-tuple-element.46.refs_0_.refs_6_.refs_11_, bf16[2048,512]{1,0:T(8,128)(2,1)} %get-tuple-element.52.refs_1_.refs_7_.refs_12_, ...), custom_call_target="tpu_custom_call" | custom-call | tf_op jit(solution)/shard_map/ffn_4/pallas_call | solution.py:430
  270.4 116.9 %back_5.1 = (bf16[2048,512]{1,0:T(8,128)(2,1)}, f32[1,512]{1,0:T(1,128)}, bf16[512,3072]{1,0:T(8,128)(2,1)}, bf16[512,3072]{1,0:T(8,128)(2,1)}) custom-call(bf16[512,2048]{1,0:T(8,128)(2,1)} %get-tuple-element.56.refs_0_, bf16[512,3072]{1,0:T(8,128)(2,1)} %refs_1_.5, bf16[512,3072]{1,0:T(8,128)(2,1)} %refs_2_.3, ...), custom_call_target="tpu_custom_call" | custom-call | tf_op jit(solution)/shard_map/back_5/pallas_call | solution.py:430
  387.4 64.8 %down_6.1 = (bf16[2048,512]{1,0:T(8,128)(2,1)}, bf16[2048,512]{1,0:T(8,128)(2,1)}, bf16[3072,512]{1,0:T(8,128)(2,1)}) custom-call(bf16[2048,512]{1,0:T(8,128)(2,1)} %bitcast.6, bf16[3072,512]{1,0:T(8,128)(2,1)} %refs_1_.6, bf16[256,3072]{1,0:T(8,128)(2,1)} %get-tuple-element.55.refs_2_, bf16[2048,512]{1,0:T(8,128)(2,1)} %get-tuple-element.60.refs_3_), custom_call_target="tpu_custom_call" | custom-call | tf_op jit(solution)/shard_map/down_6/pallas_call | solution.py:430
  452.1 134.1 %tail_7.1 = (bf16[256,4096]{1,0:T(8,128)(2,1)}, bf16[256,4096]{1,0:T(8,128)(2,1)}, bf16[512,1024]{1,0:T(8,128)(2,1)}, bf16[1024,512]{1,0:T(8,128)(2,1)}, bf16[512,512]{1,0:T(8,128)(2,1)}, /*index=5*/f32[8,128]{1,0:T(8,128)}) custom-call(bf16[2048,512]{1,0:T(8,128)(2,1)} %get-tuple-element.61.refs_0_, bf16[1024,512]{1,0:T(8,128)(2,1)} %refs_1_.7, ...), custom_call_target="tpu_custom_call" | custom-call | tf_op jit(solution)/shard_map/tail_7/pallas_call | solution.py:430
  586.2 0.0 copy-start.6
  586.3 1.4 slice_bitcast_fusion
  587.6 0.0 copy-start.5
  587.6 2.2 convert_element_type.23
  589.8 0.0 copy-done.6
  589.8 1.6 convert_element_type.22
  591.4 0.0 copy-done.5
  591.4 0.0 copy-start.3
  591.4 1.6 convert_element_type.24
  593.0 0.7 copy-done.3
  593.8 0.0 copy-start.2
  593.8 2.5 convert_element_type.21
  596.3 0.5 copy-done.2
  596.7 0.0 copy-start.1
  596.7 3.6 convert_element_type.27
  600.3 0.0 copy-done.1
  600.3 0.0 copy-start
  600.4 3.5 convert_element_type.25
  603.9 0.0 copy-done
  603.9 0.0 copy-start.4
  603.9 3.5 convert_element_type.26
  607.4 0.0 copy-done.4
  607.4 1.3 copy.22
Async XLA Ops:
  586.2 3.6 copy-start.6
  587.6 3.8 copy-start.5
  591.4 2.3 copy-start.3
  593.8 3.0 copy-start.2
  596.7 3.6 copy-start.1
  600.3 3.5 copy-start
  603.9 3.5 copy-start.4
